TPU v7x, 256 devices: a whole 4x4x8 slice. The times are simulated.
256 devices in a mesh: blk: 128 (over z, x, y_lo, core), rep: 2 (over y_hi).
Axes of the slice: x: 4, y: 4 (y_hi: 2, y_lo: 2; y = y_hi * 2 + y_lo), z: 8, core: 2. Of those that a mesh axis runs over, the one named last changes fastest.
Arguments:
- particles: bfloat16 [7168, 2048], P(('blk', 'rep')), may hold values from -0.0029907227 to 0.0029907227
- scores: bfloat16 [7168, 2048], P(('blk', 'rep')), may hold values from -60 to 60, as said below
- spread: float32 [1], replicated, may hold values from 0.00034816 to 0.00069632
Outputs:
- direction: float32 [7168, 2048], P(('blk', 'rep'))
Inputs may be any that keep to these rules, and one draw needn't show every extreme that they name: `scores`: scores of the particles' log posterior.
All inputs are finite; a program needn't handle non-finite values.
Results may differ from a plain program's by a relative error of at most 0.0003.
Values may be sent and summed in bfloat16 or wider, within the bound.
No kernel may reach another device: no remote copies, remote signals or barrier semaphores. Data moves between devices by JAX's collectives and lax.ppermute only.
A program may use at most 128 MiB of HBM per device.

v0:
```python
import jax
import jax.numpy as jnp
from jax import lax
from jax.sharding import PartitionSpec as P


def sent_to_all(value, axis):
    count = lax.axis_size(axis)
    return lax.all_to_all(
        jnp.broadcast_to(value[None], (count, *value.shape)), axis, 0, 0, tiled=True
    )


def joined_along(blocks, dim):
    dims = list(blocks.shape[1:])
    dims[dim] *= blocks.shape[0]
    return jnp.moveaxis(blocks, 0, dim).reshape(dims)


def gather_directly(value, axis, dim):
    blocks = sent_to_all(value, axis)
    return joined_along(blocks, dim)


def in_blocks(value, dim, count):
    before, after = (value.shape[:dim], value.shape[dim + 1 :])
    return jnp.moveaxis(value.reshape(*before, count, -1, *after), dim, 0)


def summed_on_arrival(value, axis, dim):
    blocks = in_blocks(value, dim, lax.axis_size(axis))
    arrived = lax.all_to_all(blocks, axis, split_axis=0, concat_axis=0, tiled=True)
    return arrived.sum(axis=0)


def kernel_weights(targets, target_norm, source_x, inverse):
    cross_dots = lax.dot_general(
        targets, source_x, (((1,), (1,)), ((), ())), preferred_element_type=jnp.float32
    )
    source_wide = source_x.astype(jnp.float32)
    source_norm = jnp.sum(source_wide * source_wide, axis=1)
    squared = jnp.maximum(target_norm[:, None] + source_norm[None, :] - 2.0 * cross_dots, 0.0)
    return jnp.exp(-squared * inverse)


def shards(particles, scores, spread):
    inverse = 1.0 / spread[0]
    own_count = particles.shape[0]
    population = own_count * lax.axis_size("blk") * lax.axis_size("rep")
    targets = gather_directly(particles, "rep", 0)
    target_wide = targets.astype(jnp.float32)
    target_norm = jnp.sum(target_wide * target_wide, axis=1)
    stacked = jnp.stack([scores, particles], axis=0)
    source = lax.all_gather(stacked, "blk", axis=1, tiled=True)
    weights = kernel_weights(targets, target_norm, source[1], inverse)
    weights_low = weights.astype(jnp.bfloat16)
    combined_step = jnp.einsum(
        "ij,cjd->cid", weights_low, source, preferred_element_type=jnp.float32
    )
    row_total = jnp.sum(weights, axis=1)
    drive_sum = combined_step[0]
    pull_sum = combined_step[1]
    partial_value = (
        drive_sum + 2.0 * inverse * (target_wide * row_total[:, None] - pull_sum)
    ) / population
    return summed_on_arrival(partial_value, "rep", 0)


def solution(mesh):
    return jax.shard_map(
        shards,
        mesh=mesh,
        in_specs=(P(("blk", "rep"), None), P(("blk", "rep"), None), P()),
        out_specs=P(("blk", "rep"), None),
        check_vma=False,
    )
```

profile of v0, /device:TPU:32, one launch (start us, length us, event | category | flops | bytes accessed | tf_op | source)
XLA Modules:
  0.0 333.5 jit_solution(15019230798505263982)
XLA Ops:
  6.5 0.0 all-gather.2.cloned.1.call-start
  6.5 1.0 pad_maximum_fusion
  7.5 0.9 copy.5
  8.5 0.0 all-gather.2.cloned.1.call-update
  8.5 1.6 broadcast_in_dim.2
  10.1 4.5 %all-to-all-start = ((bf16[2,28,2048]{2,1,0:T(8,128)(2,1)}), bf16[2,28,2048]{2,1,0:T(8,128)(2,1)S(1)}, u32[]{:S(2)}, u32[]{:S(2)}) async-start(bf16[2,28,2048]{2,1,0:T(8,128)(2,1)} %broadcast_in_dim.2), calls=%async_computation | async-start | bytes 524288 | tf_op jit(solution)/shard_map/all_to_all | solution.py:9
  15.3 6.0 %all-to-all-done = bf16[2,28,2048]{2,1,0:T(8,128)(2,1)S(1)} async-done(((bf16[2,28,2048]{2,1,0:T(8,128)(2,1)}), bf16[2,28,2048]{2,1,0:T(8,128)(2,1)S(1)}, u32[]{:S(2)}, u32[]{:S(2)}) %all-to-all-start) | async-done | bytes 229408 | tf_op jit(solution)/shard_map/all_to_all | solution.py:9
  21.3 0.1 fusion.8
  21.4 0.1 add.19
  21.5 0.1 reshape.19
  21.5 235.9 %all-gather.2.cloned.1.call-done = bf16[2,3584,2048]{2,0,1:T(2,128)(2,1)} async-done(((bf16[2,28,2048]{2,0,1:T(2,128)(2,1)}), bf16[2,3584,2048]{2,0,1:T(2,128)(2,1)}) %all-gather.2.cloned.1.call-update) | async-done | bytes 29360144 | tf_op jit(solution)/shard_map/all_gather | solution.py:54
  257.4 20.5 %copy.7 = bf16[2,3584,2048]{2,1,0:T(8,128)(2,1)} copy(bf16[2,3584,2048]{2,0,1:T(2,128)(2,1)} %all-gather.2.cloned.1.call-done) | data formatting | bytes 58720256 | tf_op jit(solution)/shard_map/all_gather | solution.py:54
  277.9 8.1 %multiply_reduce_fusion = f32[3584]{0:T(1024)S(1)} fusion(bf16[2,3584,2048]{2,1,0:T(8,128)(2,1)} %copy.7), kind=kLoop, calls=%fused_computation | loop fusion | flops 22016512 | bytes 14694400 | tf_op jit(solution)/shard_map/reduce_sum | solution.py:41
  286.0 8.2 %fusion.17 = (f32[56]{0:T(128)S(1)}, bf16[56,3584]{1,0:T(8,128)(2,1)S(1)}) fusion(f32[]{:T(128)} %bitcast.4, bf16[56,2048]{1,0:T(8,128)(2,1)S(1)} %reshape.19, bf16[2,3584,2048]{2,1,0:T(8,128)(2,1)} %copy.7, f32[3584]{0:T(1024)S(1)} %multiply_reduce_fusion, f32[56]{0:T(128)S(1)} %add.19), kind=kOutput, calls=%fused_computation.23 | convolution fusion | flops 823689152 | bytes 15326144 | tf_op jit(solution)/shard_map/dot_general | solution.py:37
  294.2 18.1 %convolution_bitcast_fusion = f32[2,56,2048]{2,1,0:T(8,128)S(1)} fusion(bf16[56,3584]{1,0:T(8,128)(2,1)S(1)} %get-tuple-element.8, bf16[2,3584,2048]{2,0,1:T(2,128)(2,1)} %all-gather.2.cloned.1.call-done), kind=kOutput, calls=%fused_computation.10 | convolution fusion | flops 1644167168 | bytes 30679040 | tf_op jit(solution)/shard_map/ij,cjd->cid/dot_general | solution.py:57
  312.4 0.1 fusion.16
  312.5 0.1 mul.52
  312.6 0.2 fusion.12
  312.8 13.1 %all_to_all.10 = f32[2,28,2048]{2,1,0:T(8,128)S(1)} all-to-all(f32[2,28,2048]{2,1,0:T(8,128)S(1)} %fusion.12), channel_id=1, replica_groups=mesh['blk'=128,'rep'=2] {'rep'}, dimensions={0} | all-to-all | bytes 917504 | tf_op jit(solution)/shard_map/all_to_all | solution.py:32
  325.9 0.7 reduce_sum.39
  (2 shorter events, 0.1 us)
Async XLA Ops:
  6.5 250.9 %all-gather.2.cloned.1.call-start = ((), (), s32[]{:S(2)}) async-start(), calls=%async_computation.2 | async-start | bytes 29589504 | tf_op jit(solution)/shard_map/all_gather | solution.py:54
  10.1 11.1 %all-to-all-start = ((bf16[2,28,2048]{2,1,0:T(8,128)(2,1)}), bf16[2,28,2048]{2,1,0:T(8,128)(2,1)S(1)}, u32[]{:S(2)}, u32[]{:S(2)}) async-start(bf16[2,28,2048]{2,1,0:T(8,128)(2,1)} %broadcast_in_dim.2), calls=%async_computation | async-start | bytes 524288 | tf_op jit(solution)/shard_map/all_to_all | solution.py:9
Sparse Core Ops, SparseCore 0:
  9.2 248.1 all-gather.1
where the time goes:
time: 334 us
  waiting for transfers between devices  242 us (72%)
  matrix products  26.3 us (8%)
  local copies, waits for them, and re-layouts  23.5 us (7%)
  between operations  14.1 us (4%)
  blocking collectives  13.1 us (4%)
  other arithmetic  10.1 us (3%)
  starting transfers between devices  4.46 us (1%)
    all_gather x1, waiting for transfers between devices, shards(): source = lax.all_gather(stacked, 'blk', axis=1, tiled=True)  236 us
    all_gather x1, local copies, waits for them, and re-layouts, shards(): source = lax.all_gather(stacked, 'blk', axis=1, tiled=True)  20.5 us
    dot_general x1, matrix products, shards(): jnp.einsum('ij,cjd->cid', weights_low, source, preferred_element_type=jnp...  18.1 us
    all_to_all x1, blocking collectives, summed_on_arrival(): lax.all_to_all(blocks, axis, split_axis=0, concat_axis=0, tiled=True)  13.1 us
    dot_general x1, matrix products, kernel_weights(): lax.dot_general(targets, source_x, (((1,), (1,)), ((), ())), preferred_el...  8.21 us
    reduce_sum x1, other arithmetic, kernel_weights(): source_norm = jnp.sum(source_wide * source_wide, axis=1)  8.09 us
  transfers between devices with their start and end apart: 2, of which 2 were waited for; matrix products, arithmetic and copies ran while one was open for 1% of the time, Pallas kernels for 0%

commit v1 on v0

v1 whole, which is shorter than its diff:
```python
import jax
import jax.numpy as jnp
from jax import lax
from jax.experimental import pallas as pl
from jax.experimental.pallas import tpu as pltpu
from jax.sharding import Mesh, PartitionSpec as P

PLANE = ("x", "yh", "yl")
AXES = ("z", "x", "yl", "c", "yh")
POPULATION = 7168
ROWS = 28
PAD = 32
DIM = 2048


def sent_to_all(value, axis):
    count = lax.axis_size(axis)
    return lax.all_to_all(
        jnp.broadcast_to(value[None], (count, *value.shape)), axis, 0, 0, tiled=True
    )


def padded(ref, index):
    rows = ref[index]
    fill = jnp.zeros((PAD - ROWS, rows.shape[1]), rows.dtype)
    return jnp.concatenate([rows, fill], axis=0)


def weights_kernel(spread_ref, t_ref, own_ref, other_ref, k_ref, q_ref, t_all, x_all):
    inverse = 1.0 / spread_ref[0]
    for i in range(8):
        t_all[pl.ds(i * PAD, PAD), :] = padded(t_ref, i)
    for i in range(16):
        x_all[pl.ds(i * PAD, PAD), :] = padded(own_ref, i)
        x_all[pl.ds((16 + i) * PAD, PAD), :] = padded(other_ref, i)
    targets = t_all[...]
    source = x_all[...]
    target_wide = targets.astype(jnp.float32)
    source_wide = source.astype(jnp.float32)
    target_norm = jnp.sum(target_wide * target_wide, axis=1, keepdims=True)
    source_norm = jnp.sum(source_wide * source_wide, axis=1, keepdims=True)
    source_norm = jnp.transpose(jnp.broadcast_to(source_norm, (source_norm.shape[0], 128)))[:1]
    dots = lax.dot_general(
        targets, source, (((1,), (1,)), ((), ())), preferred_element_type=jnp.float32
    )
    squared = jnp.maximum(target_norm + source_norm - 2.0 * dots, 0.0)
    weights = jnp.exp(-squared * inverse)
    column = lax.broadcasted_iota(jnp.int32, weights.shape, 1)
    weights = jnp.where(column % PAD < ROWS, weights, 0.0)
    low = weights.astype(jnp.bfloat16)
    k_ref[...] = low
    row_total = jnp.sum(weights, axis=1, keepdims=True)
    pull = jnp.dot(low, source, preferred_element_type=jnp.float32)
    q_ref[...] = (2.0 * inverse) * (target_wide * row_total - pull)


def kernel_weights(spread, targets, own, other):
    return pl.pallas_call(
        weights_kernel,
        in_specs=[
            pl.BlockSpec(memory_space=pltpu.SMEM),
            pl.BlockSpec(memory_space=pltpu.VMEM),
            pl.BlockSpec(memory_space=pltpu.VMEM),
            pl.BlockSpec(memory_space=pltpu.VMEM),
        ],
        out_specs=[
            pl.BlockSpec(memory_space=pltpu.VMEM),
            pl.BlockSpec(memory_space=pltpu.VMEM),
        ],
        out_shape=[
            jax.ShapeDtypeStruct((8 * PAD, 32 * PAD), jnp.bfloat16),
            jax.ShapeDtypeStruct((8 * PAD, DIM), jnp.float32),
        ],
        scratch_shapes=[
            pltpu.VMEM((8 * PAD, DIM), jnp.bfloat16),
            pltpu.VMEM((32 * PAD, DIM), jnp.bfloat16),
        ],
    )(spread, targets, own, other)


def drive_kernel(k_ref, q_ref, own_ref, other_ref, out_ref, s_all):
    for i in range(16):
        s_all[pl.ds(i * PAD, PAD), :] = padded(own_ref, i)
        s_all[pl.ds((16 + i) * PAD, PAD), :] = padded(other_ref, i)
    drive = jnp.dot(k_ref[...], s_all[...], preferred_element_type=jnp.float32)
    total = (drive + q_ref[...]) / POPULATION
    for i in range(8):
        out_ref[pl.ds(i * ROWS, ROWS), :] = total[i * PAD : i * PAD + ROWS]


def partial_direction(weights, rest, own, other):
    width = 512
    return pl.pallas_call(
        drive_kernel,
        grid=(DIM // width,),
        in_specs=[
            pl.BlockSpec((8 * PAD, 32 * PAD), lambda i: (0, 0)),
            pl.BlockSpec((8 * PAD, width), lambda i: (0, i)),
            pl.BlockSpec((16, ROWS, width), lambda i: (0, 0, i)),
            pl.BlockSpec((16, ROWS, width), lambda i: (0, 0, i)),
        ],
        out_specs=pl.BlockSpec((8 * ROWS, width), lambda i: (0, i)),
        out_shape=jax.ShapeDtypeStruct((8 * ROWS, DIM), jnp.float32),
        scratch_shapes=[pltpu.VMEM((32 * PAD, width), jnp.bfloat16)],
    )(weights, rest, own, other)


def shards(particles, scores, spread):
    swap = [(0, 1), (1, 0)]
    targets = sent_to_all(particles, "z")
    own_x = sent_to_all(particles, PLANE)
    own_s = sent_to_all(scores, PLANE)
    other_x = lax.ppermute(own_x, "c", swap)
    weights, rest = kernel_weights(spread, targets, own_x, other_x)
    other_s = lax.ppermute(own_s, "c", swap)
    partial = partial_direction(weights, rest, own_s, other_s)
    return lax.psum_scatter(partial, "z", scatter_dimension=0, tiled=True)


def solution(mesh):
    fine = Mesh(mesh.devices.reshape(8, 4, 2, 2, 2), AXES)
    return jax.shard_map(
        shards,
        mesh=fine,
        in_specs=(P(AXES, None), P(AXES, None), P()),
        out_specs=P(AXES, None),
        check_vma=False,
    )
```

time: 334 us -> 163 us (0.49)
  waiting for transfers between devices: 242 us -> 48.8 us
  blocking collectives: 13.1 us -> 63.8 us
  matrix products: 26.3 us -> 0 us
  Pallas kernels: 0 us -> 12.9 us
  between operations: 14.1 us -> 1.39 us
  starting transfers between devices: 4.46 us -> 15.1 us
  other arithmetic: 10.1 us -> 0 us
    all_gather x1 -> x0, waiting for transfers between devices: 236 us -> none  [shards(): source = lax.all_gather(stacked, 'blk', axis=1, tiled=True)]
    all_to_all x1 -> x2, waiting for transfers between devices: 5.99 us -> 44.3 us  [sent_to_all(): lax.all_to_all(jnp.broadcast_to(value[None], (count, *value.shape)), axis...]
    unnamed x0 -> x1, blocking collectives: none -> 28.4 us
    dot_general x2 -> x0, matrix products: 26.3 us -> none  [the longest x1 18.1 us: shards(): jnp.einsum('ij,cjd->cid', weights_low, source, preferred_element_type=jnp...]
    all_to_all x1, blocking collectives: 13.1 us -> 35.3 us  [sent_to_all(): lax.all_to_all(jnp.broadcast_to(value[None], (count, *value.shape)), axis...]
    all_gather x1 -> x0, local copies, waits for them, and re-layouts: 20.5 us -> none  [shards(): source = lax.all_gather(stacked, 'blk', axis=1, tiled=True)]
    pallas_call x0 -> x2, Pallas kernels: none -> 12.9 us  [the longest x1 7.16 us: kernel_weights(): pl.pallas_call(weights_kernel, in_specs=[pl.BlockSpec(memory_space=pltpu....]
    reduce_sum x3 -> x0, other arithmetic: 8.96 us -> none  [the longest x1 8.09 us: kernel_weights(): source_norm = jnp.sum(source_wide * source_wide, axis=1)]
  transfers between devices with their start and end apart: 2 -> 5, of which waited for: 2 -> 3; matrix products, arithmetic and copies ran while one was open for 1% -> 10% of each run, Pallas kernels for 0% -> 0%
where the time goes in v1:
time: 163 us; the launch traced here: 162 us
  blocking collectives  63.8 us (39%)
  waiting for transfers between devices  48.8 us (30%)
  local copies, waits for them, and re-layouts  20.3 us (12%)
  starting transfers between devices  15.1 us (9%)
  Pallas kernels  12.9 us (8%)
    all_to_all x2, waiting for transfers between devices, sent_to_all(): lax.all_to_all(jnp.broadcast_to(value[None], (count, *value.shape)), axis...  44.3 us
    all_to_all x1, blocking collectives, sent_to_all(): lax.all_to_all(jnp.broadcast_to(value[None], (count, *value.shape)), axis...  35.3 us
    unnamed x1, blocking collectives  28.4 us
    all_to_all x2, starting transfers between devices, sent_to_all(): lax.all_to_all(jnp.broadcast_to(value[None], (count, *value.shape)), axis...  12.4 us
    pallas_call x1, Pallas kernels, kernel_weights(): pl.pallas_call(weights_kernel, in_specs=[pl.BlockSpec(memory_space=pltpu....  7.16 us
    all_to_all x2, local copies, waits for them, and re-layouts, sent_to_all(): lax.all_to_all(jnp.broadcast_to(value[None], (count, *value.shape)), axis...  6.08 us
    pallas_call x1, Pallas kernels, partial_direction(): pl.pallas_call(drive_kernel, grid=(DIM // width,), in_specs=[pl.BlockSpec...  5.71 us
    unnamed x1, waiting for transfers between devices  4.52 us
  transfers between devices with their start and end apart: 5, of which 3 were waited for; matrix products, arithmetic and copies ran while one was open for 10% of the time, Pallas kernels for 0%

profile of v1, /device:TPU:32, one launch (start us, length us, event | category | flops | bytes accessed | tf_op | source)
XLA Modules:
  0.0 162.2 jit_solution(14425190275788225426)
XLA Ops:
  0.0 1.1 broadcast_in_dim.7
  1.2 0.0 copy-start.3
  1.2 35.3 %all_to_all.15.own_ref = bf16[16,28,2048]{2,1,0:T(8,128)(2,1)} all-to-all(bf16[16,28,2048]{2,1,0:T(8,128)(2,1)S(1)} %broadcast_in_dim.7), channel_id=1, replica_groups=mesh['z'=8,'x'=4,'yl'=2,'c'=2,'yh'=2] {'x','yh','yl'}, dimensions={0} | all-to-all | bytes 3670016 | tf_op jit(solution)/shard_map/all_to_all | solution.py:18
  36.5 0.0 copy-done.3
  36.5 1.6 broadcast_in_dim.8
  38.1 3.9 %all-to-all-start.2 = ((bf16[16,28,2048]{2,1,0:T(8,128)(2,1)}), bf16[16,28,2048]{2,1,0:T(8,128)(2,1)S(1)}, u32[]{:S(2)}, u32[]{:S(2)}) async-start(bf16[16,28,2048]{2,1,0:T(8,128)(2,1)} %broadcast_in_dim.8), calls=%async_computation.2 | async-start | bytes 4194304 | tf_op jit(solution)/shard_map/all_to_all | solution.py:18
  41.9 3.8 %copy.4 = bf16[16,28,2048]{2,0,1:T(8,128)(2,1)} copy(bf16[16,28,2048]{2,1,0:T(8,128)(2,1)} %all_to_all.15.own_ref) | data formatting | bytes 3670016 | tf_op jit(solution)/shard_map/all_to_all | solution.py:18
  45.8 0.0 copy-start.2
  45.8 0.0 collective-permute-start
  45.8 24.8 %all-to-all-done.2.own_ref = bf16[16,28,2048]{2,1,0:T(8,128)(2,1)S(1)} async-done(((bf16[16,28,2048]{2,1,0:T(8,128)(2,1)}), bf16[16,28,2048]{2,1,0:T(8,128)(2,1)S(1)}, u32[]{:S(2)}, u32[]{:S(2)}) %all-to-all-start.2) | async-done | bytes 1835040 | tf_op jit(solution)/shard_map/all_to_all | solution.py:18
  70.5 0.0 copy-start
  70.5 2.2 %copy.6 = bf16[16,28,2048]{2,0,1:T(8,128)(2,1)} copy(bf16[16,28,2048]{2,1,0:T(8,128)(2,1)S(1)} %all-to-all-done.2.own_ref) | data formatting | bytes 3670016 | tf_op jit(solution)/shard_map/all_to_all | solution.py:18
  72.8 0.0 collective-permute-start.1
  72.8 0.0 copy-done.2
  72.8 1.1 broadcast_in_dim.6
  73.9 0.0 copy-done
  73.9 8.6 %all-to-all-start = ((bf16[8,28,2048]{2,1,0:T(8,128)(2,1)}), bf16[8,28,2048]{2,1,0:T(8,128)(2,1)S(1)}, u32[]{:S(2)}, u32[]{:S(2)}) async-start(bf16[8,28,2048]{2,1,0:T(8,128)(2,1)} %broadcast_in_dim.6), calls=%async_computation | async-start | bytes 2097152 | tf_op jit(solution)/shard_map/all_to_all | solution.py:18
  83.1 0.0 collective-permute-done
  83.2 3.9 %copy.5.other_ref = bf16[16,28,2048]{2,1,0:T(8,128)(2,1)} copy(bf16[16,28,2048]{2,0,1:T(8,128)(2,1)} %collective-permute-done) | data formatting | bytes 3670016 | tf_op jit(solution)/shard_map/ppermute | solution.py:113
  87.0 0.0 collective-permute-done.1
  87.0 3.9 %copy.7.other_ref = bf16[16,28,2048]{2,1,0:T(8,128)(2,1)} copy(bf16[16,28,2048]{2,0,1:T(8,128)(2,1)} %collective-permute-done.1) | data formatting | bytes 3670016 | tf_op jit(solution)/shard_map/ppermute | solution.py:115
  90.9 19.6 %all-to-all-done.t_ref = bf16[8,28,2048]{2,1,0:T(8,128)(2,1)S(1)} async-done(((bf16[8,28,2048]{2,1,0:T(8,128)(2,1)}), bf16[8,28,2048]{2,1,0:T(8,128)(2,1)S(1)}, u32[]{:S(2)}, u32[]{:S(2)}) %all-to-all-start) | async-done | bytes 917536 | tf_op jit(solution)/shard_map/all_to_all | solution.py:18
  110.4 1.0 copy-done.1
  111.4 7.2 %shard_map.37 = (bf16[256,1024]{1,0:T(8,128)(2,1)}, f32[256,2048]{1,0:T(8,128)}) custom-call(f32[1]{0:T(128)S(6)} %copy.8.spread_ref, bf16[8,28,2048]{2,1,0:T(8,128)(2,1)} %copy-done.1, bf16[16,28,2048]{2,1,0:T(8,128)(2,1)} %all_to_all.15.own_ref, bf16[16,28,2048]{2,1,0:T(8,128)(2,1)} %copy.5.other_ref), custom_call_target="tpu_custom_call" | custom-call | tf_op jit(solution)/shard_map/pallas_call | solution.py:58
  118.6 5.7 %shard_map.38 = f32[224,2048]{1,0:T(8,128)} custom-call(bf16[256,1024]{1,0:T(8,128)(2,1)} %get-tuple-element.7.k_ref, f32[256,2048]{1,0:T(8,128)} %get-tuple-element.8.q_ref, bf16[16,28,2048]{2,1,0:T(8,128)(2,1)} %copy-done, bf16[16,28,2048]{2,1,0:T(8,128)(2,1)} %copy.7.other_ref), custom_call_target="tpu_custom_call" | custom-call | tf_op jit(solution)/shard_map/pallas_call | solution.py:93
  124.3 28.4 %fusion = f32[32,2048]{1,0:T(8,128)S(1)} fusion(f32[224,2048]{1,0:T(8,128)} %shard_map.38), kind=kCustom, calls=%all-reduce-scatter | all-reduce-scatter fusion | flops 524289 | bytes 2098176
  152.8 2.7 %collective-permute-start.2 = (f32[28,2048]{1,0:T(8,128)S(1)}, f32[28,2048]{1,0:T(8,128)S(1)}, u32[]{:S(2)}, u32[]{:S(2)}) collective-permute-start(f32[28,2048]{1,0:T(8,128)S(1)} %slice), channel_id=1, source_target_pairs={{0,32},{32,64},{64,96},{96,128},{128,160},{160,192},{192,224},{1,3... | collective-permute-start | bytes 688136
  155.5 0.0 copy-done.4
  155.5 0.6 dynamic-slice.4
  156.7 4.5 %collective-permute-done.2 = f32[28,2048]{1,0:T(8,128)S(1)} collective-permute-done((f32[28,2048]{1,0:T(8,128)S(1)}, f32[28,2048]{1,0:T(8,128)S(1)}, u32[]{:S(2)}, u32[]{:S(2)}) %collective-permute-start.2) | collective-permute-done | bytes 229408
  161.2 0.2 concatenate
  161.5 0.7 constant_dynamic-slice_fusion
  (3 shorter events, 0.0 us)
Async XLA Ops:
  1.2 35.3 %copy-start.3 = (bf16[28,2048]{1,0:T(8,128)(2,1)S(1)}, bf16[28,2048]{1,0:T(8,128)(2,1)}, u32[]{:S(2)}) copy-start(bf16[28,2048]{1,0:T(8,128)(2,1)} %param.4) | copy-start | bytes 344068
  38.1 32.5 %all-to-all-start.2 = ((bf16[16,28,2048]{2,1,0:T(8,128)(2,1)}), bf16[16,28,2048]{2,1,0:T(8,128)(2,1)S(1)}, u32[]{:S(2)}, u32[]{:S(2)}) async-start(bf16[16,28,2048]{2,1,0:T(8,128)(2,1)} %broadcast_in_dim.8), calls=%async_computation.2 | async-start | bytes 4194304 | tf_op jit(solution)/shard_map/all_to_all | solution.py:18
  45.8 27.0 %copy-start.2 = (bf16[28,2048]{1,0:T(8,128)(2,1)S(1)}, bf16[28,2048]{1,0:T(8,128)(2,1)}, u32[]{:S(2)}) copy-start(bf16[28,2048]{1,0:T(8,128)(2,1)} %param.3) | copy-start | bytes 344068
  45.8 37.4 %collective-permute-start = (bf16[16,28,2048]{2,0,1:T(8,128)(2,1)}, bf16[16,28,2048]{2,0,1:T(8,128)(2,1)}, u32[]{:S(2)}, u32[]{:S(2)}) collective-permute-start(bf16[16,28,2048]{2,0,1:T(8,128)(2,1)} %copy.4), channel_id=1, source_target_pairs={{0,2},{2,0},{1,3},{3,1},{4,6},{6,4},{5,7},{7,5},{8,10},{10,8},{9,1... | collective-permute-start | bytes 5505032 | tf_op jit(solution)/shard_map/ppermute | solution.py:113
  70.5 3.4 %copy-start = (bf16[16,28,2048]{2,1,0:T(8,128)(2,1)}, bf16[16,28,2048]{2,1,0:T(8,128)(2,1)S(1)}, u32[]{:S(2)}) copy-start(bf16[16,28,2048]{2,1,0:T(8,128)(2,1)S(1)} %all-to-all-done.2.own_ref) | copy-start | bytes 5505028
  72.8 14.2 %collective-permute-start.1 = (bf16[16,28,2048]{2,0,1:T(8,128)(2,1)}, bf16[16,28,2048]{2,0,1:T(8,128)(2,1)}, u32[]{:S(2)}, u32[]{:S(2)}) collective-permute-start(bf16[16,28,2048]{2,0,1:T(8,128)(2,1)} %copy.6), channel_id=1, source_target_pairs={{0,2},{2,0},{1,3},{3,1},{4,6},{6,4},{5,7},{7,5},{8,10},{10,8},{9,1... | collective-permute-start | bytes 5505032 | tf_op jit(solution)/shard_map/ppermute | solution.py:115
  73.9 36.5 %all-to-all-start = ((bf16[8,28,2048]{2,1,0:T(8,128)(2,1)}), bf16[8,28,2048]{2,1,0:T(8,128)(2,1)S(1)}, u32[]{:S(2)}, u32[]{:S(2)}) async-start(bf16[8,28,2048]{2,1,0:T(8,128)(2,1)} %broadcast_in_dim.6), calls=%async_computation | async-start | bytes 2097152 | tf_op jit(solution)/shard_map/all_to_all | solution.py:18
  110.4 1.0 copy-start.1
  124.3 31.2 %copy-start.4 = (u32[256]{0:T(256)S(1)}, u32[256]{0:T(256)}, u32[]{:S(2)}) copy-start(u32[256]{0:T(256)} %constant.4) | copy-start | bytes 3076
  152.8 8.4 %collective-permute-start.2 = (f32[28,2048]{1,0:T(8,128)S(1)}, f32[28,2048]{1,0:T(8,128)S(1)}, u32[]{:S(2)}, u32[]{:S(2)}) collective-permute-start(f32[28,2048]{1,0:T(8,128)S(1)} %slice), channel_id=1, source_target_pairs={{0,32},{32,64},{64,96},{96,128},{128,160},{160,192},{192,224},{1,3... | collective-permute-start | bytes 688136

commit v2 on v1

v2 whole, which is shorter than its diff:
```python
import jax
import jax.numpy as jnp
from jax import lax
from jax.experimental import pallas as pl
from jax.experimental.pallas import tpu as pltpu
from jax.sharding import Mesh, PartitionSpec as P


PLANE = ("x", "yh", "yl")
AXES = ("z", "x", "yl", "c", "yh")
POPULATION = 7168
ROWS = 28
PAD = 32
DIM = 2048
TARGETS = 8
PIECES = 16
STEP = 8


def sent_to_all(value, axis):
    count = lax.axis_size(axis)
    return lax.all_to_all(
        jnp.broadcast_to(value[None], (count, *value.shape)), axis, 0, 0, tiled=True
    )


def padded(rows):
    fill = jnp.zeros((PAD - ROWS, rows.shape[1]), rows.dtype)
    return jnp.concatenate([rows, fill], axis=0)


def row_norms(rows):
    wide = rows.astype(jnp.float32)
    return jnp.sum(wide * wide, axis=1, keepdims=True)


def prepare_kernel(at_ref, *refs):
    t_refs, (t_all, norm_ref) = refs[:TARGETS], refs[TARGETS:]
    for i in range(TARGETS):
        rows = pl.ds(pl.multiple_of(lax.rem(at_ref[0] + TARGETS - i, TARGETS) * PAD, PAD), PAD)
        piece = padded(t_refs[i][...])
        t_all[rows, :] = piece
        norm_ref[rows, :] = jnp.broadcast_to(row_norms(piece), (PAD, 128))


def prepared(at, targets):
    whole = TARGETS * PAD
    return pl.pallas_call(
        prepare_kernel,
        in_specs=[pl.BlockSpec(memory_space=pltpu.SMEM)]
        + [pl.BlockSpec(memory_space=pltpu.VMEM)] * TARGETS,
        out_specs=[pl.BlockSpec(memory_space=pltpu.VMEM)] * 2,
        out_shape=[
            jax.ShapeDtypeStruct((whole, DIM), jnp.bfloat16),
            jax.ShapeDtypeStruct((whole, 128), jnp.float32),
        ],
    )(at, *targets)


def half_kernel(first, spread_ref, t_all, norm_ref, source_ref, *refs):
    if first:
        out_ref, x_all, s_all = refs
    else:
        before_ref, out_ref, x_all, s_all, total_ref = refs
    step = pl.program_id(0)
    inverse = 1.0 / spread_ref[0]
    for i in range(STEP):
        x_all[pl.ds(i * PAD, PAD), :] = padded(source_ref[i, :ROWS])
        s_all[pl.ds(i * PAD, PAD), :] = padded(source_ref[i, ROWS:])
    targets = t_all[...]
    source = x_all[...]
    source_norm = row_norms(source)
    source_norm = jnp.transpose(jnp.broadcast_to(source_norm, (STEP * PAD, 128)))[:1]
    dots = lax.dot_general(
        targets, source, (((1,), (1,)), ((), ())), preferred_element_type=jnp.float32
    )
    squared = jnp.maximum(norm_ref[:, :1] + source_norm - 2.0 * dots, 0.0)
    weights = jnp.exp(-squared * inverse)
    column = lax.broadcasted_iota(jnp.int32, weights.shape, 1)
    weights = jnp.where(column % PAD < ROWS, weights, 0.0)
    low = weights.astype(jnp.bfloat16)
    row_total = jnp.sum(weights, axis=1, keepdims=True)
    pull = jnp.dot(low, source, preferred_element_type=jnp.float32)
    drive = jnp.dot(low, s_all[...], preferred_element_type=jnp.float32)
    added = drive + (2.0 * inverse) * (targets.astype(jnp.float32) * row_total - pull)
    last = pl.num_programs(0) - 1
    if first:

        @pl.when(step == 0)
        def _():
            out_ref[...] = added

        @pl.when(step > 0)
        def _():
            out_ref[...] += added

    else:

        @pl.when(step == 0)
        def _():
            total_ref[...] = before_ref[...] + added

        @pl.when(step == last)
        def _():
            total = (total_ref[...] + added) / POPULATION
            for i in range(TARGETS):
                out_ref[pl.ds(i * ROWS, ROWS), :] = total[i * PAD : i * PAD + ROWS]


def half(spread, targets, norms, source, before=None):
    first = before is None
    whole = TARGETS * PAD
    rows = whole if first else TARGETS * ROWS
    in_specs = [
        pl.BlockSpec(memory_space=pltpu.SMEM),
        pl.BlockSpec((whole, DIM), lambda i: (0, 0)),
        pl.BlockSpec((whole, 128), lambda i: (0, 0)),
        pl.BlockSpec((STEP, 2 * ROWS, DIM), lambda i: (i, 0, 0)),
    ]
    args = [spread, targets, norms, source]
    scratch = [pltpu.VMEM((STEP * PAD, DIM), jnp.bfloat16)] * 2
    if not first:
        in_specs.append(pl.BlockSpec((whole, DIM), lambda i: (0, 0)))
        args.append(before)
        scratch.append(pltpu.VMEM((whole, DIM), jnp.float32))

    def body(*refs):
        half_kernel(first, *refs)

    return pl.pallas_call(
        body,
        grid=(PIECES // STEP,),
        in_specs=in_specs,
        out_specs=pl.BlockSpec((rows, DIM), lambda i: (0, 0)),
        out_shape=jax.ShapeDtypeStruct((rows, DIM), jnp.float32),
        scratch_shapes=scratch,
        compiler_params=pltpu.CompilerParams(dimension_semantics=("arbitrary",)),
    )(*args)


def direction(particles, scores, spread):
    swap = [(0, 1), (1, 0)]
    at = lax.axis_index("z").astype(jnp.int32)[None]
    pieces = [particles] + [
        lax.ppermute(particles, "z", [(i, (i + k) % TARGETS) for i in range(TARGETS)])
        for k in range(1, TARGETS)
    ]
    targets, norms = prepared(at, pieces)
    own = sent_to_all(jnp.concatenate([particles, scores], axis=0), PLANE)
    other = lax.ppermute(own, "c", swap)
    before = half(spread, targets, norms, own)
    partial = half(spread, targets, norms, other, before)
    return lax.psum_scatter(partial, "z", scatter_dimension=0, tiled=True)


def solution(mesh):
    fine = Mesh(mesh.devices.reshape(8, 4, 2, 2, 2), AXES)
    return jax.shard_map(
        direction,
        mesh=fine,
        in_specs=(P(AXES, None), P(AXES, None), P()),
        out_specs=P(AXES, None),
        check_vma=False,
    )
```

time: 163 us -> 146 us (0.90)
  waiting for transfers between devices: 48.8 us -> 23.9 us
  local copies, waits for them, and re-layouts: 20.3 us -> 2.71 us
  blocking collectives: 63.8 us -> 80.6 us
  Pallas kernels: 12.9 us -> 17.1 us
  starting transfers between devices: 15.1 us -> 19 us
    all_to_all x2 -> x0, waiting for transfers between devices: 44.3 us -> none  [sent_to_all(): lax.all_to_all(jnp.broadcast_to(value[None], (count, *value.shape)), axis...]
    ppermute x2 -> x8, waiting for transfers between devices: 0.01 us -> 19.2 us  [the longest x7 19.2 us: direction(): lax.ppermute(particles, 'z', [(i, (i + k) % TARGETS) for i in range(TARGE...]
    all_to_all x1, blocking collectives: 35.3 us -> 52.2 us  [sent_to_all(): lax.all_to_all(jnp.broadcast_to(value[None], (count, *value.shape)), axis...]
    ppermute x2 -> x8, starting transfers between devices: 0.01 us -> 16.1 us  [the longest x7 16.1 us: direction(): lax.ppermute(particles, 'z', [(i, (i + k) % TARGETS) for i in range(TARGE...]
    all_to_all x2 -> x0, starting transfers between devices: 12.4 us -> none  [sent_to_all(): lax.all_to_all(jnp.broadcast_to(value[None], (count, *value.shape)), axis...]
    ppermute x2 -> x0, local copies, waits for them, and re-layouts: 7.73 us -> none  [the longest x1 3.87 us: shards(): other_x = lax.ppermute(own_x, 'c', swap)]
    all_to_all x2 -> x0, local copies, waits for them, and re-layouts: 6.08 us -> none  [sent_to_all(): lax.all_to_all(jnp.broadcast_to(value[None], (count, *value.shape)), axis...]
    pallas_call x2 -> x3, Pallas kernels: 12.9 us -> 17.1 us  [the longest x2 14.6 us: half(): pl.pallas_call(body, grid=(PIECES // STEP,), in_specs=in_specs, out_specs...]
  transfers between devices with their start and end apart: 5 -> 9, of which waited for: 3 -> 6; matrix products, arithmetic and copies ran while one was open for 10% -> 0% of each run, Pallas kernels for 0% -> 6%
where the time goes in v2:
time: 146 us
  blocking collectives  80.6 us (55%)
  waiting for transfers between devices  23.9 us (16%)
  starting transfers between devices  19 us (13%)
  Pallas kernels  17.1 us (12%)
  local copies, waits for them, and re-layouts  2.71 us (2%)
    all_to_all x1, blocking collectives, sent_to_all(): lax.all_to_all(jnp.broadcast_to(value[None], (count, *value.shape)), axis...  52.2 us
    unnamed x1, blocking collectives  28.4 us
    ppermute x7, waiting for transfers between devices, direction(): lax.ppermute(particles, 'z', [(i, (i + k) % TARGETS) for i in range(TARGE...  19.2 us
    ppermute x7, starting transfers between devices, direction(): lax.ppermute(particles, 'z', [(i, (i + k) % TARGETS) for i in range(TARGE...  16.1 us
    pallas_call x2, Pallas kernels, half(): pl.pallas_call(body, grid=(PIECES // STEP,), in_specs=in_specs, out_specs...  14.6 us
    unnamed x1, waiting for transfers between devices  4.67 us
  transfers between devices with their start and end apart: 9, of which 6 were waited for; matrix products, arithmetic and copies ran while one was open for 0% of the time, Pallas kernels for 6%

profile of v2, /device:TPU:32, one launch (start us, length us, event | category | flops | bytes accessed | tf_op | source)
XLA Modules:
  0.0 145.7 jit_solution(812105492899530864)
XLA Ops:
  0.0 1.0 pad_maximum_fusion
  1.0 0.4 broadcast_in_dim.10
  1.5 0.0 copy-start
  1.5 52.2 %all_to_all.5.refs_3_ = bf16[16,56,2048]{2,1,0:T(8,128)(2,1)} all-to-all(bf16[16,56,2048]{2,1,0:T(8,128)(2,1)S(1)} %broadcast_in_dim.10), channel_id=1, replica_groups=mesh['z'=8,'x'=4,'yl'=2,'c'=2,'yh'=2] {'x','yh','yl'}, dimensions={0} | all-to-all | bytes 7340032 | tf_op jit(solution)/shard_map/all_to_all | solution.py:22
  53.6 0.0 collective-permute-start.7
  53.7 0.0 copy-done
  53.7 1.9 %collective-permute-start = (bf16[28,2048]{1,0:T(8,128)(2,1)S(1)}, bf16[28,2048]{1,0:T(8,128)(2,1)S(1)}, u32[]{:S(2)}, u32[]{:S(2)}) collective-permute-start(bf16[28,2048]{1,0:T(8,128)(2,1)S(1)} %copy-done), channel_id=1, source_target_pairs={{0,32},{32,64},{64,96},{96,128},{128,160},{160,192},{192,224},{224... | collective-permute-start | bytes 344072 | tf_op jit(solution)/shard_map/ppermute | solution.py:145
  55.6 4.5 %collective-permute-start.1 = (bf16[28,2048]{1,0:T(8,128)(2,1)S(1)}, bf16[28,2048]{1,0:T(8,128)(2,1)S(1)}, u32[]{:S(2)}, u32[]{:S(2)}) collective-permute-start(bf16[28,2048]{1,0:T(8,128)(2,1)S(1)} %copy-done), channel_id=1, source_target_pairs={{0,64},{32,96},{64,128},{96,160},{128,192},{160,224},{192,0},{224,... | collective-permute-start | bytes 344072 | tf_op jit(solution)/shard_map/ppermute | solution.py:145
  60.1 1.9 %collective-permute-start.2 = (bf16[28,2048]{1,0:T(8,128)(2,1)S(1)}, bf16[28,2048]{1,0:T(8,128)(2,1)S(1)}, u32[]{:S(2)}, u32[]{:S(2)}) collective-permute-start(bf16[28,2048]{1,0:T(8,128)(2,1)S(1)} %copy-done), channel_id=1, source_target_pairs={{0,96},{32,128},{64,160},{96,192},{128,224},{160,0},{192,32},{224,... | collective-permute-start | bytes 344072 | tf_op jit(solution)/shard_map/ppermute | solution.py:145
  62.0 1.4 collective-permute-start.3
  63.4 0.0 collective-permute-done.refs_1_
  63.4 3.1 %collective-permute-start.4 = (bf16[28,2048]{1,0:T(8,128)(2,1)S(1)}, bf16[28,2048]{1,0:T(8,128)(2,1)S(1)}, u32[]{:S(2)}, u32[]{:S(2)}) collective-permute-start(bf16[28,2048]{1,0:T(8,128)(2,1)S(1)} %copy-done), channel_id=1, source_target_pairs={{0,160},{32,192},{64,224},{96,0},{128,32},{160,64},{192,96},{224,1... | collective-permute-start | bytes 344072 | tf_op jit(solution)/shard_map/ppermute | solution.py:145
  66.5 2.9 %collective-permute-done.1.refs_2_ = bf16[28,2048]{1,0:T(8,128)(2,1)S(1)} collective-permute-done((bf16[28,2048]{1,0:T(8,128)(2,1)S(1)}, bf16[28,2048]{1,0:T(8,128)(2,1)S(1)}, u32[]{:S(2)}, u32[]{:S(2)}) %collective-permute-start.1) | collective-permute-done | bytes 114720 | tf_op jit(solution)/shard_map/ppermute | solution.py:145
  69.5 3.3 %collective-permute-start.5 = (bf16[28,2048]{1,0:T(8,128)(2,1)S(1)}, bf16[28,2048]{1,0:T(8,128)(2,1)S(1)}, u32[]{:S(2)}, u32[]{:S(2)}) collective-permute-start(bf16[28,2048]{1,0:T(8,128)(2,1)S(1)} %copy-done), channel_id=1, source_target_pairs={{0,192},{32,224},{64,0},{96,32},{128,64},{160,96},{192,128},{224,1... | collective-permute-start | bytes 344072 | tf_op jit(solution)/shard_map/ppermute | solution.py:145
  72.7 9.0 %collective-permute-done.2.refs_3_ = bf16[28,2048]{1,0:T(8,128)(2,1)S(1)} collective-permute-done((bf16[28,2048]{1,0:T(8,128)(2,1)S(1)}, bf16[28,2048]{1,0:T(8,128)(2,1)S(1)}, u32[]{:S(2)}, u32[]{:S(2)}) %collective-permute-start.2) | collective-permute-done | bytes 114720 | tf_op jit(solution)/shard_map/ppermute | solution.py:145
  81.7 0.0 collective-permute-start.6
  82.4 0.0 collective-permute-done.3.refs_4_
  82.4 2.1 %collective-permute-done.4.refs_5_ = bf16[28,2048]{1,0:T(8,128)(2,1)S(1)} collective-permute-done((bf16[28,2048]{1,0:T(8,128)(2,1)S(1)}, bf16[28,2048]{1,0:T(8,128)(2,1)S(1)}, u32[]{:S(2)}, u32[]{:S(2)}) %collective-permute-start.4) | collective-permute-done | bytes 114720 | tf_op jit(solution)/shard_map/ppermute | solution.py:145
  84.5 3.0 %collective-permute-done.5.refs_6_ = bf16[28,2048]{1,0:T(8,128)(2,1)S(1)} collective-permute-done((bf16[28,2048]{1,0:T(8,128)(2,1)S(1)}, bf16[28,2048]{1,0:T(8,128)(2,1)S(1)}, u32[]{:S(2)}, u32[]{:S(2)}) %collective-permute-start.5) | collective-permute-done | bytes 114720 | tf_op jit(solution)/shard_map/ppermute | solution.py:145
  87.5 2.2 %collective-permute-done.6.refs_7_ = bf16[28,2048]{1,0:T(8,128)(2,1)S(1)} collective-permute-done((bf16[28,2048]{1,0:T(8,128)(2,1)S(1)}, bf16[28,2048]{1,0:T(8,128)(2,1)S(1)}, u32[]{:S(2)}, u32[]{:S(2)}) %collective-permute-start.6) | collective-permute-done | bytes 114720 | tf_op jit(solution)/shard_map/ppermute | solution.py:145
  89.7 0.0 copy-done.3
  89.8 0.6 copy-done.7
  90.4 2.4 %shard_map.37 = (bf16[256,2048]{1,0:T(8,128)(2,1)}, f32[256,128]{1,0:T(8,128)}) custom-call(s32[1]{0:T(128)} %bitcast.at_ref, bf16[28,2048]{1,0:T(8,128)(2,1)} %refs_0_.3, bf16[28,2048]{1,0:T(8,128)(2,1)} %copy-done.1, bf16[28,2048]{1,0:T(8,128)(2,1)} %copy-done.2, bf16[28,2048]{1,0:T(8,128)(2,1)} %copy-done.3, bf16[28,2048]{1,0:T(8,128)(2,1)} %copy-done.4, ...), custom_call_target="tpu_custom_call" | custom-call | tf_op jit(solution)/shard_map/pallas_call | solution.py:48
  92.8 6.9 %shard_map.38.refs_4_ = f32[256,2048]{1,0:T(8,128)} custom-call(f32[1]{0:T(128)S(6)} %copy.4.refs_0_, bf16[256,2048]{1,0:T(8,128)(2,1)} %get-tuple-element.7.refs_1_, f32[256,128]{1,0:T(8,128)} %get-tuple-element.8.refs_2_, bf16[16,56,2048]{2,1,0:T(8,128)(2,1)} %all_to_all.5.refs_3_), custom_call_target="tpu_custom_call" | custom-call | tf_op jit(solution)/shard_map/pallas_call | solution.py:130
  99.8 0.0 collective-permute-done.7.refs_3_
  99.8 7.7 %shard_map.39 = f32[224,2048]{1,0:T(8,128)} custom-call(f32[1]{0:T(128)S(6)} %copy.4.refs_0_, bf16[256,2048]{1,0:T(8,128)(2,1)} %get-tuple-element.7.refs_1_, f32[256,128]{1,0:T(8,128)} %get-tuple-element.8.refs_2_, bf16[16,56,2048]{2,1,0:T(8,128)(2,1)} %collective-permute-done.7.refs_3_, f32[256,2048]{1,0:T(8,128)} %shard_map.38.refs_4_), custom_call_target="tpu_custom_call" | custom-call | tf_op jit(solution)/shard_map/pallas_call | solution.py:130
  107.5 28.4 %fusion = f32[32,2048]{1,0:T(8,128)S(1)} fusion(f32[224,2048]{1,0:T(8,128)} %shard_map.39), kind=kCustom, calls=%all-reduce-scatter | all-reduce-scatter fusion | flops 524289 | bytes 2098176
  136.0 2.8 %collective-permute-start.8 = (f32[28,2048]{1,0:T(8,128)S(1)}, f32[28,2048]{1,0:T(8,128)S(1)}, u32[]{:S(2)}, u32[]{:S(2)}) collective-permute-start(f32[28,2048]{1,0:T(8,128)S(1)} %slice), channel_id=1, source_target_pairs={{0,32},{32,64},{64,96},{96,128},{128,160},{160,192},{192,224},{1,3... | collective-permute-start | bytes 688136
  138.8 0.6 dynamic-slice.4
  140.0 4.7 %collective-permute-done.8 = f32[28,2048]{1,0:T(8,128)S(1)} collective-permute-done((f32[28,2048]{1,0:T(8,128)S(1)}, f32[28,2048]{1,0:T(8,128)S(1)}, u32[]{:S(2)}, u32[]{:S(2)}) %collective-permute-start.8) | collective-permute-done | bytes 229408
  144.7 0.2 concatenate.4
  145.0 0.7 constant_dynamic-slice_fusion
  (15 shorter events, 0.0 us)
Async XLA Ops:
  1.5 52.2 %copy-start = (bf16[28,2048]{1,0:T(8,128)(2,1)S(1)}, bf16[28,2048]{1,0:T(8,128)(2,1)}, u32[]{:S(2)}) copy-start(bf16[28,2048]{1,0:T(8,128)(2,1)} %refs_0_.3) | copy-start | bytes 344068
  53.6 46.1 %collective-permute-start.7 = (bf16[16,56,2048]{2,1,0:T(8,128)(2,1)}, bf16[16,56,2048]{2,1,0:T(8,128)(2,1)}, u32[]{:S(2)}, u32[]{:S(2)}) collective-permute-start(bf16[16,56,2048]{2,1,0:T(8,128)(2,1)} %all_to_all.5.refs_3_), channel_id=1, source_target_pairs={{0,2},{2,0},{1,3},{3,1},{4,6},{6,4},{5,7},{7,5},{8,10},{10,8},{9,1... | collective-permute-start | bytes 11010056 | tf_op jit(solution)/shard_map/ppermute | solution.py:150
  53.7 9.8 %collective-permute-start = (bf16[28,2048]{1,0:T(8,128)(2,1)S(1)}, bf16[28,2048]{1,0:T(8,128)(2,1)S(1)}, u32[]{:S(2)}, u32[]{:S(2)}) collective-permute-start(bf16[28,2048]{1,0:T(8,128)(2,1)S(1)} %copy-done), channel_id=1, source_target_pairs={{0,32},{32,64},{64,96},{96,128},{128,160},{160,192},{192,224},{224... | collective-permute-start | bytes 344072 | tf_op jit(solution)/shard_map/ppermute | solution.py:145
  55.6 13.9 %collective-permute-start.1 = (bf16[28,2048]{1,0:T(8,128)(2,1)S(1)}, bf16[28,2048]{1,0:T(8,128)(2,1)S(1)}, u32[]{:S(2)}, u32[]{:S(2)}) collective-permute-start(bf16[28,2048]{1,0:T(8,128)(2,1)S(1)} %copy-done), channel_id=1, source_target_pairs={{0,64},{32,96},{64,128},{96,160},{128,192},{160,224},{192,0},{224,... | collective-permute-start | bytes 344072 | tf_op jit(solution)/shard_map/ppermute | solution.py:145
  60.1 21.7 %collective-permute-start.2 = (bf16[28,2048]{1,0:T(8,128)(2,1)S(1)}, bf16[28,2048]{1,0:T(8,128)(2,1)S(1)}, u32[]{:S(2)}, u32[]{:S(2)}) collective-permute-start(bf16[28,2048]{1,0:T(8,128)(2,1)S(1)} %copy-done), channel_id=1, source_target_pairs={{0,96},{32,128},{64,160},{96,192},{128,224},{160,0},{192,32},{224,... | collective-permute-start | bytes 344072 | tf_op jit(solution)/shard_map/ppermute | solution.py:145
  62.0 20.4 %collective-permute-start.3 = (bf16[28,2048]{1,0:T(8,128)(2,1)S(1)}, bf16[28,2048]{1,0:T(8,128)(2,1)S(1)}, u32[]{:S(2)}, u32[]{:S(2)}) collective-permute-start(bf16[28,2048]{1,0:T(8,128)(2,1)S(1)} %copy-done), channel_id=1, source_target_pairs={{0,128},{32,160},{64,192},{96,224},{128,0},{160,32},{192,64},{224,... | collective-permute-start | bytes 344072 | tf_op jit(solution)/shard_map/ppermute | solution.py:145
  63.4 26.3 %copy-start.1 = (bf16[28,2048]{1,0:T(8,128)(2,1)}, bf16[28,2048]{1,0:T(8,128)(2,1)S(1)}, u32[]{:S(2)}) copy-start(bf16[28,2048]{1,0:T(8,128)(2,1)S(1)} %collective-permute-done.refs_1_) | copy-start | bytes 344068
  63.4 21.1 %collective-permute-start.4 = (bf16[28,2048]{1,0:T(8,128)(2,1)S(1)}, bf16[28,2048]{1,0:T(8,128)(2,1)S(1)}, u32[]{:S(2)}, u32[]{:S(2)}) collective-permute-start(bf16[28,2048]{1,0:T(8,128)(2,1)S(1)} %copy-done), channel_id=1, source_target_pairs={{0,160},{32,192},{64,224},{96,0},{128,32},{160,64},{192,96},{224,1... | collective-permute-start | bytes 344072 | tf_op jit(solution)/shard_map/ppermute | solution.py:145
  69.5 20.2 %copy-start.2 = (bf16[28,2048]{1,0:T(8,128)(2,1)}, bf16[28,2048]{1,0:T(8,128)(2,1)S(1)}, u32[]{:S(2)}) copy-start(bf16[28,2048]{1,0:T(8,128)(2,1)S(1)} %collective-permute-done.1.refs_2_) | copy-start | bytes 344068
  69.5 18.0 %collective-permute-start.5 = (bf16[28,2048]{1,0:T(8,128)(2,1)S(1)}, bf16[28,2048]{1,0:T(8,128)(2,1)S(1)}, u32[]{:S(2)}, u32[]{:S(2)}) collective-permute-start(bf16[28,2048]{1,0:T(8,128)(2,1)S(1)} %copy-done), channel_id=1, source_target_pairs={{0,192},{32,224},{64,0},{96,32},{128,64},{160,96},{192,128},{224,1... | collective-permute-start | bytes 344072 | tf_op jit(solution)/shard_map/ppermute | solution.py:145
  81.7 8.0 %copy-start.3 = (bf16[28,2048]{1,0:T(8,128)(2,1)}, bf16[28,2048]{1,0:T(8,128)(2,1)S(1)}, u32[]{:S(2)}) copy-start(bf16[28,2048]{1,0:T(8,128)(2,1)S(1)} %collective-permute-done.2.refs_3_) | copy-start | bytes 344068
  81.7 8.0 %collective-permute-start.6 = (bf16[28,2048]{1,0:T(8,128)(2,1)S(1)}, bf16[28,2048]{1,0:T(8,128)(2,1)S(1)}, u32[]{:S(2)}, u32[]{:S(2)}) collective-permute-start(bf16[28,2048]{1,0:T(8,128)(2,1)S(1)} %copy-done), channel_id=1, source_target_pairs={{0,224},{32,0},{64,32},{96,64},{128,96},{160,128},{192,160},{224,1... | collective-permute-start | bytes 344072 | tf_op jit(solution)/shard_map/ppermute | solution.py:145
  82.4 7.3 %copy-start.4 = (bf16[28,2048]{1,0:T(8,128)(2,1)}, bf16[28,2048]{1,0:T(8,128)(2,1)S(1)}, u32[]{:S(2)}) copy-start(bf16[28,2048]{1,0:T(8,128)(2,1)S(1)} %collective-permute-done.3.refs_4_) | copy-start | bytes 344068
  84.5 5.2 %copy-start.5 = (bf16[28,2048]{1,0:T(8,128)(2,1)}, bf16[28,2048]{1,0:T(8,128)(2,1)S(1)}, u32[]{:S(2)}) copy-start(bf16[28,2048]{1,0:T(8,128)(2,1)S(1)} %collective-permute-done.4.refs_5_) | copy-start | bytes 344068
  87.5 2.2 %copy-start.6 = (bf16[28,2048]{1,0:T(8,128)(2,1)}, bf16[28,2048]{1,0:T(8,128)(2,1)S(1)}, u32[]{:S(2)}) copy-start(bf16[28,2048]{1,0:T(8,128)(2,1)S(1)} %collective-permute-done.5.refs_6_) | copy-start | bytes 344068
  89.7 0.7 copy-start.7
  107.5 31.3 %copy-start.8 = (u32[256]{0:T(256)S(1)}, u32[256]{0:T(256)}, u32[]{:S(2)}) copy-start(u32[256]{0:T(256)} %constant.10) | copy-start | bytes 3076
  136.0 8.7 %collective-permute-start.8 = (f32[28,2048]{1,0:T(8,128)S(1)}, f32[28,2048]{1,0:T(8,128)S(1)}, u32[]{:S(2)}, u32[]{:S(2)}) collective-permute-start(f32[28,2048]{1,0:T(8,128)S(1)} %slice), channel_id=1, source_target_pairs={{0,32},{32,64},{64,96},{96,128},{128,160},{160,192},{192,224},{1,3... | collective-permute-start | bytes 688136

commit v3 on v2

--- a/solution.py
+++ b/solution.py
@@ -34,27 +34,44 @@
     return jnp.sum(wide * wide, axis=1, keepdims=True)
 
 
-def prepare_kernel(at_ref, *refs):
-    t_refs, (t_all, norm_ref) = refs[:TARGETS], refs[TARGETS:]
-    for i in range(TARGETS):
-        rows = pl.ds(pl.multiple_of(lax.rem(at_ref[0] + TARGETS - i, TARGETS) * PAD, PAD), PAD)
-        piece = padded(t_refs[i][...])
-        t_all[rows, :] = piece
-        norm_ref[rows, :] = jnp.broadcast_to(row_norms(piece), (PAD, 128))
+def prepare_kernel(at_ref, own_ref, up_ref, down_ref, far_up_ref, far_down_ref, t_all, norm_ref):
+    half = DIM // 2
+
+    def put(offset, ref, index):
+        slot = lax.rem(at_ref[0] + TARGETS + offset, TARGETS)
+        rows = pl.ds(pl.multiple_of(slot * PAD, PAD), PAD)
+        at = index * 2 * ROWS
+        left = padded(ref[at : at + ROWS])
+        right = padded(ref[at + ROWS : at + 2 * ROWS])
+        t_all[rows, :half] = left
+        t_all[rows, half:] = right
+        norm_ref[rows, :] = jnp.broadcast_to(row_norms(left) + row_norms(right), (PAD, 128))
+
+    put(0, own_ref, 0)
+    put(-1, up_ref, 0)
+    put(1, down_ref, 0)
+    for i, offset in enumerate((-2, -3, -4)):
+        put(offset, far_up_ref, i)
+    for i, offset in enumerate((2, 3)):
+        put(offset, far_down_ref, i)
 
 
-def prepared(at, targets):
+def prepared(at, pieces):
     whole = TARGETS * PAD
     return pl.pallas_call(
         prepare_kernel,
         in_specs=[pl.BlockSpec(memory_space=pltpu.SMEM)]
-        + [pl.BlockSpec(memory_space=pltpu.VMEM)] * TARGETS,
+        + [pl.BlockSpec(memory_space=pltpu.VMEM)] * len(pieces),
         out_specs=[pl.BlockSpec(memory_space=pltpu.VMEM)] * 2,
         out_shape=[
             jax.ShapeDtypeStruct((whole, DIM), jnp.bfloat16),
             jax.ShapeDtypeStruct((whole, 128), jnp.float32),
         ],
-    )(at, *targets)
+    )(at, *pieces)
+
+
+def moved(value, steps):
+    return lax.ppermute(value, "z", [(i, (i + steps) % TARGETS) for i in range(TARGETS)])
 
 
 def half_kernel(first, spread_ref, t_all, norm_ref, source_ref, *refs):
@@ -141,10 +158,11 @@
 def direction(particles, scores, spread):
     swap = [(0, 1), (1, 0)]
     at = lax.axis_index("z").astype(jnp.int32)[None]
-    pieces = [particles] + [
-        lax.ppermute(particles, "z", [(i, (i + k) % TARGETS) for i in range(TARGETS)])
-        for k in range(1, TARGETS)
-    ]
+    own_piece = jnp.concatenate([particles[:, : DIM // 2], particles[:, DIM // 2 :]], axis=0)
+    up, down = moved(own_piece, 1), moved(own_piece, -1)
+    far_up = moved(jnp.concatenate([down, own_piece, up], axis=0), 3)
+    far_down = moved(jnp.concatenate([up, own_piece], axis=0), -3)
+    pieces = [own_piece, up, down, far_up, far_down]
     targets, norms = prepared(at, pieces)
     own = sent_to_all(jnp.concatenate([particles, scores], axis=0), PLANE)
     other = lax.ppermute(own, "c", swap)

time: 146 us -> 145 us (level)
  starting transfers between devices: 19 us -> 10.1 us
  waiting for transfers between devices: 23.9 us -> 31 us
    ppermute x7 -> x4, starting transfers between devices: 16.1 us -> 7.5 us  [moved(): lax.ppermute(value, 'z', [(i, (i + steps) % TARGETS) for i in range(TARGE...]
    ppermute x7 -> x4, waiting for transfers between devices: 19.2 us -> 26.6 us  [moved(): lax.ppermute(value, 'z', [(i, (i + steps) % TARGETS) for i in range(TARGE...]
  transfers between devices with their start and end apart: 9 -> 6, of which waited for: 6 -> 5; matrix products, arithmetic and copies ran while one was open for 0% -> 0% of each run, Pallas kernels for 6% -> 6%
where the time goes in v3:
time: 145 us
  blocking collectives  81.6 us (56%)
  waiting for transfers between devices  31 us (21%)
  Pallas kernels  17 us (12%)
  starting transfers between devices  10.1 us (7%)
  local copies, waits for them, and re-layouts  2.77 us (2%)
    all_to_all x1, blocking collectives, sent_to_all(): lax.all_to_all(jnp.broadcast_to(value[None], (count, *value.shape)), axis...  52.2 us
    unnamed x1, blocking collectives  29.4 us
    ppermute x4, waiting for transfers between devices, moved(): lax.ppermute(value, 'z', [(i, (i + steps) % TARGETS) for i in range(TARGE...  26.6 us
    pallas_call x2, Pallas kernels, half(): pl.pallas_call(body, grid=(PIECES // STEP,), in_specs=in_specs, out_specs...  14.6 us
    ppermute x4, starting transfers between devices, moved(): lax.ppermute(value, 'z', [(i, (i + steps) % TARGETS) for i in range(TARGE...  7.5 us
    unnamed x1, waiting for transfers between devices  4.38 us
  transfers between devices with their start and end apart: 6, of which 5 were waited for; matrix products, arithmetic and copies ran while one was open for 0% of the time, Pallas kernels for 6%

profile of v3, /device:TPU:32, one launch (start us, length us, event | category | flops | bytes accessed | tf_op | source)
XLA Modules:
  0.0 145.0 jit_solution(16442723652168044674)
XLA Ops:
  0.0 1.0 pad_maximum_fusion.2
  1.0 0.4 broadcast_in_dim.10
  1.5 0.0 copy-start.1
  1.5 52.2 %all_to_all.5.refs_3_ = bf16[16,56,2048]{2,1,0:T(8,128)(2,1)} all-to-all(bf16[16,56,2048]{2,1,0:T(8,128)(2,1)S(1)} %broadcast_in_dim.10), channel_id=1, replica_groups=mesh['z'=8,'x'=4,'yl'=2,'c'=2,'yh'=2] {'x','yh','yl'}, dimensions={0} | all-to-all | bytes 7340032 | tf_op jit(solution)/shard_map/all_to_all | solution.py:22
  53.6 0.0 collective-permute-start.4
  53.7 0.0 copy-done.1
  53.7 0.0 copy-start.2
  53.7 2.0 %collective-permute-start = (bf16[56,1024]{1,0:T(8,128)(2,1)S(1)}, bf16[56,1024]{1,0:T(8,128)(2,1)S(1)}, u32[]{:S(2)}, u32[]{:S(2)}) collective-permute-start(bf16[56,1024]{1,0:T(8,128)(2,1)S(1)} %pad_maximum_fusion.3.own_ref), channel_id=1, source_target_pairs={{0,32},{32,64},{64,96},{96,128},{128,160},{160,192},{192,224},{224... | collective-permute-start | bytes 344072 | tf_op jit(solution)/shard_map/ppermute | solution.py:74
  55.7 0.1 collective-permute-start.1
  55.8 3.5 %collective-permute-done.up_ref = bf16[56,1024]{1,0:T(8,128)(2,1)S(1)} collective-permute-done((bf16[56,1024]{1,0:T(8,128)(2,1)S(1)}, bf16[56,1024]{1,0:T(8,128)(2,1)S(1)}, u32[]{:S(2)}, u32[]{:S(2)}) %collective-permute-start) | collective-permute-done | bytes 114720 | tf_op jit(solution)/shard_map/ppermute | solution.py:74
  59.3 0.0 copy-start
  59.3 1.8 %collective-permute-done.1.down_ref = bf16[56,1024]{1,0:T(8,128)(2,1)S(1)} collective-permute-done((bf16[56,1024]{1,0:T(8,128)(2,1)S(1)}, bf16[56,1024]{1,0:T(8,128)(2,1)S(1)}, u32[]{:S(2)}, u32[]{:S(2)}) %collective-permute-start.1) | collective-permute-done | bytes 114720 | tf_op jit(solution)/shard_map/ppermute | solution.py:74
  61.2 5.3 %collective-permute-start.2 = (bf16[168,1024]{1,0:T(8,128)(2,1)S(1)}, bf16[168,1024]{1,0:T(8,128)(2,1)S(1)}, u32[]{:S(2)}, u32[]{:S(2)}) collective-permute-start(bf16[168,1024]{1,0:T(8,128)(2,1)S(1)} %pad_maximum_fusion), channel_id=1, source_target_pairs={{0,96},{32,128},{64,160},{96,192},{128,224},{160,0},{192,32},{224,... | collective-permute-start | bytes 1032200 | tf_op jit(solution)/shard_map/ppermute | solution.py:74
  66.6 0.1 collective-permute-start.3
  67.3 17.0 %collective-permute-done.3.far_down_ref = bf16[112,1024]{1,0:T(8,128)(2,1)S(1)} collective-permute-done((bf16[112,1024]{1,0:T(8,128)(2,1)S(1)}, bf16[112,1024]{1,0:T(8,128)(2,1)S(1)}, u32[]{:S(2)}, u32[]{:S(2)}) %collective-permute-start.3) | collective-permute-done | bytes 229408 | tf_op jit(solution)/shard_map/ppermute | solution.py:74
  84.3 4.2 %collective-permute-done.2.far_up_ref = bf16[168,1024]{1,0:T(8,128)(2,1)S(1)} collective-permute-done((bf16[168,1024]{1,0:T(8,128)(2,1)S(1)}, bf16[168,1024]{1,0:T(8,128)(2,1)S(1)}, u32[]{:S(2)}, u32[]{:S(2)}) %collective-permute-start.2) | collective-permute-done | bytes 344096 | tf_op jit(solution)/shard_map/ppermute | solution.py:74
  88.5 0.0 copy-done.2
  88.5 0.0 copy-done
  88.5 0.0 copy-done.3
  88.6 0.0 copy-done.5
  88.6 0.7 copy-done.4
  89.3 2.4 %shard_map.37 = (bf16[256,2048]{1,0:T(8,128)(2,1)}, f32[256,128]{1,0:T(8,128)}) custom-call(s32[1]{0:T(128)} %bitcast.at_ref, bf16[56,1024]{1,0:T(8,128)(2,1)} %copy-done.2, bf16[56,1024]{1,0:T(8,128)(2,1)} %copy-done, bf16[56,1024]{1,0:T(8,128)(2,1)} %copy-done.3, bf16[168,1024]{1,0:T(8,128)(2,1)} %copy-done.4, bf16[112,1024]{1,0:T(8,128)(2,1)} %copy-done.5), custom_call_target="tpu_custom_call" | custom-call | tf_op jit(solution)/shard_map/pallas_call | solution.py:61
  91.7 6.9 %shard_map.38.refs_4_ = f32[256,2048]{1,0:T(8,128)} custom-call(f32[1]{0:T(128)S(6)} %copy.4.refs_0_, bf16[256,2048]{1,0:T(8,128)(2,1)} %get-tuple-element.7.refs_1_, f32[256,128]{1,0:T(8,128)} %get-tuple-element.8.refs_2_, bf16[16,56,2048]{2,1,0:T(8,128)(2,1)} %all_to_all.5.refs_3_), custom_call_target="tpu_custom_call" | custom-call | tf_op jit(solution)/shard_map/pallas_call | solution.py:147
  98.6 0.0 collective-permute-done.4.refs_3_
  98.6 7.7 %shard_map.39 = f32[224,2048]{1,0:T(8,128)} custom-call(f32[1]{0:T(128)S(6)} %copy.4.refs_0_, bf16[256,2048]{1,0:T(8,128)(2,1)} %get-tuple-element.7.refs_1_, f32[256,128]{1,0:T(8,128)} %get-tuple-element.8.refs_2_, bf16[16,56,2048]{2,1,0:T(8,128)(2,1)} %collective-permute-done.4.refs_3_, f32[256,2048]{1,0:T(8,128)} %shard_map.38.refs_4_), custom_call_target="tpu_custom_call" | custom-call | tf_op jit(solution)/shard_map/pallas_call | solution.py:147
  106.3 29.4 %fusion = f32[32,2048]{1,0:T(8,128)S(1)} fusion(f32[224,2048]{1,0:T(8,128)} %shard_map.39), kind=kCustom, calls=%all-reduce-scatter | all-reduce-scatter fusion | flops 524289 | bytes 2098176
  135.8 2.6 %collective-permute-start.5 = (f32[28,2048]{1,0:T(8,128)S(1)}, f32[28,2048]{1,0:T(8,128)S(1)}, u32[]{:S(2)}, u32[]{:S(2)}) collective-permute-start(f32[28,2048]{1,0:T(8,128)S(1)} %slice.8), channel_id=1, source_target_pairs={{0,32},{32,64},{64,96},{96,128},{128,160},{160,192},{192,224},{1,3... | collective-permute-start | bytes 688136
  138.4 0.0 copy-done.6
  138.4 0.6 dynamic-slice.4
  139.6 4.4 %collective-permute-done.5 = f32[28,2048]{1,0:T(8,128)S(1)} collective-permute-done((f32[28,2048]{1,0:T(8,128)S(1)}, f32[28,2048]{1,0:T(8,128)S(1)}, u32[]{:S(2)}, u32[]{:S(2)}) %collective-permute-start.5) | collective-permute-done | bytes 229408
  144.0 0.2 concatenate.18
  144.3 0.7 constant_dynamic-slice_fusion
  (9 shorter events, 0.1 us)
Async XLA Ops:
  1.5 52.2 %copy-start.1 = (bf16[28,2048]{1,0:T(8,128)(2,1)S(1)}, bf16[28,2048]{1,0:T(8,128)(2,1)}, u32[]{:S(2)}) copy-start(bf16[28,2048]{1,0:T(8,128)(2,1)} %param.3) | copy-start | bytes 344068
  53.6 45.0 %collective-permute-start.4 = (bf16[16,56,2048]{2,1,0:T(8,128)(2,1)}, bf16[16,56,2048]{2,1,0:T(8,128)(2,1)}, u32[]{:S(2)}, u32[]{:S(2)}) collective-permute-start(bf16[16,56,2048]{2,1,0:T(8,128)(2,1)} %all_to_all.5.refs_3_), channel_id=1, source_target_pairs={{0,2},{2,0},{1,3},{3,1},{4,6},{6,4},{5,7},{7,5},{8,10},{10,8},{9,1... | collective-permute-start | bytes 11010056 | tf_op jit(solution)/shard_map/ppermute | solution.py:168
  53.7 34.8 %copy-start.2 = (bf16[56,1024]{1,0:T(8,128)(2,1)}, bf16[56,1024]{1,0:T(8,128)(2,1)S(1)}, u32[]{:S(2)}) copy-start(bf16[56,1024]{1,0:T(8,128)(2,1)S(1)} %pad_maximum_fusion.3.own_ref) | copy-start | bytes 344068
  53.7 5.6 %collective-permute-start = (bf16[56,1024]{1,0:T(8,128)(2,1)S(1)}, bf16[56,1024]{1,0:T(8,128)(2,1)S(1)}, u32[]{:S(2)}, u32[]{:S(2)}) collective-permute-start(bf16[56,1024]{1,0:T(8,128)(2,1)S(1)} %pad_maximum_fusion.3.own_ref), channel_id=1, source_target_pairs={{0,32},{32,64},{64,96},{96,128},{128,160},{160,192},{192,224},{224... | collective-permute-start | bytes 344072 | tf_op jit(solution)/shard_map/ppermute | solution.py:74
  55.7 5.5 %collective-permute-start.1 = (bf16[56,1024]{1,0:T(8,128)(2,1)S(1)}, bf16[56,1024]{1,0:T(8,128)(2,1)S(1)}, u32[]{:S(2)}, u32[]{:S(2)}) collective-permute-start(bf16[56,1024]{1,0:T(8,128)(2,1)S(1)} %pad_maximum_fusion.3.own_ref), channel_id=1, source_target_pairs={{0,224},{32,0},{64,32},{96,64},{128,96},{160,128},{192,160},{224,1... | collective-permute-start | bytes 344072 | tf_op jit(solution)/shard_map/ppermute | solution.py:74
  59.3 29.2 %copy-start = (bf16[56,1024]{1,0:T(8,128)(2,1)}, bf16[56,1024]{1,0:T(8,128)(2,1)S(1)}, u32[]{:S(2)}) copy-start(bf16[56,1024]{1,0:T(8,128)(2,1)S(1)} %collective-permute-done.up_ref) | copy-start | bytes 344068
  61.2 27.4 %copy-start.3 = (bf16[56,1024]{1,0:T(8,128)(2,1)}, bf16[56,1024]{1,0:T(8,128)(2,1)S(1)}, u32[]{:S(2)}) copy-start(bf16[56,1024]{1,0:T(8,128)(2,1)S(1)} %collective-permute-done.1.down_ref) | copy-start | bytes 344068
  61.2 27.3 %collective-permute-start.2 = (bf16[168,1024]{1,0:T(8,128)(2,1)S(1)}, bf16[168,1024]{1,0:T(8,128)(2,1)S(1)}, u32[]{:S(2)}, u32[]{:S(2)}) collective-permute-start(bf16[168,1024]{1,0:T(8,128)(2,1)S(1)} %pad_maximum_fusion), channel_id=1, source_target_pairs={{0,96},{32,128},{64,160},{96,192},{128,224},{160,0},{192,32},{224,... | collective-permute-start | bytes 1032200 | tf_op jit(solution)/shard_map/ppermute | solution.py:74
  66.6 17.8 %collective-permute-start.3 = (bf16[112,1024]{1,0:T(8,128)(2,1)S(1)}, bf16[112,1024]{1,0:T(8,128)(2,1)S(1)}, u32[]{:S(2)}, u32[]{:S(2)}) collective-permute-start(bf16[112,1024]{1,0:T(8,128)(2,1)S(1)} %pad_maximum_fusion.1), channel_id=1, source_target_pairs={{0,160},{32,192},{64,224},{96,0},{128,32},{160,64},{192,96},{224,1... | collective-permute-start | bytes 688136 | tf_op jit(solution)/shard_map/ppermute | solution.py:74
  84.3 4.2 %copy-start.5 = (bf16[112,1024]{1,0:T(8,128)(2,1)}, bf16[112,1024]{1,0:T(8,128)(2,1)S(1)}, u32[]{:S(2)}) copy-start(bf16[112,1024]{1,0:T(8,128)(2,1)S(1)} %collective-permute-done.3.far_down_ref) | copy-start | bytes 688132
  88.5 0.7 copy-start.4
  106.3 32.1 %copy-start.6 = (u32[256]{0:T(256)S(1)}, u32[256]{0:T(256)}, u32[]{:S(2)}) copy-start(u32[256]{0:T(256)} %constant.10) | copy-start | bytes 3076
  135.8 8.3 %collective-permute-start.5 = (f32[28,2048]{1,0:T(8,128)S(1)}, f32[28,2048]{1,0:T(8,128)S(1)}, u32[]{:S(2)}, u32[]{:S(2)}) collective-permute-start(f32[28,2048]{1,0:T(8,128)S(1)} %slice.8), channel_id=1, source_target_pairs={{0,32},{32,64},{64,96},{96,128},{128,160},{160,192},{192,224},{1,3... | collective-permute-start | bytes 688136

commit v4 on v3

--- a/solution.py
+++ b/solution.py
@@ -11,6 +11,7 @@
 POPULATION = 7168
 ROWS = 28
 PAD = 32
+SPAN = 31
 DIM = 2048
 TARGETS = 8
 PIECES = 16
@@ -74,11 +75,7 @@
     return lax.ppermute(value, "z", [(i, (i + steps) % TARGETS) for i in range(TARGETS)])
 
 
-def half_kernel(first, spread_ref, t_all, norm_ref, source_ref, *refs):
-    if first:
-        out_ref, x_all, s_all = refs
-    else:
-        before_ref, out_ref, x_all, s_all, total_ref = refs
+def half_kernel(spread_ref, t_all, norm_ref, source_ref, out_ref, x_all, s_all, total_ref):
     step = pl.program_id(0)
     inverse = 1.0 / spread_ref[0]
     for i in range(STEP):
@@ -101,58 +98,38 @@
     drive = jnp.dot(low, s_all[...], preferred_element_type=jnp.float32)
     added = drive + (2.0 * inverse) * (targets.astype(jnp.float32) * row_total - pull)
     last = pl.num_programs(0) - 1
-    if first:
 
-        @pl.when(step == 0)
-        def _():
-            out_ref[...] = added
+    @pl.when(step == 0)
+    def _():
+        total_ref[...] = added
 
-        @pl.when(step > 0)
-        def _():
-            out_ref[...] += added
-
-    else:
-
-        @pl.when(step == 0)
-        def _():
-            total_ref[...] = before_ref[...] + added
-
-        @pl.when(step == last)
-        def _():
-            total = (total_ref[...] + added) / POPULATION
-            for i in range(TARGETS):
-                out_ref[pl.ds(i * ROWS, ROWS), :] = total[i * PAD : i * PAD + ROWS]
+    @pl.when(step == last)
+    def _():
+        total = total_ref[...] + added
+        for i in range(TARGETS):
+            out_ref[pl.ds(i * SPAN, SPAN), :] = total[i * PAD : i * PAD + SPAN]
 
 
-def half(spread, targets, norms, source, before=None):
-    first = before is None
+def half(spread, targets, norms, source):
     whole = TARGETS * PAD
-    rows = whole if first else TARGETS * ROWS
-    in_specs = [
-        pl.BlockSpec(memory_space=pltpu.SMEM),
-        pl.BlockSpec((whole, DIM), lambda i: (0, 0)),
-        pl.BlockSpec((whole, 128), lambda i: (0, 0)),
-        pl.BlockSpec((STEP, 2 * ROWS, DIM), lambda i: (i, 0, 0)),
-    ]
-    args = [spread, targets, norms, source]
-    scratch = [pltpu.VMEM((STEP * PAD, DIM), jnp.bfloat16)] * 2
-    if not first:
-        in_specs.append(pl.BlockSpec((whole, DIM), lambda i: (0, 0)))
-        args.append(before)
-        scratch.append(pltpu.VMEM((whole, DIM), jnp.float32))
-
-    def body(*refs):
-        half_kernel(first, *refs)
-
     return pl.pallas_call(
-        body,
+        half_kernel,
         grid=(PIECES // STEP,),
-        in_specs=in_specs,
-        out_specs=pl.BlockSpec((rows, DIM), lambda i: (0, 0)),
-        out_shape=jax.ShapeDtypeStruct((rows, DIM), jnp.float32),
-        scratch_shapes=scratch,
+        in_specs=[
+            pl.BlockSpec(memory_space=pltpu.SMEM),
+            pl.BlockSpec((whole, DIM), lambda i: (0, 0)),
+            pl.BlockSpec((whole, 128), lambda i: (0, 0)),
+            pl.BlockSpec((STEP, 2 * ROWS, DIM), lambda i: (i, 0, 0)),
+        ],
+        out_specs=pl.BlockSpec((TARGETS * SPAN, DIM), lambda i: (0, 0)),
+        out_shape=jax.ShapeDtypeStruct((TARGETS * SPAN, DIM), jnp.float32),
+        scratch_shapes=[
+            pltpu.VMEM((STEP * PAD, DIM), jnp.bfloat16),
+            pltpu.VMEM((STEP * PAD, DIM), jnp.bfloat16),
+            pltpu.VMEM((whole, DIM), jnp.float32),
+        ],
         compiler_params=pltpu.CompilerParams(dimension_semantics=("arbitrary",)),
-    )(*args)
+    )(spread, targets, norms, source)
 
 
 def direction(particles, scores, spread):
@@ -166,9 +143,11 @@
     targets, norms = prepared(at, pieces)
     own = sent_to_all(jnp.concatenate([particles, scores], axis=0), PLANE)
     other = lax.ppermute(own, "c", swap)
-    before = half(spread, targets, norms, own)
-    partial = half(spread, targets, norms, other, before)
-    return lax.psum_scatter(partial, "z", scatter_dimension=0, tiled=True)
+    mine = half(spread, targets, norms, own)
+    theirs = half(spread, targets, norms, other)
+    partial = (mine + theirs) / POPULATION
+    total = lax.psum_scatter(partial, "z", scatter_dimension=0, tiled=True)
+    return lax.optimization_barrier(total)[:ROWS]
 
 
 def solution(mesh):

time: 145 us -> 144 us (level)
  other arithmetic: 1.1 us -> 3.57 us
  waiting for transfers between devices: 31 us -> 28.8 us
    div x0 -> x1, other arithmetic: none -> 2.47 us  [direction(): partial = (mine + theirs) / POPULATION]
    unnamed x1, waiting for transfers between devices: 4.38 us -> 2.26 us
where the time goes in v4:
time: 144 us
  blocking collectives  81 us (56%)
  waiting for transfers between devices  28.8 us (20%)
  Pallas kernels  16.2 us (11%)
  starting transfers between devices  10.2 us (7%)
  other arithmetic  3.57 us (2%)
  local copies, waits for them, and re-layouts  2.75 us (2%)
    all_to_all x1, blocking collectives, sent_to_all(): lax.all_to_all(jnp.broadcast_to(value[None], (count, *value.shape)), axis...  52.2 us
    unnamed x1, blocking collectives  28.8 us
    ppermute x4, waiting for transfers between devices, moved(): lax.ppermute(value, 'z', [(i, (i + steps) % TARGETS) for i in range(TARGE...  26.6 us
    pallas_call x2, Pallas kernels, half(): pl.pallas_call(half_kernel, grid=(PIECES // STEP,), in_specs=[pl.BlockSpe...  13.8 us
    ppermute x4, starting transfers between devices, moved(): lax.ppermute(value, 'z', [(i, (i + steps) % TARGETS) for i in range(TARGE...  7.5 us
  transfers between devices with their start and end apart: 6, of which 5 were waited for; matrix products, arithmetic and copies ran while one was open for 0% of the time, Pallas kernels for 6%

profile of v4, /device:TPU:32, one launch (start us, length us, event | category | flops | bytes accessed | tf_op | source)
XLA Modules:
  0.0 143.9 jit_solution(2910567895920837518)
XLA Ops:
  0.0 1.0 pad_maximum_fusion.2
  1.0 0.4 broadcast_in_dim.10
  1.5 0.0 copy-start.1
  1.5 52.2 %all_to_all.5.source_ref = bf16[16,56,2048]{2,1,0:T(8,128)(2,1)} all-to-all(bf16[16,56,2048]{2,1,0:T(8,128)(2,1)S(1)} %broadcast_in_dim.10), channel_id=1, replica_groups=mesh['z'=8,'x'=4,'yl'=2,'c'=2,'yh'=2] {'x','yh','yl'}, dimensions={0} | all-to-all | bytes 7340032 | tf_op jit(solution)/shard_map/all_to_all | solution.py:23
  53.6 0.0 collective-permute-start.4
  53.7 0.0 copy-done.1
  53.7 0.0 copy-start.2
  53.7 2.0 %collective-permute-start = (bf16[56,1024]{1,0:T(8,128)(2,1)S(1)}, bf16[56,1024]{1,0:T(8,128)(2,1)S(1)}, u32[]{:S(2)}, u32[]{:S(2)}) collective-permute-start(bf16[56,1024]{1,0:T(8,128)(2,1)S(1)} %pad_maximum_fusion.3.own_ref), channel_id=1, source_target_pairs={{0,32},{32,64},{64,96},{96,128},{128,160},{160,192},{192,224},{224... | collective-permute-start | bytes 344072 | tf_op jit(solution)/shard_map/ppermute | solution.py:75
  55.7 0.1 collective-permute-start.1
  55.8 3.5 %collective-permute-done.up_ref = bf16[56,1024]{1,0:T(8,128)(2,1)S(1)} collective-permute-done((bf16[56,1024]{1,0:T(8,128)(2,1)S(1)}, bf16[56,1024]{1,0:T(8,128)(2,1)S(1)}, u32[]{:S(2)}, u32[]{:S(2)}) %collective-permute-start) | collective-permute-done | bytes 114720 | tf_op jit(solution)/shard_map/ppermute | solution.py:75
  59.3 1.8 %collective-permute-done.1.down_ref = bf16[56,1024]{1,0:T(8,128)(2,1)S(1)} collective-permute-done((bf16[56,1024]{1,0:T(8,128)(2,1)S(1)}, bf16[56,1024]{1,0:T(8,128)(2,1)S(1)}, u32[]{:S(2)}, u32[]{:S(2)}) %collective-permute-start.1) | collective-permute-done | bytes 114720 | tf_op jit(solution)/shard_map/ppermute | solution.py:75
  61.2 5.3 %collective-permute-start.2 = (bf16[168,1024]{1,0:T(8,128)(2,1)S(1)}, bf16[168,1024]{1,0:T(8,128)(2,1)S(1)}, u32[]{:S(2)}, u32[]{:S(2)}) collective-permute-start(bf16[168,1024]{1,0:T(8,128)(2,1)S(1)} %pad_maximum_fusion), channel_id=1, source_target_pairs={{0,96},{32,128},{64,160},{96,192},{128,224},{160,0},{192,32},{224,... | collective-permute-start | bytes 1032200 | tf_op jit(solution)/shard_map/ppermute | solution.py:75
  66.6 0.1 collective-permute-start.3
  67.3 17.0 %collective-permute-done.3.far_down_ref = bf16[112,1024]{1,0:T(8,128)(2,1)S(1)} collective-permute-done((bf16[112,1024]{1,0:T(8,128)(2,1)S(1)}, bf16[112,1024]{1,0:T(8,128)(2,1)S(1)}, u32[]{:S(2)}, u32[]{:S(2)}) %collective-permute-start.3) | collective-permute-done | bytes 229408 | tf_op jit(solution)/shard_map/ppermute | solution.py:75
  84.3 4.2 %collective-permute-done.2.far_up_ref = bf16[168,1024]{1,0:T(8,128)(2,1)S(1)} collective-permute-done((bf16[168,1024]{1,0:T(8,128)(2,1)S(1)}, bf16[168,1024]{1,0:T(8,128)(2,1)S(1)}, u32[]{:S(2)}, u32[]{:S(2)}) %collective-permute-start.2) | collective-permute-done | bytes 344096 | tf_op jit(solution)/shard_map/ppermute | solution.py:75
  88.5 0.0 copy-done.2
  88.5 0.0 copy-done
  88.5 0.0 copy-done.3
  88.6 0.7 copy-done.4
  89.3 2.4 %shard_map.37 = (bf16[256,2048]{1,0:T(8,128)(2,1)}, f32[256,128]{1,0:T(8,128)}) custom-call(s32[1]{0:T(128)} %bitcast.at_ref, bf16[56,1024]{1,0:T(8,128)(2,1)} %copy-done.2, bf16[56,1024]{1,0:T(8,128)(2,1)} %copy-done, bf16[56,1024]{1,0:T(8,128)(2,1)} %copy-done.3, bf16[168,1024]{1,0:T(8,128)(2,1)} %copy-done.4, bf16[112,1024]{1,0:T(8,128)(2,1)} %copy-done.5), custom_call_target="tpu_custom_call" | custom-call | tf_op jit(solution)/shard_map/pallas_call | solution.py:62
  91.6 7.0 %shard_map.38 = f32[248,2048]{1,0:T(8,128)} custom-call(f32[1]{0:T(128)S(6)} %copy.4.spread_ref, bf16[256,2048]{1,0:T(8,128)(2,1)} %get-tuple-element.7.t_all, f32[256,128]{1,0:T(8,128)} %get-tuple-element.8.norm_ref, bf16[16,56,2048]{2,1,0:T(8,128)(2,1)} %all_to_all.5.source_ref), custom_call_target="tpu_custom_call" | custom-call | tf_op jit(solution)/shard_map/pallas_call | solution.py:115
  98.6 0.0 collective-permute-done.4.source_ref
  98.6 6.9 %shard_map.39 = f32[248,2048]{1,0:T(8,128)} custom-call(f32[1]{0:T(128)S(6)} %copy.4.spread_ref, bf16[256,2048]{1,0:T(8,128)(2,1)} %get-tuple-element.7.t_all, f32[256,128]{1,0:T(8,128)} %get-tuple-element.8.norm_ref, bf16[16,56,2048]{2,1,0:T(8,128)(2,1)} %collective-permute-done.4.source_ref), custom_call_target="tpu_custom_call" | custom-call | tf_op jit(solution)/shard_map/pallas_call | solution.py:115
  105.5 2.5 %add_multiply_fusion = f32[248,2048]{1,0:T(8,128)S(1)} fusion(f32[248,2048]{1,0:T(8,128)} %shard_map.38, f32[248,2048]{1,0:T(8,128)} %shard_map.39), kind=kLoop, calls=%fused_computation | loop fusion | flops 1015808 | bytes 6094848 | tf_op jit(solution)/shard_map/div | solution.py:148
  108.0 0.0 copy-start.6
  108.0 28.8 %fusion = f32[32,2048]{1,0:T(8,128)S(1)} fusion(f32[248,2048]{1,0:T(8,128)S(1)} %add_multiply_fusion), kind=kCustom, calls=%all-reduce-scatter | all-reduce-scatter fusion | flops 524289 | bytes 2294784
  136.8 2.6 %collective-permute-start.5 = (f32[7,2048]{1,0:T(8,128)S(1)}, f32[7,2048]{1,0:T(8,128)S(1)}, u32[]{:S(2)}, u32[]{:S(2)}) collective-permute-start(f32[7,2048]{1,0:T(8,128)S(1)} %slice.13), channel_id=1, source_target_pairs={{0,32},{32,64},{64,96},{96,128},{128,160},{160,192},{192,224},{1,3... | collective-permute-start | bytes 172040
  139.4 0.0 copy-done.6
  139.4 0.6 dynamic-slice.4
  140.7 2.3 %collective-permute-done.5 = f32[7,2048]{1,0:T(8,128)S(1)} collective-permute-done((f32[7,2048]{1,0:T(8,128)S(1)}, f32[7,2048]{1,0:T(8,128)S(1)}, u32[]{:S(2)}, u32[]{:S(2)}) %collective-permute-start.5) | collective-permute-done | bytes 57376
  142.9 0.2 concatenate.18
  143.2 0.7 constant_dynamic-slice_fusion
  (10 shorter events, 0.1 us)
Async XLA Ops:
  1.5 52.2 %copy-start.1 = (bf16[28,2048]{1,0:T(8,128)(2,1)S(1)}, bf16[28,2048]{1,0:T(8,128)(2,1)}, u32[]{:S(2)}) copy-start(bf16[28,2048]{1,0:T(8,128)(2,1)} %param.3) | copy-start | bytes 344068
  53.6 45.0 %collective-permute-start.4 = (bf16[16,56,2048]{2,1,0:T(8,128)(2,1)}, bf16[16,56,2048]{2,1,0:T(8,128)(2,1)}, u32[]{:S(2)}, u32[]{:S(2)}) collective-permute-start(bf16[16,56,2048]{2,1,0:T(8,128)(2,1)} %all_to_all.5.source_ref), channel_id=1, source_target_pairs={{0,2},{2,0},{1,3},{3,1},{4,6},{6,4},{5,7},{7,5},{8,10},{10,8},{9,1... | collective-permute-start | bytes 11010056 | tf_op jit(solution)/shard_map/ppermute | solution.py:145
  53.7 34.8 %copy-start.2 = (bf16[56,1024]{1,0:T(8,128)(2,1)}, bf16[56,1024]{1,0:T(8,128)(2,1)S(1)}, u32[]{:S(2)}) copy-start(bf16[56,1024]{1,0:T(8,128)(2,1)S(1)} %pad_maximum_fusion.3.own_ref) | copy-start | bytes 344068
  53.7 5.6 %collective-permute-start = (bf16[56,1024]{1,0:T(8,128)(2,1)S(1)}, bf16[56,1024]{1,0:T(8,128)(2,1)S(1)}, u32[]{:S(2)}, u32[]{:S(2)}) collective-permute-start(bf16[56,1024]{1,0:T(8,128)(2,1)S(1)} %pad_maximum_fusion.3.own_ref), channel_id=1, source_target_pairs={{0,32},{32,64},{64,96},{96,128},{128,160},{160,192},{192,224},{224... | collective-permute-start | bytes 344072 | tf_op jit(solution)/shard_map/ppermute | solution.py:75
  55.7 5.5 %collective-permute-start.1 = (bf16[56,1024]{1,0:T(8,128)(2,1)S(1)}, bf16[56,1024]{1,0:T(8,128)(2,1)S(1)}, u32[]{:S(2)}, u32[]{:S(2)}) collective-permute-start(bf16[56,1024]{1,0:T(8,128)(2,1)S(1)} %pad_maximum_fusion.3.own_ref), channel_id=1, source_target_pairs={{0,224},{32,0},{64,32},{96,64},{128,96},{160,128},{192,160},{224,1... | collective-permute-start | bytes 344072 | tf_op jit(solution)/shard_map/ppermute | solution.py:75
  59.3 29.2 %copy-start = (bf16[56,1024]{1,0:T(8,128)(2,1)}, bf16[56,1024]{1,0:T(8,128)(2,1)S(1)}, u32[]{:S(2)}) copy-start(bf16[56,1024]{1,0:T(8,128)(2,1)S(1)} %collective-permute-done.up_ref) | copy-start | bytes 344068
  61.2 27.4 %copy-start.3 = (bf16[56,1024]{1,0:T(8,128)(2,1)}, bf16[56,1024]{1,0:T(8,128)(2,1)S(1)}, u32[]{:S(2)}) copy-start(bf16[56,1024]{1,0:T(8,128)(2,1)S(1)} %collective-permute-done.1.down_ref) | copy-start | bytes 344068
  61.2 27.3 %collective-permute-start.2 = (bf16[168,1024]{1,0:T(8,128)(2,1)S(1)}, bf16[168,1024]{1,0:T(8,128)(2,1)S(1)}, u32[]{:S(2)}, u32[]{:S(2)}) collective-permute-start(bf16[168,1024]{1,0:T(8,128)(2,1)S(1)} %pad_maximum_fusion), channel_id=1, source_target_pairs={{0,96},{32,128},{64,160},{96,192},{128,224},{160,0},{192,32},{224,... | collective-permute-start | bytes 1032200 | tf_op jit(solution)/shard_map/ppermute | solution.py:75
  66.6 17.8 %collective-permute-start.3 = (bf16[112,1024]{1,0:T(8,128)(2,1)S(1)}, bf16[112,1024]{1,0:T(8,128)(2,1)S(1)}, u32[]{:S(2)}, u32[]{:S(2)}) collective-permute-start(bf16[112,1024]{1,0:T(8,128)(2,1)S(1)} %pad_maximum_fusion.1), channel_id=1, source_target_pairs={{0,160},{32,192},{64,224},{96,0},{128,32},{160,64},{192,96},{224,1... | collective-permute-start | bytes 688136 | tf_op jit(solution)/shard_map/ppermute | solution.py:75
  84.3 4.2 %copy-start.5 = (bf16[112,1024]{1,0:T(8,128)(2,1)}, bf16[112,1024]{1,0:T(8,128)(2,1)S(1)}, u32[]{:S(2)}) copy-start(bf16[112,1024]{1,0:T(8,128)(2,1)S(1)} %collective-permute-done.3.far_down_ref) | copy-start | bytes 688132
  88.5 0.7 copy-start.4
  108.0 31.5 %copy-start.6 = (u32[256]{0:T(256)S(1)}, u32[256]{0:T(256)}, u32[]{:S(2)}) copy-start(u32[256]{0:T(256)} %constant.13) | copy-start | bytes 3076
  136.8 6.2 %collective-permute-start.5 = (f32[7,2048]{1,0:T(8,128)S(1)}, f32[7,2048]{1,0:T(8,128)S(1)}, u32[]{:S(2)}, u32[]{:S(2)}) collective-permute-start(f32[7,2048]{1,0:T(8,128)S(1)} %slice.13), channel_id=1, source_target_pairs={{0,32},{32,64},{64,96},{96,128},{128,160},{160,192},{192,224},{1,3... | collective-permute-start | bytes 172040

commit v5 on v4

--- a/solution.py
+++ b/solution.py
@@ -6,7 +6,6 @@
 from jax.sharding import Mesh, PartitionSpec as P
 
 
-PLANE = ("x", "yh", "yl")
 AXES = ("z", "x", "yl", "c", "yh")
 POPULATION = 7168
 ROWS = 28
@@ -18,11 +17,33 @@
 STEP = 8
 
 
-def sent_to_all(value, axis):
-    count = lax.axis_size(axis)
-    return lax.all_to_all(
-        jnp.broadcast_to(value[None], (count, *value.shape)), axis, 0, 0, tiled=True
+def device_at(z, x, y, core):
+    return (((z * 4 + x) * 2 + y % 2) * 2 + core) * 2 + y // 2
+
+
+def plane_lines(along_x):
+    groups = []
+    for z in range(TARGETS):
+        for core in range(2):
+            for at in range(4):
+                if (core == 0) == along_x:
+                    groups.append([device_at(z, i, at, core) for i in range(4)])
+                else:
+                    groups.append([device_at(z, at, i, core) for i in range(4)])
+    return groups
+
+
+def sent_along(value, groups):
+    count = len(groups[0])
+    arrived = lax.all_to_all(
+        jnp.broadcast_to(value[None], (count, *value.shape)),
+        AXES,
+        0,
+        0,
+        tiled=True,
+        axis_index_groups=groups,
     )
+    return arrived.reshape(count * value.shape[0], *value.shape[1:])
 
 
 def padded(rows):
@@ -139,9 +160,9 @@
     up, down = moved(own_piece, 1), moved(own_piece, -1)
     far_up = moved(jnp.concatenate([down, own_piece, up], axis=0), 3)
     far_down = moved(jnp.concatenate([up, own_piece], axis=0), -3)
-    pieces = [own_piece, up, down, far_up, far_down]
-    targets, norms = prepared(at, pieces)
-    own = sent_to_all(jnp.concatenate([particles, scores], axis=0), PLANE)
+    targets, norms = prepared(at, [own_piece, up, down, far_up, far_down])
+    line = sent_along(jnp.concatenate([particles, scores], axis=0), plane_lines(True))
+    own = sent_along(line, plane_lines(False)).reshape(PIECES, 2 * ROWS, DIM)
     other = lax.ppermute(own, "c", swap)
     mine = half(spread, targets, norms, own)
     theirs = half(spread, targets, norms, other)

time: 144 us -> 136 us (0.944)
  blocking collectives: 81 us -> 72.5 us
    all_to_all x1 -> x2, blocking collectives: 52.2 us -> 43.7 us  [sent_along(): lax.all_to_all(jnp.broadcast_to(value[None], (count, *value.shape)), AXES...]
  transfers between devices with their start and end apart: 6 -> 6, of which waited for: 5 -> 5; matrix products, arithmetic and copies ran while one was open for 0% -> 1% of each run, Pallas kernels for 6% -> 7%
where the time goes in v5:
time: 136 us
  blocking collectives  72.5 us (53%)
  waiting for transfers between devices  28.8 us (21%)
  Pallas kernels  16.2 us (12%)
  starting transfers between devices  10.2 us (7%)
  other arithmetic  3.57 us (3%)
  local copies, waits for them, and re-layouts  2.85 us (2%)
  between operations  1.44 us (1%)
    all_to_all x2, blocking collectives, sent_along(): lax.all_to_all(jnp.broadcast_to(value[None], (count, *value.shape)), AXES...  43.7 us
    unnamed x1, blocking collectives  28.8 us
    ppermute x4, waiting for transfers between devices, moved(): lax.ppermute(value, 'z', [(i, (i + steps) % TARGETS) for i in range(TARGE...  26.6 us
    pallas_call x2, Pallas kernels, half(): pl.pallas_call(half_kernel, grid=(PIECES // STEP,), in_specs=[pl.BlockSpe...  13.8 us
    ppermute x4, starting transfers between devices, moved(): lax.ppermute(value, 'z', [(i, (i + steps) % TARGETS) for i in range(TARGE...  7.5 us
  transfers between devices with their start and end apart: 6, of which 5 were waited for; matrix products, arithmetic and copies ran while one was open for 1% of the time, Pallas kernels for 7%

profile of v5, /device:TPU:32, one launch (start us, length us, event | category | flops | bytes accessed | tf_op | source)
XLA Modules:
  0.0 135.6 jit_solution(7497120118430312794)
XLA Ops:
  0.0 1.0 pad_maximum_fusion.2
  1.0 0.1 broadcast_in_dim.17
  1.1 14.3 %all_to_all.10 = bf16[4,56,2048]{2,1,0:T(8,128)(2,1)S(1)} all-to-all(bf16[4,56,2048]{2,1,0:T(8,128)(2,1)S(1)} %broadcast_in_dim.17), channel_id=1, replica_groups={{0,8,16,24},{4,12,20,28},{1,9,17,25},{5,13,21,29},{2,6,3,7},{10,14,11,1..., dimensions={0} | all-to-all | bytes 1835008 | tf_op jit(solution)/shard_map/all_to_all | solution.py:38
  15.4 0.5 broadcast_in_dim.19
  15.9 0.0 copy-start.1
  15.9 29.4 %all_to_all.11 = bf16[4,224,2048]{2,1,0:T(8,128)(2,1)} all-to-all(bf16[4,224,2048]{2,1,0:T(8,128)(2,1)S(1)} %broadcast_in_dim.19), channel_id=1, replica_groups={{0,4,1,5},{8,12,9,13},{16,20,17,21},{24,28,25,29},{2,10,18,26},{6,14,22..., dimensions={0} | all-to-all | bytes 7340032 | tf_op jit(solution)/shard_map/all_to_all | solution.py:38
  45.3 0.0 collective-permute-start.4
  45.3 0.0 copy-done.1
  45.4 0.0 copy-start.2
  45.4 2.0 %collective-permute-start = (bf16[56,1024]{1,0:T(8,128)(2,1)S(1)}, bf16[56,1024]{1,0:T(8,128)(2,1)S(1)}, u32[]{:S(2)}, u32[]{:S(2)}) collective-permute-start(bf16[56,1024]{1,0:T(8,128)(2,1)S(1)} %pad_maximum_fusion.3.own_ref), channel_id=1, source_target_pairs={{0,32},{32,64},{64,96},{96,128},{128,160},{160,192},{192,224},{224... | collective-permute-start | bytes 344072 | tf_op jit(solution)/shard_map/ppermute | solution.py:96
  47.4 0.1 collective-permute-start.1
  47.5 3.5 %collective-permute-done.up_ref = bf16[56,1024]{1,0:T(8,128)(2,1)S(1)} collective-permute-done((bf16[56,1024]{1,0:T(8,128)(2,1)S(1)}, bf16[56,1024]{1,0:T(8,128)(2,1)S(1)}, u32[]{:S(2)}, u32[]{:S(2)}) %collective-permute-start) | collective-permute-done | bytes 114720 | tf_op jit(solution)/shard_map/ppermute | solution.py:96
  51.0 1.8 %collective-permute-done.1.down_ref = bf16[56,1024]{1,0:T(8,128)(2,1)S(1)} collective-permute-done((bf16[56,1024]{1,0:T(8,128)(2,1)S(1)}, bf16[56,1024]{1,0:T(8,128)(2,1)S(1)}, u32[]{:S(2)}, u32[]{:S(2)}) %collective-permute-start.1) | collective-permute-done | bytes 114720 | tf_op jit(solution)/shard_map/ppermute | solution.py:96
  52.9 5.3 %collective-permute-start.2 = (bf16[168,1024]{1,0:T(8,128)(2,1)S(1)}, bf16[168,1024]{1,0:T(8,128)(2,1)S(1)}, u32[]{:S(2)}, u32[]{:S(2)}) collective-permute-start(bf16[168,1024]{1,0:T(8,128)(2,1)S(1)} %pad_maximum_fusion), channel_id=1, source_target_pairs={{0,96},{32,128},{64,160},{96,192},{128,224},{160,0},{192,32},{224,... | collective-permute-start | bytes 1032200 | tf_op jit(solution)/shard_map/ppermute | solution.py:96
  58.2 0.1 collective-permute-start.3
  59.0 17.0 %collective-permute-done.3.far_down_ref = bf16[112,1024]{1,0:T(8,128)(2,1)S(1)} collective-permute-done((bf16[112,1024]{1,0:T(8,128)(2,1)S(1)}, bf16[112,1024]{1,0:T(8,128)(2,1)S(1)}, u32[]{:S(2)}, u32[]{:S(2)}) %collective-permute-start.3) | collective-permute-done | bytes 229408 | tf_op jit(solution)/shard_map/ppermute | solution.py:96
  76.0 4.2 %collective-permute-done.2.far_up_ref = bf16[168,1024]{1,0:T(8,128)(2,1)S(1)} collective-permute-done((bf16[168,1024]{1,0:T(8,128)(2,1)S(1)}, bf16[168,1024]{1,0:T(8,128)(2,1)S(1)}, u32[]{:S(2)}, u32[]{:S(2)}) %collective-permute-start.2) | collective-permute-done | bytes 344096 | tf_op jit(solution)/shard_map/ppermute | solution.py:96
  80.2 0.0 copy-done.2
  80.2 0.0 copy-done
  80.2 0.7 copy-done.4
  80.9 2.4 %shard_map.37 = (bf16[256,2048]{1,0:T(8,128)(2,1)}, f32[256,128]{1,0:T(8,128)}) custom-call(s32[1]{0:T(128)} %bitcast.at_ref, bf16[56,1024]{1,0:T(8,128)(2,1)} %copy-done.2, bf16[56,1024]{1,0:T(8,128)(2,1)} %copy-done, bf16[56,1024]{1,0:T(8,128)(2,1)} %copy-done.3, bf16[168,1024]{1,0:T(8,128)(2,1)} %copy-done.4, bf16[112,1024]{1,0:T(8,128)(2,1)} %copy-done.5), custom_call_target="tpu_custom_call" | custom-call | tf_op jit(solution)/shard_map/pallas_call | solution.py:83
  83.3 7.0 %shard_map.38 = f32[248,2048]{1,0:T(8,128)} custom-call(f32[1]{0:T(128)S(6)} %copy.4.spread_ref, bf16[256,2048]{1,0:T(8,128)(2,1)} %get-tuple-element.7.t_all, f32[256,128]{1,0:T(8,128)} %get-tuple-element.8.norm_ref, bf16[16,56,2048]{2,1,0:T(8,128)(2,1)} %bitcast.2.source_ref), custom_call_target="tpu_custom_call" | custom-call | tf_op jit(solution)/shard_map/pallas_call | solution.py:136
  90.3 0.0 collective-permute-done.4.source_ref
  90.3 6.9 %shard_map.39 = f32[248,2048]{1,0:T(8,128)} custom-call(f32[1]{0:T(128)S(6)} %copy.4.spread_ref, bf16[256,2048]{1,0:T(8,128)(2,1)} %get-tuple-element.7.t_all, f32[256,128]{1,0:T(8,128)} %get-tuple-element.8.norm_ref, bf16[16,56,2048]{2,1,0:T(8,128)(2,1)} %collective-permute-done.4.source_ref), custom_call_target="tpu_custom_call" | custom-call | tf_op jit(solution)/shard_map/pallas_call | solution.py:136
  97.1 2.5 %add_multiply_fusion = f32[248,2048]{1,0:T(8,128)S(1)} fusion(f32[248,2048]{1,0:T(8,128)} %shard_map.38, f32[248,2048]{1,0:T(8,128)} %shard_map.39), kind=kLoop, calls=%fused_computation | loop fusion | flops 1015808 | bytes 6094848 | tf_op jit(solution)/shard_map/div | solution.py:169
  99.6 0.0 copy-start.6
  99.6 28.8 %fusion = f32[32,2048]{1,0:T(8,128)S(1)} fusion(f32[248,2048]{1,0:T(8,128)S(1)} %add_multiply_fusion), kind=kCustom, calls=%all-reduce-scatter | all-reduce-scatter fusion | flops 524289 | bytes 2294784
  128.4 2.6 %collective-permute-start.5 = (f32[7,2048]{1,0:T(8,128)S(1)}, f32[7,2048]{1,0:T(8,128)S(1)}, u32[]{:S(2)}, u32[]{:S(2)}) collective-permute-start(f32[7,2048]{1,0:T(8,128)S(1)} %slice.13), channel_id=1, source_target_pairs={{0,32},{32,64},{64,96},{96,128},{128,160},{160,192},{192,224},{1,3... | collective-permute-start | bytes 172040
  131.1 0.6 dynamic-slice.4
  132.3 2.3 %collective-permute-done.5 = f32[7,2048]{1,0:T(8,128)S(1)} collective-permute-done((f32[7,2048]{1,0:T(8,128)S(1)}, f32[7,2048]{1,0:T(8,128)S(1)}, u32[]{:S(2)}, u32[]{:S(2)}) %collective-permute-start.5) | collective-permute-done | bytes 57376
  134.6 0.2 concatenate.18
  134.9 0.7 constant_dynamic-slice_fusion
  (12 shorter events, 0.1 us)
Async XLA Ops:
  15.9 29.5 %copy-start.1 = (bf16[28,2048]{1,0:T(8,128)(2,1)S(1)}, bf16[28,2048]{1,0:T(8,128)(2,1)}, u32[]{:S(2)}) copy-start(bf16[28,2048]{1,0:T(8,128)(2,1)} %param.3) | copy-start | bytes 344068
  45.3 45.0 %collective-permute-start.4 = (bf16[16,56,2048]{2,1,0:T(8,128)(2,1)}, bf16[16,56,2048]{2,1,0:T(8,128)(2,1)}, u32[]{:S(2)}, u32[]{:S(2)}) collective-permute-start(bf16[16,56,2048]{2,1,0:T(8,128)(2,1)} %bitcast.2.source_ref), channel_id=1, source_target_pairs={{0,2},{2,0},{1,3},{3,1},{4,6},{6,4},{5,7},{7,5},{8,10},{10,8},{9,1... | collective-permute-start | bytes 11010056 | tf_op jit(solution)/shard_map/ppermute | solution.py:166
  45.4 34.8 %copy-start.2 = (bf16[56,1024]{1,0:T(8,128)(2,1)}, bf16[56,1024]{1,0:T(8,128)(2,1)S(1)}, u32[]{:S(2)}) copy-start(bf16[56,1024]{1,0:T(8,128)(2,1)S(1)} %pad_maximum_fusion.3.own_ref) | copy-start | bytes 344068
  45.4 5.6 %collective-permute-start = (bf16[56,1024]{1,0:T(8,128)(2,1)S(1)}, bf16[56,1024]{1,0:T(8,128)(2,1)S(1)}, u32[]{:S(2)}, u32[]{:S(2)}) collective-permute-start(bf16[56,1024]{1,0:T(8,128)(2,1)S(1)} %pad_maximum_fusion.3.own_ref), channel_id=1, source_target_pairs={{0,32},{32,64},{64,96},{96,128},{128,160},{160,192},{192,224},{224... | collective-permute-start | bytes 344072 | tf_op jit(solution)/shard_map/ppermute | solution.py:96
  47.4 5.5 %collective-permute-start.1 = (bf16[56,1024]{1,0:T(8,128)(2,1)S(1)}, bf16[56,1024]{1,0:T(8,128)(2,1)S(1)}, u32[]{:S(2)}, u32[]{:S(2)}) collective-permute-start(bf16[56,1024]{1,0:T(8,128)(2,1)S(1)} %pad_maximum_fusion.3.own_ref), channel_id=1, source_target_pairs={{0,224},{32,0},{64,32},{96,64},{128,96},{160,128},{192,160},{224,1... | collective-permute-start | bytes 344072 | tf_op jit(solution)/shard_map/ppermute | solution.py:96
  51.0 29.2 %copy-start = (bf16[56,1024]{1,0:T(8,128)(2,1)}, bf16[56,1024]{1,0:T(8,128)(2,1)S(1)}, u32[]{:S(2)}) copy-start(bf16[56,1024]{1,0:T(8,128)(2,1)S(1)} %collective-permute-done.up_ref) | copy-start | bytes 344068
  52.8 27.4 %copy-start.3 = (bf16[56,1024]{1,0:T(8,128)(2,1)}, bf16[56,1024]{1,0:T(8,128)(2,1)S(1)}, u32[]{:S(2)}) copy-start(bf16[56,1024]{1,0:T(8,128)(2,1)S(1)} %collective-permute-done.1.down_ref) | copy-start | bytes 344068
  52.9 27.3 %collective-permute-start.2 = (bf16[168,1024]{1,0:T(8,128)(2,1)S(1)}, bf16[168,1024]{1,0:T(8,128)(2,1)S(1)}, u32[]{:S(2)}, u32[]{:S(2)}) collective-permute-start(bf16[168,1024]{1,0:T(8,128)(2,1)S(1)} %pad_maximum_fusion), channel_id=1, source_target_pairs={{0,96},{32,128},{64,160},{96,192},{128,224},{160,0},{192,32},{224,... | collective-permute-start | bytes 1032200 | tf_op jit(solution)/shard_map/ppermute | solution.py:96
  58.2 17.8 %collective-permute-start.3 = (bf16[112,1024]{1,0:T(8,128)(2,1)S(1)}, bf16[112,1024]{1,0:T(8,128)(2,1)S(1)}, u32[]{:S(2)}, u32[]{:S(2)}) collective-permute-start(bf16[112,1024]{1,0:T(8,128)(2,1)S(1)} %pad_maximum_fusion.1), channel_id=1, source_target_pairs={{0,160},{32,192},{64,224},{96,0},{128,32},{160,64},{192,96},{224,1... | collective-permute-start | bytes 688136 | tf_op jit(solution)/shard_map/ppermute | solution.py:96
  76.0 4.2 %copy-start.5 = (bf16[112,1024]{1,0:T(8,128)(2,1)}, bf16[112,1024]{1,0:T(8,128)(2,1)S(1)}, u32[]{:S(2)}) copy-start(bf16[112,1024]{1,0:T(8,128)(2,1)S(1)} %collective-permute-done.3.far_down_ref) | copy-start | bytes 688132
  80.2 0.7 copy-start.4
  99.6 31.5 %copy-start.6 = (u32[256]{0:T(256)S(1)}, u32[256]{0:T(256)}, u32[]{:S(2)}) copy-start(u32[256]{0:T(256)} %constant.13) | copy-start | bytes 3076
  128.4 6.2 %collective-permute-start.5 = (f32[7,2048]{1,0:T(8,128)S(1)}, f32[7,2048]{1,0:T(8,128)S(1)}, u32[]{:S(2)}, u32[]{:S(2)}) collective-permute-start(f32[7,2048]{1,0:T(8,128)S(1)} %slice.13), channel_id=1, source_target_pairs={{0,32},{32,64},{64,96},{96,128},{128,160},{160,192},{192,224},{1,3... | collective-permute-start | bytes 172040

commit v6 on v5

v6 whole, which is shorter than its diff:
```python
import jax
import jax.numpy as jnp
from jax import lax
from jax.experimental import pallas as pl
from jax.experimental.pallas import tpu as pltpu
from jax.sharding import Mesh, PartitionSpec as P


AXES = ("z", "x", "yl", "c", "yh")
POPULATION = 7168
ROWS = 28
PAD = 32
SPAN = 31
CUT = 32
DIM = 2048
TARGETS = 8
PIECES = 16
STEP = 8
CHUNK = 4
WIDTH = 512


def device_at(z, x, y, core):
    return (((z * 4 + x) * 2 + y % 2) * 2 + core) * 2 + y // 2


def plane_lines(along_x):
    groups = []
    for z in range(TARGETS):
        for core in range(2):
            for at in range(4):
                if (core == 0) == along_x:
                    groups.append([device_at(z, i, at, core) for i in range(4)])
                else:
                    groups.append([device_at(z, at, i, core) for i in range(4)])
    return groups


def sent_along(value, groups):
    count = len(groups[0])
    arrived = lax.all_to_all(
        jnp.broadcast_to(value[None], (count, *value.shape)),
        AXES,
        0,
        0,
        tiled=True,
        axis_index_groups=groups,
    )
    return arrived.reshape(count * value.shape[0], *value.shape[1:])


def padded(rows):
    fill = jnp.zeros((PAD - ROWS, rows.shape[1]), rows.dtype)
    return jnp.concatenate([rows, fill], axis=0)


def row_norms(rows):
    wide = rows.astype(jnp.float32)
    return jnp.sum(wide * wide, axis=1, keepdims=True)


def prepare_kernel(at_ref, own_ref, up_ref, down_ref, far_up_ref, far_down_ref, low_ref, high_ref, t_all, norm_ref):
    half = DIM // 2

    def put(offset, piece):
        slot = lax.rem(at_ref[0] + TARGETS + offset, TARGETS)
        rows = pl.ds(pl.multiple_of(slot * PAD, PAD), PAD)
        left = padded(piece[:ROWS])
        right = padded(piece[ROWS:])
        t_all[rows, :half] = left
        t_all[rows, half:] = right
        norm_ref[rows, :] = jnp.broadcast_to(row_norms(left) + row_norms(right), (PAD, 128))

    put(0, own_ref[...])
    put(-1, up_ref[...])
    put(1, down_ref[...])
    put(-2, far_up_ref[: 2 * ROWS])
    put(-3, far_up_ref[2 * ROWS :])
    put(2, far_down_ref[: 2 * ROWS])
    put(3, far_down_ref[2 * ROWS :])
    put(4, jnp.concatenate([low_ref[...], high_ref[...]], axis=0))


def prepared(at, pieces):
    whole = TARGETS * PAD
    return pl.pallas_call(
        prepare_kernel,
        in_specs=[pl.BlockSpec(memory_space=pltpu.SMEM)]
        + [pl.BlockSpec(memory_space=pltpu.VMEM)] * len(pieces),
        out_specs=[pl.BlockSpec(memory_space=pltpu.VMEM)] * 2,
        out_shape=[
            jax.ShapeDtypeStruct((whole, DIM), jnp.bfloat16),
            jax.ShapeDtypeStruct((whole, 128), jnp.float32),
        ],
    )(at, *pieces)


def moved(value, steps):
    return lax.ppermute(value, "z", [(i, (i + steps) % TARGETS) for i in range(TARGETS)])


def half_kernel(first, spread_ref, t_hbm, norm_hbm, source_hbm, *refs):
    if first:
        out_hbm, t_all, norms, pieces, x_all, s_all, low_all, out, sems, out_sems = refs
    else:
        before_hbm, out_hbm, t_all, norms, pieces, x_all, s_all, low_all, out, before, sems, out_sems = refs
    inverse = 1.0 / spread_ref[0]
    chunks = PIECES // CHUNK
    loads = [
        pltpu.make_async_copy(
            source_hbm.at[pl.ds(j * CHUNK, CHUNK)], pieces.at[pl.ds(j * CHUNK, CHUNK)], sems.at[j]
        )
        for j in range(chunks)
    ]
    t_load = pltpu.make_async_copy(t_hbm, t_all, sems.at[chunks])
    norm_load = pltpu.make_async_copy(norm_hbm, norms, sems.at[chunks + 1])
    loads[0].start()
    t_load.start()
    norm_load.start()
    for load in loads[1:]:
        load.start()
    if not first:
        before_load = pltpu.make_async_copy(before_hbm, before, sems.at[chunks + 2])
        before_load.start()
    row_total = jnp.zeros((TARGETS * PAD, 1), jnp.float32)
    per_step = STEP // CHUNK
    for step in range(PIECES // STEP):
        for j in range(step * per_step, (step + 1) * per_step):
            loads[j].wait()
            for i in range(j * CHUNK, (j + 1) * CHUNK):
                x_all[pl.ds(i * PAD, PAD), :] = padded(pieces[i, :ROWS])
                s_all[pl.ds(i * PAD, PAD), :] = padded(pieces[i, ROWS:])
        if step == 0:
            t_load.wait()
            norm_load.wait()
        rows = pl.ds(step * STEP * PAD, STEP * PAD)
        source = x_all[rows, :]
        source_norm = row_norms(source)
        source_norm = jnp.transpose(jnp.broadcast_to(source_norm, (STEP * PAD, 128)))[:1]
        dots = lax.dot_general(
            t_all[...], source, (((1,), (1,)), ((), ())), preferred_element_type=jnp.float32
        )
        squared = jnp.maximum(norms[:, :1] + source_norm - 2.0 * dots, 0.0)
        weights = jnp.exp(-squared * inverse)
        column = lax.broadcasted_iota(jnp.int32, weights.shape, 1)
        weights = jnp.where(column % PAD < ROWS, weights, 0.0)
        low_all[:, rows] = weights.astype(jnp.bfloat16)
        row_total = row_total + jnp.sum(weights, axis=1, keepdims=True)
    if not first:
        before_load.wait()
    stores = []
    for n in range(DIM // WIDTH):
        columns = pl.ds(n * WIDTH, WIDTH)
        low = low_all[...]
        pull = jnp.dot(low, x_all[:, columns], preferred_element_type=jnp.float32)
        drive = jnp.dot(low, s_all[:, columns], preferred_element_type=jnp.float32)
        wide = t_all[:, columns].astype(jnp.float32)
        added = drive + (2.0 * inverse) * (wide * row_total - pull)
        for i in range(TARGETS):
            span = pl.ds(i * SPAN, SPAN)
            part = added[i * PAD : i * PAD + SPAN]
            if not first:
                part = (before[span, columns] + part) / POPULATION
            out[span, columns] = part
        stores.append(
            pltpu.make_async_copy(out.at[:, columns], out_hbm.at[:, columns], out_sems.at[n])
        )
        stores[-1].start()
    for store in stores:
        store.wait()


def half(spread, targets, norms, source, before=None):
    first = before is None
    whole = TARGETS * PAD
    result = (TARGETS * SPAN, DIM)
    args = [spread, targets, norms, source] + ([] if first else [before])
    scratch = [
        pltpu.VMEM((whole, DIM), jnp.bfloat16),
        pltpu.VMEM((whole, 128), jnp.float32),
        pltpu.VMEM((PIECES, 2 * ROWS, DIM), jnp.bfloat16),
        pltpu.VMEM((PIECES * PAD, DIM), jnp.bfloat16),
        pltpu.VMEM((PIECES * PAD, DIM), jnp.bfloat16),
        pltpu.VMEM((whole, PIECES * PAD), jnp.bfloat16),
        pltpu.VMEM(result, jnp.float32),
    ]
    if not first:
        scratch.append(pltpu.VMEM(result, jnp.float32))
    scratch += [
        pltpu.SemaphoreType.DMA((PIECES // CHUNK + 3,)),
        pltpu.SemaphoreType.DMA((DIM // WIDTH,)),
    ]

    def body(*refs):
        half_kernel(first, *refs)

    return pl.pallas_call(
        body,
        in_specs=[pl.BlockSpec(memory_space=pltpu.SMEM)]
        + [pl.BlockSpec(memory_space=pl.ANY)] * (len(args) - 1),
        out_specs=pl.BlockSpec(memory_space=pl.ANY),
        out_shape=jax.ShapeDtypeStruct(result, jnp.float32),
        scratch_shapes=scratch,
    )(*args)


def direction(particles, scores, spread):
    swap = [(0, 1), (1, 0)]
    at = lax.axis_index("z").astype(jnp.int32)[None]
    own_piece = jnp.concatenate([particles[:, : DIM // 2], particles[:, DIM // 2 :]], axis=0)
    up, down = moved(own_piece, 1), moved(own_piece, -1)
    far_up = moved(jnp.concatenate([own_piece, up], axis=0), 2)
    far_down = moved(jnp.concatenate([own_piece, down], axis=0), -2)
    low = moved(up[:CUT], 3)
    high = moved(down[CUT:], -3)
    targets, norms = prepared(at, [own_piece, up, down, far_up, far_down, low, high])
    line = sent_along(jnp.concatenate([particles, scores], axis=0), plane_lines(True))
    own = sent_along(line, plane_lines(False)).reshape(PIECES, 2 * ROWS, DIM)
    other = lax.ppermute(own, "c", swap)
    mine = half(spread, targets, norms, own)
    partial = half(spread, targets, norms, other, mine)
    total = lax.psum_scatter(partial, "z", scatter_dimension=0, tiled=True)
    return lax.optimization_barrier(total)[:ROWS]


def solution(mesh):
    fine = Mesh(mesh.devices.reshape(8, 4, 2, 2, 2), AXES)
    return jax.shard_map(
        direction,
        mesh=fine,
        in_specs=(P(AXES, None), P(AXES, None), P()),
        out_specs=P(AXES, None),
        check_vma=False,
    )
```

time: 136 us -> 126 us (0.926)
  waiting for transfers between devices: 28.8 us -> 18.8 us
  starting transfers between devices: 10.2 us -> 15.3 us
  other arithmetic: 3.57 us -> 1.08 us
  Pallas kernels: 16.2 us -> 14.2 us
    ppermute x4 -> x6, waiting for transfers between devices: 26.6 us -> 16.3 us  [moved(): lax.ppermute(value, 'z', [(i, (i + steps) % TARGETS) for i in range(TARGE...]
    ppermute x4 -> x6, starting transfers between devices: 7.5 us -> 12.8 us  [moved(): lax.ppermute(value, 'z', [(i, (i + steps) % TARGETS) for i in range(TARGE...]
    div x1 -> x0, other arithmetic: 2.47 us -> none  [direction(): partial = (mine + theirs) / POPULATION]
    pallas_call x2, Pallas kernels: 13.8 us -> 11.8 us  [half(): pl.pallas_call(body, in_specs=[pl.BlockSpec(memory_space=pltpu.SMEM)] + [...]
  transfers between devices with their start and end apart: 6 -> 8, of which waited for: 5 -> 4; matrix products, arithmetic and copies ran while one was open for 1% -> 1% of each run, Pallas kernels for 7% -> 6%
where the time goes in v6:
time: 126 us
  blocking collectives  72 us (57%)
  waiting for transfers between devices  18.8 us (15%)
  starting transfers between devices  15.3 us (12%)
  Pallas kernels  14.2 us (11%)
  local copies, waits for them, and re-layouts  2.88 us (2%)
  between operations  1.5 us (1%)
    all_to_all x2, blocking collectives, sent_along(): lax.all_to_all(jnp.broadcast_to(value[None], (count, *value.shape)), AXES...  43.7 us
    unnamed x1, blocking collectives  28.3 us
    ppermute x6, waiting for transfers between devices, moved(): lax.ppermute(value, 'z', [(i, (i + steps) % TARGETS) for i in range(TARGE...  16.3 us
    ppermute x6, starting transfers between devices, moved(): lax.ppermute(value, 'z', [(i, (i + steps) % TARGETS) for i in range(TARGE...  12.8 us
    pallas_call x2, Pallas kernels, half(): pl.pallas_call(body, in_specs=[pl.BlockSpec(memory_space=pltpu.SMEM)] + [...  11.8 us
  transfers between devices with their start and end apart: 8, of which 4 were waited for; matrix products, arithmetic and copies ran while one was open for 1% of the time, Pallas kernels for 6%

profile of v6, /device:TPU:32, one launch (start us, length us, event | category | flops | bytes accessed | tf_op | source)
XLA Modules:
  0.0 125.8 jit_solution(17451201600962103574)
XLA Ops:
  0.0 1.0 pad_maximum_fusion.3
  1.0 0.1 broadcast_in_dim.17
  1.1 14.3 %all_to_all.10 = bf16[4,56,2048]{2,1,0:T(8,128)(2,1)S(1)} all-to-all(bf16[4,56,2048]{2,1,0:T(8,128)(2,1)S(1)} %broadcast_in_dim.17), channel_id=1, replica_groups={{0,8,16,24},{4,12,20,28},{1,9,17,25},{5,13,21,29},{2,6,3,7},{10,14,11,1..., dimensions={0} | all-to-all | bytes 1835008 | tf_op jit(solution)/shard_map/all_to_all | solution.py:41
  15.4 0.5 broadcast_in_dim.19
  15.9 0.0 copy-start.2
  15.9 29.4 %all_to_all.11 = bf16[4,224,2048]{2,1,0:T(8,128)(2,1)} all-to-all(bf16[4,224,2048]{2,1,0:T(8,128)(2,1)S(1)} %broadcast_in_dim.19), channel_id=1, replica_groups={{0,4,1,5},{8,12,9,13},{16,20,17,21},{24,28,25,29},{2,10,18,26},{6,14,22..., dimensions={0} | all-to-all | bytes 7340032 | tf_op jit(solution)/shard_map/all_to_all | solution.py:41
  45.4 2.0 %collective-permute-start = (bf16[56,1024]{1,0:T(8,128)(2,1)S(1)}, bf16[56,1024]{1,0:T(8,128)(2,1)S(1)}, u32[]{:S(2)}, u32[]{:S(2)}) collective-permute-start(bf16[56,1024]{1,0:T(8,128)(2,1)S(1)} %pad_maximum_fusion.4.own_ref), channel_id=1, source_target_pairs={{0,32},{32,64},{64,96},{96,128},{128,160},{160,192},{192,224},{224... | collective-permute-start | bytes 344072 | tf_op jit(solution)/shard_map/ppermute | solution.py:99
  47.4 0.1 collective-permute-start.1
  47.5 3.5 %collective-permute-done.up_ref = bf16[56,1024]{1,0:T(8,128)(2,1)S(1)} collective-permute-done((bf16[56,1024]{1,0:T(8,128)(2,1)S(1)}, bf16[56,1024]{1,0:T(8,128)(2,1)S(1)}, u32[]{:S(2)}, u32[]{:S(2)}) %collective-permute-start) | collective-permute-done | bytes 114720 | tf_op jit(solution)/shard_map/ppermute | solution.py:99
  51.0 1.8 %collective-permute-done.1.down_ref = bf16[56,1024]{1,0:T(8,128)(2,1)S(1)} collective-permute-done((bf16[56,1024]{1,0:T(8,128)(2,1)S(1)}, bf16[56,1024]{1,0:T(8,128)(2,1)S(1)}, u32[]{:S(2)}, u32[]{:S(2)}) %collective-permute-start.1) | collective-permute-done | bytes 114720 | tf_op jit(solution)/shard_map/ppermute | solution.py:99
  52.8 0.1 pad_maximum_fusion.2
  52.9 5.6 %collective-permute-start.2 = (bf16[112,1024]{1,0:T(8,128)(2,1)S(1)}, bf16[112,1024]{1,0:T(8,128)(2,1)S(1)}, u32[]{:S(2)}, u32[]{:S(2)}) collective-permute-start(bf16[112,1024]{1,0:T(8,128)(2,1)S(1)} %get-tuple-element.10), channel_id=1, source_target_pairs={{0,64},{32,96},{64,128},{96,160},{128,192},{160,224},{192,0},{224,... | collective-permute-start | bytes 688136 | tf_op jit(solution)/shard_map/ppermute | solution.py:99
  58.5 0.0 collective-permute-start.3
  58.5 3.9 %collective-permute-start.4 = (bf16[32,1024]{1,0:T(8,128)(2,1)S(1)}, bf16[32,1024]{1,0:T(8,128)(2,1)S(1)}, u32[]{:S(2)}, u32[]{:S(2)}) collective-permute-start(bf16[32,1024]{1,0:T(8,128)(2,1)S(1)} %slice.20), channel_id=1, source_target_pairs={{0,96},{32,128},{64,160},{96,192},{128,224},{160,0},{192,32},{224,... | collective-permute-start | bytes 196616 | tf_op jit(solution)/shard_map/ppermute | solution.py:99
  62.3 1.3 %collective-permute-start.5 = (bf16[24,1024]{1,0:T(8,128)(2,1)S(1)}, bf16[24,1024]{1,0:T(8,128)(2,1)S(1)}, u32[]{:S(2)}, u32[]{:S(2)}) collective-permute-start(bf16[24,1024]{1,0:T(8,128)(2,1)S(1)} %slice.21), channel_id=1, source_target_pairs={{0,160},{32,192},{64,224},{96,0},{128,32},{160,64},{192,96},{224,1... | collective-permute-start | bytes 147464 | tf_op jit(solution)/shard_map/ppermute | solution.py:99
  64.3 11.0 %collective-permute-done.5.high_ref = bf16[24,1024]{1,0:T(8,128)(2,1)S(1)} collective-permute-done((bf16[24,1024]{1,0:T(8,128)(2,1)S(1)}, bf16[24,1024]{1,0:T(8,128)(2,1)S(1)}, u32[]{:S(2)}, u32[]{:S(2)}) %collective-permute-start.5) | collective-permute-done | bytes 49184 | tf_op jit(solution)/shard_map/ppermute | solution.py:99
  75.2 0.0 collective-permute-done.4.low_ref
  75.3 0.0 copy-start.4
  75.3 0.5 copy-done.7
  75.9 0.0 copy-done.6
  75.9 0.1 copy-done.4
  76.0 0.1 copy-done.5
  76.0 2.4 %shard_map.37 = (bf16[256,2048]{1,0:T(8,128)(2,1)}, f32[256,128]{1,0:T(8,128)}) custom-call(s32[1]{0:T(128)} %bitcast.at_ref, bf16[56,1024]{1,0:T(8,128)(2,1)} %copy-done.3, bf16[56,1024]{1,0:T(8,128)(2,1)} %copy-done, bf16[56,1024]{1,0:T(8,128)(2,1)} %copy-done.1, bf16[112,1024]{1,0:T(8,128)(2,1)} %copy-done.4, bf16[112,1024]{1,0:T(8,128)(2,1)} %copy-done.5, ...), custom_call_target="tpu_custom_call" | custom-call | tf_op jit(solution)/shard_map/pallas_call | solution.py:86
  78.5 5.7 %shard_map.38.refs_4_ = f32[248,2048]{1,0:T(8,128)} custom-call(f32[1]{0:T(128)S(6)} %copy.4.refs_0_, bf16[256,2048]{1,0:T(8,128)(2,1)} %get-tuple-element.7.refs_1_, f32[256,128]{1,0:T(8,128)} %get-tuple-element.8.refs_2_, bf16[16,56,2048]{2,1,0:T(8,128)(2,1)} %bitcast.2.refs_3_), custom_call_target="tpu_custom_call" | custom-call | tf_op jit(solution)/shard_map/pallas_call | solution.py:197
  84.2 6.1 %shard_map.39 = f32[248,2048]{1,0:T(8,128)} custom-call(f32[1]{0:T(128)S(6)} %copy.4.refs_0_, bf16[256,2048]{1,0:T(8,128)(2,1)} %get-tuple-element.7.refs_1_, f32[256,128]{1,0:T(8,128)} %get-tuple-element.8.refs_2_, bf16[16,56,2048]{2,1,0:T(8,128)(2,1)} %collective-permute-done.6.refs_3_, f32[248,2048]{1,0:T(8,128)} %shard_map.38.refs_4_), custom_call_target="tpu_custom_call" | custom-call | tf_op jit(solution)/shard_map/pallas_call | solution.py:197
  90.3 0.0 copy-start.8
  90.3 28.3 %fusion = f32[32,2048]{1,0:T(8,128)S(1)} fusion(f32[248,2048]{1,0:T(8,128)} %shard_map.39), kind=kCustom, calls=%all-reduce-scatter | all-reduce-scatter fusion | flops 524289 | bytes 2294784
  118.7 2.5 %collective-permute-start.7 = (f32[7,2048]{1,0:T(8,128)S(1)}, f32[7,2048]{1,0:T(8,128)S(1)}, u32[]{:S(2)}, u32[]{:S(2)}) collective-permute-start(f32[7,2048]{1,0:T(8,128)S(1)} %slice.23), channel_id=1, source_target_pairs={{0,32},{32,64},{64,96},{96,128},{128,160},{160,192},{192,224},{1,3... | collective-permute-start | bytes 172040
  121.1 0.6 dynamic-slice.4
  122.4 2.4 %collective-permute-done.7 = f32[7,2048]{1,0:T(8,128)S(1)} collective-permute-done((f32[7,2048]{1,0:T(8,128)S(1)}, f32[7,2048]{1,0:T(8,128)S(1)}, u32[]{:S(2)}, u32[]{:S(2)}) %collective-permute-start.7) | collective-permute-done | bytes 57376
  124.8 0.2 concatenate.18
  125.1 0.7 constant_dynamic-slice_fusion
  (20 shorter events, 0.1 us)
Async XLA Ops:
  15.9 29.5 %copy-start.2 = (bf16[28,2048]{1,0:T(8,128)(2,1)S(1)}, bf16[28,2048]{1,0:T(8,128)(2,1)}, u32[]{:S(2)}) copy-start(bf16[28,2048]{1,0:T(8,128)(2,1)} %param.3) | copy-start | bytes 344068
  45.3 38.9 %collective-permute-start.6 = (bf16[16,56,2048]{2,1,0:T(8,128)(2,1)}, bf16[16,56,2048]{2,1,0:T(8,128)(2,1)}, u32[]{:S(2)}, u32[]{:S(2)}) collective-permute-start(bf16[16,56,2048]{2,1,0:T(8,128)(2,1)} %bitcast.2.refs_3_), channel_id=1, source_target_pairs={{0,2},{2,0},{1,3},{3,1},{4,6},{6,4},{5,7},{7,5},{8,10},{10,8},{9,1... | collective-permute-start | bytes 11010056 | tf_op jit(solution)/shard_map/ppermute | solution.py:219
  45.4 29.9 %copy-start.3 = (bf16[56,1024]{1,0:T(8,128)(2,1)}, bf16[56,1024]{1,0:T(8,128)(2,1)S(1)}, u32[]{:S(2)}) copy-start(bf16[56,1024]{1,0:T(8,128)(2,1)S(1)} %pad_maximum_fusion.4.own_ref) | copy-start | bytes 344068
  45.4 5.6 %collective-permute-start = (bf16[56,1024]{1,0:T(8,128)(2,1)S(1)}, bf16[56,1024]{1,0:T(8,128)(2,1)S(1)}, u32[]{:S(2)}, u32[]{:S(2)}) collective-permute-start(bf16[56,1024]{1,0:T(8,128)(2,1)S(1)} %pad_maximum_fusion.4.own_ref), channel_id=1, source_target_pairs={{0,32},{32,64},{64,96},{96,128},{128,160},{160,192},{192,224},{224... | collective-permute-start | bytes 344072 | tf_op jit(solution)/shard_map/ppermute | solution.py:99
  47.4 5.5 %collective-permute-start.1 = (bf16[56,1024]{1,0:T(8,128)(2,1)S(1)}, bf16[56,1024]{1,0:T(8,128)(2,1)S(1)}, u32[]{:S(2)}, u32[]{:S(2)}) collective-permute-start(bf16[56,1024]{1,0:T(8,128)(2,1)S(1)} %pad_maximum_fusion.4.own_ref), channel_id=1, source_target_pairs={{0,224},{32,0},{64,32},{96,64},{128,96},{160,128},{192,160},{224,1... | collective-permute-start | bytes 344072 | tf_op jit(solution)/shard_map/ppermute | solution.py:99
  51.0 24.3 %copy-start = (bf16[56,1024]{1,0:T(8,128)(2,1)}, bf16[56,1024]{1,0:T(8,128)(2,1)S(1)}, u32[]{:S(2)}) copy-start(bf16[56,1024]{1,0:T(8,128)(2,1)S(1)} %collective-permute-done.up_ref) | copy-start | bytes 344068
  52.8 22.5 %copy-start.1 = (bf16[56,1024]{1,0:T(8,128)(2,1)}, bf16[56,1024]{1,0:T(8,128)(2,1)S(1)}, u32[]{:S(2)}) copy-start(bf16[56,1024]{1,0:T(8,128)(2,1)S(1)} %collective-permute-done.1.down_ref) | copy-start | bytes 344068
  52.9 22.4 %collective-permute-start.2 = (bf16[112,1024]{1,0:T(8,128)(2,1)S(1)}, bf16[112,1024]{1,0:T(8,128)(2,1)S(1)}, u32[]{:S(2)}, u32[]{:S(2)}) collective-permute-start(bf16[112,1024]{1,0:T(8,128)(2,1)S(1)} %get-tuple-element.10), channel_id=1, source_target_pairs={{0,64},{32,96},{64,128},{96,160},{128,192},{160,224},{192,0},{224,... | collective-permute-start | bytes 688136 | tf_op jit(solution)/shard_map/ppermute | solution.py:99
  58.5 16.8 %collective-permute-start.3 = (bf16[112,1024]{1,0:T(8,128)(2,1)S(1)}, bf16[112,1024]{1,0:T(8,128)(2,1)S(1)}, u32[]{:S(2)}, u32[]{:S(2)}) collective-permute-start(bf16[112,1024]{1,0:T(8,128)(2,1)S(1)} %get-tuple-element.9), channel_id=1, source_target_pairs={{0,192},{32,224},{64,0},{96,32},{128,64},{160,96},{192,128},{224,1... | collective-permute-start | bytes 688136 | tf_op jit(solution)/shard_map/ppermute | solution.py:99
  58.5 16.8 %collective-permute-start.4 = (bf16[32,1024]{1,0:T(8,128)(2,1)S(1)}, bf16[32,1024]{1,0:T(8,128)(2,1)S(1)}, u32[]{:S(2)}, u32[]{:S(2)}) collective-permute-start(bf16[32,1024]{1,0:T(8,128)(2,1)S(1)} %slice.20), channel_id=1, source_target_pairs={{0,96},{32,128},{64,160},{96,192},{128,224},{160,0},{192,32},{224,... | collective-permute-start | bytes 196616 | tf_op jit(solution)/shard_map/ppermute | solution.py:99
  62.3 12.9 %collective-permute-start.5 = (bf16[24,1024]{1,0:T(8,128)(2,1)S(1)}, bf16[24,1024]{1,0:T(8,128)(2,1)S(1)}, u32[]{:S(2)}, u32[]{:S(2)}) collective-permute-start(bf16[24,1024]{1,0:T(8,128)(2,1)S(1)} %slice.21), channel_id=1, source_target_pairs={{0,160},{32,192},{64,224},{96,0},{128,32},{160,64},{192,96},{224,1... | collective-permute-start | bytes 147464 | tf_op jit(solution)/shard_map/ppermute | solution.py:99
  75.2 0.6 copy-start.7
  75.3 0.6 copy-start.6
  75.3 0.7 copy-start.4
  75.3 0.8 copy-start.5
  90.3 30.8 %copy-start.8 = (u32[256]{0:T(256)S(1)}, u32[256]{0:T(256)}, u32[]{:S(2)}) copy-start(u32[256]{0:T(256)} %constant.10) | copy-start | bytes 3076
  118.7 6.2 %collective-permute-start.7 = (f32[7,2048]{1,0:T(8,128)S(1)}, f32[7,2048]{1,0:T(8,128)S(1)}, u32[]{:S(2)}, u32[]{:S(2)}) collective-permute-start(f32[7,2048]{1,0:T(8,128)S(1)} %slice.23), channel_id=1, source_target_pairs={{0,32},{32,64},{64,96},{96,128},{128,160},{160,192},{192,224},{1,3... | collective-permute-start | bytes 172040

commit v7 on v6

--- a/solution.py
+++ b/solution.py
@@ -16,8 +16,8 @@
 TARGETS = 8
 PIECES = 16
 STEP = 8
-CHUNK = 4
 WIDTH = 512
+VMEM_BYTES = 24 * 2**20
 
 
 def device_at(z, x, y, core):
@@ -92,6 +92,7 @@
             jax.ShapeDtypeStruct((whole, DIM), jnp.bfloat16),
             jax.ShapeDtypeStruct((whole, 128), jnp.float32),
         ],
+        compiler_params=pltpu.CompilerParams(vmem_limit_bytes=VMEM_BYTES),
     )(at, *pieces)
 
 
@@ -99,40 +100,17 @@
     return lax.ppermute(value, "z", [(i, (i + steps) % TARGETS) for i in range(TARGETS)])
 
 
-def half_kernel(first, spread_ref, t_hbm, norm_hbm, source_hbm, *refs):
+def half_kernel(first, spread_ref, t_all, norms, pieces, *refs):
     if first:
-        out_hbm, t_all, norms, pieces, x_all, s_all, low_all, out, sems, out_sems = refs
+        out, x_all, s_all, low_all = refs
     else:
-        before_hbm, out_hbm, t_all, norms, pieces, x_all, s_all, low_all, out, before, sems, out_sems = refs
+        before, out, x_all, s_all, low_all = refs
     inverse = 1.0 / spread_ref[0]
-    chunks = PIECES // CHUNK
-    loads = [
-        pltpu.make_async_copy(
-            source_hbm.at[pl.ds(j * CHUNK, CHUNK)], pieces.at[pl.ds(j * CHUNK, CHUNK)], sems.at[j]
-        )
-        for j in range(chunks)
-    ]
-    t_load = pltpu.make_async_copy(t_hbm, t_all, sems.at[chunks])
-    norm_load = pltpu.make_async_copy(norm_hbm, norms, sems.at[chunks + 1])
-    loads[0].start()
-    t_load.start()
-    norm_load.start()
-    for load in loads[1:]:
-        load.start()
-    if not first:
-        before_load = pltpu.make_async_copy(before_hbm, before, sems.at[chunks + 2])
-        before_load.start()
     row_total = jnp.zeros((TARGETS * PAD, 1), jnp.float32)
-    per_step = STEP // CHUNK
     for step in range(PIECES // STEP):
-        for j in range(step * per_step, (step + 1) * per_step):
-            loads[j].wait()
-            for i in range(j * CHUNK, (j + 1) * CHUNK):
-                x_all[pl.ds(i * PAD, PAD), :] = padded(pieces[i, :ROWS])
-                s_all[pl.ds(i * PAD, PAD), :] = padded(pieces[i, ROWS:])
-        if step == 0:
-            t_load.wait()
-            norm_load.wait()
+        for i in range(step * STEP, (step + 1) * STEP):
+            x_all[pl.ds(i * PAD, PAD), :] = padded(pieces[i, :ROWS])
+            s_all[pl.ds(i * PAD, PAD), :] = padded(pieces[i, ROWS:])
         rows = pl.ds(step * STEP * PAD, STEP * PAD)
         source = x_all[rows, :]
         source_norm = row_norms(source)
@@ -146,9 +124,6 @@
         weights = jnp.where(column % PAD < ROWS, weights, 0.0)
         low_all[:, rows] = weights.astype(jnp.bfloat16)
         row_total = row_total + jnp.sum(weights, axis=1, keepdims=True)
-    if not first:
-        before_load.wait()
-    stores = []
     for n in range(DIM // WIDTH):
         columns = pl.ds(n * WIDTH, WIDTH)
         low = low_all[...]
@@ -162,34 +137,14 @@
             if not first:
                 part = (before[span, columns] + part) / POPULATION
             out[span, columns] = part
-        stores.append(
-            pltpu.make_async_copy(out.at[:, columns], out_hbm.at[:, columns], out_sems.at[n])
-        )
-        stores[-1].start()
-    for store in stores:
-        store.wait()
 
 
 def half(spread, targets, norms, source, before=None):
     first = before is None
     whole = TARGETS * PAD
     result = (TARGETS * SPAN, DIM)
-    args = [spread, targets, norms, source] + ([] if first else [before])
-    scratch = [
-        pltpu.VMEM((whole, DIM), jnp.bfloat16),
-        pltpu.VMEM((whole, 128), jnp.float32),
-        pltpu.VMEM((PIECES, 2 * ROWS, DIM), jnp.bfloat16),
-        pltpu.VMEM((PIECES * PAD, DIM), jnp.bfloat16),
-        pltpu.VMEM((PIECES * PAD, DIM), jnp.bfloat16),
-        pltpu.VMEM((whole, PIECES * PAD), jnp.bfloat16),
-        pltpu.VMEM(result, jnp.float32),
-    ]
-    if not first:
-        scratch.append(pltpu.VMEM(result, jnp.float32))
-    scratch += [
-        pltpu.SemaphoreType.DMA((PIECES // CHUNK + 3,)),
-        pltpu.SemaphoreType.DMA((DIM // WIDTH,)),
-    ]
+    args = [targets, norms, source] + ([] if first else [before])
+    args = [pltpu.with_memory_space_constraint(a, pltpu.VMEM) for a in args]
 
     def body(*refs):
         half_kernel(first, *refs)
@@ -197,11 +152,16 @@
     return pl.pallas_call(
         body,
         in_specs=[pl.BlockSpec(memory_space=pltpu.SMEM)]
-        + [pl.BlockSpec(memory_space=pl.ANY)] * (len(args) - 1),
-        out_specs=pl.BlockSpec(memory_space=pl.ANY),
-        out_shape=jax.ShapeDtypeStruct(result, jnp.float32),
-        scratch_shapes=scratch,
-    )(*args)
+        + [pl.BlockSpec(memory_space=pltpu.VMEM)] * len(args),
+        out_specs=pl.BlockSpec(memory_space=pltpu.VMEM),
+        out_shape=pltpu.VMEM(result, jnp.float32),
+        scratch_shapes=[
+            pltpu.VMEM((PIECES * PAD, DIM), jnp.bfloat16),
+            pltpu.VMEM((PIECES * PAD, DIM), jnp.bfloat16),
+            pltpu.VMEM((whole, PIECES * PAD), jnp.bfloat16),
+        ],
+        compiler_params=pltpu.CompilerParams(vmem_limit_bytes=VMEM_BYTES),
+    )(spread, *args)
 
 
 def direction(particles, scores, spread):

time: 126 us -> 120 us (0.952)
  Pallas kernels: 14.2 us -> 9.24 us
    pallas_call x2, Pallas kernels: 11.8 us -> 8.99 us  [half(): pl.pallas_call(body, in_specs=[pl.BlockSpec(memory_space=pltpu.SMEM)] + [...]
    pallas_call x1, Pallas kernels: 2.43 us -> 0.25 us  [prepared(): pl.pallas_call(prepare_kernel, in_specs=[pl.BlockSpec(memory_space=pltpu....]
  transfers between devices with their start and end apart: 8 -> 8, of which waited for: 4 -> 4; matrix products, arithmetic and copies ran while one was open for 1% -> 1% of each run, Pallas kernels for 6% -> 4%
where the time goes in v7:
time: 120 us
  blocking collectives  71.5 us (60%)
  waiting for transfers between devices  18.8 us (16%)
  starting transfers between devices  15.3 us (13%)
  Pallas kernels  9.24 us (8%)
  local copies, waits for them, and re-layouts  2.15 us (2%)
  between operations  1.45 us (1%)
    all_to_all x2, blocking collectives, sent_along(): lax.all_to_all(jnp.broadcast_to(value[None], (count, *value.shape)), AXES...  43.7 us
    unnamed x1, blocking collectives  27.8 us
    ppermute x6, waiting for transfers between devices, moved(): lax.ppermute(value, 'z', [(i, (i + steps) % TARGETS) for i in range(TARGE...  16.3 us
    ppermute x6, starting transfers between devices, moved(): lax.ppermute(value, 'z', [(i, (i + steps) % TARGETS) for i in range(TARGE...  12.8 us
    pallas_call x2, Pallas kernels, half(): pl.pallas_call(body, in_specs=[pl.BlockSpec(memory_space=pltpu.SMEM)] + [...  8.99 us
    unnamed x1, waiting for transfers between devices  2.47 us
    unnamed x1, starting transfers between devices  2.44 us
  transfers between devices with their start and end apart: 8, of which 4 were waited for; matrix products, arithmetic and copies ran while one was open for 1% of the time, Pallas kernels for 4%

profile of v7, /device:TPU:32, one launch (start us, length us, event | category | flops | bytes accessed | tf_op | source)
XLA Modules:
  0.0 119.5 jit_solution(9139082527832785729)
XLA Ops:
  0.0 1.0 pad_maximum_fusion.3
  1.0 0.1 broadcast_in_dim.17
  1.1 14.3 %all_to_all.10 = bf16[4,56,2048]{2,1,0:T(8,128)(2,1)S(1)} all-to-all(bf16[4,56,2048]{2,1,0:T(8,128)(2,1)S(1)} %broadcast_in_dim.17), channel_id=1, replica_groups={{0,8,16,24},{4,12,20,28},{1,9,17,25},{5,13,21,29},{2,6,3,7},{10,14,11,1..., dimensions={0} | all-to-all | bytes 1835008 | tf_op jit(solution)/shard_map/all_to_all | solution.py:41
  15.4 0.5 broadcast_in_dim.19
  15.9 0.0 copy-start
  15.9 29.4 %all_to_all.11 = bf16[4,224,2048]{2,1,0:T(8,128)(2,1)} all-to-all(bf16[4,224,2048]{2,1,0:T(8,128)(2,1)S(1)} %broadcast_in_dim.19), channel_id=1, replica_groups={{0,4,1,5},{8,12,9,13},{16,20,17,21},{24,28,25,29},{2,10,18,26},{6,14,22..., dimensions={0} | all-to-all | bytes 7340032 | tf_op jit(solution)/shard_map/all_to_all | solution.py:41
  45.3 0.0 collective-permute-start.6
  45.4 2.0 %collective-permute-start = (bf16[56,1024]{1,0:T(8,128)(2,1)S(1)}, bf16[56,1024]{1,0:T(8,128)(2,1)S(1)}, u32[]{:S(2)}, u32[]{:S(2)}) collective-permute-start(bf16[56,1024]{1,0:T(8,128)(2,1)S(1)} %pad_maximum_fusion.4.own_ref), channel_id=1, source_target_pairs={{0,32},{32,64},{64,96},{96,128},{128,160},{160,192},{192,224},{224... | collective-permute-start | bytes 344072 | tf_op jit(solution)/shard_map/ppermute | solution.py:100
  47.4 0.1 collective-permute-start.1
  47.5 3.5 %collective-permute-done.up_ref = bf16[56,1024]{1,0:T(8,128)(2,1)S(1)} collective-permute-done((bf16[56,1024]{1,0:T(8,128)(2,1)S(1)}, bf16[56,1024]{1,0:T(8,128)(2,1)S(1)}, u32[]{:S(2)}, u32[]{:S(2)}) %collective-permute-start) | collective-permute-done | bytes 114720 | tf_op jit(solution)/shard_map/ppermute | solution.py:100
  51.0 1.8 %collective-permute-done.1.down_ref = bf16[56,1024]{1,0:T(8,128)(2,1)S(1)} collective-permute-done((bf16[56,1024]{1,0:T(8,128)(2,1)S(1)}, bf16[56,1024]{1,0:T(8,128)(2,1)S(1)}, u32[]{:S(2)}, u32[]{:S(2)}) %collective-permute-start.1) | collective-permute-done | bytes 114720 | tf_op jit(solution)/shard_map/ppermute | solution.py:100
  52.8 0.1 pad_maximum_fusion.2
  52.9 5.6 %collective-permute-start.2 = (bf16[112,1024]{1,0:T(8,128)(2,1)S(1)}, bf16[112,1024]{1,0:T(8,128)(2,1)S(1)}, u32[]{:S(2)}, u32[]{:S(2)}) collective-permute-start(bf16[112,1024]{1,0:T(8,128)(2,1)S(1)} %get-tuple-element.10), channel_id=1, source_target_pairs={{0,64},{32,96},{64,128},{96,160},{128,192},{160,224},{192,0},{224,... | collective-permute-start | bytes 688136 | tf_op jit(solution)/shard_map/ppermute | solution.py:100
  58.5 0.0 collective-permute-start.3
  58.5 3.9 %collective-permute-start.4 = (bf16[32,1024]{1,0:T(8,128)(2,1)S(1)}, bf16[32,1024]{1,0:T(8,128)(2,1)S(1)}, u32[]{:S(2)}, u32[]{:S(2)}) collective-permute-start(bf16[32,1024]{1,0:T(8,128)(2,1)S(1)} %slice.20), channel_id=1, source_target_pairs={{0,96},{32,128},{64,160},{96,192},{128,224},{160,0},{192,32},{224,... | collective-permute-start | bytes 196616 | tf_op jit(solution)/shard_map/ppermute | solution.py:100
  62.3 1.3 %collective-permute-start.5 = (bf16[24,1024]{1,0:T(8,128)(2,1)S(1)}, bf16[24,1024]{1,0:T(8,128)(2,1)S(1)}, u32[]{:S(2)}, u32[]{:S(2)}) collective-permute-start(bf16[24,1024]{1,0:T(8,128)(2,1)S(1)} %slice.21), channel_id=1, source_target_pairs={{0,160},{32,192},{64,224},{96,0},{128,32},{160,64},{192,96},{224,1... | collective-permute-start | bytes 147464 | tf_op jit(solution)/shard_map/ppermute | solution.py:100
  64.2 11.0 %collective-permute-done.5.high_ref = bf16[24,1024]{1,0:T(8,128)(2,1)S(1)} collective-permute-done((bf16[24,1024]{1,0:T(8,128)(2,1)S(1)}, bf16[24,1024]{1,0:T(8,128)(2,1)S(1)}, u32[]{:S(2)}, u32[]{:S(2)}) %collective-permute-start.5) | collective-permute-done | bytes 49184 | tf_op jit(solution)/shard_map/ppermute | solution.py:100
  75.2 0.0 collective-permute-done.4.low_ref
  75.2 0.0 collective-permute-done.2.far_up_ref
  75.2 0.0 collective-permute-done.3.far_down_ref
  75.2 0.2 shard_map.37
  75.5 4.4 %shard_map.38.refs_4_ = f32[248,2048]{1,0:T(8,128)S(1)} custom-call(f32[1]{0:T(128)S(6)} %copy.4.refs_0_, bf16[256,2048]{1,0:T(8,128)(2,1)S(1)} %get-tuple-element.7.refs_1_, f32[256,128]{1,0:T(8,128)S(1)} %get-tuple-element.8.refs_2_, bf16[16,56,2048]{2,1,0:T(8,128)(2,1)} %bitcast.2.refs_3_), custom_call_target="tpu_custom_call" | custom-call | tf_op jit(solution)/shard_map/pallas_call | solution.py:152
  79.9 0.0 collective-permute-done.6.refs_3_
  79.9 4.6 %shard_map.39 = f32[248,2048]{1,0:T(8,128)S(1)} custom-call(f32[1]{0:T(128)S(6)} %copy.4.refs_0_, bf16[256,2048]{1,0:T(8,128)(2,1)S(1)} %get-tuple-element.7.refs_1_, f32[256,128]{1,0:T(8,128)S(1)} %get-tuple-element.8.refs_2_, bf16[16,56,2048]{2,1,0:T(8,128)(2,1)} %collective-permute-done.6.refs_3_, f32[248,2048]{1,0:T(8,128)S(1)} %shard_map.38.refs_4_), custom_call_target="tpu_custom_call" | custom-call | tf_op jit(solution)/shard_map/pallas_call | solution.py:152
  84.5 0.0 copy-start.1
  84.5 27.8 %fusion = f32[32,2048]{1,0:T(8,128)S(1)} fusion(f32[248,2048]{1,0:T(8,128)S(1)} %shard_map.39), kind=kCustom, calls=%all-reduce-scatter | all-reduce-scatter fusion | flops 524289 | bytes 2294784
  112.4 2.4 %collective-permute-start.7 = (f32[7,2048]{1,0:T(8,128)S(1)}, f32[7,2048]{1,0:T(8,128)S(1)}, u32[]{:S(2)}, u32[]{:S(2)}) collective-permute-start(f32[7,2048]{1,0:T(8,128)S(1)} %slice.23), channel_id=1, source_target_pairs={{0,32},{32,64},{64,96},{96,128},{128,160},{160,192},{192,224},{1,3... | collective-permute-start | bytes 172040
  114.8 0.0 copy-done.1
  114.8 0.6 dynamic-slice.4
  116.1 2.5 %collective-permute-done.7 = f32[7,2048]{1,0:T(8,128)S(1)} collective-permute-done((f32[7,2048]{1,0:T(8,128)S(1)}, f32[7,2048]{1,0:T(8,128)S(1)}, u32[]{:S(2)}, u32[]{:S(2)}) %collective-permute-start.7) | collective-permute-done | bytes 57376
  118.5 0.2 concatenate.18
  118.8 0.7 constant_dynamic-slice_fusion
  (6 shorter events, 0.1 us)
Async XLA Ops:
  15.9 29.5 %copy-start = (bf16[28,2048]{1,0:T(8,128)(2,1)S(1)}, bf16[28,2048]{1,0:T(8,128)(2,1)}, u32[]{:S(2)}) copy-start(bf16[28,2048]{1,0:T(8,128)(2,1)} %param.3) | copy-start | bytes 344068
  45.3 34.6 %collective-permute-start.6 = (bf16[16,56,2048]{2,1,0:T(8,128)(2,1)}, bf16[16,56,2048]{2,1,0:T(8,128)(2,1)}, u32[]{:S(2)}, u32[]{:S(2)}) collective-permute-start(bf16[16,56,2048]{2,1,0:T(8,128)(2,1)} %bitcast.2.refs_3_), channel_id=1, source_target_pairs={{0,2},{2,0},{1,3},{3,1},{4,6},{6,4},{5,7},{7,5},{8,10},{10,8},{9,1... | collective-permute-start | bytes 11010056 | tf_op jit(solution)/shard_map/ppermute | solution.py:179
  45.4 5.6 %collective-permute-start = (bf16[56,1024]{1,0:T(8,128)(2,1)S(1)}, bf16[56,1024]{1,0:T(8,128)(2,1)S(1)}, u32[]{:S(2)}, u32[]{:S(2)}) collective-permute-start(bf16[56,1024]{1,0:T(8,128)(2,1)S(1)} %pad_maximum_fusion.4.own_ref), channel_id=1, source_target_pairs={{0,32},{32,64},{64,96},{96,128},{128,160},{160,192},{192,224},{224... | collective-permute-start | bytes 344072 | tf_op jit(solution)/shard_map/ppermute | solution.py:100
  47.4 5.5 %collective-permute-start.1 = (bf16[56,1024]{1,0:T(8,128)(2,1)S(1)}, bf16[56,1024]{1,0:T(8,128)(2,1)S(1)}, u32[]{:S(2)}, u32[]{:S(2)}) collective-permute-start(bf16[56,1024]{1,0:T(8,128)(2,1)S(1)} %pad_maximum_fusion.4.own_ref), channel_id=1, source_target_pairs={{0,224},{32,0},{64,32},{96,64},{128,96},{160,128},{192,160},{224,1... | collective-permute-start | bytes 344072 | tf_op jit(solution)/shard_map/ppermute | solution.py:100
  52.9 22.4 %collective-permute-start.2 = (bf16[112,1024]{1,0:T(8,128)(2,1)S(1)}, bf16[112,1024]{1,0:T(8,128)(2,1)S(1)}, u32[]{:S(2)}, u32[]{:S(2)}) collective-permute-start(bf16[112,1024]{1,0:T(8,128)(2,1)S(1)} %get-tuple-element.10), channel_id=1, source_target_pairs={{0,64},{32,96},{64,128},{96,160},{128,192},{160,224},{192,0},{224,... | collective-permute-start | bytes 688136 | tf_op jit(solution)/shard_map/ppermute | solution.py:100
  58.5 16.8 %collective-permute-start.3 = (bf16[112,1024]{1,0:T(8,128)(2,1)S(1)}, bf16[112,1024]{1,0:T(8,128)(2,1)S(1)}, u32[]{:S(2)}, u32[]{:S(2)}) collective-permute-start(bf16[112,1024]{1,0:T(8,128)(2,1)S(1)} %get-tuple-element.9), channel_id=1, source_target_pairs={{0,192},{32,224},{64,0},{96,32},{128,64},{160,96},{192,128},{224,1... | collective-permute-start | bytes 688136 | tf_op jit(solution)/shard_map/ppermute | solution.py:100
  58.5 16.8 %collective-permute-start.4 = (bf16[32,1024]{1,0:T(8,128)(2,1)S(1)}, bf16[32,1024]{1,0:T(8,128)(2,1)S(1)}, u32[]{:S(2)}, u32[]{:S(2)}) collective-permute-start(bf16[32,1024]{1,0:T(8,128)(2,1)S(1)} %slice.20), channel_id=1, source_target_pairs={{0,96},{32,128},{64,160},{96,192},{128,224},{160,0},{192,32},{224,... | collective-permute-start | bytes 196616 | tf_op jit(solution)/shard_map/ppermute | solution.py:100
  62.3 12.9 %collective-permute-start.5 = (bf16[24,1024]{1,0:T(8,128)(2,1)S(1)}, bf16[24,1024]{1,0:T(8,128)(2,1)S(1)}, u32[]{:S(2)}, u32[]{:S(2)}) collective-permute-start(bf16[24,1024]{1,0:T(8,128)(2,1)S(1)} %slice.21), channel_id=1, source_target_pairs={{0,160},{32,192},{64,224},{96,0},{128,32},{160,64},{192,96},{224,1... | collective-permute-start | bytes 147464 | tf_op jit(solution)/shard_map/ppermute | solution.py:100
  84.5 30.3 %copy-start.1 = (u32[256]{0:T(256)S(1)}, u32[256]{0:T(256)}, u32[]{:S(2)}) copy-start(u32[256]{0:T(256)} %constant.10) | copy-start | bytes 3076
  112.4 6.2 %collective-permute-start.7 = (f32[7,2048]{1,0:T(8,128)S(1)}, f32[7,2048]{1,0:T(8,128)S(1)}, u32[]{:S(2)}, u32[]{:S(2)}) collective-permute-start(f32[7,2048]{1,0:T(8,128)S(1)} %slice.23), channel_id=1, source_target_pairs={{0,32},{32,64},{64,96},{96,128},{128,160},{160,192},{192,224},{1,3... | collective-permute-start | bytes 172040

commit v8 on v7

--- a/solution.py
+++ b/solution.py
@@ -59,7 +59,7 @@
     return jnp.sum(wide * wide, axis=1, keepdims=True)
 
 
-def prepare_kernel(at_ref, own_ref, up_ref, down_ref, far_up_ref, far_down_ref, low_ref, high_ref, t_all, norm_ref):
+def prepare_kernel(at_ref, own_ref, up_ref, down_ref, far_up_ref, far_down_ref, low_ref, high_ref, t_all):
     half = DIM // 2
 
     def put(offset, piece):
@@ -69,7 +69,6 @@
         right = padded(piece[ROWS:])
         t_all[rows, :half] = left
         t_all[rows, half:] = right
-        norm_ref[rows, :] = jnp.broadcast_to(row_norms(left) + row_norms(right), (PAD, 128))
 
     put(0, own_ref[...])
     put(-1, up_ref[...])
@@ -82,43 +81,50 @@
 
 
 def prepared(at, pieces):
-    whole = TARGETS * PAD
     return pl.pallas_call(
         prepare_kernel,
         in_specs=[pl.BlockSpec(memory_space=pltpu.SMEM)]
         + [pl.BlockSpec(memory_space=pltpu.VMEM)] * len(pieces),
-        out_specs=[pl.BlockSpec(memory_space=pltpu.VMEM)] * 2,
-        out_shape=[
-            jax.ShapeDtypeStruct((whole, DIM), jnp.bfloat16),
-            jax.ShapeDtypeStruct((whole, 128), jnp.float32),
-        ],
+        out_specs=pl.BlockSpec(memory_space=pltpu.VMEM),
+        out_shape=pltpu.VMEM((TARGETS * PAD, DIM), jnp.bfloat16),
         compiler_params=pltpu.CompilerParams(vmem_limit_bytes=VMEM_BYTES),
     )(at, *pieces)
+
+
+def moved_across(value, steps):
+    pairs = [
+        (group[i], group[(i + steps) % 4]) for group in plane_lines(False) for i in range(4)
+    ]
+    return lax.ppermute(value, AXES, sorted(pairs))
 
 
 def moved(value, steps):
     return lax.ppermute(value, "z", [(i, (i + steps) % TARGETS) for i in range(TARGETS)])
 
 
-def half_kernel(first, spread_ref, t_all, norms, pieces, *refs):
-    if first:
-        out, x_all, s_all, low_all = refs
-    else:
-        before, out, x_all, s_all, low_all = refs
+def part_kernel(spread_ref, t_all, line_ref, back_ref, ahead_ref, low_ref, high_ref, out, x_all, s_all, low_all):
     inverse = 1.0 / spread_ref[0]
+    targets = t_all[...]
+    target_norm = row_norms(targets)
     row_total = jnp.zeros((TARGETS * PAD, 1), jnp.float32)
+    pieces = [
+        (ref, i * 2 * ROWS)
+        for ref, count in ((line_ref, 4), (back_ref, 4), (ahead_ref, 4), (low_ref, 2), (high_ref, 2))
+        for i in range(count)
+    ]
     for step in range(PIECES // STEP):
         for i in range(step * STEP, (step + 1) * STEP):
-            x_all[pl.ds(i * PAD, PAD), :] = padded(pieces[i, :ROWS])
-            s_all[pl.ds(i * PAD, PAD), :] = padded(pieces[i, ROWS:])
+            ref, at = pieces[i]
+            x_all[pl.ds(i * PAD, PAD), :] = padded(ref[at : at + ROWS])
+            s_all[pl.ds(i * PAD, PAD), :] = padded(ref[at + ROWS : at + 2 * ROWS])
         rows = pl.ds(step * STEP * PAD, STEP * PAD)
         source = x_all[rows, :]
         source_norm = row_norms(source)
         source_norm = jnp.transpose(jnp.broadcast_to(source_norm, (STEP * PAD, 128)))[:1]
         dots = lax.dot_general(
-            t_all[...], source, (((1,), (1,)), ((), ())), preferred_element_type=jnp.float32
+            targets, source, (((1,), (1,)), ((), ())), preferred_element_type=jnp.float32
         )
-        squared = jnp.maximum(norms[:, :1] + source_norm - 2.0 * dots, 0.0)
+        squared = jnp.maximum(target_norm + source_norm - 2.0 * dots, 0.0)
         weights = jnp.exp(-squared * inverse)
         column = lax.broadcasted_iota(jnp.int32, weights.shape, 1)
         weights = jnp.where(column % PAD < ROWS, weights, 0.0)
@@ -132,33 +138,21 @@
         wide = t_all[:, columns].astype(jnp.float32)
         added = drive + (2.0 * inverse) * (wide * row_total - pull)
         for i in range(TARGETS):
-            span = pl.ds(i * SPAN, SPAN)
-            part = added[i * PAD : i * PAD + SPAN]
-            if not first:
-                part = (before[span, columns] + part) / POPULATION
-            out[span, columns] = part
+            out[pl.ds(i * SPAN, SPAN), columns] = added[i * PAD : i * PAD + SPAN]
 
 
-def half(spread, targets, norms, source, before=None):
-    first = before is None
-    whole = TARGETS * PAD
-    result = (TARGETS * SPAN, DIM)
-    args = [targets, norms, source] + ([] if first else [before])
-    args = [pltpu.with_memory_space_constraint(a, pltpu.VMEM) for a in args]
-
-    def body(*refs):
-        half_kernel(first, *refs)
-
+def part(spread, targets, sources):
+    args = [pltpu.with_memory_space_constraint(a, pltpu.VMEM) for a in (targets, *sources)]
     return pl.pallas_call(
-        body,
+        part_kernel,
         in_specs=[pl.BlockSpec(memory_space=pltpu.SMEM)]
         + [pl.BlockSpec(memory_space=pltpu.VMEM)] * len(args),
         out_specs=pl.BlockSpec(memory_space=pltpu.VMEM),
-        out_shape=pltpu.VMEM(result, jnp.float32),
+        out_shape=pltpu.VMEM((TARGETS * SPAN, DIM), jnp.float32),
         scratch_shapes=[
             pltpu.VMEM((PIECES * PAD, DIM), jnp.bfloat16),
             pltpu.VMEM((PIECES * PAD, DIM), jnp.bfloat16),
-            pltpu.VMEM((whole, PIECES * PAD), jnp.bfloat16),
+            pltpu.VMEM((TARGETS * PAD, PIECES * PAD), jnp.bfloat16),
         ],
         compiler_params=pltpu.CompilerParams(vmem_limit_bytes=VMEM_BYTES),
     )(spread, *args)
@@ -173,12 +167,18 @@
     far_down = moved(jnp.concatenate([own_piece, down], axis=0), -2)
     low = moved(up[:CUT], 3)
     high = moved(down[CUT:], -3)
-    targets, norms = prepared(at, [own_piece, up, down, far_up, far_down, low, high])
+    targets = prepared(at, [own_piece, up, down, far_up, far_down, low, high])
+    others = lax.ppermute(targets, "c", swap)
     line = sent_along(jnp.concatenate([particles, scores], axis=0), plane_lines(True))
-    own = sent_along(line, plane_lines(False)).reshape(PIECES, 2 * ROWS, DIM)
-    other = lax.ppermute(own, "c", swap)
-    mine = half(spread, targets, norms, own)
-    partial = half(spread, targets, norms, other, mine)
+    back, ahead = moved_across(line, 1), moved_across(line, -1)
+    middle = 4 * ROWS
+    low_half, high_half = back[:middle], ahead[middle:]
+    opposite = [moved_across(low_half, 1), moved_across(high_half, -1)]
+    sources = [line, back, ahead, *opposite]
+    theirs = part(spread, others, sources)
+    arrived = lax.ppermute(theirs, "c", swap)
+    mine = part(spread, targets, sources)
+    partial = (mine + arrived) / POPULATION
     total = lax.psum_scatter(partial, "z", scatter_dimension=0, tiled=True)
     return lax.optimization_barrier(total)[:ROWS]
 

time: 120 us -> 105 us (0.88)
  blocking collectives: 71.5 us -> 27.7 us
  waiting for transfers between devices: 18.8 us -> 36.9 us
  starting transfers between devices: 15.3 us -> 25.4 us
  Pallas kernels: 9.24 us -> 5.87 us
  local copies, waits for them, and re-layouts: 2.15 us -> 4.74 us
    all_to_all x2 -> x0, blocking collectives: 43.7 us -> none  [sent_along(): lax.all_to_all(jnp.broadcast_to(value[None], (count, *value.shape)), AXES...]
    all_to_all x0 -> x1, waiting for transfers between devices: none -> 8.04 us  [sent_along(): lax.all_to_all(jnp.broadcast_to(value[None], (count, *value.shape)), AXES...]
    ppermute x1 -> x6, waiting for transfers between devices: 0.01 us -> 7.26 us  [the longest x4 5.68 us: moved_across(): return lax.ppermute(value, AXES, sorted(pairs))]
    ppermute x1 -> x6, starting transfers between devices: 0.01 us -> 6.99 us  [the longest x4 6.63 us: moved_across(): return lax.ppermute(value, AXES, sorted(pairs))]
    all_to_all x0 -> x1, starting transfers between devices: none -> 4.29 us  [sent_along(): lax.all_to_all(jnp.broadcast_to(value[None], (count, *value.shape)), AXES...]
    pallas_call x2, Pallas kernels: 8.99 us -> 4.93 us  [part(): pl.pallas_call(part_kernel, in_specs=[pl.BlockSpec(memory_space=pltpu.SME...]
    ppermute x6, waiting for transfers between devices: 16.3 us -> 19.5 us  [moved(): lax.ppermute(value, 'z', [(i, (i + steps) % TARGETS) for i in range(TARGE...]
    ppermute x6, starting transfers between devices: 12.8 us -> 11.3 us  [moved(): lax.ppermute(value, 'z', [(i, (i + steps) % TARGETS) for i in range(TARGE...]
  transfers between devices with their start and end apart: 8 -> 14, of which waited for: 4 -> 6; matrix products, arithmetic and copies ran while one was open for 1% -> 2% of each run, Pallas kernels for 4% -> 3%
where the time goes in v8:
time: 105 us; the launch traced here: 104 us
  waiting for transfers between devices  36.9 us (35%)
  blocking collectives  27.7 us (26%)
  starting transfers between devices  25.4 us (24%)
  Pallas kernels  5.87 us (6%)
  local copies, waits for them, and re-layouts  4.74 us (5%)
  other arithmetic  2.19 us (2%)
  between operations  1.46 us (1%)
    unnamed x1, blocking collectives  27.7 us
    ppermute x6, waiting for transfers between devices, moved(): lax.ppermute(value, 'z', [(i, (i + steps) % TARGETS) for i in range(TARGE...  19.5 us
    ppermute x6, starting transfers between devices, moved(): lax.ppermute(value, 'z', [(i, (i + steps) % TARGETS) for i in range(TARGE...  11.3 us
    all_to_all x1, waiting for transfers between devices, sent_along(): lax.all_to_all(jnp.broadcast_to(value[None], (count, *value.shape)), AXES...  8.04 us
    ppermute x4, starting transfers between devices, moved_across(): return lax.ppermute(value, AXES, sorted(pairs))  6.63 us
    ppermute x4, waiting for transfers between devices, moved_across(): return lax.ppermute(value, AXES, sorted(pairs))  5.68 us
    pallas_call x2, Pallas kernels, part(): pl.pallas_call(part_kernel, in_specs=[pl.BlockSpec(memory_space=pltpu.SME...  4.93 us
    all_to_all x1, starting transfers between devices, sent_along(): lax.all_to_all(jnp.broadcast_to(value[None], (count, *value.shape)), AXES...  4.29 us
  transfers between devices with their start and end apart: 14, of which 6 were waited for; matrix products, arithmetic and copies ran while one was open for 2% of the time, Pallas kernels for 3%

profile of v8, /device:TPU:32, one launch (start us, length us, event | category | flops | bytes accessed | tf_op | source)
XLA Modules:
  0.0 104.2 jit_solution(5293722144484745200)
XLA Ops:
  0.0 1.0 %pad_maximum_fusion.3 = bf16[56,2048]{1,0:T(8,128)(2,1)S(1)} fusion(bf16[28,2048]{1,0:T(8,128)(2,1)} %param.4, bf16[28,2048]{1,0:T(8,128)(2,1)} %param.3), kind=kLoop, calls=%fused_computation.4 | loop fusion | flops 458752 | bytes 458752 | tf_op jit(solution)/shard_map/concatenate | solution.py:172
  1.1 1.0 broadcast_in_dim.10
  2.1 4.3 %all-to-all-start = ((bf16[4,56,2048]{2,1,0:T(8,128)(2,1)}), bf16[4,56,2048]{2,1,0:T(8,128)(2,1)S(1)}, u32[]{:S(2)}, u32[]{:S(2)}) async-start(bf16[4,56,2048]{2,1,0:T(8,128)(2,1)} %broadcast_in_dim.10), calls=%async_computation | async-start | bytes 1835008 | tf_op jit(solution)/shard_map/all_to_all | solution.py:41
  6.4 2.0 %collective-permute-start = (bf16[56,1024]{1,0:T(8,128)(2,1)S(1)}, bf16[56,1024]{1,0:T(8,128)(2,1)S(1)}, u32[]{:S(2)}, u32[]{:S(2)}) collective-permute-start(bf16[56,1024]{1,0:T(8,128)(2,1)S(1)} %pad_maximum_fusion.4.own_ref), channel_id=1, source_target_pairs={{0,32},{32,64},{64,96},{96,128},{128,160},{160,192},{192,224},{224... | collective-permute-start | bytes 344072 | tf_op jit(solution)/shard_map/ppermute | solution.py:102
  8.5 8.0 %all-to-all-done = bf16[4,56,2048]{2,1,0:T(8,128)(2,1)S(1)} async-done(((bf16[4,56,2048]{2,1,0:T(8,128)(2,1)}), bf16[4,56,2048]{2,1,0:T(8,128)(2,1)S(1)}, u32[]{:S(2)}, u32[]{:S(2)}) %all-to-all-start) | async-done | bytes 917536 | tf_op jit(solution)/shard_map/all_to_all | solution.py:41
  16.6 1.6 %collective-permute-start.6 = (bf16[224,2048]{1,0:T(8,128)(2,1)S(1)}, bf16[224,2048]{1,0:T(8,128)(2,1)S(1)}, u32[]{:S(2)}, u32[]{:S(2)}) collective-permute-start(bf16[224,2048]{1,0:T(8,128)(2,1)S(1)} %bitcast.6), channel_id=1, source_target_pairs={{0,4},{1,5},{2,10},{3,11},{4,1},{5,0},{6,14},{7,15},{8,12},{9,13},... | collective-permute-start | bytes 2752520 | tf_op jit(solution)/shard_map/ppermute | solution.py:98
  18.1 1.7 %collective-permute-start.7 = (bf16[224,2048]{1,0:T(8,128)(2,1)S(1)}, bf16[224,2048]{1,0:T(8,128)(2,1)S(1)}, u32[]{:S(2)}, u32[]{:S(2)}) collective-permute-start(bf16[224,2048]{1,0:T(8,128)(2,1)S(1)} %bitcast.7), channel_id=1, source_target_pairs={{0,5},{1,4},{2,26},{3,27},{4,0},{5,1},{6,30},{7,31},{8,13},{9,12},... | collective-permute-start | bytes 2752520 | tf_op jit(solution)/shard_map/ppermute | solution.py:98
  19.8 0.8 pad_maximum_fusion.2
  20.6 3.3 %collective-permute-start.2 = (bf16[112,1024]{1,0:T(8,128)(2,1)}, bf16[112,1024]{1,0:T(8,128)(2,1)S(1)}, u32[]{:S(2)}, u32[]{:S(2)}) collective-permute-start(bf16[112,1024]{1,0:T(8,128)(2,1)} %get-tuple-element.6), channel_id=1, source_target_pairs={{0,64},{32,96},{64,128},{96,160},{128,192},{160,224},{192,0},{224,... | collective-permute-start | bytes 688136 | tf_op jit(solution)/shard_map/ppermute | solution.py:102
  23.9 2.1 %collective-permute-start.3 = (bf16[112,1024]{1,0:T(8,128)(2,1)}, bf16[112,1024]{1,0:T(8,128)(2,1)S(1)}, u32[]{:S(2)}, u32[]{:S(2)}) collective-permute-start(bf16[112,1024]{1,0:T(8,128)(2,1)} %get-tuple-element.5), channel_id=1, source_target_pairs={{0,192},{32,224},{64,0},{96,32},{128,64},{160,96},{192,128},{224,1... | collective-permute-start | bytes 688136 | tf_op jit(solution)/shard_map/ppermute | solution.py:102
  26.1 3.4 %collective-permute-start.5 = (bf16[24,1024]{1,0:T(8,128)(2,1)S(1)}, bf16[24,1024]{1,0:T(8,128)(2,1)S(1)}, u32[]{:S(2)}, u32[]{:S(2)}) collective-permute-start(bf16[24,1024]{1,0:T(8,128)(2,1)S(1)} %slice.29), channel_id=1, source_target_pairs={{0,160},{32,192},{64,224},{96,0},{128,32},{160,64},{192,96},{224,1... | collective-permute-start | bytes 147464 | tf_op jit(solution)/shard_map/ppermute | solution.py:102
  29.4 0.6 slice.28
  30.1 12.4 %collective-permute-done.5.high_ref = bf16[24,1024]{1,0:T(8,128)(2,1)S(1)} collective-permute-done((bf16[24,1024]{1,0:T(8,128)(2,1)S(1)}, bf16[24,1024]{1,0:T(8,128)(2,1)S(1)}, u32[]{:S(2)}, u32[]{:S(2)}) %collective-permute-start.5) | collective-permute-done | bytes 49184 | tf_op jit(solution)/shard_map/ppermute | solution.py:102
  42.4 0.6 copy-done
  43.0 0.5 collective-permute-start.4
  43.5 7.1 %collective-permute-done.4.low_ref = bf16[32,1024]{1,0:T(8,128)(2,1)} collective-permute-done((bf16[32,1024]{1,0:T(8,128)(2,1)}, bf16[32,1024]{1,0:T(8,128)(2,1)}, u32[]{:S(2)}, u32[]{:S(2)}) %collective-permute-start.4) | collective-permute-done | bytes 65568 | tf_op jit(solution)/shard_map/ppermute | solution.py:102
  50.6 0.8 copy-done.1
  51.4 0.9 shard_map.37.t_all
  52.5 0.6 collective-permute-start.8
  53.2 2.7 %collective-permute-start.9 = (bf16[112,2048]{1,0:T(8,128)(2,1)S(1)}, bf16[112,2048]{1,0:T(8,128)(2,1)S(1)}, u32[]{:S(2)}, u32[]{:S(2)}) collective-permute-start(bf16[112,2048]{1,0:T(8,128)(2,1)S(1)} %slice.31), channel_id=1, source_target_pairs={{0,5},{1,4},{2,26},{3,27},{4,0},{5,1},{6,30},{7,31},{8,13},{9,12},... | collective-permute-start | bytes 1376264 | tf_op jit(solution)/shard_map/ppermute | solution.py:98
  56.6 5.7 %collective-permute-done.8.low_ref = bf16[112,2048]{1,0:T(8,128)(2,1)S(1)} collective-permute-done((bf16[112,2048]{1,0:T(8,128)(2,1)S(1)}, bf16[112,2048]{1,0:T(8,128)(2,1)S(1)}, u32[]{:S(2)}, u32[]{:S(2)}) %collective-permute-start.8) | collective-permute-done | bytes 458784 | tf_op jit(solution)/shard_map/ppermute | solution.py:98
  62.3 2.5 %shard_map.39 = f32[248,2048]{1,0:T(8,128)S(1)} custom-call(f32[1]{0:T(128)S(6)} %copy.4.spread_ref, bf16[256,2048]{1,0:T(8,128)(2,1)S(1)} %collective-permute-done.10.t_all, bf16[224,2048]{1,0:T(8,128)(2,1)S(1)} %bitcast.8, bf16[224,2048]{1,0:T(8,128)(2,1)S(1)} %collective-permute-done.6.back_ref, bf16[224,2048]{1,0:T(8,128)(2,1)S(1)} %collective-permute-done.7.ahead_ref, ...), custom_call_target="tpu_custom_call" | custom-call | tf_op jit(solution)/shard_map/pallas_call | solution.py:146
  64.8 0.3 collective-permute-start.11
  65.0 2.5 %shard_map.38 = f32[248,2048]{1,0:T(8,128)S(1)} custom-call(f32[1]{0:T(128)S(6)} %copy.4.spread_ref, bf16[256,2048]{1,0:T(8,128)(2,1)S(1)} %shard_map.37.t_all, bf16[224,2048]{1,0:T(8,128)(2,1)S(1)} %bitcast.9, bf16[224,2048]{1,0:T(8,128)(2,1)S(1)} %collective-permute-done.6.back_ref, bf16[224,2048]{1,0:T(8,128)(2,1)S(1)} %collective-permute-done.7.ahead_ref, ...), custom_call_target="tpu_custom_call" | custom-call | tf_op jit(solution)/shard_map/pallas_call | solution.py:146
  67.5 1.6 %collective-permute-done.11 = f32[248,2048]{1,0:T(8,128)S(1)} collective-permute-done((f32[248,2048]{1,0:T(8,128)S(1)}, f32[248,2048]{1,0:T(8,128)S(1)}, u32[]{:S(2)}, u32[]{:S(2)}) %collective-permute-start.11) | collective-permute-done | bytes 2031648 | tf_op jit(solution)/shard_map/ppermute | solution.py:179
  69.1 0.3 add_multiply_fusion
  69.4 27.7 %fusion = f32[32,2048]{1,0:T(8,128)S(1)} fusion(f32[248,2048]{1,0:T(8,128)S(1)} %add_multiply_fusion), kind=kCustom, calls=%all-reduce-scatter | all-reduce-scatter fusion | flops 524289 | bytes 2294784
  97.1 2.8 %collective-permute-start.12 = (f32[7,2048]{1,0:T(8,128)S(1)}, f32[7,2048]{1,0:T(8,128)S(1)}, u32[]{:S(2)}, u32[]{:S(2)}) collective-permute-start(f32[7,2048]{1,0:T(8,128)S(1)} %slice.33), channel_id=1, source_target_pairs={{0,32},{32,64},{64,96},{96,128},{128,160},{160,192},{192,224},{1,3... | collective-permute-start | bytes 172040
  99.9 0.6 dynamic-slice.4
  101.1 2.1 %collective-permute-done.12 = f32[7,2048]{1,0:T(8,128)S(1)} collective-permute-done((f32[7,2048]{1,0:T(8,128)S(1)}, f32[7,2048]{1,0:T(8,128)S(1)}, u32[]{:S(2)}, u32[]{:S(2)}) %collective-permute-start.12) | collective-permute-done | bytes 57376
  103.3 0.2 concatenate.18
  103.5 0.7 constant_dynamic-slice_fusion
  (22 shorter events, 0.3 us)
Async XLA Ops:
  0.0 6.4 %copy-start.2 = (bf16[28,2048]{1,0:T(8,128)(2,1)S(1)}, bf16[28,2048]{1,0:T(8,128)(2,1)}, u32[]{:S(2)}) copy-start(bf16[28,2048]{1,0:T(8,128)(2,1)} %param.3) | copy-start | bytes 344068
  2.1 14.5 %all-to-all-start = ((bf16[4,56,2048]{2,1,0:T(8,128)(2,1)}), bf16[4,56,2048]{2,1,0:T(8,128)(2,1)S(1)}, u32[]{:S(2)}, u32[]{:S(2)}) async-start(bf16[4,56,2048]{2,1,0:T(8,128)(2,1)} %broadcast_in_dim.10), calls=%async_computation | async-start | bytes 1835008 | tf_op jit(solution)/shard_map/all_to_all | solution.py:41
  6.4 13.4 %collective-permute-start = (bf16[56,1024]{1,0:T(8,128)(2,1)S(1)}, bf16[56,1024]{1,0:T(8,128)(2,1)S(1)}, u32[]{:S(2)}, u32[]{:S(2)}) collective-permute-start(bf16[56,1024]{1,0:T(8,128)(2,1)S(1)} %pad_maximum_fusion.4.own_ref), channel_id=1, source_target_pairs={{0,32},{32,64},{64,96},{96,128},{128,160},{160,192},{192,224},{224... | collective-permute-start | bytes 344072 | tf_op jit(solution)/shard_map/ppermute | solution.py:102
  8.4 11.4 %collective-permute-start.1 = (bf16[56,1024]{1,0:T(8,128)(2,1)S(1)}, bf16[56,1024]{1,0:T(8,128)(2,1)S(1)}, u32[]{:S(2)}, u32[]{:S(2)}) collective-permute-start(bf16[56,1024]{1,0:T(8,128)(2,1)S(1)} %pad_maximum_fusion.4.own_ref), channel_id=1, source_target_pairs={{0,224},{32,0},{64,32},{96,64},{128,96},{160,128},{192,160},{224,1... | collective-permute-start | bytes 344072 | tf_op jit(solution)/shard_map/ppermute | solution.py:102
  16.6 35.9 %collective-permute-start.6 = (bf16[224,2048]{1,0:T(8,128)(2,1)S(1)}, bf16[224,2048]{1,0:T(8,128)(2,1)S(1)}, u32[]{:S(2)}, u32[]{:S(2)}) collective-permute-start(bf16[224,2048]{1,0:T(8,128)(2,1)S(1)} %bitcast.6), channel_id=1, source_target_pairs={{0,4},{1,5},{2,10},{3,11},{4,1},{5,0},{6,14},{7,15},{8,12},{9,13},... | collective-permute-start | bytes 2752520 | tf_op jit(solution)/shard_map/ppermute | solution.py:98
  18.1 35.0 %collective-permute-start.7 = (bf16[224,2048]{1,0:T(8,128)(2,1)S(1)}, bf16[224,2048]{1,0:T(8,128)(2,1)S(1)}, u32[]{:S(2)}, u32[]{:S(2)}) collective-permute-start(bf16[224,2048]{1,0:T(8,128)(2,1)S(1)} %bitcast.7), channel_id=1, source_target_pairs={{0,5},{1,4},{2,26},{3,27},{4,0},{5,1},{6,30},{7,31},{8,13},{9,12},... | collective-permute-start | bytes 2752520 | tf_op jit(solution)/shard_map/ppermute | solution.py:98
  20.6 30.0 %collective-permute-start.2 = (bf16[112,1024]{1,0:T(8,128)(2,1)}, bf16[112,1024]{1,0:T(8,128)(2,1)S(1)}, u32[]{:S(2)}, u32[]{:S(2)}) collective-permute-start(bf16[112,1024]{1,0:T(8,128)(2,1)} %get-tuple-element.6), channel_id=1, source_target_pairs={{0,64},{32,96},{64,128},{96,160},{128,192},{160,224},{192,0},{224,... | collective-permute-start | bytes 688136 | tf_op jit(solution)/shard_map/ppermute | solution.py:102
  23.9 26.7 %collective-permute-start.3 = (bf16[112,1024]{1,0:T(8,128)(2,1)}, bf16[112,1024]{1,0:T(8,128)(2,1)S(1)}, u32[]{:S(2)}, u32[]{:S(2)}) collective-permute-start(bf16[112,1024]{1,0:T(8,128)(2,1)} %get-tuple-element.5), channel_id=1, source_target_pairs={{0,192},{32,224},{64,0},{96,32},{128,64},{160,96},{192,128},{224,1... | collective-permute-start | bytes 688136 | tf_op jit(solution)/shard_map/ppermute | solution.py:102
  26.1 16.4 %collective-permute-start.5 = (bf16[24,1024]{1,0:T(8,128)(2,1)S(1)}, bf16[24,1024]{1,0:T(8,128)(2,1)S(1)}, u32[]{:S(2)}, u32[]{:S(2)}) collective-permute-start(bf16[24,1024]{1,0:T(8,128)(2,1)S(1)} %slice.29), channel_id=1, source_target_pairs={{0,160},{32,192},{64,224},{96,0},{128,32},{160,64},{192,96},{224,1... | collective-permute-start | bytes 147464 | tf_op jit(solution)/shard_map/ppermute | solution.py:102
  42.4 0.6 copy-start
  43.0 7.6 %collective-permute-start.4 = (bf16[32,1024]{1,0:T(8,128)(2,1)}, bf16[32,1024]{1,0:T(8,128)(2,1)}, u32[]{:S(2)}, u32[]{:S(2)}) collective-permute-start(bf16[32,1024]{1,0:T(8,128)(2,1)} %slice.28), channel_id=1, source_target_pairs={{0,96},{32,128},{64,160},{96,192},{128,224},{160,0},{192,32},{224,... | collective-permute-start | bytes 196616 | tf_op jit(solution)/shard_map/ppermute | solution.py:102
  50.6 0.8 copy-start.1
  52.4 4.2 %collective-permute-start.10 = (bf16[256,2048]{1,0:T(8,128)(2,1)S(1)}, bf16[256,2048]{1,0:T(8,128)(2,1)S(1)}, u32[]{:S(2)}, u32[]{:S(2)}) collective-permute-start(bf16[256,2048]{1,0:T(8,128)(2,1)S(1)} %shard_map.37.t_all), channel_id=1, source_target_pairs={{0,2},{2,0},{1,3},{3,1},{4,6},{6,4},{5,7},{7,5},{8,10},{10,8},{9,1... | collective-permute-start | bytes 3145736 | tf_op jit(solution)/shard_map/ppermute | solution.py:171
  52.5 9.8 %collective-permute-start.8 = (bf16[112,2048]{1,0:T(8,128)(2,1)S(1)}, bf16[112,2048]{1,0:T(8,128)(2,1)S(1)}, u32[]{:S(2)}, u32[]{:S(2)}) collective-permute-start(bf16[112,2048]{1,0:T(8,128)(2,1)S(1)} %slice.30), channel_id=1, source_target_pairs={{0,4},{1,5},{2,10},{3,11},{4,1},{5,0},{6,14},{7,15},{8,12},{9,13},... | collective-permute-start | bytes 1376264 | tf_op jit(solution)/shard_map/ppermute | solution.py:98
  53.2 9.1 %collective-permute-start.9 = (bf16[112,2048]{1,0:T(8,128)(2,1)S(1)}, bf16[112,2048]{1,0:T(8,128)(2,1)S(1)}, u32[]{:S(2)}, u32[]{:S(2)}) collective-permute-start(bf16[112,2048]{1,0:T(8,128)(2,1)S(1)} %slice.31), channel_id=1, source_target_pairs={{0,5},{1,4},{2,26},{3,27},{4,0},{5,1},{6,30},{7,31},{8,13},{9,12},... | collective-permute-start | bytes 1376264 | tf_op jit(solution)/shard_map/ppermute | solution.py:98
  64.8 4.3 %collective-permute-start.11 = (f32[248,2048]{1,0:T(8,128)S(1)}, f32[248,2048]{1,0:T(8,128)S(1)}, u32[]{:S(2)}, u32[]{:S(2)}) collective-permute-start(f32[248,2048]{1,0:T(8,128)S(1)} %shard_map.39), channel_id=1, source_target_pairs={{0,2},{2,0},{1,3},{3,1},{4,6},{6,4},{5,7},{7,5},{8,10},{10,8},{9,1... | collective-permute-start | bytes 6094856 | tf_op jit(solution)/shard_map/ppermute | solution.py:179
  69.4 30.5 %copy-start.3 = (u32[256]{0:T(256)S(1)}, u32[256]{0:T(256)}, u32[]{:S(2)}) copy-start(u32[256]{0:T(256)} %constant.13) | copy-start | bytes 3076
  97.1 6.2 %collective-permute-start.12 = (f32[7,2048]{1,0:T(8,128)S(1)}, f32[7,2048]{1,0:T(8,128)S(1)}, u32[]{:S(2)}, u32[]{:S(2)}) collective-permute-start(f32[7,2048]{1,0:T(8,128)S(1)} %slice.33), channel_id=1, source_target_pairs={{0,32},{32,64},{64,96},{96,128},{128,160},{160,192},{192,224},{1,3... | collective-permute-start | bytes 172040

commit v9 on v8

--- a/solution.py
+++ b/solution.py
@@ -46,7 +46,7 @@
         tiled=True,
         axis_index_groups=groups,
     )
-    return arrived.reshape(count * value.shape[0], *value.shape[1:])
+    return arrived.reshape(count * arrived.shape[1], *arrived.shape[2:])
 
 
 def padded(rows):
@@ -59,7 +59,7 @@
     return jnp.sum(wide * wide, axis=1, keepdims=True)
 
 
-def prepare_kernel(at_ref, own_ref, up_ref, down_ref, far_up_ref, far_down_ref, low_ref, high_ref, t_all):
+def prepare_kernel(at_ref, own_ref, up_ref, down_ref, up2_ref, down2_ref, far_up_ref, far_down_ref, t_all):
     half = DIM // 2
 
     def put(offset, piece):
@@ -73,11 +73,11 @@
     put(0, own_ref[...])
     put(-1, up_ref[...])
     put(1, down_ref[...])
-    put(-2, far_up_ref[: 2 * ROWS])
-    put(-3, far_up_ref[2 * ROWS :])
-    put(2, far_down_ref[: 2 * ROWS])
-    put(3, far_down_ref[2 * ROWS :])
-    put(4, jnp.concatenate([low_ref[...], high_ref[...]], axis=0))
+    put(-2, up2_ref[...])
+    put(2, down2_ref[...])
+    put(-3, far_up_ref[: 2 * ROWS])
+    put(3, far_down_ref[: 2 * ROWS])
+    put(4, jnp.concatenate([far_up_ref[2 * ROWS :], far_down_ref[2 * ROWS :]], axis=0))
 
 
 def prepared(at, pieces):
@@ -163,11 +163,10 @@
     at = lax.axis_index("z").astype(jnp.int32)[None]
     own_piece = jnp.concatenate([particles[:, : DIM // 2], particles[:, DIM // 2 :]], axis=0)
     up, down = moved(own_piece, 1), moved(own_piece, -1)
-    far_up = moved(jnp.concatenate([own_piece, up], axis=0), 2)
-    far_down = moved(jnp.concatenate([own_piece, down], axis=0), -2)
-    low = moved(up[:CUT], 3)
-    high = moved(down[CUT:], -3)
-    targets = prepared(at, [own_piece, up, down, far_up, far_down, low, high])
+    up2, down2 = moved(up, 1), moved(down, -1)
+    far_up = moved(jnp.concatenate([up, up2[:CUT]], axis=0), 2)
+    far_down = moved(jnp.concatenate([down, down2[CUT:]], axis=0), -2)
+    targets = prepared(at, [own_piece, up, down, up2, down2, far_up, far_down])
     others = lax.ppermute(targets, "c", swap)
     line = sent_along(jnp.concatenate([particles, scores], axis=0), plane_lines(True))
     back, ahead = moved_across(line, 1), moved_across(line, -1)

time: 105 us -> 90.7 us (0.86)
  waiting for transfers between devices: 36.9 us -> 21.9 us
  blocking collectives: 27.7 us -> 30.5 us
  local copies, waits for them, and re-layouts: 4.74 us -> 2.69 us
    all_to_all x1, waiting for transfers between devices: 8.04 us -> 0.01 us  [sent_along(): lax.all_to_all(jnp.broadcast_to(value[None], (count, *value.shape)), AXES...]
    ppermute x6, waiting for transfers between devices: 19.5 us -> 12.8 us  [moved(): lax.ppermute(value, 'z', [(i, (i + steps) % TARGETS) for i in range(TARGE...]
    unnamed x1, blocking collectives: 27.7 us -> 30.5 us
    unnamed x12 -> x8, local copies, waits for them, and re-layouts: 2.99 us -> 1.58 us
  transfers between devices with their start and end apart: 14 -> 14, of which waited for: 6 -> 6; matrix products, arithmetic and copies ran while one was open for 2% -> 2% of each run, Pallas kernels for 3% -> 4%
where the time goes in v9:
time: 90.7 us; the launch traced here: 90.1 us
  blocking collectives  30.5 us (34%)
  starting transfers between devices  24.9 us (27%)
  waiting for transfers between devices  21.9 us (24%)
  Pallas kernels  5.95 us (7%)
  other arithmetic  2.72 us (3%)
  local copies, waits for them, and re-layouts  2.69 us (3%)
  between operations  1.47 us (2%)
    unnamed x1, blocking collectives  30.5 us
    ppermute x6, waiting for transfers between devices, moved(): lax.ppermute(value, 'z', [(i, (i + steps) % TARGETS) for i in range(TARGE...  12.8 us
    ppermute x6, starting transfers between devices, moved(): lax.ppermute(value, 'z', [(i, (i + steps) % TARGETS) for i in range(TARGE...  10.5 us
    ppermute x4, starting transfers between devices, moved_across(): return lax.ppermute(value, AXES, sorted(pairs))  6.69 us
    ppermute x4, waiting for transfers between devices, moved_across(): return lax.ppermute(value, AXES, sorted(pairs))  5.68 us
    pallas_call x2, Pallas kernels, part(): pl.pallas_call(part_kernel, in_specs=[pl.BlockSpec(memory_space=pltpu.SME...  4.93 us
    all_to_all x1, starting transfers between devices, sent_along(): lax.all_to_all(jnp.broadcast_to(value[None], (count, *value.shape)), AXES...  4.29 us
    unnamed x1, starting transfers between devices  3.1 us
  transfers between devices with their start and end apart: 14, of which 6 were waited for; matrix products, arithmetic and copies ran while one was open for 2% of the time, Pallas kernels for 4%

profile of v9, /device:TPU:32, one launch (start us, length us, event | category | flops | bytes accessed | tf_op | source)
XLA Modules:
  0.0 90.1 jit_solution(15591146652017436179)
XLA Ops:
  0.0 1.0 %pad_maximum_fusion = bf16[56,2048]{1,0:T(8,128)(2,1)S(1)} fusion(bf16[28,2048]{1,0:T(8,128)(2,1)} %param.4, bf16[28,2048]{1,0:T(8,128)(2,1)} %param.3), kind=kLoop, calls=%fused_computation.1 | loop fusion | flops 458752 | bytes 458752 | tf_op jit(solution)/shard_map/concatenate | solution.py:171
  1.1 1.0 %broadcast_in_dim.10 = bf16[4,56,2048]{2,1,0:T(8,128)(2,1)} broadcast(bf16[56,2048]{1,0:T(8,128)(2,1)S(1)} %pad_maximum_fusion), dimensions={1,2} | broadcast | bytes 1146880 | tf_op jit(solution)/shard_map/broadcast_in_dim | solution.py:42
  2.1 4.3 %all-to-all-start = ((bf16[4,56,2048]{2,1,0:T(8,128)(2,1)}), bf16[4,56,2048]{2,1,0:T(8,128)(2,1)S(1)}, u32[]{:S(2)}, u32[]{:S(2)}) async-start(bf16[4,56,2048]{2,1,0:T(8,128)(2,1)} %broadcast_in_dim.10), calls=%async_computation | async-start | bytes 1835008 | tf_op jit(solution)/shard_map/all_to_all | solution.py:41
  6.4 2.0 %collective-permute-start = (bf16[56,1024]{1,0:T(8,128)(2,1)S(1)}, bf16[56,1024]{1,0:T(8,128)(2,1)S(1)}, u32[]{:S(2)}, u32[]{:S(2)}) collective-permute-start(bf16[56,1024]{1,0:T(8,128)(2,1)S(1)} %pad_maximum_fusion.3.own_ref), channel_id=1, source_target_pairs={{0,32},{32,64},{64,96},{96,128},{128,160},{160,192},{192,224},{224... | collective-permute-start | bytes 344072 | tf_op jit(solution)/shard_map/ppermute | solution.py:102
  8.4 0.1 collective-permute-start.1
  8.5 2.8 %collective-permute-done.up_ref = bf16[56,1024]{1,0:T(8,128)(2,1)S(1)} collective-permute-done((bf16[56,1024]{1,0:T(8,128)(2,1)S(1)}, bf16[56,1024]{1,0:T(8,128)(2,1)S(1)}, u32[]{:S(2)}, u32[]{:S(2)}) %collective-permute-start) | collective-permute-done | bytes 114720 | tf_op jit(solution)/shard_map/ppermute | solution.py:102
  11.3 1.9 %collective-permute-start.2 = (bf16[56,1024]{1,0:T(8,128)(2,1)S(1)}, bf16[56,1024]{1,0:T(8,128)(2,1)S(1)}, u32[]{:S(2)}, u32[]{:S(2)}) collective-permute-start(bf16[56,1024]{1,0:T(8,128)(2,1)S(1)} %collective-permute-done.up_ref), channel_id=1, source_target_pairs={{0,32},{32,64},{64,96},{96,128},{128,160},{160,192},{192,224},{224... | collective-permute-start | bytes 344072 | tf_op jit(solution)/shard_map/ppermute | solution.py:102
  13.2 2.3 %collective-permute-start.3 = (bf16[56,1024]{1,0:T(8,128)(2,1)S(1)}, bf16[56,1024]{1,0:T(8,128)(2,1)S(1)}, u32[]{:S(2)}, u32[]{:S(2)}) collective-permute-start(bf16[56,1024]{1,0:T(8,128)(2,1)S(1)} %collective-permute-done.1.down_ref), channel_id=1, source_target_pairs={{0,224},{32,0},{64,32},{96,64},{128,96},{160,128},{192,160},{224,1... | collective-permute-start | bytes 344072 | tf_op jit(solution)/shard_map/ppermute | solution.py:102
  15.5 2.8 %collective-permute-done.2.up2_ref = bf16[56,1024]{1,0:T(8,128)(2,1)S(1)} collective-permute-done((bf16[56,1024]{1,0:T(8,128)(2,1)S(1)}, bf16[56,1024]{1,0:T(8,128)(2,1)S(1)}, u32[]{:S(2)}, u32[]{:S(2)}) %collective-permute-start.2) | collective-permute-done | bytes 114720 | tf_op jit(solution)/shard_map/ppermute | solution.py:102
  18.3 1.8 %collective-permute-start.6 = (bf16[224,2048]{1,0:T(8,128)(2,1)S(1)}, bf16[224,2048]{1,0:T(8,128)(2,1)S(1)}, u32[]{:S(2)}, u32[]{:S(2)}) collective-permute-start(bf16[224,2048]{1,0:T(8,128)(2,1)S(1)} %bitcast.6), channel_id=1, source_target_pairs={{0,4},{1,5},{2,10},{3,11},{4,1},{5,0},{6,14},{7,15},{8,12},{9,13},... | collective-permute-start | bytes 2752520 | tf_op jit(solution)/shard_map/ppermute | solution.py:98
  20.1 1.5 %collective-permute-start.7 = (bf16[224,2048]{1,0:T(8,128)(2,1)S(1)}, bf16[224,2048]{1,0:T(8,128)(2,1)S(1)}, u32[]{:S(2)}, u32[]{:S(2)}) collective-permute-start(bf16[224,2048]{1,0:T(8,128)(2,1)S(1)} %bitcast.7), channel_id=1, source_target_pairs={{0,5},{1,4},{2,26},{3,27},{4,0},{5,1},{6,30},{7,31},{8,13},{9,12},... | collective-permute-start | bytes 2752520 | tf_op jit(solution)/shard_map/ppermute | solution.py:98
  21.6 0.7 pad_maximum_fusion.1
  22.3 3.0 %collective-permute-start.4 = (bf16[88,1024]{1,0:T(8,128)(2,1)}, bf16[88,1024]{1,0:T(8,128)(2,1)S(1)}, u32[]{:S(2)}, u32[]{:S(2)}) collective-permute-start(bf16[88,1024]{1,0:T(8,128)(2,1)} %pad_maximum_fusion.1), channel_id=1, source_target_pairs={{0,64},{32,96},{64,128},{96,160},{128,192},{160,224},{192,0},{224,... | collective-permute-start | bytes 540680 | tf_op jit(solution)/shard_map/ppermute | solution.py:102
  25.3 0.7 pad_maximum_fusion.2
  26.0 1.1 %collective-permute-start.5 = (bf16[80,1024]{1,0:T(8,128)(2,1)}, bf16[80,1024]{1,0:T(8,128)(2,1)}, u32[]{:S(2)}, u32[]{:S(2)}) collective-permute-start(bf16[80,1024]{1,0:T(8,128)(2,1)} %pad_maximum_fusion.2), channel_id=1, source_target_pairs={{0,192},{32,224},{64,0},{96,32},{128,64},{160,96},{192,128},{224,1... | collective-permute-start | bytes 491528 | tf_op jit(solution)/shard_map/ppermute | solution.py:102
  27.1 7.3 %collective-permute-done.5.far_down_ref = bf16[80,1024]{1,0:T(8,128)(2,1)} collective-permute-done((bf16[80,1024]{1,0:T(8,128)(2,1)}, bf16[80,1024]{1,0:T(8,128)(2,1)}, u32[]{:S(2)}, u32[]{:S(2)}) %collective-permute-start.5) | collective-permute-done | bytes 163872 | tf_op jit(solution)/shard_map/ppermute | solution.py:102
  34.4 1.0 %shard_map.37.t_all = bf16[256,2048]{1,0:T(8,128)(2,1)S(1)} custom-call(s32[1]{0:T(128)} %bitcast.at_ref, bf16[56,1024]{1,0:T(8,128)(2,1)S(1)} %pad_maximum_fusion.3.own_ref, bf16[56,1024]{1,0:T(8,128)(2,1)S(1)} %collective-permute-done.up_ref, bf16[56,1024]{1,0:T(8,128)(2,1)S(1)} %collective-permute-done.1.down_ref, ...), custom_call_target="tpu_custom_call" | custom-call | tf_op jit(solution)/shard_map/pallas_call | solution.py:84
  35.4 0.1 collective-permute-start.10
  35.5 0.1 collective-permute-start.8
  35.7 3.3 %collective-permute-start.9 = (bf16[112,2048]{1,0:T(8,128)(2,1)S(1)}, bf16[112,2048]{1,0:T(8,128)(2,1)S(1)}, u32[]{:S(2)}, u32[]{:S(2)}) collective-permute-start(bf16[112,2048]{1,0:T(8,128)(2,1)S(1)} %slice.31), channel_id=1, source_target_pairs={{0,5},{1,4},{2,26},{3,27},{4,0},{5,1},{6,30},{7,31},{8,13},{9,12},... | collective-permute-start | bytes 1376264 | tf_op jit(solution)/shard_map/ppermute | solution.py:98
  39.6 5.7 %collective-permute-done.8.low_ref = bf16[112,2048]{1,0:T(8,128)(2,1)S(1)} collective-permute-done((bf16[112,2048]{1,0:T(8,128)(2,1)S(1)}, bf16[112,2048]{1,0:T(8,128)(2,1)S(1)}, u32[]{:S(2)}, u32[]{:S(2)}) %collective-permute-start.8) | collective-permute-done | bytes 458784 | tf_op jit(solution)/shard_map/ppermute | solution.py:98
  45.3 2.5 %shard_map.39 = f32[248,2048]{1,0:T(8,128)S(1)} custom-call(f32[1]{0:T(128)S(6)} %copy.4.spread_ref, bf16[256,2048]{1,0:T(8,128)(2,1)S(1)} %collective-permute-done.10.t_all, bf16[224,2048]{1,0:T(8,128)(2,1)S(1)} %bitcast.8, bf16[224,2048]{1,0:T(8,128)(2,1)S(1)} %collective-permute-done.6.back_ref, bf16[224,2048]{1,0:T(8,128)(2,1)S(1)} %collective-permute-done.7.ahead_ref, ...), custom_call_target="tpu_custom_call" | custom-call | tf_op jit(solution)/shard_map/pallas_call | solution.py:146
  47.8 0.3 collective-permute-start.11
  48.1 2.5 %shard_map.38 = f32[248,2048]{1,0:T(8,128)S(1)} custom-call(f32[1]{0:T(128)S(6)} %copy.4.spread_ref, bf16[256,2048]{1,0:T(8,128)(2,1)S(1)} %shard_map.37.t_all, bf16[224,2048]{1,0:T(8,128)(2,1)S(1)} %bitcast.9, bf16[224,2048]{1,0:T(8,128)(2,1)S(1)} %collective-permute-done.6.back_ref, bf16[224,2048]{1,0:T(8,128)(2,1)S(1)} %collective-permute-done.7.ahead_ref, ...), custom_call_target="tpu_custom_call" | custom-call | tf_op jit(solution)/shard_map/pallas_call | solution.py:146
  50.5 1.6 %collective-permute-done.11 = f32[248,2048]{1,0:T(8,128)S(1)} collective-permute-done((f32[248,2048]{1,0:T(8,128)S(1)}, f32[248,2048]{1,0:T(8,128)S(1)}, u32[]{:S(2)}, u32[]{:S(2)}) %collective-permute-start.11) | collective-permute-done | bytes 2031648 | tf_op jit(solution)/shard_map/ppermute | solution.py:178
  52.1 0.3 add_multiply_fusion
  52.4 30.5 %fusion = f32[32,2048]{1,0:T(8,128)S(1)} fusion(f32[248,2048]{1,0:T(8,128)S(1)} %add_multiply_fusion), kind=kCustom, calls=%all-reduce-scatter | all-reduce-scatter fusion | flops 524289 | bytes 2294784
  83.0 3.1 %collective-permute-start.12 = (f32[7,2048]{1,0:T(8,128)S(1)}, f32[7,2048]{1,0:T(8,128)S(1)}, u32[]{:S(2)}, u32[]{:S(2)}) collective-permute-start(f32[7,2048]{1,0:T(8,128)S(1)} %slice.33), channel_id=1, source_target_pairs={{0,32},{32,64},{64,96},{96,128},{128,160},{160,192},{192,224},{1,3... | collective-permute-start | bytes 172040
  86.1 0.6 dynamic-slice.4
  87.3 1.8 %collective-permute-done.12 = f32[7,2048]{1,0:T(8,128)S(1)} collective-permute-done((f32[7,2048]{1,0:T(8,128)S(1)}, f32[7,2048]{1,0:T(8,128)S(1)}, u32[]{:S(2)}, u32[]{:S(2)}) %collective-permute-start.12) | collective-permute-done | bytes 57376
  89.1 0.2 concatenate.16
  89.4 0.7 constant_dynamic-slice_fusion
  (19 shorter events, 0.1 us)
Async XLA Ops:
  0.0 6.4 %copy-start = (bf16[28,2048]{1,0:T(8,128)(2,1)S(1)}, bf16[28,2048]{1,0:T(8,128)(2,1)}, u32[]{:S(2)}) copy-start(bf16[28,2048]{1,0:T(8,128)(2,1)} %param.3) | copy-start | bytes 344068
  2.1 16.2 %all-to-all-start = ((bf16[4,56,2048]{2,1,0:T(8,128)(2,1)}), bf16[4,56,2048]{2,1,0:T(8,128)(2,1)S(1)}, u32[]{:S(2)}, u32[]{:S(2)}) async-start(bf16[4,56,2048]{2,1,0:T(8,128)(2,1)} %broadcast_in_dim.10), calls=%async_computation | async-start | bytes 1835008 | tf_op jit(solution)/shard_map/all_to_all | solution.py:41
  6.4 4.9 %collective-permute-start = (bf16[56,1024]{1,0:T(8,128)(2,1)S(1)}, bf16[56,1024]{1,0:T(8,128)(2,1)S(1)}, u32[]{:S(2)}, u32[]{:S(2)}) collective-permute-start(bf16[56,1024]{1,0:T(8,128)(2,1)S(1)} %pad_maximum_fusion.3.own_ref), channel_id=1, source_target_pairs={{0,32},{32,64},{64,96},{96,128},{128,160},{160,192},{192,224},{224... | collective-permute-start | bytes 344072 | tf_op jit(solution)/shard_map/ppermute | solution.py:102
  8.4 4.8 %collective-permute-start.1 = (bf16[56,1024]{1,0:T(8,128)(2,1)S(1)}, bf16[56,1024]{1,0:T(8,128)(2,1)S(1)}, u32[]{:S(2)}, u32[]{:S(2)}) collective-permute-start(bf16[56,1024]{1,0:T(8,128)(2,1)S(1)} %pad_maximum_fusion.3.own_ref), channel_id=1, source_target_pairs={{0,224},{32,0},{64,32},{96,64},{128,96},{160,128},{192,160},{224,1... | collective-permute-start | bytes 344072 | tf_op jit(solution)/shard_map/ppermute | solution.py:102
  11.3 7.0 %collective-permute-start.2 = (bf16[56,1024]{1,0:T(8,128)(2,1)S(1)}, bf16[56,1024]{1,0:T(8,128)(2,1)S(1)}, u32[]{:S(2)}, u32[]{:S(2)}) collective-permute-start(bf16[56,1024]{1,0:T(8,128)(2,1)S(1)} %collective-permute-done.up_ref), channel_id=1, source_target_pairs={{0,32},{32,64},{64,96},{96,128},{128,160},{160,192},{192,224},{224... | collective-permute-start | bytes 344072 | tf_op jit(solution)/shard_map/ppermute | solution.py:102
  13.2 12.1 %collective-permute-start.3 = (bf16[56,1024]{1,0:T(8,128)(2,1)S(1)}, bf16[56,1024]{1,0:T(8,128)(2,1)S(1)}, u32[]{:S(2)}, u32[]{:S(2)}) collective-permute-start(bf16[56,1024]{1,0:T(8,128)(2,1)S(1)} %collective-permute-done.1.down_ref), channel_id=1, source_target_pairs={{0,224},{32,0},{64,32},{96,64},{128,96},{160,128},{192,160},{224,1... | collective-permute-start | bytes 344072 | tf_op jit(solution)/shard_map/ppermute | solution.py:102
  18.3 17.2 %collective-permute-start.6 = (bf16[224,2048]{1,0:T(8,128)(2,1)S(1)}, bf16[224,2048]{1,0:T(8,128)(2,1)S(1)}, u32[]{:S(2)}, u32[]{:S(2)}) collective-permute-start(bf16[224,2048]{1,0:T(8,128)(2,1)S(1)} %bitcast.6), channel_id=1, source_target_pairs={{0,4},{1,5},{2,10},{3,11},{4,1},{5,0},{6,14},{7,15},{8,12},{9,13},... | collective-permute-start | bytes 2752520 | tf_op jit(solution)/shard_map/ppermute | solution.py:98
  20.1 15.5 %collective-permute-start.7 = (bf16[224,2048]{1,0:T(8,128)(2,1)S(1)}, bf16[224,2048]{1,0:T(8,128)(2,1)S(1)}, u32[]{:S(2)}, u32[]{:S(2)}) collective-permute-start(bf16[224,2048]{1,0:T(8,128)(2,1)S(1)} %bitcast.7), channel_id=1, source_target_pairs={{0,5},{1,4},{2,26},{3,27},{4,0},{5,1},{6,30},{7,31},{8,13},{9,12},... | collective-permute-start | bytes 2752520 | tf_op jit(solution)/shard_map/ppermute | solution.py:98
  22.3 12.1 %collective-permute-start.4 = (bf16[88,1024]{1,0:T(8,128)(2,1)}, bf16[88,1024]{1,0:T(8,128)(2,1)S(1)}, u32[]{:S(2)}, u32[]{:S(2)}) collective-permute-start(bf16[88,1024]{1,0:T(8,128)(2,1)} %pad_maximum_fusion.1), channel_id=1, source_target_pairs={{0,64},{32,96},{64,128},{96,160},{128,192},{160,224},{192,0},{224,... | collective-permute-start | bytes 540680 | tf_op jit(solution)/shard_map/ppermute | solution.py:102
  26.0 8.4 %collective-permute-start.5 = (bf16[80,1024]{1,0:T(8,128)(2,1)}, bf16[80,1024]{1,0:T(8,128)(2,1)}, u32[]{:S(2)}, u32[]{:S(2)}) collective-permute-start(bf16[80,1024]{1,0:T(8,128)(2,1)} %pad_maximum_fusion.2), channel_id=1, source_target_pairs={{0,192},{32,224},{64,0},{96,32},{128,64},{160,96},{192,128},{224,1... | collective-permute-start | bytes 491528 | tf_op jit(solution)/shard_map/ppermute | solution.py:102
  35.4 4.2 %collective-permute-start.10 = (bf16[256,2048]{1,0:T(8,128)(2,1)S(1)}, bf16[256,2048]{1,0:T(8,128)(2,1)S(1)}, u32[]{:S(2)}, u32[]{:S(2)}) collective-permute-start(bf16[256,2048]{1,0:T(8,128)(2,1)S(1)} %shard_map.37.t_all), channel_id=1, source_target_pairs={{0,2},{2,0},{1,3},{3,1},{4,6},{6,4},{5,7},{7,5},{8,10},{10,8},{9,1... | collective-permute-start | bytes 3145736 | tf_op jit(solution)/shard_map/ppermute | solution.py:170
  35.5 9.8 %collective-permute-start.8 = (bf16[112,2048]{1,0:T(8,128)(2,1)S(1)}, bf16[112,2048]{1,0:T(8,128)(2,1)S(1)}, u32[]{:S(2)}, u32[]{:S(2)}) collective-permute-start(bf16[112,2048]{1,0:T(8,128)(2,1)S(1)} %slice.30), channel_id=1, source_target_pairs={{0,4},{1,5},{2,10},{3,11},{4,1},{5,0},{6,14},{7,15},{8,12},{9,13},... | collective-permute-start | bytes 1376264 | tf_op jit(solution)/shard_map/ppermute | solution.py:98
  35.7 9.6 %collective-permute-start.9 = (bf16[112,2048]{1,0:T(8,128)(2,1)S(1)}, bf16[112,2048]{1,0:T(8,128)(2,1)S(1)}, u32[]{:S(2)}, u32[]{:S(2)}) collective-permute-start(bf16[112,2048]{1,0:T(8,128)(2,1)S(1)} %slice.31), channel_id=1, source_target_pairs={{0,5},{1,4},{2,26},{3,27},{4,0},{5,1},{6,30},{7,31},{8,13},{9,12},... | collective-permute-start | bytes 1376264 | tf_op jit(solution)/shard_map/ppermute | solution.py:98
  47.8 4.3 %collective-permute-start.11 = (f32[248,2048]{1,0:T(8,128)S(1)}, f32[248,2048]{1,0:T(8,128)S(1)}, u32[]{:S(2)}, u32[]{:S(2)}) collective-permute-start(f32[248,2048]{1,0:T(8,128)S(1)} %shard_map.39), channel_id=1, source_target_pairs={{0,2},{2,0},{1,3},{3,1},{4,6},{6,4},{5,7},{7,5},{8,10},{10,8},{9,1... | collective-permute-start | bytes 6094856 | tf_op jit(solution)/shard_map/ppermute | solution.py:178
  52.4 33.7 %copy-start.1 = (u32[256]{0:T(256)S(1)}, u32[256]{0:T(256)}, u32[]{:S(2)}) copy-start(u32[256]{0:T(256)} %constant.13) | copy-start | bytes 3076
  83.0 6.2 %collective-permute-start.12 = (f32[7,2048]{1,0:T(8,128)S(1)}, f32[7,2048]{1,0:T(8,128)S(1)}, u32[]{:S(2)}, u32[]{:S(2)}) collective-permute-start(f32[7,2048]{1,0:T(8,128)S(1)} %slice.33), channel_id=1, source_target_pairs={{0,32},{32,64},{64,96},{96,128},{128,160},{160,192},{192,224},{1,3... | collective-permute-start | bytes 172040

commit v10 on v9

--- a/solution.py
+++ b/solution.py
@@ -102,14 +102,15 @@
     return lax.ppermute(value, "z", [(i, (i + steps) % TARGETS) for i in range(TARGETS)])
 
 
-def part_kernel(spread_ref, t_all, line_ref, back_ref, ahead_ref, low_ref, high_ref, out, x_all, s_all, low_all):
+def part_kernel(spread_ref, t_all, line_ref, *refs):
+    half_refs, (out, x_all, s_all, low_all) = refs[:6], refs[6:]
     inverse = 1.0 / spread_ref[0]
     targets = t_all[...]
     target_norm = row_norms(targets)
     row_total = jnp.zeros((TARGETS * PAD, 1), jnp.float32)
     pieces = [
         (ref, i * 2 * ROWS)
-        for ref, count in ((line_ref, 4), (back_ref, 4), (ahead_ref, 4), (low_ref, 2), (high_ref, 2))
+        for ref, count in ((line_ref, 4), *((half, 2) for half in half_refs))
         for i in range(count)
     ]
     for step in range(PIECES // STEP):
@@ -169,11 +170,13 @@
     targets = prepared(at, [own_piece, up, down, up2, down2, far_up, far_down])
     others = lax.ppermute(targets, "c", swap)
     line = sent_along(jnp.concatenate([particles, scores], axis=0), plane_lines(True))
-    back, ahead = moved_across(line, 1), moved_across(line, -1)
     middle = 4 * ROWS
-    low_half, high_half = back[:middle], ahead[middle:]
-    opposite = [moved_across(low_half, 1), moved_across(high_half, -1)]
-    sources = [line, back, ahead, *opposite]
+    back_low = moved_across(line[:middle], 1)
+    ahead_high = moved_across(line[middle:], -1)
+    back_high = moved_across(line[middle:], 1)
+    ahead_low = moved_across(line[:middle], -1)
+    opposite = [moved_across(back_low, 1), moved_across(ahead_high, -1)]
+    sources = [line, back_low, back_high, ahead_low, ahead_high, *opposite]
     theirs = part(spread, others, sources)
     arrived = lax.ppermute(theirs, "c", swap)
     mine = part(spread, targets, sources)

time: 90.7 us -> 95.4 us (1.052)
  starting transfers between devices: 24.9 us -> 29.8 us
  waiting for transfers between devices: 21.9 us -> 23.8 us
  other arithmetic: 2.72 us -> 1.39 us
    ppermute x4 -> x6, waiting for transfers between devices: 5.68 us -> 9.25 us  [moved_across(): return lax.ppermute(value, AXES, sorted(pairs))]
    ppermute x4 -> x6, starting transfers between devices: 6.69 us -> 10.1 us  [moved_across(): return lax.ppermute(value, AXES, sorted(pairs))]
    ppermute x6, starting transfers between devices: 10.5 us -> 12.3 us  [moved(): lax.ppermute(value, 'z', [(i, (i + steps) % TARGETS) for i in range(TARGE...]
    ppermute x6, waiting for transfers between devices: 12.8 us -> 11 us  [moved(): lax.ppermute(value, 'z', [(i, (i + steps) % TARGETS) for i in range(TARGE...]
  transfers between devices with their start and end apart: 14 -> 16, of which waited for: 6 -> 10; matrix products, arithmetic and copies ran while one was open for 2% -> 1% of each run, Pallas kernels for 4% -> 3%
where the time goes in v10:
time: 95.4 us; the launch traced here: 95.2 us
  blocking collectives  31.1 us (33%)
  starting transfers between devices  29.8 us (31%)
  waiting for transfers between devices  23.8 us (25%)
  Pallas kernels  5.04 us (5%)
  local copies, waits for them, and re-layouts  2.69 us (3%)
  between operations  1.45 us (2%)
  other arithmetic  1.39 us (1%)
    unnamed x1, blocking collectives  31.1 us
    ppermute x6, starting transfers between devices, moved(): lax.ppermute(value, 'z', [(i, (i + steps) % TARGETS) for i in range(TARGE...  12.3 us
    ppermute x6, waiting for transfers between devices, moved(): lax.ppermute(value, 'z', [(i, (i + steps) % TARGETS) for i in range(TARGE...  11 us
    ppermute x6, starting transfers between devices, moved_across(): return lax.ppermute(value, AXES, sorted(pairs))  10.1 us
    ppermute x6, waiting for transfers between devices, moved_across(): return lax.ppermute(value, AXES, sorted(pairs))  9.25 us
    pallas_call x2, Pallas kernels, part(): pl.pallas_call(part_kernel, in_specs=[pl.BlockSpec(memory_space=pltpu.SME...  4.94 us
    all_to_all x1, starting transfers between devices, sent_along(): lax.all_to_all(jnp.broadcast_to(value[None], (count, *value.shape)), AXES...  4.29 us
    unnamed x1, starting transfers between devices  2.92 us
  transfers between devices with their start and end apart: 16, of which 10 were waited for; matrix products, arithmetic and copies ran while one was open for 1% of the time, Pallas kernels for 3%

profile of v10, /device:TPU:32, one launch (start us, length us, event | category | flops | bytes accessed | tf_op | source)
XLA Modules:
  0.0 95.2 jit_solution(3278624628516500003)
XLA Ops:
  0.0 1.0 %pad_maximum_fusion = bf16[56,2048]{1,0:T(8,128)(2,1)S(1)} fusion(bf16[28,2048]{1,0:T(8,128)(2,1)} %param.4, bf16[28,2048]{1,0:T(8,128)(2,1)} %param.3), kind=kLoop, calls=%fused_computation.1 | loop fusion | flops 458752 | bytes 458752 | tf_op jit(solution)/shard_map/concatenate | solution.py:172
  1.1 1.0 %broadcast_in_dim.10 = bf16[4,56,2048]{2,1,0:T(8,128)(2,1)} broadcast(bf16[56,2048]{1,0:T(8,128)(2,1)S(1)} %pad_maximum_fusion), dimensions={1,2} | broadcast | bytes 1146880 | tf_op jit(solution)/shard_map/broadcast_in_dim | solution.py:42
  2.1 4.3 %all-to-all-start = ((bf16[4,56,2048]{2,1,0:T(8,128)(2,1)}), bf16[4,56,2048]{2,1,0:T(8,128)(2,1)S(1)}, u32[]{:S(2)}, u32[]{:S(2)}) async-start(bf16[4,56,2048]{2,1,0:T(8,128)(2,1)} %broadcast_in_dim.10), calls=%async_computation | async-start | bytes 1835008 | tf_op jit(solution)/shard_map/all_to_all | solution.py:41
  6.4 2.0 %collective-permute-start = (bf16[56,1024]{1,0:T(8,128)(2,1)S(1)}, bf16[56,1024]{1,0:T(8,128)(2,1)S(1)}, u32[]{:S(2)}, u32[]{:S(2)}) collective-permute-start(bf16[56,1024]{1,0:T(8,128)(2,1)S(1)} %pad_maximum_fusion.3.own_ref), channel_id=1, source_target_pairs={{0,32},{32,64},{64,96},{96,128},{128,160},{160,192},{192,224},{224... | collective-permute-start | bytes 344072 | tf_op jit(solution)/shard_map/ppermute | solution.py:102
  8.5 2.8 %collective-permute-done.up_ref = bf16[56,1024]{1,0:T(8,128)(2,1)S(1)} collective-permute-done((bf16[56,1024]{1,0:T(8,128)(2,1)S(1)}, bf16[56,1024]{1,0:T(8,128)(2,1)S(1)}, u32[]{:S(2)}, u32[]{:S(2)}) %collective-permute-start) | collective-permute-done | bytes 114720 | tf_op jit(solution)/shard_map/ppermute | solution.py:102
  11.3 1.9 %collective-permute-start.2 = (bf16[56,1024]{1,0:T(8,128)(2,1)S(1)}, bf16[56,1024]{1,0:T(8,128)(2,1)S(1)}, u32[]{:S(2)}, u32[]{:S(2)}) collective-permute-start(bf16[56,1024]{1,0:T(8,128)(2,1)S(1)} %collective-permute-done.up_ref), channel_id=1, source_target_pairs={{0,32},{32,64},{64,96},{96,128},{128,160},{160,192},{192,224},{224... | collective-permute-start | bytes 344072 | tf_op jit(solution)/shard_map/ppermute | solution.py:102
  13.2 2.3 %collective-permute-start.3 = (bf16[56,1024]{1,0:T(8,128)(2,1)S(1)}, bf16[56,1024]{1,0:T(8,128)(2,1)S(1)}, u32[]{:S(2)}, u32[]{:S(2)}) collective-permute-start(bf16[56,1024]{1,0:T(8,128)(2,1)S(1)} %collective-permute-done.1.down_ref), channel_id=1, source_target_pairs={{0,224},{32,0},{64,32},{96,64},{128,96},{160,128},{192,160},{224,1... | collective-permute-start | bytes 344072 | tf_op jit(solution)/shard_map/ppermute | solution.py:102
  15.5 2.8 %collective-permute-done.2.up2_ref = bf16[56,1024]{1,0:T(8,128)(2,1)S(1)} collective-permute-done((bf16[56,1024]{1,0:T(8,128)(2,1)S(1)}, bf16[56,1024]{1,0:T(8,128)(2,1)S(1)}, u32[]{:S(2)}, u32[]{:S(2)}) %collective-permute-start.2) | collective-permute-done | bytes 114720 | tf_op jit(solution)/shard_map/ppermute | solution.py:102
  18.3 3.1 %collective-permute-start.4 = (bf16[88,1024]{1,0:T(8,128)(2,1)S(1)}, bf16[88,1024]{1,0:T(8,128)(2,1)S(1)}, u32[]{:S(2)}, u32[]{:S(2)}) collective-permute-start(bf16[88,1024]{1,0:T(8,128)(2,1)S(1)} %pad_maximum_fusion.1), channel_id=1, source_target_pairs={{0,64},{32,96},{64,128},{96,160},{128,192},{160,224},{192,0},{224,... | collective-permute-start | bytes 540680 | tf_op jit(solution)/shard_map/ppermute | solution.py:102
  21.4 2.9 %collective-permute-start.5 = (bf16[80,1024]{1,0:T(8,128)(2,1)S(1)}, bf16[80,1024]{1,0:T(8,128)(2,1)S(1)}, u32[]{:S(2)}, u32[]{:S(2)}) collective-permute-start(bf16[80,1024]{1,0:T(8,128)(2,1)S(1)} %pad_maximum_fusion.2), channel_id=1, source_target_pairs={{0,192},{32,224},{64,0},{96,32},{128,64},{160,96},{192,128},{224,1... | collective-permute-start | bytes 491528 | tf_op jit(solution)/shard_map/ppermute | solution.py:102
  24.3 5.4 %collective-permute-done.5.far_down_ref = bf16[80,1024]{1,0:T(8,128)(2,1)S(1)} collective-permute-done((bf16[80,1024]{1,0:T(8,128)(2,1)S(1)}, bf16[80,1024]{1,0:T(8,128)(2,1)S(1)}, u32[]{:S(2)}, u32[]{:S(2)}) %collective-permute-start.5) | collective-permute-done | bytes 163872 | tf_op jit(solution)/shard_map/ppermute | solution.py:102
  30.0 1.7 %collective-permute-start.6 = (bf16[112,2048]{1,0:T(8,128)(2,1)S(1)}, bf16[112,2048]{1,0:T(8,128)(2,1)S(1)}, u32[]{:S(2)}, u32[]{:S(2)}) collective-permute-start(bf16[112,2048]{1,0:T(8,128)(2,1)S(1)} %bitcast.10), channel_id=1, source_target_pairs={{0,4},{1,5},{2,10},{3,11},{4,1},{5,0},{6,14},{7,15},{8,12},{9,13},... | collective-permute-start | bytes 1376264 | tf_op jit(solution)/shard_map/ppermute | solution.py:98
  31.7 1.8 %collective-permute-start.9 = (bf16[112,2048]{1,0:T(8,128)(2,1)S(1)}, bf16[112,2048]{1,0:T(8,128)(2,1)S(1)}, u32[]{:S(2)}, u32[]{:S(2)}) collective-permute-start(bf16[112,2048]{1,0:T(8,128)(2,1)S(1)} %bitcast.12), channel_id=1, source_target_pairs={{0,5},{1,4},{2,26},{3,27},{4,0},{5,1},{6,30},{7,31},{8,13},{9,12},... | collective-permute-start | bytes 1376264 | tf_op jit(solution)/shard_map/ppermute | solution.py:98
  33.5 0.2 collective-permute-start.7
  33.7 3.1 %collective-permute-start.8 = (bf16[112,2048]{1,0:T(8,128)(2,1)S(1)}, bf16[112,2048]{1,0:T(8,128)(2,1)S(1)}, u32[]{:S(2)}, u32[]{:S(2)}) collective-permute-start(bf16[112,2048]{1,0:T(8,128)(2,1)S(1)} %bitcast.11), channel_id=1, source_target_pairs={{0,5},{1,4},{2,26},{3,27},{4,0},{5,1},{6,30},{7,31},{8,13},{9,12},... | collective-permute-start | bytes 1376264 | tf_op jit(solution)/shard_map/ppermute | solution.py:98
  36.8 3.1 %collective-permute-done.6.refs_0_ = bf16[112,2048]{1,0:T(8,128)(2,1)S(1)} collective-permute-done((bf16[112,2048]{1,0:T(8,128)(2,1)S(1)}, bf16[112,2048]{1,0:T(8,128)(2,1)S(1)}, u32[]{:S(2)}, u32[]{:S(2)}) %collective-permute-start.6) | collective-permute-done | bytes 458784 | tf_op jit(solution)/shard_map/ppermute | solution.py:98
  39.9 0.3 collective-permute-start.10
  40.2 3.1 %collective-permute-start.11 = (bf16[112,2048]{1,0:T(8,128)(2,1)S(1)}, bf16[112,2048]{1,0:T(8,128)(2,1)S(1)}, u32[]{:S(2)}, u32[]{:S(2)}) collective-permute-start(bf16[112,2048]{1,0:T(8,128)(2,1)S(1)} %collective-permute-done.9.refs_3_), channel_id=1, source_target_pairs={{0,5},{1,4},{2,26},{3,27},{4,0},{5,1},{6,30},{7,31},{8,13},{9,12},... | collective-permute-start | bytes 1376264 | tf_op jit(solution)/shard_map/ppermute | solution.py:98
  43.9 0.9 collective-permute-done.7.refs_1_
  44.8 0.3 collective-permute-done.8.refs_2_
  45.1 4.6 %collective-permute-done.10.refs_4_ = bf16[112,2048]{1,0:T(8,128)(2,1)S(1)} collective-permute-done((bf16[112,2048]{1,0:T(8,128)(2,1)S(1)}, bf16[112,2048]{1,0:T(8,128)(2,1)S(1)}, u32[]{:S(2)}, u32[]{:S(2)}) %collective-permute-start.10) | collective-permute-done | bytes 458784 | tf_op jit(solution)/shard_map/ppermute | solution.py:98
  49.7 0.3 collective-permute-done.11.refs_5_
  50.0 2.5 %shard_map.39 = f32[248,2048]{1,0:T(8,128)S(1)} custom-call(f32[1]{0:T(128)S(6)} %copy.4.spread_ref, bf16[256,2048]{1,0:T(8,128)(2,1)S(1)} %collective-permute-done.12.t_all, bf16[224,2048]{1,0:T(8,128)(2,1)S(1)} %bitcast.8, bf16[112,2048]{1,0:T(8,128)(2,1)S(1)} %collective-permute-done.6.refs_0_, bf16[112,2048]{1,0:T(8,128)(2,1)S(1)} %collective-permute-done.7.refs_1_, ...), custom_call_target="tpu_custom_call" | custom-call | tf_op jit(solution)/shard_map/pallas_call | solution.py:147
  52.6 2.5 %shard_map.38 = f32[248,2048]{1,0:T(8,128)S(1)} custom-call(f32[1]{0:T(128)S(6)} %copy.4.spread_ref, bf16[256,2048]{1,0:T(8,128)(2,1)S(1)} %shard_map.37.t_all, bf16[224,2048]{1,0:T(8,128)(2,1)S(1)} %bitcast.9, bf16[112,2048]{1,0:T(8,128)(2,1)S(1)} %collective-permute-done.6.refs_0_, bf16[112,2048]{1,0:T(8,128)(2,1)S(1)} %collective-permute-done.7.refs_1_, ...), custom_call_target="tpu_custom_call" | custom-call | tf_op jit(solution)/shard_map/pallas_call | solution.py:147
  55.1 1.6 %collective-permute-done.13 = f32[248,2048]{1,0:T(8,128)S(1)} collective-permute-done((f32[248,2048]{1,0:T(8,128)S(1)}, f32[248,2048]{1,0:T(8,128)S(1)}, u32[]{:S(2)}, u32[]{:S(2)}) %collective-permute-start.13) | collective-permute-done | bytes 2031648 | tf_op jit(solution)/shard_map/ppermute | solution.py:181
  56.6 0.3 add_multiply_fusion
  56.9 31.1 %fusion = f32[32,2048]{1,0:T(8,128)S(1)} fusion(f32[248,2048]{1,0:T(8,128)S(1)} %add_multiply_fusion), kind=kCustom, calls=%all-reduce-scatter | all-reduce-scatter fusion | flops 524289 | bytes 2294784
  88.1 2.9 %collective-permute-start.14 = (f32[7,2048]{1,0:T(8,128)S(1)}, f32[7,2048]{1,0:T(8,128)S(1)}, u32[]{:S(2)}, u32[]{:S(2)}) collective-permute-start(f32[7,2048]{1,0:T(8,128)S(1)} %slice.43), channel_id=1, source_target_pairs={{0,32},{32,64},{64,96},{96,128},{128,160},{160,192},{192,224},{1,3... | collective-permute-start | bytes 172040
  91.0 0.6 dynamic-slice.4
  92.3 2.0 %collective-permute-done.14 = f32[7,2048]{1,0:T(8,128)S(1)} collective-permute-done((f32[7,2048]{1,0:T(8,128)S(1)}, f32[7,2048]{1,0:T(8,128)S(1)}, u32[]{:S(2)}, u32[]{:S(2)}) %collective-permute-start.14) | collective-permute-done | bytes 57376
  94.2 0.2 concatenate.16
  94.5 0.7 constant_dynamic-slice_fusion
  (22 shorter events, 0.6 us)
Async XLA Ops:
  0.0 6.4 %copy-start = (bf16[28,2048]{1,0:T(8,128)(2,1)S(1)}, bf16[28,2048]{1,0:T(8,128)(2,1)}, u32[]{:S(2)}) copy-start(bf16[28,2048]{1,0:T(8,128)(2,1)} %param.3) | copy-start | bytes 344068
  2.1 27.9 %all-to-all-start = ((bf16[4,56,2048]{2,1,0:T(8,128)(2,1)}), bf16[4,56,2048]{2,1,0:T(8,128)(2,1)S(1)}, u32[]{:S(2)}, u32[]{:S(2)}) async-start(bf16[4,56,2048]{2,1,0:T(8,128)(2,1)} %broadcast_in_dim.10), calls=%async_computation | async-start | bytes 1835008 | tf_op jit(solution)/shard_map/all_to_all | solution.py:41
  6.4 4.9 %collective-permute-start = (bf16[56,1024]{1,0:T(8,128)(2,1)S(1)}, bf16[56,1024]{1,0:T(8,128)(2,1)S(1)}, u32[]{:S(2)}, u32[]{:S(2)}) collective-permute-start(bf16[56,1024]{1,0:T(8,128)(2,1)S(1)} %pad_maximum_fusion.3.own_ref), channel_id=1, source_target_pairs={{0,32},{32,64},{64,96},{96,128},{128,160},{160,192},{192,224},{224... | collective-permute-start | bytes 344072 | tf_op jit(solution)/shard_map/ppermute | solution.py:102
  8.4 4.8 %collective-permute-start.1 = (bf16[56,1024]{1,0:T(8,128)(2,1)S(1)}, bf16[56,1024]{1,0:T(8,128)(2,1)S(1)}, u32[]{:S(2)}, u32[]{:S(2)}) collective-permute-start(bf16[56,1024]{1,0:T(8,128)(2,1)S(1)} %pad_maximum_fusion.3.own_ref), channel_id=1, source_target_pairs={{0,224},{32,0},{64,32},{96,64},{128,96},{160,128},{192,160},{224,1... | collective-permute-start | bytes 344072 | tf_op jit(solution)/shard_map/ppermute | solution.py:102
  11.3 7.0 %collective-permute-start.2 = (bf16[56,1024]{1,0:T(8,128)(2,1)S(1)}, bf16[56,1024]{1,0:T(8,128)(2,1)S(1)}, u32[]{:S(2)}, u32[]{:S(2)}) collective-permute-start(bf16[56,1024]{1,0:T(8,128)(2,1)S(1)} %collective-permute-done.up_ref), channel_id=1, source_target_pairs={{0,32},{32,64},{64,96},{96,128},{128,160},{160,192},{192,224},{224... | collective-permute-start | bytes 344072 | tf_op jit(solution)/shard_map/ppermute | solution.py:102
  13.2 8.2 %collective-permute-start.3 = (bf16[56,1024]{1,0:T(8,128)(2,1)S(1)}, bf16[56,1024]{1,0:T(8,128)(2,1)S(1)}, u32[]{:S(2)}, u32[]{:S(2)}) collective-permute-start(bf16[56,1024]{1,0:T(8,128)(2,1)S(1)} %collective-permute-done.1.down_ref), channel_id=1, source_target_pairs={{0,224},{32,0},{64,32},{96,64},{128,96},{160,128},{192,160},{224,1... | collective-permute-start | bytes 344072 | tf_op jit(solution)/shard_map/ppermute | solution.py:102
  18.3 11.4 %collective-permute-start.4 = (bf16[88,1024]{1,0:T(8,128)(2,1)S(1)}, bf16[88,1024]{1,0:T(8,128)(2,1)S(1)}, u32[]{:S(2)}, u32[]{:S(2)}) collective-permute-start(bf16[88,1024]{1,0:T(8,128)(2,1)S(1)} %pad_maximum_fusion.1), channel_id=1, source_target_pairs={{0,64},{32,96},{64,128},{96,160},{128,192},{160,224},{192,0},{224,... | collective-permute-start | bytes 540680 | tf_op jit(solution)/shard_map/ppermute | solution.py:102
  21.4 8.3 %collective-permute-start.5 = (bf16[80,1024]{1,0:T(8,128)(2,1)S(1)}, bf16[80,1024]{1,0:T(8,128)(2,1)S(1)}, u32[]{:S(2)}, u32[]{:S(2)}) collective-permute-start(bf16[80,1024]{1,0:T(8,128)(2,1)S(1)} %pad_maximum_fusion.2), channel_id=1, source_target_pairs={{0,192},{32,224},{64,0},{96,32},{128,64},{160,96},{192,128},{224,1... | collective-permute-start | bytes 491528 | tf_op jit(solution)/shard_map/ppermute | solution.py:102
  29.8 15.3 %collective-permute-start.12 = (bf16[256,2048]{1,0:T(8,128)(2,1)S(1)}, bf16[256,2048]{1,0:T(8,128)(2,1)S(1)}, u32[]{:S(2)}, u32[]{:S(2)}) collective-permute-start(bf16[256,2048]{1,0:T(8,128)(2,1)S(1)} %shard_map.37.t_all), channel_id=1, source_target_pairs={{0,2},{2,0},{1,3},{3,1},{4,6},{6,4},{5,7},{7,5},{8,10},{10,8},{9,1... | collective-permute-start | bytes 3145736 | tf_op jit(solution)/shard_map/ppermute | solution.py:171
  30.0 9.9 %collective-permute-start.6 = (bf16[112,2048]{1,0:T(8,128)(2,1)S(1)}, bf16[112,2048]{1,0:T(8,128)(2,1)S(1)}, u32[]{:S(2)}, u32[]{:S(2)}) collective-permute-start(bf16[112,2048]{1,0:T(8,128)(2,1)S(1)} %bitcast.10), channel_id=1, source_target_pairs={{0,4},{1,5},{2,10},{3,11},{4,1},{5,0},{6,14},{7,15},{8,12},{9,13},... | collective-permute-start | bytes 1376264 | tf_op jit(solution)/shard_map/ppermute | solution.py:98
  31.7 8.5 %collective-permute-start.9 = (bf16[112,2048]{1,0:T(8,128)(2,1)S(1)}, bf16[112,2048]{1,0:T(8,128)(2,1)S(1)}, u32[]{:S(2)}, u32[]{:S(2)}) collective-permute-start(bf16[112,2048]{1,0:T(8,128)(2,1)S(1)} %bitcast.12), channel_id=1, source_target_pairs={{0,5},{1,4},{2,26},{3,27},{4,0},{5,1},{6,30},{7,31},{8,13},{9,12},... | collective-permute-start | bytes 1376264 | tf_op jit(solution)/shard_map/ppermute | solution.py:98
  33.5 11.3 %collective-permute-start.7 = (bf16[112,2048]{1,0:T(8,128)(2,1)S(1)}, bf16[112,2048]{1,0:T(8,128)(2,1)S(1)}, u32[]{:S(2)}, u32[]{:S(2)}) collective-permute-start(bf16[112,2048]{1,0:T(8,128)(2,1)S(1)} %bitcast.13), channel_id=1, source_target_pairs={{0,4},{1,5},{2,10},{3,11},{4,1},{5,0},{6,14},{7,15},{8,12},{9,13},... | collective-permute-start | bytes 1376264 | tf_op jit(solution)/shard_map/ppermute | solution.py:98
  33.7 11.4 %collective-permute-start.8 = (bf16[112,2048]{1,0:T(8,128)(2,1)S(1)}, bf16[112,2048]{1,0:T(8,128)(2,1)S(1)}, u32[]{:S(2)}, u32[]{:S(2)}) collective-permute-start(bf16[112,2048]{1,0:T(8,128)(2,1)S(1)} %bitcast.11), channel_id=1, source_target_pairs={{0,5},{1,4},{2,26},{3,27},{4,0},{5,1},{6,30},{7,31},{8,13},{9,12},... | collective-permute-start | bytes 1376264 | tf_op jit(solution)/shard_map/ppermute | solution.py:98
  39.9 9.8 %collective-permute-start.10 = (bf16[112,2048]{1,0:T(8,128)(2,1)S(1)}, bf16[112,2048]{1,0:T(8,128)(2,1)S(1)}, u32[]{:S(2)}, u32[]{:S(2)}) collective-permute-start(bf16[112,2048]{1,0:T(8,128)(2,1)S(1)} %collective-permute-done.6.refs_0_), channel_id=1, source_target_pairs={{0,4},{1,5},{2,10},{3,11},{4,1},{5,0},{6,14},{7,15},{8,12},{9,13},... | collective-permute-start | bytes 1376264 | tf_op jit(solution)/shard_map/ppermute | solution.py:98
  40.2 9.8 %collective-permute-start.11 = (bf16[112,2048]{1,0:T(8,128)(2,1)S(1)}, bf16[112,2048]{1,0:T(8,128)(2,1)S(1)}, u32[]{:S(2)}, u32[]{:S(2)}) collective-permute-start(bf16[112,2048]{1,0:T(8,128)(2,1)S(1)} %collective-permute-done.9.refs_3_), channel_id=1, source_target_pairs={{0,5},{1,4},{2,26},{3,27},{4,0},{5,1},{6,30},{7,31},{8,13},{9,12},... | collective-permute-start | bytes 1376264 | tf_op jit(solution)/shard_map/ppermute | solution.py:98
  52.5 4.2 %collective-permute-start.13 = (f32[248,2048]{1,0:T(8,128)S(1)}, f32[248,2048]{1,0:T(8,128)S(1)}, u32[]{:S(2)}, u32[]{:S(2)}) collective-permute-start(f32[248,2048]{1,0:T(8,128)S(1)} %shard_map.39), channel_id=1, source_target_pairs={{0,2},{2,0},{1,3},{3,1},{4,6},{6,4},{5,7},{7,5},{8,10},{10,8},{9,1... | collective-permute-start | bytes 6094856 | tf_op jit(solution)/shard_map/ppermute | solution.py:181
  56.9 34.1 %copy-start.1 = (u32[256]{0:T(256)S(1)}, u32[256]{0:T(256)}, u32[]{:S(2)}) copy-start(u32[256]{0:T(256)} %constant.13) | copy-start | bytes 3076
  88.1 6.2 %collective-permute-start.14 = (f32[7,2048]{1,0:T(8,128)S(1)}, f32[7,2048]{1,0:T(8,128)S(1)}, u32[]{:S(2)}, u32[]{:S(2)}) collective-permute-start(f32[7,2048]{1,0:T(8,128)S(1)} %slice.43), channel_id=1, source_target_pairs={{0,32},{32,64},{64,96},{96,128},{128,160},{160,192},{192,224},{1,3... | collective-permute-start | bytes 172040

commit v11 on v10

--- a/solution.py
+++ b/solution.py
@@ -10,7 +10,6 @@
 POPULATION = 7168
 ROWS = 28
 PAD = 32
-SPAN = 31
 CUT = 32
 DIM = 2048
 TARGETS = 8
@@ -59,12 +58,11 @@
     return jnp.sum(wide * wide, axis=1, keepdims=True)
 
 
-def prepare_kernel(at_ref, own_ref, up_ref, down_ref, up2_ref, down2_ref, far_up_ref, far_down_ref, t_all):
+def prepare_kernel(own_ref, up_ref, down_ref, up2_ref, down2_ref, far_up_ref, far_down_ref, t_all):
     half = DIM // 2
 
     def put(offset, piece):
-        slot = lax.rem(at_ref[0] + TARGETS + offset, TARGETS)
-        rows = pl.ds(pl.multiple_of(slot * PAD, PAD), PAD)
+        rows = pl.ds(offset % TARGETS * PAD, PAD)
         left = padded(piece[:ROWS])
         right = padded(piece[ROWS:])
         t_all[rows, :half] = left
@@ -80,15 +78,14 @@
     put(4, jnp.concatenate([far_up_ref[2 * ROWS :], far_down_ref[2 * ROWS :]], axis=0))
 
 
-def prepared(at, pieces):
+def prepared(pieces):
     return pl.pallas_call(
         prepare_kernel,
-        in_specs=[pl.BlockSpec(memory_space=pltpu.SMEM)]
-        + [pl.BlockSpec(memory_space=pltpu.VMEM)] * len(pieces),
+        in_specs=[pl.BlockSpec(memory_space=pltpu.VMEM)] * len(pieces),
         out_specs=pl.BlockSpec(memory_space=pltpu.VMEM),
         out_shape=pltpu.VMEM((TARGETS * PAD, DIM), jnp.bfloat16),
         compiler_params=pltpu.CompilerParams(vmem_limit_bytes=VMEM_BYTES),
-    )(at, *pieces)
+    )(*pieces)
 
 
 def moved_across(value, steps):
@@ -103,7 +100,7 @@
 
 
 def part_kernel(spread_ref, t_all, line_ref, *refs):
-    half_refs, (out, x_all, s_all, low_all) = refs[:6], refs[6:]
+    half_refs, outs, (x_all, s_all, low_all) = refs[:6], refs[6:8], refs[8:]
     inverse = 1.0 / spread_ref[0]
     targets = t_all[...]
     target_norm = row_norms(targets)
@@ -139,7 +136,8 @@
         wide = t_all[:, columns].astype(jnp.float32)
         added = drive + (2.0 * inverse) * (wide * row_total - pull)
         for i in range(TARGETS):
-            out[pl.ds(i * SPAN, SPAN), columns] = added[i * PAD : i * PAD + SPAN]
+            rows = pl.ds((2 * i + n % 2) * ROWS, ROWS)
+            outs[n // 2][rows, :] = added[i * PAD : i * PAD + ROWS]
 
 
 def part(spread, targets, sources):
@@ -148,8 +146,8 @@
         part_kernel,
         in_specs=[pl.BlockSpec(memory_space=pltpu.SMEM)]
         + [pl.BlockSpec(memory_space=pltpu.VMEM)] * len(args),
-        out_specs=pl.BlockSpec(memory_space=pltpu.VMEM),
-        out_shape=pltpu.VMEM((TARGETS * SPAN, DIM), jnp.float32),
+        out_specs=[pl.BlockSpec(memory_space=pltpu.VMEM)] * 2,
+        out_shape=[pltpu.VMEM((2 * TARGETS * ROWS, WIDTH), jnp.float32)] * 2,
         scratch_shapes=[
             pltpu.VMEM((PIECES * PAD, DIM), jnp.bfloat16),
             pltpu.VMEM((PIECES * PAD, DIM), jnp.bfloat16),
@@ -161,13 +159,12 @@
 
 def direction(particles, scores, spread):
     swap = [(0, 1), (1, 0)]
-    at = lax.axis_index("z").astype(jnp.int32)[None]
     own_piece = jnp.concatenate([particles[:, : DIM // 2], particles[:, DIM // 2 :]], axis=0)
     up, down = moved(own_piece, 1), moved(own_piece, -1)
     up2, down2 = moved(up, 1), moved(down, -1)
     far_up = moved(jnp.concatenate([up, up2[:CUT]], axis=0), 2)
     far_down = moved(jnp.concatenate([down, down2[CUT:]], axis=0), -2)
-    targets = prepared(at, [own_piece, up, down, up2, down2, far_up, far_down])
+    targets = prepared([own_piece, up, down, up2, down2, far_up, far_down])
     others = lax.ppermute(targets, "c", swap)
     line = sent_along(jnp.concatenate([particles, scores], axis=0), plane_lines(True))
     middle = 4 * ROWS
@@ -178,11 +175,23 @@
     opposite = [moved_across(back_low, 1), moved_across(ahead_high, -1)]
     sources = [line, back_low, back_high, ahead_low, ahead_high, *opposite]
     theirs = part(spread, others, sources)
-    arrived = lax.ppermute(theirs, "c", swap)
+    arrived = [lax.ppermute(t, "c", swap) for t in theirs]
     mine = part(spread, targets, sources)
-    partial = (mine + arrived) / POPULATION
-    total = lax.psum_scatter(partial, "z", scatter_dimension=0, tiled=True)
-    return lax.optimization_barrier(total)[:ROWS]
+    halves = [summed_along_z((m + a) / POPULATION) for m, a in zip(mine, arrived)]
+    return jnp.concatenate([rows for h in halves for rows in (h[:ROWS], h[ROWS:])], axis=1)
+
+
+def summed_along_z(partial):
+    chunk = [partial[2 * ROWS * k : 2 * ROWS * (k + 1)] for k in range(TARGETS)]
+    up = moved(chunk[4][:CUT], 1)
+    down = moved(chunk[4][CUT:], -1)
+    up = moved(jnp.concatenate([chunk[3][:CUT] + up, chunk[3][CUT:]], axis=0), 1)
+    down = moved(jnp.concatenate([chunk[5][:CUT], chunk[5][CUT:] + down], axis=0), -1)
+    up = moved(chunk[2] + up, 1)
+    down = moved(chunk[6] + down, -1)
+    up = moved(chunk[1] + up, 1)
+    down = moved(chunk[7] + down, -1)
+    return chunk[0] + up + down
 
 
 def solution(mesh):

time: 95.4 us -> 101 us (1.059)
  the two profiles are of different devices: /device:TPU:32 before, /device:TPU:96 now
where the time goes in v11:
time: 101 us
  starting transfers between devices  48.3 us (48%)
  waiting for transfers between devices  42.7 us (42%)
  Pallas kernels  4.99 us (5%)
  other arithmetic  2.47 us (2%)
  local copies, waits for them, and re-layouts  1.17 us (1%)
    ppermute x22, starting transfers between devices, moved(): lax.ppermute(value, 'z', [(i, (i + steps) % TARGETS) for i in range(TARGE...  34.6 us
    ppermute x22, waiting for transfers between devices, moved(): lax.ppermute(value, 'z', [(i, (i + steps) % TARGETS) for i in range(TARGE...  31.6 us
    ppermute x6, waiting for transfers between devices, moved_across(): return lax.ppermute(value, AXES, sorted(pairs))  11 us
    ppermute x6, starting transfers between devices, moved_across(): return lax.ppermute(value, AXES, sorted(pairs))  8.58 us
    pallas_call x2, Pallas kernels, part(): pl.pallas_call(part_kernel, in_specs=[pl.BlockSpec(memory_space=pltpu.SME...  4.89 us
    all_to_all x1, starting transfers between devices, sent_along(): lax.all_to_all(jnp.broadcast_to(value[None], (count, *value.shape)), AXES...  4.42 us
  transfers between devices with their start and end apart: 32, of which 14 were waited for; matrix products, arithmetic and copies ran while one was open for 1% of the time, Pallas kernels for 3%

profile of v11, /device:TPU:96, one launch (start us, length us, event | category | flops | bytes accessed | tf_op | source)
XLA Modules:
  0.0 100.5 jit_solution(10278681508521593041)
XLA Ops:
  1.0 1.0 %broadcast_in_dim.2 = bf16[4,56,2048]{2,1,0:T(8,128)(2,1)} broadcast(bf16[56,2048]{1,0:T(8,128)(2,1)S(1)} %pad_maximum_fusion.1), dimensions={1,2} | broadcast | bytes 1146880 | tf_op jit(solution)/shard_map/broadcast_in_dim | solution.py:41
  2.1 4.4 %all-to-all-start = ((bf16[4,56,2048]{2,1,0:T(8,128)(2,1)}), bf16[4,56,2048]{2,1,0:T(8,128)(2,1)S(1)}, u32[]{:S(2)}, u32[]{:S(2)}) async-start(bf16[4,56,2048]{2,1,0:T(8,128)(2,1)} %broadcast_in_dim.2), calls=%async_computation | async-start | bytes 1835008 | tf_op jit(solution)/shard_map/all_to_all | solution.py:40
  6.5 3.2 %collective-permute-start = (bf16[56,1024]{1,0:T(8,128)(2,1)S(1)}, bf16[56,1024]{1,0:T(8,128)(2,1)S(1)}, u32[]{:S(2)}, u32[]{:S(2)}) collective-permute-start(bf16[56,1024]{1,0:T(8,128)(2,1)S(1)} %pad_maximum_fusion.4.own_ref), channel_id=1, source_target_pairs={{0,32},{32,64},{64,96},{96,128},{128,160},{160,192},{192,224},{224... | collective-permute-start | bytes 344072 | tf_op jit(solution)/shard_map/ppermute | solution.py:99
  9.7 2.4 %collective-permute-done.up_ref = bf16[56,1024]{1,0:T(8,128)(2,1)S(1)} collective-permute-done((bf16[56,1024]{1,0:T(8,128)(2,1)S(1)}, bf16[56,1024]{1,0:T(8,128)(2,1)S(1)}, u32[]{:S(2)}, u32[]{:S(2)}) %collective-permute-start) | collective-permute-done | bytes 114720 | tf_op jit(solution)/shard_map/ppermute | solution.py:99
  12.1 3.6 %collective-permute-start.2 = (bf16[56,1024]{1,0:T(8,128)(2,1)S(1)}, bf16[56,1024]{1,0:T(8,128)(2,1)S(1)}, u32[]{:S(2)}, u32[]{:S(2)}) collective-permute-start(bf16[56,1024]{1,0:T(8,128)(2,1)S(1)} %collective-permute-done.up_ref), channel_id=1, source_target_pairs={{0,32},{32,64},{64,96},{96,128},{128,160},{160,192},{192,224},{224... | collective-permute-start | bytes 344072 | tf_op jit(solution)/shard_map/ppermute | solution.py:99
  15.7 2.4 %collective-permute-done.2.up2_ref = bf16[56,1024]{1,0:T(8,128)(2,1)S(1)} collective-permute-done((bf16[56,1024]{1,0:T(8,128)(2,1)S(1)}, bf16[56,1024]{1,0:T(8,128)(2,1)S(1)}, u32[]{:S(2)}, u32[]{:S(2)}) %collective-permute-start.2) | collective-permute-done | bytes 114720 | tf_op jit(solution)/shard_map/ppermute | solution.py:99
  18.1 1.9 %collective-permute-start.4 = (bf16[88,1024]{1,0:T(8,128)(2,1)S(1)}, bf16[88,1024]{1,0:T(8,128)(2,1)S(1)}, u32[]{:S(2)}, u32[]{:S(2)}) collective-permute-start(bf16[88,1024]{1,0:T(8,128)(2,1)S(1)} %pad_maximum_fusion.2), channel_id=1, source_target_pairs={{0,64},{32,96},{64,128},{96,160},{128,192},{160,224},{192,0},{224,... | collective-permute-start | bytes 540680 | tf_op jit(solution)/shard_map/ppermute | solution.py:99
  20.1 1.7 %collective-permute-done.3.down2_ref = bf16[56,1024]{1,0:T(8,128)(2,1)S(1)} collective-permute-done((bf16[56,1024]{1,0:T(8,128)(2,1)S(1)}, bf16[56,1024]{1,0:T(8,128)(2,1)S(1)}, u32[]{:S(2)}, u32[]{:S(2)}) %collective-permute-start.3) | collective-permute-done | bytes 114720 | tf_op jit(solution)/shard_map/ppermute | solution.py:99
  21.9 9.2 %collective-permute-done.5.far_down_ref = bf16[80,1024]{1,0:T(8,128)(2,1)S(1)} collective-permute-done((bf16[80,1024]{1,0:T(8,128)(2,1)S(1)}, bf16[80,1024]{1,0:T(8,128)(2,1)S(1)}, u32[]{:S(2)}, u32[]{:S(2)}) %collective-permute-start.5) | collective-permute-done | bytes 163872 | tf_op jit(solution)/shard_map/ppermute | solution.py:99
  31.3 1.9 %collective-permute-start.6 = (bf16[112,2048]{1,0:T(8,128)(2,1)S(1)}, bf16[112,2048]{1,0:T(8,128)(2,1)S(1)}, u32[]{:S(2)}, u32[]{:S(2)}) collective-permute-start(bf16[112,2048]{1,0:T(8,128)(2,1)S(1)} %bitcast.7), channel_id=1, source_target_pairs={{0,4},{1,5},{2,10},{3,11},{4,1},{5,0},{6,14},{7,15},{8,12},{9,13},... | collective-permute-start | bytes 1376264 | tf_op jit(solution)/shard_map/ppermute | solution.py:95
  33.3 1.4 %collective-permute-start.9 = (bf16[112,2048]{1,0:T(8,128)(2,1)S(1)}, bf16[112,2048]{1,0:T(8,128)(2,1)S(1)}, u32[]{:S(2)}, u32[]{:S(2)}) collective-permute-start(bf16[112,2048]{1,0:T(8,128)(2,1)S(1)} %bitcast.5), channel_id=1, source_target_pairs={{0,5},{1,4},{2,26},{3,27},{4,0},{5,1},{6,30},{7,31},{8,13},{9,12},... | collective-permute-start | bytes 1376264 | tf_op jit(solution)/shard_map/ppermute | solution.py:95
  34.7 1.6 %collective-permute-start.8 = (bf16[112,2048]{1,0:T(8,128)(2,1)S(1)}, bf16[112,2048]{1,0:T(8,128)(2,1)S(1)}, u32[]{:S(2)}, u32[]{:S(2)}) collective-permute-start(bf16[112,2048]{1,0:T(8,128)(2,1)S(1)} %bitcast.8), channel_id=1, source_target_pairs={{0,5},{1,4},{2,26},{3,27},{4,0},{5,1},{6,30},{7,31},{8,13},{9,12},... | collective-permute-start | bytes 1376264 | tf_op jit(solution)/shard_map/ppermute | solution.py:95
  36.7 4.4 %collective-permute-done.6.refs_0_ = bf16[112,2048]{1,0:T(8,128)(2,1)S(1)} collective-permute-done((bf16[112,2048]{1,0:T(8,128)(2,1)S(1)}, bf16[112,2048]{1,0:T(8,128)(2,1)S(1)}, u32[]{:S(2)}, u32[]{:S(2)}) %collective-permute-start.6) | collective-permute-done | bytes 458784 | tf_op jit(solution)/shard_map/ppermute | solution.py:95
  41.8 2.6 %collective-permute-start.11 = (bf16[112,2048]{1,0:T(8,128)(2,1)S(1)}, bf16[112,2048]{1,0:T(8,128)(2,1)S(1)}, u32[]{:S(2)}, u32[]{:S(2)}) collective-permute-start(bf16[112,2048]{1,0:T(8,128)(2,1)S(1)} %collective-permute-done.9.refs_3_), channel_id=1, source_target_pairs={{0,5},{1,4},{2,26},{3,27},{4,0},{5,1},{6,30},{7,31},{8,13},{9,12},... | collective-permute-start | bytes 1376264 | tf_op jit(solution)/shard_map/ppermute | solution.py:95
  45.0 1.7 %collective-permute-done.8.refs_2_ = bf16[112,2048]{1,0:T(8,128)(2,1)S(1)} collective-permute-done((bf16[112,2048]{1,0:T(8,128)(2,1)S(1)}, bf16[112,2048]{1,0:T(8,128)(2,1)S(1)}, u32[]{:S(2)}, u32[]{:S(2)}) %collective-permute-start.8) | collective-permute-done | bytes 458784 | tf_op jit(solution)/shard_map/ppermute | solution.py:95
  46.7 4.2 %collective-permute-done.10.refs_4_ = bf16[112,2048]{1,0:T(8,128)(2,1)S(1)} collective-permute-done((bf16[112,2048]{1,0:T(8,128)(2,1)S(1)}, bf16[112,2048]{1,0:T(8,128)(2,1)S(1)}, u32[]{:S(2)}, u32[]{:S(2)}) %collective-permute-start.10) | collective-permute-done | bytes 458784 | tf_op jit(solution)/shard_map/ppermute | solution.py:95
  51.6 2.4 %shard_map.39 = (f32[448,512]{1,0:T(8,128)S(1)}, f32[448,512]{1,0:T(8,128)S(1)}) custom-call(f32[1]{0:T(128)S(6)} %copy.4.spread_ref, bf16[256,2048]{1,0:T(8,128)(2,1)S(1)} %collective-permute-done.12.t_all, bf16[224,2048]{1,0:T(8,128)(2,1)S(1)} %bitcast.3, bf16[112,2048]{1,0:T(8,128)(2,1)S(1)} %collective-permute-done.6.refs_0_, ...), custom_call_target="tpu_custom_call" | custom-call | tf_op jit(solution)/shard_map/pallas_call | solution.py:145
  54.6 2.4 %shard_map.38 = (f32[448,512]{1,0:T(8,128)S(1)}, f32[448,512]{1,0:T(8,128)S(1)}) custom-call(f32[1]{0:T(128)S(6)} %copy.4.spread_ref, bf16[256,2048]{1,0:T(8,128)(2,1)S(1)} %shard_map.37.t_all, bf16[224,2048]{1,0:T(8,128)(2,1)S(1)} %bitcast.4, bf16[112,2048]{1,0:T(8,128)(2,1)S(1)} %collective-permute-done.6.refs_0_, ...), custom_call_target="tpu_custom_call" | custom-call | tf_op jit(solution)/shard_map/pallas_call | solution.py:145
  57.3 1.7 %collective-permute-start.18 = (f32[24,512]{1,0:T(8,128)S(1)}, f32[24,512]{1,0:T(8,128)S(1)}, u32[]{:S(2)}, u32[]{:S(2)}) collective-permute-start(f32[24,512]{1,0:T(8,128)S(1)} %get-tuple-element.18), channel_id=1, source_target_pairs={{0,224},{32,0},{64,32},{96,64},{128,96},{160,128},{192,160},{224,1... | collective-permute-start | bytes 147464 | tf_op jit(solution)/shard_map/ppermute | solution.py:99
  59.3 1.7 %collective-permute-start.14 = (f32[32,512]{1,0:T(8,128)S(1)}, f32[32,512]{1,0:T(8,128)S(1)}, u32[]{:S(2)}, u32[]{:S(2)}) collective-permute-start(f32[32,512]{1,0:T(8,128)S(1)} %slice.164), channel_id=1, source_target_pairs={{0,32},{32,64},{64,96},{96,128},{128,160},{160,192},{192,224},{224... | collective-permute-start | bytes 196616 | tf_op jit(solution)/shard_map/ppermute | solution.py:99
  61.1 1.9 %collective-permute-start.27 = (f32[24,512]{1,0:T(8,128)S(1)}, f32[24,512]{1,0:T(8,128)S(1)}, u32[]{:S(2)}, u32[]{:S(2)}) collective-permute-start(f32[24,512]{1,0:T(8,128)S(1)} %get-tuple-element.24), channel_id=1, source_target_pairs={{0,224},{32,0},{64,32},{96,64},{128,96},{160,128},{192,160},{224,1... | collective-permute-start | bytes 147464 | tf_op jit(solution)/shard_map/ppermute | solution.py:99
  63.0 3.4 %collective-permute-done.27 = f32[24,512]{1,0:T(8,128)S(1)} collective-permute-done((f32[24,512]{1,0:T(8,128)S(1)}, f32[24,512]{1,0:T(8,128)S(1)}, u32[]{:S(2)}, u32[]{:S(2)}) %collective-permute-start.27) | collective-permute-done | bytes 49184 | tf_op jit(solution)/shard_map/ppermute | solution.py:99
  67.2 2.6 %collective-permute-start.15 = (f32[56,512]{1,0:T(8,128)S(1)}, f32[56,512]{1,0:T(8,128)S(1)}, u32[]{:S(2)}, u32[]{:S(2)}) collective-permute-start(f32[56,512]{1,0:T(8,128)S(1)} %pad_maximum_fusion.5), channel_id=1, source_target_pairs={{0,32},{32,64},{64,96},{96,128},{128,160},{160,192},{192,224},{224... | collective-permute-start | bytes 344072 | tf_op jit(solution)/shard_map/ppermute | solution.py:99
  70.0 3.5 %collective-permute-start.24 = (f32[56,512]{1,0:T(8,128)S(1)}, f32[56,512]{1,0:T(8,128)S(1)}, u32[]{:S(2)}, u32[]{:S(2)}) collective-permute-start(f32[56,512]{1,0:T(8,128)S(1)} %pad_maximum_fusion.7), channel_id=1, source_target_pairs={{0,32},{32,64},{64,96},{96,128},{128,160},{160,192},{192,224},{224... | collective-permute-start | bytes 344072 | tf_op jit(solution)/shard_map/ppermute | solution.py:99
  73.5 3.4 %collective-permute-start.16 = (f32[56,512]{1,0:T(8,128)S(1)}, f32[56,512]{1,0:T(8,128)S(1)}, u32[]{:S(2)}, u32[]{:S(2)}) collective-permute-start(f32[56,512]{1,0:T(8,128)S(1)} %slice_add_fusion.7), channel_id=1, source_target_pairs={{0,32},{32,64},{64,96},{96,128},{128,160},{160,192},{192,224},{224... | collective-permute-start | bytes 344072 | tf_op jit(solution)/shard_map/ppermute | solution.py:99
  76.9 2.7 %collective-permute-start.25 = (f32[56,512]{1,0:T(8,128)S(1)}, f32[56,512]{1,0:T(8,128)S(1)}, u32[]{:S(2)}, u32[]{:S(2)}) collective-permute-start(f32[56,512]{1,0:T(8,128)S(1)} %slice_add_fusion.2), channel_id=1, source_target_pairs={{0,32},{32,64},{64,96},{96,128},{128,160},{160,192},{192,224},{224... | collective-permute-start | bytes 344072 | tf_op jit(solution)/shard_map/ppermute | solution.py:99
  80.5 3.8 %collective-permute-start.17 = (f32[56,512]{1,0:T(8,128)S(1)}, f32[56,512]{1,0:T(8,128)S(1)}, u32[]{:S(2)}, u32[]{:S(2)}) collective-permute-start(f32[56,512]{1,0:T(8,128)S(1)} %get-tuple-element.13), channel_id=1, source_target_pairs={{0,32},{32,64},{64,96},{96,128},{128,160},{160,192},{192,224},{224... | collective-permute-start | bytes 344072 | tf_op jit(solution)/shard_map/ppermute | solution.py:99
  84.3 3.3 %collective-permute-start.26 = (f32[56,512]{1,0:T(8,128)S(1)}, f32[56,512]{1,0:T(8,128)S(1)}, u32[]{:S(2)}, u32[]{:S(2)}) collective-permute-start(f32[56,512]{1,0:T(8,128)S(1)} %get-tuple-element.19), channel_id=1, source_target_pairs={{0,32},{32,64},{64,96},{96,128},{128,160},{160,192},{192,224},{224... | collective-permute-start | bytes 344072 | tf_op jit(solution)/shard_map/ppermute | solution.py:99
  87.6 2.6 %collective-permute-done.20 = f32[56,512]{1,0:T(8,128)S(1)} collective-permute-done((f32[56,512]{1,0:T(8,128)S(1)}, f32[56,512]{1,0:T(8,128)S(1)}, u32[]{:S(2)}, u32[]{:S(2)}) %collective-permute-start.20) | collective-permute-done | bytes 114720 | tf_op jit(solution)/shard_map/ppermute | solution.py:99
  90.4 3.3 %collective-permute-done.29 = f32[56,512]{1,0:T(8,128)S(1)} collective-permute-done((f32[56,512]{1,0:T(8,128)S(1)}, f32[56,512]{1,0:T(8,128)S(1)}, u32[]{:S(2)}, u32[]{:S(2)}) %collective-permute-start.29) | collective-permute-done | bytes 114720 | tf_op jit(solution)/shard_map/ppermute | solution.py:99
  93.8 2.6 %collective-permute-done.21 = f32[56,512]{1,0:T(8,128)S(1)} collective-permute-done((f32[56,512]{1,0:T(8,128)S(1)}, f32[56,512]{1,0:T(8,128)S(1)}, u32[]{:S(2)}, u32[]{:S(2)}) %collective-permute-start.21) | collective-permute-done | bytes 114720 | tf_op jit(solution)/shard_map/ppermute | solution.py:99
  96.4 3.3 %collective-permute-done.30 = f32[56,512]{1,0:T(8,128)S(1)} collective-permute-done((f32[56,512]{1,0:T(8,128)S(1)}, f32[56,512]{1,0:T(8,128)S(1)}, u32[]{:S(2)}, u32[]{:S(2)}) %collective-permute-start.30) | collective-permute-done | bytes 114720 | tf_op jit(solution)/shard_map/ppermute | solution.py:99
  (71 shorter events, 7.3 us)
Async XLA Ops:
  2.1 29.2 %all-to-all-start = ((bf16[4,56,2048]{2,1,0:T(8,128)(2,1)}), bf16[4,56,2048]{2,1,0:T(8,128)(2,1)S(1)}, u32[]{:S(2)}, u32[]{:S(2)}) async-start(bf16[4,56,2048]{2,1,0:T(8,128)(2,1)} %broadcast_in_dim.2), calls=%async_computation | async-start | bytes 1835008 | tf_op jit(solution)/shard_map/all_to_all | solution.py:40
  6.5 5.6 %collective-permute-start = (bf16[56,1024]{1,0:T(8,128)(2,1)S(1)}, bf16[56,1024]{1,0:T(8,128)(2,1)S(1)}, u32[]{:S(2)}, u32[]{:S(2)}) collective-permute-start(bf16[56,1024]{1,0:T(8,128)(2,1)S(1)} %pad_maximum_fusion.4.own_ref), channel_id=1, source_target_pairs={{0,32},{32,64},{64,96},{96,128},{128,160},{160,192},{192,224},{224... | collective-permute-start | bytes 344072 | tf_op jit(solution)/shard_map/ppermute | solution.py:99
  9.7 6.0 %collective-permute-start.1 = (bf16[56,1024]{1,0:T(8,128)(2,1)S(1)}, bf16[56,1024]{1,0:T(8,128)(2,1)S(1)}, u32[]{:S(2)}, u32[]{:S(2)}) collective-permute-start(bf16[56,1024]{1,0:T(8,128)(2,1)S(1)} %pad_maximum_fusion.4.own_ref), channel_id=1, source_target_pairs={{0,224},{32,0},{64,32},{96,64},{128,96},{160,128},{192,160},{224,1... | collective-permute-start | bytes 344072 | tf_op jit(solution)/shard_map/ppermute | solution.py:99
  12.1 6.0 %collective-permute-start.2 = (bf16[56,1024]{1,0:T(8,128)(2,1)S(1)}, bf16[56,1024]{1,0:T(8,128)(2,1)S(1)}, u32[]{:S(2)}, u32[]{:S(2)}) collective-permute-start(bf16[56,1024]{1,0:T(8,128)(2,1)S(1)} %collective-permute-done.up_ref), channel_id=1, source_target_pairs={{0,32},{32,64},{64,96},{96,128},{128,160},{160,192},{192,224},{224... | collective-permute-start | bytes 344072 | tf_op jit(solution)/shard_map/ppermute | solution.py:99
  15.7 6.0 %collective-permute-start.3 = (bf16[56,1024]{1,0:T(8,128)(2,1)S(1)}, bf16[56,1024]{1,0:T(8,128)(2,1)S(1)}, u32[]{:S(2)}, u32[]{:S(2)}) collective-permute-start(bf16[56,1024]{1,0:T(8,128)(2,1)S(1)} %collective-permute-done.1.down_ref), channel_id=1, source_target_pairs={{0,224},{32,0},{64,32},{96,64},{128,96},{160,128},{192,160},{224,1... | collective-permute-start | bytes 344072 | tf_op jit(solution)/shard_map/ppermute | solution.py:99
  18.1 12.9 %collective-permute-start.4 = (bf16[88,1024]{1,0:T(8,128)(2,1)S(1)}, bf16[88,1024]{1,0:T(8,128)(2,1)S(1)}, u32[]{:S(2)}, u32[]{:S(2)}) collective-permute-start(bf16[88,1024]{1,0:T(8,128)(2,1)S(1)} %pad_maximum_fusion.2), channel_id=1, source_target_pairs={{0,64},{32,96},{64,128},{96,160},{128,192},{160,224},{192,0},{224,... | collective-permute-start | bytes 540680 | tf_op jit(solution)/shard_map/ppermute | solution.py:99
  21.8 9.3 %collective-permute-start.5 = (bf16[80,1024]{1,0:T(8,128)(2,1)S(1)}, bf16[80,1024]{1,0:T(8,128)(2,1)S(1)}, u32[]{:S(2)}, u32[]{:S(2)}) collective-permute-start(bf16[80,1024]{1,0:T(8,128)(2,1)S(1)} %pad_maximum_fusion.3), channel_id=1, source_target_pairs={{0,192},{32,224},{64,0},{96,32},{128,64},{160,96},{192,128},{224,1... | collective-permute-start | bytes 491528 | tf_op jit(solution)/shard_map/ppermute | solution.py:99
  31.2 15.5 %collective-permute-start.12 = (bf16[256,2048]{1,0:T(8,128)(2,1)S(1)}, bf16[256,2048]{1,0:T(8,128)(2,1)S(1)}, u32[]{:S(2)}, u32[]{:S(2)}) collective-permute-start(bf16[256,2048]{1,0:T(8,128)(2,1)S(1)} %shard_map.37.t_all), channel_id=1, source_target_pairs={{0,2},{2,0},{1,3},{3,1},{4,6},{6,4},{5,7},{7,5},{8,10},{10,8},{9,1... | collective-permute-start | bytes 3145736 | tf_op jit(solution)/shard_map/ppermute | solution.py:168
  31.3 9.8 %collective-permute-start.6 = (bf16[112,2048]{1,0:T(8,128)(2,1)S(1)}, bf16[112,2048]{1,0:T(8,128)(2,1)S(1)}, u32[]{:S(2)}, u32[]{:S(2)}) collective-permute-start(bf16[112,2048]{1,0:T(8,128)(2,1)S(1)} %bitcast.7), channel_id=1, source_target_pairs={{0,4},{1,5},{2,10},{3,11},{4,1},{5,0},{6,14},{7,15},{8,12},{9,13},... | collective-permute-start | bytes 1376264 | tf_op jit(solution)/shard_map/ppermute | solution.py:95
  33.3 8.5 %collective-permute-start.9 = (bf16[112,2048]{1,0:T(8,128)(2,1)S(1)}, bf16[112,2048]{1,0:T(8,128)(2,1)S(1)}, u32[]{:S(2)}, u32[]{:S(2)}) collective-permute-start(bf16[112,2048]{1,0:T(8,128)(2,1)S(1)} %bitcast.5), channel_id=1, source_target_pairs={{0,5},{1,4},{2,26},{3,27},{4,0},{5,1},{6,30},{7,31},{8,13},{9,12},... | collective-permute-start | bytes 1376264 | tf_op jit(solution)/shard_map/ppermute | solution.py:95
  34.7 12.0 %collective-permute-start.8 = (bf16[112,2048]{1,0:T(8,128)(2,1)S(1)}, bf16[112,2048]{1,0:T(8,128)(2,1)S(1)}, u32[]{:S(2)}, u32[]{:S(2)}) collective-permute-start(bf16[112,2048]{1,0:T(8,128)(2,1)S(1)} %bitcast.8), channel_id=1, source_target_pairs={{0,5},{1,4},{2,26},{3,27},{4,0},{5,1},{6,30},{7,31},{8,13},{9,12},... | collective-permute-start | bytes 1376264 | tf_op jit(solution)/shard_map/ppermute | solution.py:95
  36.2 10.5 %collective-permute-start.7 = (bf16[112,2048]{1,0:T(8,128)(2,1)S(1)}, bf16[112,2048]{1,0:T(8,128)(2,1)S(1)}, u32[]{:S(2)}, u32[]{:S(2)}) collective-permute-start(bf16[112,2048]{1,0:T(8,128)(2,1)S(1)} %bitcast.6), channel_id=1, source_target_pairs={{0,4},{1,5},{2,10},{3,11},{4,1},{5,0},{6,14},{7,15},{8,12},{9,13},... | collective-permute-start | bytes 1376264 | tf_op jit(solution)/shard_map/ppermute | solution.py:95
  41.1 9.8 %collective-permute-start.10 = (bf16[112,2048]{1,0:T(8,128)(2,1)S(1)}, bf16[112,2048]{1,0:T(8,128)(2,1)S(1)}, u32[]{:S(2)}, u32[]{:S(2)}) collective-permute-start(bf16[112,2048]{1,0:T(8,128)(2,1)S(1)} %collective-permute-done.6.refs_0_), channel_id=1, source_target_pairs={{0,4},{1,5},{2,10},{3,11},{4,1},{5,0},{6,14},{7,15},{8,12},{9,13},... | collective-permute-start | bytes 1376264 | tf_op jit(solution)/shard_map/ppermute | solution.py:95
  41.8 9.8 %collective-permute-start.11 = (bf16[112,2048]{1,0:T(8,128)(2,1)S(1)}, bf16[112,2048]{1,0:T(8,128)(2,1)S(1)}, u32[]{:S(2)}, u32[]{:S(2)}) collective-permute-start(bf16[112,2048]{1,0:T(8,128)(2,1)S(1)} %collective-permute-done.9.refs_3_), channel_id=1, source_target_pairs={{0,5},{1,4},{2,26},{3,27},{4,0},{5,1},{6,30},{7,31},{8,13},{9,12},... | collective-permute-start | bytes 1376264 | tf_op jit(solution)/shard_map/ppermute | solution.py:95
  54.1 3.1 %collective-permute-start.13 = (f32[448,512]{1,0:T(8,128)S(1)}, f32[448,512]{1,0:T(8,128)S(1)}, u32[]{:S(2)}, u32[]{:S(2)}) collective-permute-start(f32[448,512]{1,0:T(8,128)S(1)} %get-tuple-element.10), channel_id=1, source_target_pairs={{0,2},{2,0},{1,3},{3,1},{4,6},{6,4},{5,7},{7,5},{8,10},{10,8},{9,1... | collective-permute-start | bytes 2752520 | tf_op jit(solution)/shard_map/ppermute | solution.py:178
  54.2 4.9 %collective-permute-start.22 = (f32[448,512]{1,0:T(8,128)S(1)}, f32[448,512]{1,0:T(8,128)S(1)}, u32[]{:S(2)}, u32[]{:S(2)}) collective-permute-start(f32[448,512]{1,0:T(8,128)S(1)} %get-tuple-element.12), channel_id=1, source_target_pairs={{0,2},{2,0},{1,3},{3,1},{4,6},{6,4},{5,7},{7,5},{8,10},{10,8},{9,1... | collective-permute-start | bytes 2752520 | tf_op jit(solution)/shard_map/ppermute | solution.py:178
  57.3 5.7 %collective-permute-start.18 = (f32[24,512]{1,0:T(8,128)S(1)}, f32[24,512]{1,0:T(8,128)S(1)}, u32[]{:S(2)}, u32[]{:S(2)}) collective-permute-start(f32[24,512]{1,0:T(8,128)S(1)} %get-tuple-element.18), channel_id=1, source_target_pairs={{0,224},{32,0},{64,32},{96,64},{128,96},{160,128},{192,160},{224,1... | collective-permute-start | bytes 147464 | tf_op jit(solution)/shard_map/ppermute | solution.py:99
  59.3 7.1 %collective-permute-start.14 = (f32[32,512]{1,0:T(8,128)S(1)}, f32[32,512]{1,0:T(8,128)S(1)}, u32[]{:S(2)}, u32[]{:S(2)}) collective-permute-start(f32[32,512]{1,0:T(8,128)S(1)} %slice.164), channel_id=1, source_target_pairs={{0,32},{32,64},{64,96},{96,128},{128,160},{160,192},{192,224},{224... | collective-permute-start | bytes 196616 | tf_op jit(solution)/shard_map/ppermute | solution.py:99
  61.0 8.9 %collective-permute-start.23 = (f32[32,512]{1,0:T(8,128)S(1)}, f32[32,512]{1,0:T(8,128)S(1)}, u32[]{:S(2)}, u32[]{:S(2)}) collective-permute-start(f32[32,512]{1,0:T(8,128)S(1)} %slice.177), channel_id=1, source_target_pairs={{0,32},{32,64},{64,96},{96,128},{128,160},{160,192},{192,224},{224... | collective-permute-start | bytes 196616 | tf_op jit(solution)/shard_map/ppermute | solution.py:99
  61.1 5.3 %collective-permute-start.27 = (f32[24,512]{1,0:T(8,128)S(1)}, f32[24,512]{1,0:T(8,128)S(1)}, u32[]{:S(2)}, u32[]{:S(2)}) collective-permute-start(f32[24,512]{1,0:T(8,128)S(1)} %get-tuple-element.24), channel_id=1, source_target_pairs={{0,224},{32,0},{64,32},{96,64},{128,96},{160,128},{192,160},{224,1... | collective-permute-start | bytes 147464 | tf_op jit(solution)/shard_map/ppermute | solution.py:99
  66.4 13.2 %collective-permute-start.19 = (f32[56,512]{1,0:T(8,128)S(1)}, f32[56,512]{1,0:T(8,128)S(1)}, u32[]{:S(2)}, u32[]{:S(2)}) collective-permute-start(f32[56,512]{1,0:T(8,128)S(1)} %pad_maximum_fusion.6), channel_id=1, source_target_pairs={{0,224},{32,0},{64,32},{96,64},{128,96},{160,128},{192,160},{224,1... | collective-permute-start | bytes 344072 | tf_op jit(solution)/shard_map/ppermute | solution.py:99
  67.2 6.3 %collective-permute-start.15 = (f32[56,512]{1,0:T(8,128)S(1)}, f32[56,512]{1,0:T(8,128)S(1)}, u32[]{:S(2)}, u32[]{:S(2)}) collective-permute-start(f32[56,512]{1,0:T(8,128)S(1)} %pad_maximum_fusion.5), channel_id=1, source_target_pairs={{0,32},{32,64},{64,96},{96,128},{128,160},{160,192},{192,224},{224... | collective-permute-start | bytes 344072 | tf_op jit(solution)/shard_map/ppermute | solution.py:99
  69.9 14.4 %collective-permute-start.28 = (f32[56,512]{1,0:T(8,128)S(1)}, f32[56,512]{1,0:T(8,128)S(1)}, u32[]{:S(2)}, u32[]{:S(2)}) collective-permute-start(f32[56,512]{1,0:T(8,128)S(1)} %pad_maximum_fusion.8), channel_id=1, source_target_pairs={{0,224},{32,0},{64,32},{96,64},{128,96},{160,128},{192,160},{224,1... | collective-permute-start | bytes 344072 | tf_op jit(solution)/shard_map/ppermute | solution.py:99
  70.0 6.9 %collective-permute-start.24 = (f32[56,512]{1,0:T(8,128)S(1)}, f32[56,512]{1,0:T(8,128)S(1)}, u32[]{:S(2)}, u32[]{:S(2)}) collective-permute-start(f32[56,512]{1,0:T(8,128)S(1)} %pad_maximum_fusion.7), channel_id=1, source_target_pairs={{0,32},{32,64},{64,96},{96,128},{128,160},{160,192},{192,224},{224... | collective-permute-start | bytes 344072 | tf_op jit(solution)/shard_map/ppermute | solution.py:99
  73.5 6.9 %collective-permute-start.16 = (f32[56,512]{1,0:T(8,128)S(1)}, f32[56,512]{1,0:T(8,128)S(1)}, u32[]{:S(2)}, u32[]{:S(2)}) collective-permute-start(f32[56,512]{1,0:T(8,128)S(1)} %slice_add_fusion.7), channel_id=1, source_target_pairs={{0,32},{32,64},{64,96},{96,128},{128,160},{160,192},{192,224},{224... | collective-permute-start | bytes 344072 | tf_op jit(solution)/shard_map/ppermute | solution.py:99
  76.9 7.3 %collective-permute-start.25 = (f32[56,512]{1,0:T(8,128)S(1)}, f32[56,512]{1,0:T(8,128)S(1)}, u32[]{:S(2)}, u32[]{:S(2)}) collective-permute-start(f32[56,512]{1,0:T(8,128)S(1)} %slice_add_fusion.2), channel_id=1, source_target_pairs={{0,32},{32,64},{64,96},{96,128},{128,160},{160,192},{192,224},{224... | collective-permute-start | bytes 344072 | tf_op jit(solution)/shard_map/ppermute | solution.py:99
  80.5 13.3 %collective-permute-start.17 = (f32[56,512]{1,0:T(8,128)S(1)}, f32[56,512]{1,0:T(8,128)S(1)}, u32[]{:S(2)}, u32[]{:S(2)}) collective-permute-start(f32[56,512]{1,0:T(8,128)S(1)} %get-tuple-element.13), channel_id=1, source_target_pairs={{0,32},{32,64},{64,96},{96,128},{128,160},{160,192},{192,224},{224... | collective-permute-start | bytes 344072 | tf_op jit(solution)/shard_map/ppermute | solution.py:99
  84.3 6.0 %collective-permute-start.20 = (f32[56,512]{1,0:T(8,128)S(1)}, f32[56,512]{1,0:T(8,128)S(1)}, u32[]{:S(2)}, u32[]{:S(2)}) collective-permute-start(f32[56,512]{1,0:T(8,128)S(1)} %get-tuple-element.14), channel_id=1, source_target_pairs={{0,224},{32,0},{64,32},{96,64},{128,96},{160,128},{192,160},{224,1... | collective-permute-start | bytes 344072 | tf_op jit(solution)/shard_map/ppermute | solution.py:99
  84.3 12.1 %collective-permute-start.26 = (f32[56,512]{1,0:T(8,128)S(1)}, f32[56,512]{1,0:T(8,128)S(1)}, u32[]{:S(2)}, u32[]{:S(2)}) collective-permute-start(f32[56,512]{1,0:T(8,128)S(1)} %get-tuple-element.19), channel_id=1, source_target_pairs={{0,32},{32,64},{64,96},{96,128},{128,160},{160,192},{192,224},{224... | collective-permute-start | bytes 344072 | tf_op jit(solution)/shard_map/ppermute | solution.py:99
  87.6 6.0 %collective-permute-start.29 = (f32[56,512]{1,0:T(8,128)S(1)}, f32[56,512]{1,0:T(8,128)S(1)}, u32[]{:S(2)}, u32[]{:S(2)}) collective-permute-start(f32[56,512]{1,0:T(8,128)S(1)} %get-tuple-element.20), channel_id=1, source_target_pairs={{0,224},{32,0},{64,32},{96,64},{128,96},{160,128},{192,160},{224,1... | collective-permute-start | bytes 344072 | tf_op jit(solution)/shard_map/ppermute | solution.py:99
  90.3 6.1 %collective-permute-start.21 = (f32[56,512]{1,0:T(8,128)S(1)}, f32[56,512]{1,0:T(8,128)S(1)}, u32[]{:S(2)}, u32[]{:S(2)}) collective-permute-start(f32[56,512]{1,0:T(8,128)S(1)} %slice_add_fusion.6), channel_id=1, source_target_pairs={{0,224},{32,0},{64,32},{96,64},{128,96},{160,128},{192,160},{224,1... | collective-permute-start | bytes 344072 | tf_op jit(solution)/shard_map/ppermute | solution.py:99
  93.7 6.1 %collective-permute-start.30 = (f32[56,512]{1,0:T(8,128)S(1)}, f32[56,512]{1,0:T(8,128)S(1)}, u32[]{:S(2)}, u32[]{:S(2)}) collective-permute-start(f32[56,512]{1,0:T(8,128)S(1)} %slice_add_fusion.1), channel_id=1, source_target_pairs={{0,224},{32,0},{64,32},{96,64},{128,96},{160,128},{192,160},{224,1... | collective-permute-start | bytes 344072 | tf_op jit(solution)/shard_map/ppermute | solution.py:99
  (1 other events, 4.4 us)

commit v12 on v11

--- a/solution.py
+++ b/solution.py
@@ -100,7 +100,7 @@
 
 
 def part_kernel(spread_ref, t_all, line_ref, *refs):
-    half_refs, outs, (x_all, s_all, low_all) = refs[:6], refs[6:8], refs[8:]
+    half_refs, (out, x_all, s_all, low_all) = refs[:6], refs[6:]
     inverse = 1.0 / spread_ref[0]
     targets = t_all[...]
     target_norm = row_norms(targets)
@@ -136,8 +136,8 @@
         wide = t_all[:, columns].astype(jnp.float32)
         added = drive + (2.0 * inverse) * (wide * row_total - pull)
         for i in range(TARGETS):
-            rows = pl.ds((2 * i + n % 2) * ROWS, ROWS)
-            outs[n // 2][rows, :] = added[i * PAD : i * PAD + ROWS]
+            rows = pl.ds((2 * i + n // 2) * ROWS, ROWS)
+            out[rows, pl.ds(n % 2 * WIDTH, WIDTH)] = added[i * PAD : i * PAD + ROWS]
 
 
 def part(spread, targets, sources):
@@ -146,8 +146,8 @@
         part_kernel,
         in_specs=[pl.BlockSpec(memory_space=pltpu.SMEM)]
         + [pl.BlockSpec(memory_space=pltpu.VMEM)] * len(args),
-        out_specs=[pl.BlockSpec(memory_space=pltpu.VMEM)] * 2,
-        out_shape=[pltpu.VMEM((2 * TARGETS * ROWS, WIDTH), jnp.float32)] * 2,
+        out_specs=pl.BlockSpec(memory_space=pltpu.VMEM),
+        out_shape=pltpu.VMEM((2 * TARGETS * ROWS, 2 * WIDTH), jnp.float32),
         scratch_shapes=[
             pltpu.VMEM((PIECES * PAD, DIM), jnp.bfloat16),
             pltpu.VMEM((PIECES * PAD, DIM), jnp.bfloat16),
@@ -175,10 +175,10 @@
     opposite = [moved_across(back_low, 1), moved_across(ahead_high, -1)]
     sources = [line, back_low, back_high, ahead_low, ahead_high, *opposite]
     theirs = part(spread, others, sources)
-    arrived = [lax.ppermute(t, "c", swap) for t in theirs]
+    arrived = lax.ppermute(theirs, "c", swap)
     mine = part(spread, targets, sources)
-    halves = [summed_along_z((m + a) / POPULATION) for m, a in zip(mine, arrived)]
-    return jnp.concatenate([rows for h in halves for rows in (h[:ROWS], h[ROWS:])], axis=1)
+    total = summed_along_z((mine + arrived) / POPULATION)
+    return jnp.concatenate([total[:ROWS], total[ROWS:]], axis=1)
 
 
 def summed_along_z(partial):

time: 101 us -> 96.1 us (0.951)
  the two profiles are of different devices: /device:TPU:96 before, /device:TPU:12 now
where the time goes in v12:
time: 96.1 us; the launch traced here: 96 us
  waiting for transfers between devices  52.6 us (55%)
  starting transfers between devices  33.9 us (35%)
  Pallas kernels  5 us (5%)
  other arithmetic  2.43 us (3%)
  local copies, waits for them, and re-layouts  1.19 us (1%)
    ppermute x14, waiting for transfers between devices, moved(): lax.ppermute(value, 'z', [(i, (i + steps) % TARGETS) for i in range(TARGE...  38.1 us
    ppermute x14, starting transfers between devices, moved(): lax.ppermute(value, 'z', [(i, (i + steps) % TARGETS) for i in range(TARGE...  22.7 us
    ppermute x6, waiting for transfers between devices, moved_across(): return lax.ppermute(value, AXES, sorted(pairs))  13.2 us
    ppermute x6, starting transfers between devices, moved_across(): return lax.ppermute(value, AXES, sorted(pairs))  6.16 us
    pallas_call x2, Pallas kernels, part(): pl.pallas_call(part_kernel, in_specs=[pl.BlockSpec(memory_space=pltpu.SME...  4.9 us
    all_to_all x1, starting transfers between devices, sent_along(): lax.all_to_all(jnp.broadcast_to(value[None], (count, *value.shape)), AXES...  4.8 us
  transfers between devices with their start and end apart: 23, of which 14 were waited for; matrix products, arithmetic and copies ran while one was open for 0% of the time, Pallas kernels for 3%

profile of v12, /device:TPU:12, one launch (start us, length us, event | category | flops | bytes accessed | tf_op | source)
XLA Modules:
  0.0 96.0 jit_solution(9692345356355484346)
XLA Ops:
  0.0 1.0 %pad_maximum_fusion.1 = bf16[56,2048]{1,0:T(8,128)(2,1)S(1)} fusion(bf16[28,2048]{1,0:T(8,128)(2,1)} %param.4, bf16[28,2048]{1,0:T(8,128)(2,1)} %param.3), kind=kLoop, calls=%fused_computation.8 | loop fusion | flops 458752 | bytes 458752 | tf_op jit(solution)/shard_map/concatenate | solution.py:169
  1.1 1.1 %broadcast_in_dim.2 = bf16[4,56,2048]{2,1,0:T(8,128)(2,1)} broadcast(bf16[56,2048]{1,0:T(8,128)(2,1)S(1)} %pad_maximum_fusion.1), dimensions={1,2} | broadcast | bytes 1146880 | tf_op jit(solution)/shard_map/broadcast_in_dim | solution.py:41
  2.1 4.8 %all-to-all-start = ((bf16[4,56,2048]{2,1,0:T(8,128)(2,1)}), bf16[4,56,2048]{2,1,0:T(8,128)(2,1)S(1)}, u32[]{:S(2)}, u32[]{:S(2)}) async-start(bf16[4,56,2048]{2,1,0:T(8,128)(2,1)} %broadcast_in_dim.2), calls=%async_computation | async-start | bytes 1835008 | tf_op jit(solution)/shard_map/all_to_all | solution.py:40
  7.0 2.0 %collective-permute-start = (bf16[56,1024]{1,0:T(8,128)(2,1)S(1)}, bf16[56,1024]{1,0:T(8,128)(2,1)S(1)}, u32[]{:S(2)}, u32[]{:S(2)}) collective-permute-start(bf16[56,1024]{1,0:T(8,128)(2,1)S(1)} %pad_maximum_fusion.6.own_ref), channel_id=1, source_target_pairs={{0,32},{32,64},{64,96},{96,128},{128,160},{160,192},{192,224},{224... | collective-permute-start | bytes 344072 | tf_op jit(solution)/shard_map/ppermute | solution.py:99
  8.9 4.0 %collective-permute-start.1 = (bf16[56,1024]{1,0:T(8,128)(2,1)S(1)}, bf16[56,1024]{1,0:T(8,128)(2,1)S(1)}, u32[]{:S(2)}, u32[]{:S(2)}) collective-permute-start(bf16[56,1024]{1,0:T(8,128)(2,1)S(1)} %pad_maximum_fusion.6.own_ref), channel_id=1, source_target_pairs={{0,224},{32,0},{64,32},{96,64},{128,96},{160,128},{192,160},{224,1... | collective-permute-start | bytes 344072 | tf_op jit(solution)/shard_map/ppermute | solution.py:99
  13.0 2.7 %collective-permute-done.up_ref = bf16[56,1024]{1,0:T(8,128)(2,1)S(1)} collective-permute-done((bf16[56,1024]{1,0:T(8,128)(2,1)S(1)}, bf16[56,1024]{1,0:T(8,128)(2,1)S(1)}, u32[]{:S(2)}, u32[]{:S(2)}) %collective-permute-start) | collective-permute-done | bytes 114720 | tf_op jit(solution)/shard_map/ppermute | solution.py:99
  15.7 3.3 %collective-permute-start.3 = (bf16[56,1024]{1,0:T(8,128)(2,1)S(1)}, bf16[56,1024]{1,0:T(8,128)(2,1)S(1)}, u32[]{:S(2)}, u32[]{:S(2)}) collective-permute-start(bf16[56,1024]{1,0:T(8,128)(2,1)S(1)} %collective-permute-done.1.down_ref), channel_id=1, source_target_pairs={{0,224},{32,0},{64,32},{96,64},{128,96},{160,128},{192,160},{224,1... | collective-permute-start | bytes 344072 | tf_op jit(solution)/shard_map/ppermute | solution.py:99
  19.0 2.9 %collective-permute-done.2.up2_ref = bf16[56,1024]{1,0:T(8,128)(2,1)S(1)} collective-permute-done((bf16[56,1024]{1,0:T(8,128)(2,1)S(1)}, bf16[56,1024]{1,0:T(8,128)(2,1)S(1)}, u32[]{:S(2)}, u32[]{:S(2)}) %collective-permute-start.2) | collective-permute-done | bytes 114720 | tf_op jit(solution)/shard_map/ppermute | solution.py:99
  22.0 4.2 %collective-permute-start.5 = (bf16[80,1024]{1,0:T(8,128)(2,1)S(1)}, bf16[80,1024]{1,0:T(8,128)(2,1)S(1)}, u32[]{:S(2)}, u32[]{:S(2)}) collective-permute-start(bf16[80,1024]{1,0:T(8,128)(2,1)S(1)} %pad_maximum_fusion.5), channel_id=1, source_target_pairs={{0,192},{32,224},{64,0},{96,32},{128,64},{160,96},{192,128},{224,1... | collective-permute-start | bytes 491528 | tf_op jit(solution)/shard_map/ppermute | solution.py:99
  26.2 6.1 %collective-permute-done.5.far_down_ref = bf16[80,1024]{1,0:T(8,128)(2,1)S(1)} collective-permute-done((bf16[80,1024]{1,0:T(8,128)(2,1)S(1)}, bf16[80,1024]{1,0:T(8,128)(2,1)S(1)}, u32[]{:S(2)}, u32[]{:S(2)}) %collective-permute-start.5) | collective-permute-done | bytes 163872 | tf_op jit(solution)/shard_map/ppermute | solution.py:99
  32.7 1.7 %collective-permute-start.6 = (bf16[112,2048]{1,0:T(8,128)(2,1)S(1)}, bf16[112,2048]{1,0:T(8,128)(2,1)S(1)}, u32[]{:S(2)}, u32[]{:S(2)}) collective-permute-start(bf16[112,2048]{1,0:T(8,128)(2,1)S(1)} %bitcast.7), channel_id=1, source_target_pairs={{0,4},{1,5},{2,10},{3,11},{4,1},{5,0},{6,14},{7,15},{8,12},{9,13},... | collective-permute-start | bytes 1376264 | tf_op jit(solution)/shard_map/ppermute | solution.py:95
  34.8 1.7 %collective-permute-start.8 = (bf16[112,2048]{1,0:T(8,128)(2,1)S(1)}, bf16[112,2048]{1,0:T(8,128)(2,1)S(1)}, u32[]{:S(2)}, u32[]{:S(2)}) collective-permute-start(bf16[112,2048]{1,0:T(8,128)(2,1)S(1)} %bitcast.8), channel_id=1, source_target_pairs={{0,5},{1,4},{2,26},{3,27},{4,0},{5,1},{6,30},{7,31},{8,13},{9,12},... | collective-permute-start | bytes 1376264 | tf_op jit(solution)/shard_map/ppermute | solution.py:95
  36.8 4.4 %collective-permute-done.6.refs_0_ = bf16[112,2048]{1,0:T(8,128)(2,1)S(1)} collective-permute-done((bf16[112,2048]{1,0:T(8,128)(2,1)S(1)}, bf16[112,2048]{1,0:T(8,128)(2,1)S(1)}, u32[]{:S(2)}, u32[]{:S(2)}) %collective-permute-start.6) | collective-permute-done | bytes 458784 | tf_op jit(solution)/shard_map/ppermute | solution.py:95
  41.2 1.6 %collective-permute-start.10 = (bf16[112,2048]{1,0:T(8,128)(2,1)S(1)}, bf16[112,2048]{1,0:T(8,128)(2,1)S(1)}, u32[]{:S(2)}, u32[]{:S(2)}) collective-permute-start(bf16[112,2048]{1,0:T(8,128)(2,1)S(1)} %collective-permute-done.6.refs_0_), channel_id=1, source_target_pairs={{0,4},{1,5},{2,10},{3,11},{4,1},{5,0},{6,14},{7,15},{8,12},{9,13},... | collective-permute-start | bytes 1376264 | tf_op jit(solution)/shard_map/ppermute | solution.py:95
  42.9 0.4 collective-permute-start.11
  43.9 3.9 %collective-permute-done.8.refs_2_ = bf16[112,2048]{1,0:T(8,128)(2,1)S(1)} collective-permute-done((bf16[112,2048]{1,0:T(8,128)(2,1)S(1)}, bf16[112,2048]{1,0:T(8,128)(2,1)S(1)}, u32[]{:S(2)}, u32[]{:S(2)}) %collective-permute-start.8) | collective-permute-done | bytes 458784 | tf_op jit(solution)/shard_map/ppermute | solution.py:95
  47.8 3.3 %collective-permute-done.10.refs_4_ = bf16[112,2048]{1,0:T(8,128)(2,1)S(1)} collective-permute-done((bf16[112,2048]{1,0:T(8,128)(2,1)S(1)}, bf16[112,2048]{1,0:T(8,128)(2,1)S(1)}, u32[]{:S(2)}, u32[]{:S(2)}) %collective-permute-start.10) | collective-permute-done | bytes 458784 | tf_op jit(solution)/shard_map/ppermute | solution.py:95
  51.0 1.6 %collective-permute-done.11.refs_5_ = bf16[112,2048]{1,0:T(8,128)(2,1)S(1)} collective-permute-done((bf16[112,2048]{1,0:T(8,128)(2,1)S(1)}, bf16[112,2048]{1,0:T(8,128)(2,1)S(1)}, u32[]{:S(2)}, u32[]{:S(2)}) %collective-permute-start.11) | collective-permute-done | bytes 458784 | tf_op jit(solution)/shard_map/ppermute | solution.py:95
  52.7 2.4 %shard_map.39 = f32[448,1024]{1,0:T(8,128)S(1)} custom-call(f32[1]{0:T(128)S(6)} %copy.4.spread_ref, bf16[256,2048]{1,0:T(8,128)(2,1)S(1)} %collective-permute-done.12.t_all, bf16[224,2048]{1,0:T(8,128)(2,1)S(1)} %bitcast.3, bf16[112,2048]{1,0:T(8,128)(2,1)S(1)} %collective-permute-done.6.refs_0_, bf16[112,2048]{1,0:T(8,128)(2,1)S(1)} %collective-permute-done.7.refs_1_, ...), custom_call_target="tpu_custom_call" | custom-call | tf_op jit(solution)/shard_map/pallas_call | solution.py:145
  55.2 2.5 %shard_map.38 = f32[448,1024]{1,0:T(8,128)S(1)} custom-call(f32[1]{0:T(128)S(6)} %copy.4.spread_ref, bf16[256,2048]{1,0:T(8,128)(2,1)S(1)} %shard_map.37.t_all, bf16[224,2048]{1,0:T(8,128)(2,1)S(1)} %bitcast.4, bf16[112,2048]{1,0:T(8,128)(2,1)S(1)} %collective-permute-done.6.refs_0_, bf16[112,2048]{1,0:T(8,128)(2,1)S(1)} %collective-permute-done.7.refs_1_, ...), custom_call_target="tpu_custom_call" | custom-call | tf_op jit(solution)/shard_map/pallas_call | solution.py:145
  57.7 1.3 %collective-permute-done.13 = f32[448,1024]{1,0:T(8,128)S(1)} collective-permute-done((f32[448,1024]{1,0:T(8,128)S(1)}, f32[448,1024]{1,0:T(8,128)S(1)}, u32[]{:S(2)}, u32[]{:S(2)}) %collective-permute-start.13) | collective-permute-done | bytes 1835040 | tf_op jit(solution)/shard_map/ppermute | solution.py:178
  59.5 3.3 %collective-permute-start.18 = (f32[24,1024]{1,0:T(8,128)S(1)}, f32[24,1024]{1,0:T(8,128)S(1)}, u32[]{:S(2)}, u32[]{:S(2)}) collective-permute-start(f32[24,1024]{1,0:T(8,128)S(1)} %get-tuple-element.10), channel_id=1, source_target_pairs={{0,224},{32,0},{64,32},{96,64},{128,96},{160,128},{192,160},{224,1... | collective-permute-start | bytes 294920 | tf_op jit(solution)/shard_map/ppermute | solution.py:99
  62.8 3.4 %collective-permute-done.14 = f32[32,1024]{1,0:T(8,128)S(1)} collective-permute-done((f32[32,1024]{1,0:T(8,128)S(1)}, f32[32,1024]{1,0:T(8,128)S(1)}, u32[]{:S(2)}, u32[]{:S(2)}) %collective-permute-start.14) | collective-permute-done | bytes 131104 | tf_op jit(solution)/shard_map/ppermute | solution.py:99
  66.3 1.4 %collective-permute-start.15 = (f32[56,1024]{1,0:T(8,128)S(1)}, f32[56,1024]{1,0:T(8,128)S(1)}, u32[]{:S(2)}, u32[]{:S(2)}) collective-permute-start(f32[56,1024]{1,0:T(8,128)S(1)} %pad_maximum_fusion.2), channel_id=1, source_target_pairs={{0,32},{32,64},{64,96},{96,128},{128,160},{160,192},{192,224},{224... | collective-permute-start | bytes 688136 | tf_op jit(solution)/shard_map/ppermute | solution.py:99
  67.7 2.0 %collective-permute-start.19 = (f32[56,1024]{1,0:T(8,128)S(1)}, f32[56,1024]{1,0:T(8,128)S(1)}, u32[]{:S(2)}, u32[]{:S(2)}) collective-permute-start(f32[56,1024]{1,0:T(8,128)S(1)} %pad_maximum_fusion.3), channel_id=1, source_target_pairs={{0,224},{32,0},{64,32},{96,64},{128,96},{160,128},{192,160},{224,1... | collective-permute-start | bytes 688136 | tf_op jit(solution)/shard_map/ppermute | solution.py:99
  69.7 4.6 %collective-permute-done.15 = f32[56,1024]{1,0:T(8,128)S(1)} collective-permute-done((f32[56,1024]{1,0:T(8,128)S(1)}, f32[56,1024]{1,0:T(8,128)S(1)}, u32[]{:S(2)}, u32[]{:S(2)}) %collective-permute-start.15) | collective-permute-done | bytes 229408 | tf_op jit(solution)/shard_map/ppermute | solution.py:99
  74.5 0.5 collective-permute-done.19
  75.0 6.7 %collective-permute-done.16 = f32[56,1024]{1,0:T(8,128)S(1)} collective-permute-done((f32[56,1024]{1,0:T(8,128)S(1)}, f32[56,1024]{1,0:T(8,128)S(1)}, u32[]{:S(2)}, u32[]{:S(2)}) %collective-permute-start.16) | collective-permute-done | bytes 229408 | tf_op jit(solution)/shard_map/ppermute | solution.py:99
  81.9 2.0 %collective-permute-start.17 = (f32[56,1024]{1,0:T(8,128)S(1)}, f32[56,1024]{1,0:T(8,128)S(1)}, u32[]{:S(2)}, u32[]{:S(2)}) collective-permute-start(f32[56,1024]{1,0:T(8,128)S(1)} %get-tuple-element.5), channel_id=1, source_target_pairs={{0,32},{32,64},{64,96},{96,128},{128,160},{160,192},{192,224},{224... | collective-permute-start | bytes 688136 | tf_op jit(solution)/shard_map/ppermute | solution.py:99
  83.9 5.2 %collective-permute-done.20 = f32[56,1024]{1,0:T(8,128)S(1)} collective-permute-done((f32[56,1024]{1,0:T(8,128)S(1)}, f32[56,1024]{1,0:T(8,128)S(1)}, u32[]{:S(2)}, u32[]{:S(2)}) %collective-permute-start.20) | collective-permute-done | bytes 229408 | tf_op jit(solution)/shard_map/ppermute | solution.py:99
  89.2 6.0 %collective-permute-done.21 = f32[56,1024]{1,0:T(8,128)S(1)} collective-permute-done((f32[56,1024]{1,0:T(8,128)S(1)}, f32[56,1024]{1,0:T(8,128)S(1)}, u32[]{:S(2)}, u32[]{:S(2)}) %collective-permute-start.21) | collective-permute-done | bytes 229408 | tf_op jit(solution)/shard_map/ppermute | solution.py:99
  95.2 0.7 pad_maximum_fusion
  (41 shorter events, 2.3 us)
Async XLA Ops:
  0.0 6.9 %copy-start = (bf16[28,2048]{1,0:T(8,128)(2,1)S(1)}, bf16[28,2048]{1,0:T(8,128)(2,1)}, u32[]{:S(2)}) copy-start(bf16[28,2048]{1,0:T(8,128)(2,1)} %param.3) | copy-start | bytes 344068
  2.1 30.5 %all-to-all-start = ((bf16[4,56,2048]{2,1,0:T(8,128)(2,1)}), bf16[4,56,2048]{2,1,0:T(8,128)(2,1)S(1)}, u32[]{:S(2)}, u32[]{:S(2)}) async-start(bf16[4,56,2048]{2,1,0:T(8,128)(2,1)} %broadcast_in_dim.2), calls=%async_computation | async-start | bytes 1835008 | tf_op jit(solution)/shard_map/all_to_all | solution.py:40
  7.0 8.7 %collective-permute-start = (bf16[56,1024]{1,0:T(8,128)(2,1)S(1)}, bf16[56,1024]{1,0:T(8,128)(2,1)S(1)}, u32[]{:S(2)}, u32[]{:S(2)}) collective-permute-start(bf16[56,1024]{1,0:T(8,128)(2,1)S(1)} %pad_maximum_fusion.6.own_ref), channel_id=1, source_target_pairs={{0,32},{32,64},{64,96},{96,128},{128,160},{160,192},{192,224},{224... | collective-permute-start | bytes 344072 | tf_op jit(solution)/shard_map/ppermute | solution.py:99
  8.9 6.7 %collective-permute-start.1 = (bf16[56,1024]{1,0:T(8,128)(2,1)S(1)}, bf16[56,1024]{1,0:T(8,128)(2,1)S(1)}, u32[]{:S(2)}, u32[]{:S(2)}) collective-permute-start(bf16[56,1024]{1,0:T(8,128)(2,1)S(1)} %pad_maximum_fusion.6.own_ref), channel_id=1, source_target_pairs={{0,224},{32,0},{64,32},{96,64},{128,96},{160,128},{192,160},{224,1... | collective-permute-start | bytes 344072 | tf_op jit(solution)/shard_map/ppermute | solution.py:99
  15.7 6.2 %collective-permute-start.2 = (bf16[56,1024]{1,0:T(8,128)(2,1)S(1)}, bf16[56,1024]{1,0:T(8,128)(2,1)S(1)}, u32[]{:S(2)}, u32[]{:S(2)}) collective-permute-start(bf16[56,1024]{1,0:T(8,128)(2,1)S(1)} %collective-permute-done.up_ref), channel_id=1, source_target_pairs={{0,32},{32,64},{64,96},{96,128},{128,160},{160,192},{192,224},{224... | collective-permute-start | bytes 344072 | tf_op jit(solution)/shard_map/ppermute | solution.py:99
  15.7 6.3 %collective-permute-start.3 = (bf16[56,1024]{1,0:T(8,128)(2,1)S(1)}, bf16[56,1024]{1,0:T(8,128)(2,1)S(1)}, u32[]{:S(2)}, u32[]{:S(2)}) collective-permute-start(bf16[56,1024]{1,0:T(8,128)(2,1)S(1)} %collective-permute-done.1.down_ref), channel_id=1, source_target_pairs={{0,224},{32,0},{64,32},{96,64},{128,96},{160,128},{192,160},{224,1... | collective-permute-start | bytes 344072 | tf_op jit(solution)/shard_map/ppermute | solution.py:99
  21.9 10.5 %collective-permute-start.4 = (bf16[88,1024]{1,0:T(8,128)(2,1)S(1)}, bf16[88,1024]{1,0:T(8,128)(2,1)S(1)}, u32[]{:S(2)}, u32[]{:S(2)}) collective-permute-start(bf16[88,1024]{1,0:T(8,128)(2,1)S(1)} %pad_maximum_fusion.4), channel_id=1, source_target_pairs={{0,64},{32,96},{64,128},{96,160},{128,192},{160,224},{192,0},{224,... | collective-permute-start | bytes 540680 | tf_op jit(solution)/shard_map/ppermute | solution.py:99
  22.0 10.3 %collective-permute-start.5 = (bf16[80,1024]{1,0:T(8,128)(2,1)S(1)}, bf16[80,1024]{1,0:T(8,128)(2,1)S(1)}, u32[]{:S(2)}, u32[]{:S(2)}) collective-permute-start(bf16[80,1024]{1,0:T(8,128)(2,1)S(1)} %pad_maximum_fusion.5), channel_id=1, source_target_pairs={{0,192},{32,224},{64,0},{96,32},{128,64},{160,96},{192,128},{224,1... | collective-permute-start | bytes 491528 | tf_op jit(solution)/shard_map/ppermute | solution.py:99
  32.5 15.3 %collective-permute-start.12 = (bf16[256,2048]{1,0:T(8,128)(2,1)S(1)}, bf16[256,2048]{1,0:T(8,128)(2,1)S(1)}, u32[]{:S(2)}, u32[]{:S(2)}) collective-permute-start(bf16[256,2048]{1,0:T(8,128)(2,1)S(1)} %shard_map.37.t_all), channel_id=1, source_target_pairs={{0,2},{2,0},{1,3},{3,1},{4,6},{6,4},{5,7},{7,5},{8,10},{10,8},{9,1... | collective-permute-start | bytes 3145736 | tf_op jit(solution)/shard_map/ppermute | solution.py:168
  32.7 8.6 %collective-permute-start.6 = (bf16[112,2048]{1,0:T(8,128)(2,1)S(1)}, bf16[112,2048]{1,0:T(8,128)(2,1)S(1)}, u32[]{:S(2)}, u32[]{:S(2)}) collective-permute-start(bf16[112,2048]{1,0:T(8,128)(2,1)S(1)} %bitcast.7), channel_id=1, source_target_pairs={{0,4},{1,5},{2,10},{3,11},{4,1},{5,0},{6,14},{7,15},{8,12},{9,13},... | collective-permute-start | bytes 1376264 | tf_op jit(solution)/shard_map/ppermute | solution.py:95
  34.4 8.5 %collective-permute-start.9 = (bf16[112,2048]{1,0:T(8,128)(2,1)S(1)}, bf16[112,2048]{1,0:T(8,128)(2,1)S(1)}, u32[]{:S(2)}, u32[]{:S(2)}) collective-permute-start(bf16[112,2048]{1,0:T(8,128)(2,1)S(1)} %bitcast.5), channel_id=1, source_target_pairs={{0,5},{1,4},{2,26},{3,27},{4,0},{5,1},{6,30},{7,31},{8,13},{9,12},... | collective-permute-start | bytes 1376264 | tf_op jit(solution)/shard_map/ppermute | solution.py:95
  34.8 13.0 %collective-permute-start.8 = (bf16[112,2048]{1,0:T(8,128)(2,1)S(1)}, bf16[112,2048]{1,0:T(8,128)(2,1)S(1)}, u32[]{:S(2)}, u32[]{:S(2)}) collective-permute-start(bf16[112,2048]{1,0:T(8,128)(2,1)S(1)} %bitcast.8), channel_id=1, source_target_pairs={{0,5},{1,4},{2,26},{3,27},{4,0},{5,1},{6,30},{7,31},{8,13},{9,12},... | collective-permute-start | bytes 1376264 | tf_op jit(solution)/shard_map/ppermute | solution.py:95
  36.5 11.3 %collective-permute-start.7 = (bf16[112,2048]{1,0:T(8,128)(2,1)S(1)}, bf16[112,2048]{1,0:T(8,128)(2,1)S(1)}, u32[]{:S(2)}, u32[]{:S(2)}) collective-permute-start(bf16[112,2048]{1,0:T(8,128)(2,1)S(1)} %bitcast.6), channel_id=1, source_target_pairs={{0,4},{1,5},{2,10},{3,11},{4,1},{5,0},{6,14},{7,15},{8,12},{9,13},... | collective-permute-start | bytes 1376264 | tf_op jit(solution)/shard_map/ppermute | solution.py:95
  41.2 9.8 %collective-permute-start.10 = (bf16[112,2048]{1,0:T(8,128)(2,1)S(1)}, bf16[112,2048]{1,0:T(8,128)(2,1)S(1)}, u32[]{:S(2)}, u32[]{:S(2)}) collective-permute-start(bf16[112,2048]{1,0:T(8,128)(2,1)S(1)} %collective-permute-done.6.refs_0_), channel_id=1, source_target_pairs={{0,4},{1,5},{2,10},{3,11},{4,1},{5,0},{6,14},{7,15},{8,12},{9,13},... | collective-permute-start | bytes 1376264 | tf_op jit(solution)/shard_map/ppermute | solution.py:95
  42.9 9.8 %collective-permute-start.11 = (bf16[112,2048]{1,0:T(8,128)(2,1)S(1)}, bf16[112,2048]{1,0:T(8,128)(2,1)S(1)}, u32[]{:S(2)}, u32[]{:S(2)}) collective-permute-start(bf16[112,2048]{1,0:T(8,128)(2,1)S(1)} %collective-permute-done.9.refs_3_), channel_id=1, source_target_pairs={{0,5},{1,4},{2,26},{3,27},{4,0},{5,1},{6,30},{7,31},{8,13},{9,12},... | collective-permute-start | bytes 1376264 | tf_op jit(solution)/shard_map/ppermute | solution.py:95
  55.1 3.9 %collective-permute-start.13 = (f32[448,1024]{1,0:T(8,128)S(1)}, f32[448,1024]{1,0:T(8,128)S(1)}, u32[]{:S(2)}, u32[]{:S(2)}) collective-permute-start(f32[448,1024]{1,0:T(8,128)S(1)} %shard_map.39), channel_id=1, source_target_pairs={{0,2},{2,0},{1,3},{3,1},{4,6},{6,4},{5,7},{7,5},{8,10},{10,8},{9,1... | collective-permute-start | bytes 5505032 | tf_op jit(solution)/shard_map/ppermute | solution.py:178
  59.4 6.8 %collective-permute-start.14 = (f32[32,1024]{1,0:T(8,128)S(1)}, f32[32,1024]{1,0:T(8,128)S(1)}, u32[]{:S(2)}, u32[]{:S(2)}) collective-permute-start(f32[32,1024]{1,0:T(8,128)S(1)} %slice.103), channel_id=1, source_target_pairs={{0,32},{32,64},{64,96},{96,128},{128,160},{160,192},{192,224},{224... | collective-permute-start | bytes 393224 | tf_op jit(solution)/shard_map/ppermute | solution.py:99
  59.5 8.1 %collective-permute-start.18 = (f32[24,1024]{1,0:T(8,128)S(1)}, f32[24,1024]{1,0:T(8,128)S(1)}, u32[]{:S(2)}, u32[]{:S(2)}) collective-permute-start(f32[24,1024]{1,0:T(8,128)S(1)} %get-tuple-element.10), channel_id=1, source_target_pairs={{0,224},{32,0},{64,32},{96,64},{128,96},{160,128},{192,160},{224,1... | collective-permute-start | bytes 294920 | tf_op jit(solution)/shard_map/ppermute | solution.py:99
  66.3 8.1 %collective-permute-start.15 = (f32[56,1024]{1,0:T(8,128)S(1)}, f32[56,1024]{1,0:T(8,128)S(1)}, u32[]{:S(2)}, u32[]{:S(2)}) collective-permute-start(f32[56,1024]{1,0:T(8,128)S(1)} %pad_maximum_fusion.2), channel_id=1, source_target_pairs={{0,32},{32,64},{64,96},{96,128},{128,160},{160,192},{192,224},{224... | collective-permute-start | bytes 688136 | tf_op jit(solution)/shard_map/ppermute | solution.py:99
  67.7 7.3 %collective-permute-start.19 = (f32[56,1024]{1,0:T(8,128)S(1)}, f32[56,1024]{1,0:T(8,128)S(1)}, u32[]{:S(2)}, u32[]{:S(2)}) collective-permute-start(f32[56,1024]{1,0:T(8,128)S(1)} %pad_maximum_fusion.3), channel_id=1, source_target_pairs={{0,224},{32,0},{64,32},{96,64},{128,96},{160,128},{192,160},{224,1... | collective-permute-start | bytes 688136 | tf_op jit(solution)/shard_map/ppermute | solution.py:99
  74.4 7.3 %collective-permute-start.16 = (f32[56,1024]{1,0:T(8,128)S(1)}, f32[56,1024]{1,0:T(8,128)S(1)}, u32[]{:S(2)}, u32[]{:S(2)}) collective-permute-start(f32[56,1024]{1,0:T(8,128)S(1)} %slice_add_fusion.2), channel_id=1, source_target_pairs={{0,32},{32,64},{64,96},{96,128},{128,160},{160,192},{192,224},{224... | collective-permute-start | bytes 688136 | tf_op jit(solution)/shard_map/ppermute | solution.py:99
  81.8 7.3 %collective-permute-start.20 = (f32[56,1024]{1,0:T(8,128)S(1)}, f32[56,1024]{1,0:T(8,128)S(1)}, u32[]{:S(2)}, u32[]{:S(2)}) collective-permute-start(f32[56,1024]{1,0:T(8,128)S(1)} %get-tuple-element.6), channel_id=1, source_target_pairs={{0,224},{32,0},{64,32},{96,64},{128,96},{160,128},{192,160},{224,1... | collective-permute-start | bytes 688136 | tf_op jit(solution)/shard_map/ppermute | solution.py:99
  81.9 7.3 %collective-permute-start.17 = (f32[56,1024]{1,0:T(8,128)S(1)}, f32[56,1024]{1,0:T(8,128)S(1)}, u32[]{:S(2)}, u32[]{:S(2)}) collective-permute-start(f32[56,1024]{1,0:T(8,128)S(1)} %get-tuple-element.5), channel_id=1, source_target_pairs={{0,32},{32,64},{64,96},{96,128},{128,160},{160,192},{192,224},{224... | collective-permute-start | bytes 688136 | tf_op jit(solution)/shard_map/ppermute | solution.py:99
  89.1 6.1 %collective-permute-start.21 = (f32[56,1024]{1,0:T(8,128)S(1)}, f32[56,1024]{1,0:T(8,128)S(1)}, u32[]{:S(2)}, u32[]{:S(2)}) collective-permute-start(f32[56,1024]{1,0:T(8,128)S(1)} %slice_add_fusion.1), channel_id=1, source_target_pairs={{0,224},{32,0},{64,32},{96,64},{128,96},{160,128},{192,160},{224,1... | collective-permute-start | bytes 688136 | tf_op jit(solution)/shard_map/ppermute | solution.py:99

commit v13 on v12

--- a/solution.py
+++ b/solution.py
@@ -177,21 +177,30 @@
     theirs = part(spread, others, sources)
     arrived = lax.ppermute(theirs, "c", swap)
     mine = part(spread, targets, sources)
-    total = summed_along_z((mine + arrived) / POPULATION)
+    total = summed_along_z(mine, arrived)
     return jnp.concatenate([total[:ROWS], total[ROWS:]], axis=1)
 
 
-def summed_along_z(partial):
-    chunk = [partial[2 * ROWS * k : 2 * ROWS * (k + 1)] for k in range(TARGETS)]
-    up = moved(chunk[4][:CUT], 1)
-    down = moved(chunk[4][CUT:], -1)
-    up = moved(jnp.concatenate([chunk[3][:CUT] + up, chunk[3][CUT:]], axis=0), 1)
-    down = moved(jnp.concatenate([chunk[5][:CUT], chunk[5][CUT:] + down], axis=0), -1)
-    up = moved(chunk[2] + up, 1)
-    down = moved(chunk[6] + down, -1)
-    up = moved(chunk[1] + up, 1)
-    down = moved(chunk[7] + down, -1)
-    return chunk[0] + up + down
+def summed_along_z(mine, arrived):
+    size = 2 * ROWS
+
+    def both(first, last):
+        span = slice(first * size, last * size)
+        return (mine[span] + arrived[span]) / POPULATION
+
+    ahead, behind = lax.optimization_barrier((both(1, 5), both(4, 8)))
+
+    def rows(array, index, first=0, last=size):
+        return array[index * size + first : index * size + last]
+
+    up = moved(rows(ahead, 3, 0, CUT), 1)
+    down = moved(rows(behind, 0, CUT), -1)
+    up = jnp.concatenate([rows(ahead, 2, 0, CUT) + up, rows(ahead, 2, CUT)], axis=0)
+    down = jnp.concatenate([rows(behind, 1, 0, CUT), rows(behind, 1, CUT) + down], axis=0)
+    up, down = moved(up, 1), moved(down, -1)
+    up, down = moved(rows(ahead, 1) + up, 1), moved(rows(behind, 2) + down, -1)
+    up, down = moved(rows(ahead, 0) + up, 1), moved(rows(behind, 3) + down, -1)
+    return both(0, 1) + up + down
 
 
 def solution(mesh):

time: 96.1 us -> 91.2 us (0.949)
  the two profiles are of different devices: /device:TPU:12 before, /device:TPU:24 now
where the time goes in v13:
time: 91.2 us; the launch traced here: 91 us
  waiting for transfers between devices  42.3 us (46%)
  starting transfers between devices  39.3 us (43%)
  Pallas kernels  5 us (5%)
  other arithmetic  2.37 us (3%)
  local copies, waits for them, and re-layouts  1.2 us (1%)
    ppermute x14, waiting for transfers between devices, moved(): lax.ppermute(value, 'z', [(i, (i + steps) % TARGETS) for i in range(TARGE...  29 us
    ppermute x14, starting transfers between devices, moved(): lax.ppermute(value, 'z', [(i, (i + steps) % TARGETS) for i in range(TARGE...  27.3 us
    ppermute x6, waiting for transfers between devices, moved_across(): return lax.ppermute(value, AXES, sorted(pairs))  12.1 us
    ppermute x6, starting transfers between devices, moved_across(): return lax.ppermute(value, AXES, sorted(pairs))  7.37 us
    pallas_call x2, Pallas kernels, part(): pl.pallas_call(part_kernel, in_specs=[pl.BlockSpec(memory_space=pltpu.SME...  4.9 us
    all_to_all x1, starting transfers between devices, sent_along(): lax.all_to_all(jnp.broadcast_to(value[None], (count, *value.shape)), AXES...  4.29 us
  transfers between devices with their start and end apart: 23, of which 16 were waited for; matrix products, arithmetic and copies ran while one was open for 0% of the time, Pallas kernels for 3%

profile of v13, /device:TPU:24, one launch (start us, length us, event | category | flops | bytes accessed | tf_op | source)
XLA Modules:
  0.0 91.0 jit_solution(6714927894046784360)
XLA Ops:
  0.0 1.0 %pad_maximum_fusion.1 = bf16[56,2048]{1,0:T(8,128)(2,1)S(1)} fusion(bf16[28,2048]{1,0:T(8,128)(2,1)} %param.4, bf16[28,2048]{1,0:T(8,128)(2,1)} %param.3), kind=kLoop, calls=%fused_computation.9 | loop fusion | flops 458752 | bytes 458752 | tf_op jit(solution)/shard_map/concatenate | solution.py:169
  1.1 1.1 %broadcast_in_dim.2 = bf16[4,56,2048]{2,1,0:T(8,128)(2,1)} broadcast(bf16[56,2048]{1,0:T(8,128)(2,1)S(1)} %pad_maximum_fusion.1), dimensions={1,2} | broadcast | bytes 1146880 | tf_op jit(solution)/shard_map/broadcast_in_dim | solution.py:41
  2.1 4.3 %all-to-all-start = ((bf16[4,56,2048]{2,1,0:T(8,128)(2,1)}), bf16[4,56,2048]{2,1,0:T(8,128)(2,1)S(1)}, u32[]{:S(2)}, u32[]{:S(2)}) async-start(bf16[4,56,2048]{2,1,0:T(8,128)(2,1)} %broadcast_in_dim.2), calls=%async_computation | async-start | bytes 1835008 | tf_op jit(solution)/shard_map/all_to_all | solution.py:40
  6.5 2.0 %collective-permute-start = (bf16[56,1024]{1,0:T(8,128)(2,1)S(1)}, bf16[56,1024]{1,0:T(8,128)(2,1)S(1)}, u32[]{:S(2)}, u32[]{:S(2)}) collective-permute-start(bf16[56,1024]{1,0:T(8,128)(2,1)S(1)} %pad_maximum_fusion.6.own_ref), channel_id=1, source_target_pairs={{0,32},{32,64},{64,96},{96,128},{128,160},{160,192},{192,224},{224... | collective-permute-start | bytes 344072 | tf_op jit(solution)/shard_map/ppermute | solution.py:99
  8.4 4.0 %collective-permute-start.1 = (bf16[56,1024]{1,0:T(8,128)(2,1)S(1)}, bf16[56,1024]{1,0:T(8,128)(2,1)S(1)}, u32[]{:S(2)}, u32[]{:S(2)}) collective-permute-start(bf16[56,1024]{1,0:T(8,128)(2,1)S(1)} %pad_maximum_fusion.6.own_ref), channel_id=1, source_target_pairs={{0,224},{32,0},{64,32},{96,64},{128,96},{160,128},{192,160},{224,1... | collective-permute-start | bytes 344072 | tf_op jit(solution)/shard_map/ppermute | solution.py:99
  12.5 2.9 %collective-permute-done.up_ref = bf16[56,1024]{1,0:T(8,128)(2,1)S(1)} collective-permute-done((bf16[56,1024]{1,0:T(8,128)(2,1)S(1)}, bf16[56,1024]{1,0:T(8,128)(2,1)S(1)}, u32[]{:S(2)}, u32[]{:S(2)}) %collective-permute-start) | collective-permute-done | bytes 114720 | tf_op jit(solution)/shard_map/ppermute | solution.py:99
  15.4 3.2 %collective-permute-start.3 = (bf16[56,1024]{1,0:T(8,128)(2,1)S(1)}, bf16[56,1024]{1,0:T(8,128)(2,1)S(1)}, u32[]{:S(2)}, u32[]{:S(2)}) collective-permute-start(bf16[56,1024]{1,0:T(8,128)(2,1)S(1)} %collective-permute-done.1.down_ref), channel_id=1, source_target_pairs={{0,224},{32,0},{64,32},{96,64},{128,96},{160,128},{192,160},{224,1... | collective-permute-start | bytes 344072 | tf_op jit(solution)/shard_map/ppermute | solution.py:99
  18.6 2.8 %collective-permute-done.2.up2_ref = bf16[56,1024]{1,0:T(8,128)(2,1)S(1)} collective-permute-done((bf16[56,1024]{1,0:T(8,128)(2,1)S(1)}, bf16[56,1024]{1,0:T(8,128)(2,1)S(1)}, u32[]{:S(2)}, u32[]{:S(2)}) %collective-permute-start.2) | collective-permute-done | bytes 114720 | tf_op jit(solution)/shard_map/ppermute | solution.py:99
  21.5 4.2 %collective-permute-start.5 = (bf16[80,1024]{1,0:T(8,128)(2,1)S(1)}, bf16[80,1024]{1,0:T(8,128)(2,1)S(1)}, u32[]{:S(2)}, u32[]{:S(2)}) collective-permute-start(bf16[80,1024]{1,0:T(8,128)(2,1)S(1)} %pad_maximum_fusion.5), channel_id=1, source_target_pairs={{0,192},{32,224},{64,0},{96,32},{128,64},{160,96},{192,128},{224,1... | collective-permute-start | bytes 491528 | tf_op jit(solution)/shard_map/ppermute | solution.py:99
  25.7 5.8 %collective-permute-done.5.far_down_ref = bf16[80,1024]{1,0:T(8,128)(2,1)S(1)} collective-permute-done((bf16[80,1024]{1,0:T(8,128)(2,1)S(1)}, bf16[80,1024]{1,0:T(8,128)(2,1)S(1)}, u32[]{:S(2)}, u32[]{:S(2)}) %collective-permute-start.5) | collective-permute-done | bytes 163872 | tf_op jit(solution)/shard_map/ppermute | solution.py:99
  31.8 0.6 collective-permute-start.6
  32.3 1.5 %collective-permute-start.9 = (bf16[112,2048]{1,0:T(8,128)(2,1)S(1)}, bf16[112,2048]{1,0:T(8,128)(2,1)S(1)}, u32[]{:S(2)}, u32[]{:S(2)}) collective-permute-start(bf16[112,2048]{1,0:T(8,128)(2,1)S(1)} %bitcast.5), channel_id=1, source_target_pairs={{0,5},{1,4},{2,26},{3,27},{4,0},{5,1},{6,30},{7,31},{8,13},{9,12},... | collective-permute-start | bytes 1376264 | tf_op jit(solution)/shard_map/ppermute | solution.py:95
  33.9 1.1 %collective-permute-start.8 = (bf16[112,2048]{1,0:T(8,128)(2,1)S(1)}, bf16[112,2048]{1,0:T(8,128)(2,1)S(1)}, u32[]{:S(2)}, u32[]{:S(2)}) collective-permute-start(bf16[112,2048]{1,0:T(8,128)(2,1)S(1)} %bitcast.8), channel_id=1, source_target_pairs={{0,5},{1,4},{2,26},{3,27},{4,0},{5,1},{6,30},{7,31},{8,13},{9,12},... | collective-permute-start | bytes 1376264 | tf_op jit(solution)/shard_map/ppermute | solution.py:95
  35.0 2.1 %collective-permute-start.7 = (bf16[112,2048]{1,0:T(8,128)(2,1)S(1)}, bf16[112,2048]{1,0:T(8,128)(2,1)S(1)}, u32[]{:S(2)}, u32[]{:S(2)}) collective-permute-start(bf16[112,2048]{1,0:T(8,128)(2,1)S(1)} %bitcast.6), channel_id=1, source_target_pairs={{0,4},{1,5},{2,10},{3,11},{4,1},{5,0},{6,14},{7,15},{8,12},{9,13},... | collective-permute-start | bytes 1376264 | tf_op jit(solution)/shard_map/ppermute | solution.py:95
  37.1 3.2 %collective-permute-done.6.refs_0_ = bf16[112,2048]{1,0:T(8,128)(2,1)S(1)} collective-permute-done((bf16[112,2048]{1,0:T(8,128)(2,1)S(1)}, bf16[112,2048]{1,0:T(8,128)(2,1)S(1)}, u32[]{:S(2)}, u32[]{:S(2)}) %collective-permute-start.6) | collective-permute-done | bytes 458784 | tf_op jit(solution)/shard_map/ppermute | solution.py:95
  40.3 1.7 %collective-permute-start.10 = (bf16[112,2048]{1,0:T(8,128)(2,1)S(1)}, bf16[112,2048]{1,0:T(8,128)(2,1)S(1)}, u32[]{:S(2)}, u32[]{:S(2)}) collective-permute-start(bf16[112,2048]{1,0:T(8,128)(2,1)S(1)} %collective-permute-done.6.refs_0_), channel_id=1, source_target_pairs={{0,4},{1,5},{2,10},{3,11},{4,1},{5,0},{6,14},{7,15},{8,12},{9,13},... | collective-permute-start | bytes 1376264 | tf_op jit(solution)/shard_map/ppermute | solution.py:95
  43.0 3.9 %collective-permute-done.8.refs_2_ = bf16[112,2048]{1,0:T(8,128)(2,1)S(1)} collective-permute-done((bf16[112,2048]{1,0:T(8,128)(2,1)S(1)}, bf16[112,2048]{1,0:T(8,128)(2,1)S(1)}, u32[]{:S(2)}, u32[]{:S(2)}) %collective-permute-start.8) | collective-permute-done | bytes 458784 | tf_op jit(solution)/shard_map/ppermute | solution.py:95
  46.9 3.2 %collective-permute-done.10.refs_4_ = bf16[112,2048]{1,0:T(8,128)(2,1)S(1)} collective-permute-done((bf16[112,2048]{1,0:T(8,128)(2,1)S(1)}, bf16[112,2048]{1,0:T(8,128)(2,1)S(1)}, u32[]{:S(2)}, u32[]{:S(2)}) %collective-permute-start.10) | collective-permute-done | bytes 458784 | tf_op jit(solution)/shard_map/ppermute | solution.py:95
  50.1 1.7 %collective-permute-done.11.refs_5_ = bf16[112,2048]{1,0:T(8,128)(2,1)S(1)} collective-permute-done((bf16[112,2048]{1,0:T(8,128)(2,1)S(1)}, bf16[112,2048]{1,0:T(8,128)(2,1)S(1)}, u32[]{:S(2)}, u32[]{:S(2)}) %collective-permute-start.11) | collective-permute-done | bytes 458784 | tf_op jit(solution)/shard_map/ppermute | solution.py:95
  51.8 2.5 %shard_map.39 = f32[448,1024]{1,0:T(8,128)S(1)} custom-call(f32[1]{0:T(128)S(6)} %copy.4.spread_ref, bf16[256,2048]{1,0:T(8,128)(2,1)S(1)} %collective-permute-done.12.t_all, bf16[224,2048]{1,0:T(8,128)(2,1)S(1)} %bitcast.3, bf16[112,2048]{1,0:T(8,128)(2,1)S(1)} %collective-permute-done.6.refs_0_, bf16[112,2048]{1,0:T(8,128)(2,1)S(1)} %collective-permute-done.7.refs_1_, ...), custom_call_target="tpu_custom_call" | custom-call | tf_op jit(solution)/shard_map/pallas_call | solution.py:145
  54.5 2.4 %shard_map.38 = f32[448,1024]{1,0:T(8,128)S(1)} custom-call(f32[1]{0:T(128)S(6)} %copy.4.spread_ref, bf16[256,2048]{1,0:T(8,128)(2,1)S(1)} %shard_map.37.t_all, bf16[224,2048]{1,0:T(8,128)(2,1)S(1)} %bitcast.4, bf16[112,2048]{1,0:T(8,128)(2,1)S(1)} %collective-permute-done.6.refs_0_, bf16[112,2048]{1,0:T(8,128)(2,1)S(1)} %collective-permute-done.7.refs_1_, ...), custom_call_target="tpu_custom_call" | custom-call | tf_op jit(solution)/shard_map/pallas_call | solution.py:145
  56.9 1.2 %collective-permute-done.13 = f32[448,1024]{1,0:T(8,128)S(1)} collective-permute-done((f32[448,1024]{1,0:T(8,128)S(1)}, f32[448,1024]{1,0:T(8,128)S(1)}, u32[]{:S(2)}, u32[]{:S(2)}) %collective-permute-start.13) | collective-permute-done | bytes 1835040 | tf_op jit(solution)/shard_map/ppermute | solution.py:178
  58.5 2.6 %collective-permute-start.18 = (f32[24,1024]{1,0:T(8,128)S(1)}, f32[24,1024]{1,0:T(8,128)S(1)}, u32[]{:S(2)}, u32[]{:S(2)}) collective-permute-start(f32[24,1024]{1,0:T(8,128)S(1)} %slice.103), channel_id=1, source_target_pairs={{0,224},{32,0},{64,32},{96,64},{128,96},{160,128},{192,160},{224,1... | collective-permute-start | bytes 294920 | tf_op jit(solution)/shard_map/ppermute | solution.py:99
  61.2 2.2 %collective-permute-done.18 = f32[24,1024]{1,0:T(8,128)S(1)} collective-permute-done((f32[24,1024]{1,0:T(8,128)S(1)}, f32[24,1024]{1,0:T(8,128)S(1)}, u32[]{:S(2)}, u32[]{:S(2)}) %collective-permute-start.18) | collective-permute-done | bytes 98336 | tf_op jit(solution)/shard_map/ppermute | solution.py:99
  63.5 3.8 %collective-permute-start.19 = (f32[56,1024]{1,0:T(8,128)S(1)}, f32[56,1024]{1,0:T(8,128)S(1)}, u32[]{:S(2)}, u32[]{:S(2)}) collective-permute-start(f32[56,1024]{1,0:T(8,128)S(1)} %pad_maximum_fusion.3), channel_id=1, source_target_pairs={{0,224},{32,0},{64,32},{96,64},{128,96},{160,128},{192,160},{224,1... | collective-permute-start | bytes 688136 | tf_op jit(solution)/shard_map/ppermute | solution.py:99
  67.8 4.2 %collective-permute-done.19 = f32[56,1024]{1,0:T(8,128)S(1)} collective-permute-done((f32[56,1024]{1,0:T(8,128)S(1)}, f32[56,1024]{1,0:T(8,128)S(1)}, u32[]{:S(2)}, u32[]{:S(2)}) %collective-permute-start.19) | collective-permute-done | bytes 229408 | tf_op jit(solution)/shard_map/ppermute | solution.py:99
  72.0 3.3 %collective-permute-start.20 = (f32[56,1024]{1,0:T(8,128)S(1)}, f32[56,1024]{1,0:T(8,128)S(1)}, u32[]{:S(2)}, u32[]{:S(2)}) collective-permute-start(f32[56,1024]{1,0:T(8,128)S(1)} %slice_add_fusion.3), channel_id=1, source_target_pairs={{0,224},{32,0},{64,32},{96,64},{128,96},{160,128},{192,160},{224,1... | collective-permute-start | bytes 688136 | tf_op jit(solution)/shard_map/ppermute | solution.py:99
  75.6 3.3 %collective-permute-done.20 = f32[56,1024]{1,0:T(8,128)S(1)} collective-permute-done((f32[56,1024]{1,0:T(8,128)S(1)}, f32[56,1024]{1,0:T(8,128)S(1)}, u32[]{:S(2)}, u32[]{:S(2)}) %collective-permute-start.20) | collective-permute-done | bytes 229408 | tf_op jit(solution)/shard_map/ppermute | solution.py:99
  78.9 3.8 %collective-permute-start.21 = (f32[56,1024]{1,0:T(8,128)S(1)}, f32[56,1024]{1,0:T(8,128)S(1)}, u32[]{:S(2)}, u32[]{:S(2)}) collective-permute-start(f32[56,1024]{1,0:T(8,128)S(1)} %slice_add_fusion.4), channel_id=1, source_target_pairs={{0,224},{32,0},{64,32},{96,64},{128,96},{160,128},{192,160},{224,1... | collective-permute-start | bytes 688136 | tf_op jit(solution)/shard_map/ppermute | solution.py:99
  83.0 3.3 %collective-permute-done.21 = f32[56,1024]{1,0:T(8,128)S(1)} collective-permute-done((f32[56,1024]{1,0:T(8,128)S(1)}, f32[56,1024]{1,0:T(8,128)S(1)}, u32[]{:S(2)}, u32[]{:S(2)}) %collective-permute-start.21) | collective-permute-done | bytes 229408 | tf_op jit(solution)/shard_map/ppermute | solution.py:99
  86.2 4.0 %collective-permute-done.17 = f32[56,1024]{1,0:T(8,128)S(1)} collective-permute-done((f32[56,1024]{1,0:T(8,128)S(1)}, f32[56,1024]{1,0:T(8,128)S(1)}, u32[]{:S(2)}, u32[]{:S(2)}) %collective-permute-start.17) | collective-permute-done | bytes 229408 | tf_op jit(solution)/shard_map/ppermute | solution.py:99
  90.3 0.7 pad_maximum_fusion
  (44 shorter events, 2.6 us)
Async XLA Ops:
  0.0 6.4 %copy-start = (bf16[28,2048]{1,0:T(8,128)(2,1)S(1)}, bf16[28,2048]{1,0:T(8,128)(2,1)}, u32[]{:S(2)}) copy-start(bf16[28,2048]{1,0:T(8,128)(2,1)} %param.3) | copy-start | bytes 344068
  2.1 29.6 %all-to-all-start = ((bf16[4,56,2048]{2,1,0:T(8,128)(2,1)}), bf16[4,56,2048]{2,1,0:T(8,128)(2,1)S(1)}, u32[]{:S(2)}, u32[]{:S(2)}) async-start(bf16[4,56,2048]{2,1,0:T(8,128)(2,1)} %broadcast_in_dim.2), calls=%async_computation | async-start | bytes 1835008 | tf_op jit(solution)/shard_map/all_to_all | solution.py:40
  6.5 8.9 %collective-permute-start = (bf16[56,1024]{1,0:T(8,128)(2,1)S(1)}, bf16[56,1024]{1,0:T(8,128)(2,1)S(1)}, u32[]{:S(2)}, u32[]{:S(2)}) collective-permute-start(bf16[56,1024]{1,0:T(8,128)(2,1)S(1)} %pad_maximum_fusion.6.own_ref), channel_id=1, source_target_pairs={{0,32},{32,64},{64,96},{96,128},{128,160},{160,192},{192,224},{224... | collective-permute-start | bytes 344072 | tf_op jit(solution)/shard_map/ppermute | solution.py:99
  8.4 6.9 %collective-permute-start.1 = (bf16[56,1024]{1,0:T(8,128)(2,1)S(1)}, bf16[56,1024]{1,0:T(8,128)(2,1)S(1)}, u32[]{:S(2)}, u32[]{:S(2)}) collective-permute-start(bf16[56,1024]{1,0:T(8,128)(2,1)S(1)} %pad_maximum_fusion.6.own_ref), channel_id=1, source_target_pairs={{0,224},{32,0},{64,32},{96,64},{128,96},{160,128},{192,160},{224,1... | collective-permute-start | bytes 344072 | tf_op jit(solution)/shard_map/ppermute | solution.py:99
  15.4 6.0 %collective-permute-start.2 = (bf16[56,1024]{1,0:T(8,128)(2,1)S(1)}, bf16[56,1024]{1,0:T(8,128)(2,1)S(1)}, u32[]{:S(2)}, u32[]{:S(2)}) collective-permute-start(bf16[56,1024]{1,0:T(8,128)(2,1)S(1)} %collective-permute-done.up_ref), channel_id=1, source_target_pairs={{0,32},{32,64},{64,96},{96,128},{128,160},{160,192},{192,224},{224... | collective-permute-start | bytes 344072 | tf_op jit(solution)/shard_map/ppermute | solution.py:99
  15.4 6.1 %collective-permute-start.3 = (bf16[56,1024]{1,0:T(8,128)(2,1)S(1)}, bf16[56,1024]{1,0:T(8,128)(2,1)S(1)}, u32[]{:S(2)}, u32[]{:S(2)}) collective-permute-start(bf16[56,1024]{1,0:T(8,128)(2,1)S(1)} %collective-permute-done.1.down_ref), channel_id=1, source_target_pairs={{0,224},{32,0},{64,32},{96,64},{128,96},{160,128},{192,160},{224,1... | collective-permute-start | bytes 344072 | tf_op jit(solution)/shard_map/ppermute | solution.py:99
  21.4 10.1 %collective-permute-start.4 = (bf16[88,1024]{1,0:T(8,128)(2,1)S(1)}, bf16[88,1024]{1,0:T(8,128)(2,1)S(1)}, u32[]{:S(2)}, u32[]{:S(2)}) collective-permute-start(bf16[88,1024]{1,0:T(8,128)(2,1)S(1)} %pad_maximum_fusion.4), channel_id=1, source_target_pairs={{0,64},{32,96},{64,128},{96,160},{128,192},{160,224},{192,0},{224,... | collective-permute-start | bytes 540680 | tf_op jit(solution)/shard_map/ppermute | solution.py:99
  21.5 9.9 %collective-permute-start.5 = (bf16[80,1024]{1,0:T(8,128)(2,1)S(1)}, bf16[80,1024]{1,0:T(8,128)(2,1)S(1)}, u32[]{:S(2)}, u32[]{:S(2)}) collective-permute-start(bf16[80,1024]{1,0:T(8,128)(2,1)S(1)} %pad_maximum_fusion.5), channel_id=1, source_target_pairs={{0,192},{32,224},{64,0},{96,32},{128,64},{160,96},{192,128},{224,1... | collective-permute-start | bytes 491528 | tf_op jit(solution)/shard_map/ppermute | solution.py:99
  31.6 15.3 %collective-permute-start.12 = (bf16[256,2048]{1,0:T(8,128)(2,1)S(1)}, bf16[256,2048]{1,0:T(8,128)(2,1)S(1)}, u32[]{:S(2)}, u32[]{:S(2)}) collective-permute-start(bf16[256,2048]{1,0:T(8,128)(2,1)S(1)} %shard_map.37.t_all), channel_id=1, source_target_pairs={{0,2},{2,0},{1,3},{3,1},{4,6},{6,4},{5,7},{7,5},{8,10},{10,8},{9,1... | collective-permute-start | bytes 3145736 | tf_op jit(solution)/shard_map/ppermute | solution.py:168
  31.8 8.6 %collective-permute-start.6 = (bf16[112,2048]{1,0:T(8,128)(2,1)S(1)}, bf16[112,2048]{1,0:T(8,128)(2,1)S(1)}, u32[]{:S(2)}, u32[]{:S(2)}) collective-permute-start(bf16[112,2048]{1,0:T(8,128)(2,1)S(1)} %bitcast.7), channel_id=1, source_target_pairs={{0,4},{1,5},{2,10},{3,11},{4,1},{5,0},{6,14},{7,15},{8,12},{9,13},... | collective-permute-start | bytes 1376264 | tf_op jit(solution)/shard_map/ppermute | solution.py:95
  32.3 9.7 %collective-permute-start.9 = (bf16[112,2048]{1,0:T(8,128)(2,1)S(1)}, bf16[112,2048]{1,0:T(8,128)(2,1)S(1)}, u32[]{:S(2)}, u32[]{:S(2)}) collective-permute-start(bf16[112,2048]{1,0:T(8,128)(2,1)S(1)} %bitcast.5), channel_id=1, source_target_pairs={{0,5},{1,4},{2,26},{3,27},{4,0},{5,1},{6,30},{7,31},{8,13},{9,12},... | collective-permute-start | bytes 1376264 | tf_op jit(solution)/shard_map/ppermute | solution.py:95
  33.9 13.1 %collective-permute-start.8 = (bf16[112,2048]{1,0:T(8,128)(2,1)S(1)}, bf16[112,2048]{1,0:T(8,128)(2,1)S(1)}, u32[]{:S(2)}, u32[]{:S(2)}) collective-permute-start(bf16[112,2048]{1,0:T(8,128)(2,1)S(1)} %bitcast.8), channel_id=1, source_target_pairs={{0,5},{1,4},{2,26},{3,27},{4,0},{5,1},{6,30},{7,31},{8,13},{9,12},... | collective-permute-start | bytes 1376264 | tf_op jit(solution)/shard_map/ppermute | solution.py:95
  35.0 11.9 %collective-permute-start.7 = (bf16[112,2048]{1,0:T(8,128)(2,1)S(1)}, bf16[112,2048]{1,0:T(8,128)(2,1)S(1)}, u32[]{:S(2)}, u32[]{:S(2)}) collective-permute-start(bf16[112,2048]{1,0:T(8,128)(2,1)S(1)} %bitcast.6), channel_id=1, source_target_pairs={{0,4},{1,5},{2,10},{3,11},{4,1},{5,0},{6,14},{7,15},{8,12},{9,13},... | collective-permute-start | bytes 1376264 | tf_op jit(solution)/shard_map/ppermute | solution.py:95
  40.3 9.8 %collective-permute-start.10 = (bf16[112,2048]{1,0:T(8,128)(2,1)S(1)}, bf16[112,2048]{1,0:T(8,128)(2,1)S(1)}, u32[]{:S(2)}, u32[]{:S(2)}) collective-permute-start(bf16[112,2048]{1,0:T(8,128)(2,1)S(1)} %collective-permute-done.6.refs_0_), channel_id=1, source_target_pairs={{0,4},{1,5},{2,10},{3,11},{4,1},{5,0},{6,14},{7,15},{8,12},{9,13},... | collective-permute-start | bytes 1376264 | tf_op jit(solution)/shard_map/ppermute | solution.py:95
  42.0 9.8 %collective-permute-start.11 = (bf16[112,2048]{1,0:T(8,128)(2,1)S(1)}, bf16[112,2048]{1,0:T(8,128)(2,1)S(1)}, u32[]{:S(2)}, u32[]{:S(2)}) collective-permute-start(bf16[112,2048]{1,0:T(8,128)(2,1)S(1)} %collective-permute-done.9.refs_3_), channel_id=1, source_target_pairs={{0,5},{1,4},{2,26},{3,27},{4,0},{5,1},{6,30},{7,31},{8,13},{9,12},... | collective-permute-start | bytes 1376264 | tf_op jit(solution)/shard_map/ppermute | solution.py:95
  54.3 3.9 %collective-permute-start.13 = (f32[448,1024]{1,0:T(8,128)S(1)}, f32[448,1024]{1,0:T(8,128)S(1)}, u32[]{:S(2)}, u32[]{:S(2)}) collective-permute-start(f32[448,1024]{1,0:T(8,128)S(1)} %shard_map.39), channel_id=1, source_target_pairs={{0,2},{2,0},{1,3},{3,1},{4,6},{6,4},{5,7},{7,5},{8,10},{10,8},{9,1... | collective-permute-start | bytes 5505032 | tf_op jit(solution)/shard_map/ppermute | solution.py:178
  58.5 5.0 %collective-permute-start.18 = (f32[24,1024]{1,0:T(8,128)S(1)}, f32[24,1024]{1,0:T(8,128)S(1)}, u32[]{:S(2)}, u32[]{:S(2)}) collective-permute-start(f32[24,1024]{1,0:T(8,128)S(1)} %slice.103), channel_id=1, source_target_pairs={{0,224},{32,0},{64,32},{96,64},{128,96},{160,128},{192,160},{224,1... | collective-permute-start | bytes 294920 | tf_op jit(solution)/shard_map/ppermute | solution.py:99
  61.1 6.5 %collective-permute-start.14 = (f32[32,1024]{1,0:T(8,128)S(1)}, f32[32,1024]{1,0:T(8,128)S(1)}, u32[]{:S(2)}, u32[]{:S(2)}) collective-permute-start(f32[32,1024]{1,0:T(8,128)S(1)} %slice.97), channel_id=1, source_target_pairs={{0,32},{32,64},{64,96},{96,128},{128,160},{160,192},{192,224},{224... | collective-permute-start | bytes 393224 | tf_op jit(solution)/shard_map/ppermute | solution.py:99
  63.5 8.5 %collective-permute-start.19 = (f32[56,1024]{1,0:T(8,128)S(1)}, f32[56,1024]{1,0:T(8,128)S(1)}, u32[]{:S(2)}, u32[]{:S(2)}) collective-permute-start(f32[56,1024]{1,0:T(8,128)S(1)} %pad_maximum_fusion.3), channel_id=1, source_target_pairs={{0,224},{32,0},{64,32},{96,64},{128,96},{160,128},{192,160},{224,1... | collective-permute-start | bytes 688136 | tf_op jit(solution)/shard_map/ppermute | solution.py:99
  67.7 7.8 %collective-permute-start.15 = (f32[56,1024]{1,0:T(8,128)S(1)}, f32[56,1024]{1,0:T(8,128)S(1)}, u32[]{:S(2)}, u32[]{:S(2)}) collective-permute-start(f32[56,1024]{1,0:T(8,128)S(1)} %pad_maximum_fusion.2), channel_id=1, source_target_pairs={{0,32},{32,64},{64,96},{96,128},{128,160},{160,192},{192,224},{224... | collective-permute-start | bytes 688136 | tf_op jit(solution)/shard_map/ppermute | solution.py:99
  72.0 6.9 %collective-permute-start.20 = (f32[56,1024]{1,0:T(8,128)S(1)}, f32[56,1024]{1,0:T(8,128)S(1)}, u32[]{:S(2)}, u32[]{:S(2)}) collective-permute-start(f32[56,1024]{1,0:T(8,128)S(1)} %slice_add_fusion.3), channel_id=1, source_target_pairs={{0,224},{32,0},{64,32},{96,64},{128,96},{160,128},{192,160},{224,1... | collective-permute-start | bytes 688136 | tf_op jit(solution)/shard_map/ppermute | solution.py:99
  75.5 7.3 %collective-permute-start.16 = (f32[56,1024]{1,0:T(8,128)S(1)}, f32[56,1024]{1,0:T(8,128)S(1)}, u32[]{:S(2)}, u32[]{:S(2)}) collective-permute-start(f32[56,1024]{1,0:T(8,128)S(1)} %slice_add_fusion.5), channel_id=1, source_target_pairs={{0,32},{32,64},{64,96},{96,128},{128,160},{160,192},{192,224},{224... | collective-permute-start | bytes 688136 | tf_op jit(solution)/shard_map/ppermute | solution.py:99
  78.9 7.3 %collective-permute-start.21 = (f32[56,1024]{1,0:T(8,128)S(1)}, f32[56,1024]{1,0:T(8,128)S(1)}, u32[]{:S(2)}, u32[]{:S(2)}) collective-permute-start(f32[56,1024]{1,0:T(8,128)S(1)} %slice_add_fusion.4), channel_id=1, source_target_pairs={{0,224},{32,0},{64,32},{96,64},{128,96},{160,128},{192,160},{224,1... | collective-permute-start | bytes 688136 | tf_op jit(solution)/shard_map/ppermute | solution.py:99
  82.9 7.3 %collective-permute-start.17 = (f32[56,1024]{1,0:T(8,128)S(1)}, f32[56,1024]{1,0:T(8,128)S(1)}, u32[]{:S(2)}, u32[]{:S(2)}) collective-permute-start(f32[56,1024]{1,0:T(8,128)S(1)} %slice_add_fusion.6), channel_id=1, source_target_pairs={{0,32},{32,64},{64,96},{96,128},{128,160},{160,192},{192,224},{224... | collective-permute-start | bytes 688136 | tf_op jit(solution)/shard_map/ppermute | solution.py:99

commit v14 on v13

--- a/solution.py
+++ b/solution.py
@@ -14,7 +14,7 @@
 DIM = 2048
 TARGETS = 8
 PIECES = 16
-STEP = 8
+STEP = 16
 WIDTH = 512
 VMEM_BYTES = 24 * 2**20
 
@@ -100,7 +100,7 @@
 
 
 def part_kernel(spread_ref, t_all, line_ref, *refs):
-    half_refs, (out, x_all, s_all, low_all) = refs[:6], refs[6:]
+    half_refs, outs, (x_all, s_all, low_all) = refs[:6], refs[6:8], refs[8:]
     inverse = 1.0 / spread_ref[0]
     targets = t_all[...]
     target_norm = row_norms(targets)
@@ -136,8 +136,8 @@
         wide = t_all[:, columns].astype(jnp.float32)
         added = drive + (2.0 * inverse) * (wide * row_total - pull)
         for i in range(TARGETS):
-            rows = pl.ds((2 * i + n // 2) * ROWS, ROWS)
-            out[rows, pl.ds(n % 2 * WIDTH, WIDTH)] = added[i * PAD : i * PAD + ROWS]
+            rows = pl.ds((2 * (i % 4) + n // 2) * ROWS, ROWS)
+            outs[i // 4][rows, pl.ds(n % 2 * WIDTH, WIDTH)] = added[i * PAD : i * PAD + ROWS]
 
 
 def part(spread, targets, sources):
@@ -146,8 +146,8 @@
         part_kernel,
         in_specs=[pl.BlockSpec(memory_space=pltpu.SMEM)]
         + [pl.BlockSpec(memory_space=pltpu.VMEM)] * len(args),
-        out_specs=pl.BlockSpec(memory_space=pltpu.VMEM),
-        out_shape=pltpu.VMEM((2 * TARGETS * ROWS, 2 * WIDTH), jnp.float32),
+        out_specs=[pl.BlockSpec(memory_space=pltpu.VMEM)] * 2,
+        out_shape=[pltpu.VMEM((TARGETS * ROWS, 2 * WIDTH), jnp.float32)] * 2,
         scratch_shapes=[
             pltpu.VMEM((PIECES * PAD, DIM), jnp.bfloat16),
             pltpu.VMEM((PIECES * PAD, DIM), jnp.bfloat16),
@@ -175,32 +175,29 @@
     opposite = [moved_across(back_low, 1), moved_across(ahead_high, -1)]
     sources = [line, back_low, back_high, ahead_low, ahead_high, *opposite]
     theirs = part(spread, others, sources)
-    arrived = lax.ppermute(theirs, "c", swap)
+    arrived_behind = lax.ppermute(theirs[1], "c", swap)
+    arrived_ahead = lax.ppermute(theirs[0], "c", swap)
     mine = part(spread, targets, sources)
-    total = summed_along_z(mine, arrived)
+    behind = lax.optimization_barrier((mine[1] + arrived_behind) / POPULATION)
+    ahead = lax.optimization_barrier((mine[0] + arrived_ahead) / POPULATION)
+    total = summed_along_z(ahead, behind)
     return jnp.concatenate([total[:ROWS], total[ROWS:]], axis=1)
 
 
-def summed_along_z(mine, arrived):
+def summed_along_z(ahead, behind):
     size = 2 * ROWS
-
-    def both(first, last):
-        span = slice(first * size, last * size)
-        return (mine[span] + arrived[span]) / POPULATION
-
-    ahead, behind = lax.optimization_barrier((both(1, 5), both(4, 8)))
 
     def rows(array, index, first=0, last=size):
         return array[index * size + first : index * size + last]
 
-    up = moved(rows(ahead, 3, 0, CUT), 1)
+    up = moved(rows(behind, 0, 0, CUT), 1)
     down = moved(rows(behind, 0, CUT), -1)
-    up = jnp.concatenate([rows(ahead, 2, 0, CUT) + up, rows(ahead, 2, CUT)], axis=0)
+    up = jnp.concatenate([rows(ahead, 3, 0, CUT) + up, rows(ahead, 3, CUT)], axis=0)
     down = jnp.concatenate([rows(behind, 1, 0, CUT), rows(behind, 1, CUT) + down], axis=0)
     up, down = moved(up, 1), moved(down, -1)
-    up, down = moved(rows(ahead, 1) + up, 1), moved(rows(behind, 2) + down, -1)
-    up, down = moved(rows(ahead, 0) + up, 1), moved(rows(behind, 3) + down, -1)
-    return both(0, 1) + up + down
+    up, down = moved(rows(ahead, 2) + up, 1), moved(rows(behind, 2) + down, -1)
+    up, down = moved(rows(ahead, 1) + up, 1), moved(rows(behind, 3) + down, -1)
+    return rows(ahead, 0) + up + down
 
 
 def solution(mesh):

time: 91.2 us -> 90.4 us (level)
  waiting for transfers between devices: 42.3 us -> 41.1 us
    ppermute x1 -> x2, waiting for transfers between devices: 1.22 us -> 0.01 us  [the longest x1 0.01 us: direction(): arrived_behind = lax.ppermute(theirs[1], 'c', swap)]
  transfers between devices with their start and end apart: 23 -> 24, of which waited for: 16 -> 15; matrix products, arithmetic and copies ran while one was open for 0% -> 1% of each run, Pallas kernels for 3% -> 3%
where the time goes in v14:
time: 90.4 us; the launch traced here: 90.2 us
  waiting for transfers between devices  41.1 us (45%)
  starting transfers between devices  39.7 us (44%)
  Pallas kernels  4.99 us (6%)
  other arithmetic  2.31 us (3%)
  local copies, waits for them, and re-layouts  1.18 us (1%)
    ppermute x14, waiting for transfers between devices, moved(): lax.ppermute(value, 'z', [(i, (i + steps) % TARGETS) for i in range(TARGE...  29 us
    ppermute x14, starting transfers between devices, moved(): lax.ppermute(value, 'z', [(i, (i + steps) % TARGETS) for i in range(TARGE...  27.3 us
    ppermute x6, waiting for transfers between devices, moved_across(): return lax.ppermute(value, AXES, sorted(pairs))  12.1 us
    ppermute x6, starting transfers between devices, moved_across(): return lax.ppermute(value, AXES, sorted(pairs))  7.37 us
    pallas_call x2, Pallas kernels, part(): pl.pallas_call(part_kernel, in_specs=[pl.BlockSpec(memory_space=pltpu.SME...  4.88 us
    all_to_all x1, starting transfers between devices, sent_along(): lax.all_to_all(jnp.broadcast_to(value[None], (count, *value.shape)), AXES...  4.42 us
  transfers between devices with their start and end apart: 24, of which 15 were waited for; matrix products, arithmetic and copies ran while one was open for 1% of the time, Pallas kernels for 3%

profile of v14, /device:TPU:24, one launch (start us, length us, event | category | flops | bytes accessed | tf_op | source)
XLA Modules:
  0.0 90.2 jit_solution(3236492299335930672)
XLA Ops:
  0.0 1.0 %pad_maximum_fusion.1 = bf16[56,2048]{1,0:T(8,128)(2,1)S(1)} fusion(bf16[28,2048]{1,0:T(8,128)(2,1)} %param.4, bf16[28,2048]{1,0:T(8,128)(2,1)} %param.3), kind=kLoop, calls=%fused_computation.9 | loop fusion | flops 458752 | bytes 458752 | tf_op jit(solution)/shard_map/concatenate | solution.py:169
  1.0 1.0 %broadcast_in_dim.2 = bf16[4,56,2048]{2,1,0:T(8,128)(2,1)} broadcast(bf16[56,2048]{1,0:T(8,128)(2,1)S(1)} %pad_maximum_fusion.1), dimensions={1,2} | broadcast | bytes 1146880 | tf_op jit(solution)/shard_map/broadcast_in_dim | solution.py:41
  2.1 4.4 %all-to-all-start = ((bf16[4,56,2048]{2,1,0:T(8,128)(2,1)}), bf16[4,56,2048]{2,1,0:T(8,128)(2,1)S(1)}, u32[]{:S(2)}, u32[]{:S(2)}) async-start(bf16[4,56,2048]{2,1,0:T(8,128)(2,1)} %broadcast_in_dim.2), calls=%async_computation | async-start | bytes 1835008 | tf_op jit(solution)/shard_map/all_to_all | solution.py:40
  6.5 2.0 %collective-permute-start = (bf16[56,1024]{1,0:T(8,128)(2,1)S(1)}, bf16[56,1024]{1,0:T(8,128)(2,1)S(1)}, u32[]{:S(2)}, u32[]{:S(2)}) collective-permute-start(bf16[56,1024]{1,0:T(8,128)(2,1)S(1)} %pad_maximum_fusion.6.own_ref), channel_id=1, source_target_pairs={{0,32},{32,64},{64,96},{96,128},{128,160},{160,192},{192,224},{224... | collective-permute-start | bytes 344072 | tf_op jit(solution)/shard_map/ppermute | solution.py:99
  8.5 4.0 %collective-permute-start.1 = (bf16[56,1024]{1,0:T(8,128)(2,1)S(1)}, bf16[56,1024]{1,0:T(8,128)(2,1)S(1)}, u32[]{:S(2)}, u32[]{:S(2)}) collective-permute-start(bf16[56,1024]{1,0:T(8,128)(2,1)S(1)} %pad_maximum_fusion.6.own_ref), channel_id=1, source_target_pairs={{0,224},{32,0},{64,32},{96,64},{128,96},{160,128},{192,160},{224,1... | collective-permute-start | bytes 344072 | tf_op jit(solution)/shard_map/ppermute | solution.py:99
  12.6 2.9 %collective-permute-done.up_ref = bf16[56,1024]{1,0:T(8,128)(2,1)S(1)} collective-permute-done((bf16[56,1024]{1,0:T(8,128)(2,1)S(1)}, bf16[56,1024]{1,0:T(8,128)(2,1)S(1)}, u32[]{:S(2)}, u32[]{:S(2)}) %collective-permute-start) | collective-permute-done | bytes 114720 | tf_op jit(solution)/shard_map/ppermute | solution.py:99
  15.4 3.2 %collective-permute-start.3 = (bf16[56,1024]{1,0:T(8,128)(2,1)S(1)}, bf16[56,1024]{1,0:T(8,128)(2,1)S(1)}, u32[]{:S(2)}, u32[]{:S(2)}) collective-permute-start(bf16[56,1024]{1,0:T(8,128)(2,1)S(1)} %collective-permute-done.1.down_ref), channel_id=1, source_target_pairs={{0,224},{32,0},{64,32},{96,64},{128,96},{160,128},{192,160},{224,1... | collective-permute-start | bytes 344072 | tf_op jit(solution)/shard_map/ppermute | solution.py:99
  18.7 2.8 %collective-permute-done.2.up2_ref = bf16[56,1024]{1,0:T(8,128)(2,1)S(1)} collective-permute-done((bf16[56,1024]{1,0:T(8,128)(2,1)S(1)}, bf16[56,1024]{1,0:T(8,128)(2,1)S(1)}, u32[]{:S(2)}, u32[]{:S(2)}) %collective-permute-start.2) | collective-permute-done | bytes 114720 | tf_op jit(solution)/shard_map/ppermute | solution.py:99
  21.6 4.2 %collective-permute-start.5 = (bf16[80,1024]{1,0:T(8,128)(2,1)S(1)}, bf16[80,1024]{1,0:T(8,128)(2,1)S(1)}, u32[]{:S(2)}, u32[]{:S(2)}) collective-permute-start(bf16[80,1024]{1,0:T(8,128)(2,1)S(1)} %pad_maximum_fusion.5), channel_id=1, source_target_pairs={{0,192},{32,224},{64,0},{96,32},{128,64},{160,96},{192,128},{224,1... | collective-permute-start | bytes 491528 | tf_op jit(solution)/shard_map/ppermute | solution.py:99
  25.8 5.8 %collective-permute-done.5.far_down_ref = bf16[80,1024]{1,0:T(8,128)(2,1)S(1)} collective-permute-done((bf16[80,1024]{1,0:T(8,128)(2,1)S(1)}, bf16[80,1024]{1,0:T(8,128)(2,1)S(1)}, u32[]{:S(2)}, u32[]{:S(2)}) %collective-permute-start.5) | collective-permute-done | bytes 163872 | tf_op jit(solution)/shard_map/ppermute | solution.py:99
  31.8 0.6 collective-permute-start.6
  32.4 1.5 %collective-permute-start.9 = (bf16[112,2048]{1,0:T(8,128)(2,1)S(1)}, bf16[112,2048]{1,0:T(8,128)(2,1)S(1)}, u32[]{:S(2)}, u32[]{:S(2)}) collective-permute-start(bf16[112,2048]{1,0:T(8,128)(2,1)S(1)} %bitcast.5), channel_id=1, source_target_pairs={{0,5},{1,4},{2,26},{3,27},{4,0},{5,1},{6,30},{7,31},{8,13},{9,12},... | collective-permute-start | bytes 1376264 | tf_op jit(solution)/shard_map/ppermute | solution.py:95
  33.9 1.1 %collective-permute-start.8 = (bf16[112,2048]{1,0:T(8,128)(2,1)S(1)}, bf16[112,2048]{1,0:T(8,128)(2,1)S(1)}, u32[]{:S(2)}, u32[]{:S(2)}) collective-permute-start(bf16[112,2048]{1,0:T(8,128)(2,1)S(1)} %bitcast.8), channel_id=1, source_target_pairs={{0,5},{1,4},{2,26},{3,27},{4,0},{5,1},{6,30},{7,31},{8,13},{9,12},... | collective-permute-start | bytes 1376264 | tf_op jit(solution)/shard_map/ppermute | solution.py:95
  35.1 2.1 %collective-permute-start.7 = (bf16[112,2048]{1,0:T(8,128)(2,1)S(1)}, bf16[112,2048]{1,0:T(8,128)(2,1)S(1)}, u32[]{:S(2)}, u32[]{:S(2)}) collective-permute-start(bf16[112,2048]{1,0:T(8,128)(2,1)S(1)} %bitcast.6), channel_id=1, source_target_pairs={{0,4},{1,5},{2,10},{3,11},{4,1},{5,0},{6,14},{7,15},{8,12},{9,13},... | collective-permute-start | bytes 1376264 | tf_op jit(solution)/shard_map/ppermute | solution.py:95
  37.2 3.2 %collective-permute-done.6.refs_0_ = bf16[112,2048]{1,0:T(8,128)(2,1)S(1)} collective-permute-done((bf16[112,2048]{1,0:T(8,128)(2,1)S(1)}, bf16[112,2048]{1,0:T(8,128)(2,1)S(1)}, u32[]{:S(2)}, u32[]{:S(2)}) %collective-permute-start.6) | collective-permute-done | bytes 458784 | tf_op jit(solution)/shard_map/ppermute | solution.py:95
  40.4 1.7 %collective-permute-start.10 = (bf16[112,2048]{1,0:T(8,128)(2,1)S(1)}, bf16[112,2048]{1,0:T(8,128)(2,1)S(1)}, u32[]{:S(2)}, u32[]{:S(2)}) collective-permute-start(bf16[112,2048]{1,0:T(8,128)(2,1)S(1)} %collective-permute-done.6.refs_0_), channel_id=1, source_target_pairs={{0,4},{1,5},{2,10},{3,11},{4,1},{5,0},{6,14},{7,15},{8,12},{9,13},... | collective-permute-start | bytes 1376264 | tf_op jit(solution)/shard_map/ppermute | solution.py:95
  43.1 3.9 %collective-permute-done.8.refs_2_ = bf16[112,2048]{1,0:T(8,128)(2,1)S(1)} collective-permute-done((bf16[112,2048]{1,0:T(8,128)(2,1)S(1)}, bf16[112,2048]{1,0:T(8,128)(2,1)S(1)}, u32[]{:S(2)}, u32[]{:S(2)}) %collective-permute-start.8) | collective-permute-done | bytes 458784 | tf_op jit(solution)/shard_map/ppermute | solution.py:95
  47.0 3.2 %collective-permute-done.10.refs_4_ = bf16[112,2048]{1,0:T(8,128)(2,1)S(1)} collective-permute-done((bf16[112,2048]{1,0:T(8,128)(2,1)S(1)}, bf16[112,2048]{1,0:T(8,128)(2,1)S(1)}, u32[]{:S(2)}, u32[]{:S(2)}) %collective-permute-start.10) | collective-permute-done | bytes 458784 | tf_op jit(solution)/shard_map/ppermute | solution.py:95
  50.2 1.7 %collective-permute-done.11.refs_5_ = bf16[112,2048]{1,0:T(8,128)(2,1)S(1)} collective-permute-done((bf16[112,2048]{1,0:T(8,128)(2,1)S(1)}, bf16[112,2048]{1,0:T(8,128)(2,1)S(1)}, u32[]{:S(2)}, u32[]{:S(2)}) %collective-permute-start.11) | collective-permute-done | bytes 458784 | tf_op jit(solution)/shard_map/ppermute | solution.py:95
  51.9 2.4 %shard_map.39 = (f32[224,1024]{1,0:T(8,128)S(1)}, f32[224,1024]{1,0:T(8,128)S(1)}) custom-call(f32[1]{0:T(128)S(6)} %copy.4.spread_ref, bf16[256,2048]{1,0:T(8,128)(2,1)S(1)} %collective-permute-done.12.t_all, bf16[224,2048]{1,0:T(8,128)(2,1)S(1)} %bitcast.3, bf16[112,2048]{1,0:T(8,128)(2,1)S(1)} %collective-permute-done.6.refs_0_, ...), custom_call_target="tpu_custom_call" | custom-call | tf_op jit(solution)/shard_map/pallas_call | solution.py:145
  55.0 2.4 %shard_map.38 = (f32[224,1024]{1,0:T(8,128)S(1)}, f32[224,1024]{1,0:T(8,128)S(1)}) custom-call(f32[1]{0:T(128)S(6)} %copy.4.spread_ref, bf16[256,2048]{1,0:T(8,128)(2,1)S(1)} %shard_map.37.t_all, bf16[224,2048]{1,0:T(8,128)(2,1)S(1)} %bitcast.4, bf16[112,2048]{1,0:T(8,128)(2,1)S(1)} %collective-permute-done.6.refs_0_, ...), custom_call_target="tpu_custom_call" | custom-call | tf_op jit(solution)/shard_map/pallas_call | solution.py:145
  57.6 2.6 %collective-permute-start.19 = (f32[24,1024]{1,0:T(8,128)S(1)}, f32[24,1024]{1,0:T(8,128)S(1)}, u32[]{:S(2)}, u32[]{:S(2)}) collective-permute-start(f32[24,1024]{1,0:T(8,128)S(1)} %slice.100), channel_id=1, source_target_pairs={{0,224},{32,0},{64,32},{96,64},{128,96},{160,128},{192,160},{224,1... | collective-permute-start | bytes 294920 | tf_op jit(solution)/shard_map/ppermute | solution.py:99
  60.5 2.0 %collective-permute-done.19 = f32[24,1024]{1,0:T(8,128)S(1)} collective-permute-done((f32[24,1024]{1,0:T(8,128)S(1)}, f32[24,1024]{1,0:T(8,128)S(1)}, u32[]{:S(2)}, u32[]{:S(2)}) %collective-permute-start.19) | collective-permute-done | bytes 98336 | tf_op jit(solution)/shard_map/ppermute | solution.py:99
  62.5 3.8 %collective-permute-start.20 = (f32[56,1024]{1,0:T(8,128)S(1)}, f32[56,1024]{1,0:T(8,128)S(1)}, u32[]{:S(2)}, u32[]{:S(2)}) collective-permute-start(f32[56,1024]{1,0:T(8,128)S(1)} %pad_maximum_fusion.3), channel_id=1, source_target_pairs={{0,224},{32,0},{64,32},{96,64},{128,96},{160,128},{192,160},{224,1... | collective-permute-start | bytes 688136 | tf_op jit(solution)/shard_map/ppermute | solution.py:99
  66.3 0.6 collective-permute-done.15
  67.0 4.1 %collective-permute-done.20 = f32[56,1024]{1,0:T(8,128)S(1)} collective-permute-done((f32[56,1024]{1,0:T(8,128)S(1)}, f32[56,1024]{1,0:T(8,128)S(1)}, u32[]{:S(2)}, u32[]{:S(2)}) %collective-permute-start.20) | collective-permute-done | bytes 229408 | tf_op jit(solution)/shard_map/ppermute | solution.py:99
  71.1 3.3 %collective-permute-start.21 = (f32[56,1024]{1,0:T(8,128)S(1)}, f32[56,1024]{1,0:T(8,128)S(1)}, u32[]{:S(2)}, u32[]{:S(2)}) collective-permute-start(f32[56,1024]{1,0:T(8,128)S(1)} %slice_add_fusion), channel_id=1, source_target_pairs={{0,224},{32,0},{64,32},{96,64},{128,96},{160,128},{192,160},{224,1... | collective-permute-start | bytes 688136 | tf_op jit(solution)/shard_map/ppermute | solution.py:99
  74.8 3.1 %collective-permute-done.21 = f32[56,1024]{1,0:T(8,128)S(1)} collective-permute-done((f32[56,1024]{1,0:T(8,128)S(1)}, f32[56,1024]{1,0:T(8,128)S(1)}, u32[]{:S(2)}, u32[]{:S(2)}) %collective-permute-start.21) | collective-permute-done | bytes 229408 | tf_op jit(solution)/shard_map/ppermute | solution.py:99
  78.0 3.8 %collective-permute-start.22 = (f32[56,1024]{1,0:T(8,128)S(1)}, f32[56,1024]{1,0:T(8,128)S(1)}, u32[]{:S(2)}, u32[]{:S(2)}) collective-permute-start(f32[56,1024]{1,0:T(8,128)S(1)} %slice_add_fusion.1), channel_id=1, source_target_pairs={{0,224},{32,0},{64,32},{96,64},{128,96},{160,128},{192,160},{224,1... | collective-permute-start | bytes 688136 | tf_op jit(solution)/shard_map/ppermute | solution.py:99
  82.2 3.1 %collective-permute-done.22 = f32[56,1024]{1,0:T(8,128)S(1)} collective-permute-done((f32[56,1024]{1,0:T(8,128)S(1)}, f32[56,1024]{1,0:T(8,128)S(1)}, u32[]{:S(2)}, u32[]{:S(2)}) %collective-permute-start.22) | collective-permute-done | bytes 229408 | tf_op jit(solution)/shard_map/ppermute | solution.py:99
  85.3 4.1 %collective-permute-done.18 = f32[56,1024]{1,0:T(8,128)S(1)} collective-permute-done((f32[56,1024]{1,0:T(8,128)S(1)}, f32[56,1024]{1,0:T(8,128)S(1)}, u32[]{:S(2)}, u32[]{:S(2)}) %collective-permute-start.18) | collective-permute-done | bytes 229408 | tf_op jit(solution)/shard_map/ppermute | solution.py:99
  89.5 0.7 pad_maximum_fusion
  (46 shorter events, 2.9 us)
Async XLA Ops:
  2.1 4.4 %copy-start = (bf16[28,2048]{1,0:T(8,128)(2,1)S(1)}, bf16[28,2048]{1,0:T(8,128)(2,1)}, u32[]{:S(2)}) copy-start(bf16[28,2048]{1,0:T(8,128)(2,1)} %param.3) | copy-start | bytes 344068
  2.1 29.7 %all-to-all-start = ((bf16[4,56,2048]{2,1,0:T(8,128)(2,1)}), bf16[4,56,2048]{2,1,0:T(8,128)(2,1)S(1)}, u32[]{:S(2)}, u32[]{:S(2)}) async-start(bf16[4,56,2048]{2,1,0:T(8,128)(2,1)} %broadcast_in_dim.2), calls=%async_computation | async-start | bytes 1835008 | tf_op jit(solution)/shard_map/all_to_all | solution.py:40
  6.5 8.9 %collective-permute-start = (bf16[56,1024]{1,0:T(8,128)(2,1)S(1)}, bf16[56,1024]{1,0:T(8,128)(2,1)S(1)}, u32[]{:S(2)}, u32[]{:S(2)}) collective-permute-start(bf16[56,1024]{1,0:T(8,128)(2,1)S(1)} %pad_maximum_fusion.6.own_ref), channel_id=1, source_target_pairs={{0,32},{32,64},{64,96},{96,128},{128,160},{160,192},{192,224},{224... | collective-permute-start | bytes 344072 | tf_op jit(solution)/shard_map/ppermute | solution.py:99
  8.5 6.9 %collective-permute-start.1 = (bf16[56,1024]{1,0:T(8,128)(2,1)S(1)}, bf16[56,1024]{1,0:T(8,128)(2,1)S(1)}, u32[]{:S(2)}, u32[]{:S(2)}) collective-permute-start(bf16[56,1024]{1,0:T(8,128)(2,1)S(1)} %pad_maximum_fusion.6.own_ref), channel_id=1, source_target_pairs={{0,224},{32,0},{64,32},{96,64},{128,96},{160,128},{192,160},{224,1... | collective-permute-start | bytes 344072 | tf_op jit(solution)/shard_map/ppermute | solution.py:99
  15.4 6.0 %collective-permute-start.2 = (bf16[56,1024]{1,0:T(8,128)(2,1)S(1)}, bf16[56,1024]{1,0:T(8,128)(2,1)S(1)}, u32[]{:S(2)}, u32[]{:S(2)}) collective-permute-start(bf16[56,1024]{1,0:T(8,128)(2,1)S(1)} %collective-permute-done.up_ref), channel_id=1, source_target_pairs={{0,32},{32,64},{64,96},{96,128},{128,160},{160,192},{192,224},{224... | collective-permute-start | bytes 344072 | tf_op jit(solution)/shard_map/ppermute | solution.py:99
  15.4 6.1 %collective-permute-start.3 = (bf16[56,1024]{1,0:T(8,128)(2,1)S(1)}, bf16[56,1024]{1,0:T(8,128)(2,1)S(1)}, u32[]{:S(2)}, u32[]{:S(2)}) collective-permute-start(bf16[56,1024]{1,0:T(8,128)(2,1)S(1)} %collective-permute-done.1.down_ref), channel_id=1, source_target_pairs={{0,224},{32,0},{64,32},{96,64},{128,96},{160,128},{192,160},{224,1... | collective-permute-start | bytes 344072 | tf_op jit(solution)/shard_map/ppermute | solution.py:99
  21.5 10.1 %collective-permute-start.4 = (bf16[88,1024]{1,0:T(8,128)(2,1)S(1)}, bf16[88,1024]{1,0:T(8,128)(2,1)S(1)}, u32[]{:S(2)}, u32[]{:S(2)}) collective-permute-start(bf16[88,1024]{1,0:T(8,128)(2,1)S(1)} %pad_maximum_fusion.4), channel_id=1, source_target_pairs={{0,64},{32,96},{64,128},{96,160},{128,192},{160,224},{192,0},{224,... | collective-permute-start | bytes 540680 | tf_op jit(solution)/shard_map/ppermute | solution.py:99
  21.6 9.9 %collective-permute-start.5 = (bf16[80,1024]{1,0:T(8,128)(2,1)S(1)}, bf16[80,1024]{1,0:T(8,128)(2,1)S(1)}, u32[]{:S(2)}, u32[]{:S(2)}) collective-permute-start(bf16[80,1024]{1,0:T(8,128)(2,1)S(1)} %pad_maximum_fusion.5), channel_id=1, source_target_pairs={{0,192},{32,224},{64,0},{96,32},{128,64},{160,96},{192,128},{224,1... | collective-permute-start | bytes 491528 | tf_op jit(solution)/shard_map/ppermute | solution.py:99
  31.6 15.3 %collective-permute-start.12 = (bf16[256,2048]{1,0:T(8,128)(2,1)S(1)}, bf16[256,2048]{1,0:T(8,128)(2,1)S(1)}, u32[]{:S(2)}, u32[]{:S(2)}) collective-permute-start(bf16[256,2048]{1,0:T(8,128)(2,1)S(1)} %shard_map.37.t_all), channel_id=1, source_target_pairs={{0,2},{2,0},{1,3},{3,1},{4,6},{6,4},{5,7},{7,5},{8,10},{10,8},{9,1... | collective-permute-start | bytes 3145736 | tf_op jit(solution)/shard_map/ppermute | solution.py:168
  31.8 8.6 %collective-permute-start.6 = (bf16[112,2048]{1,0:T(8,128)(2,1)S(1)}, bf16[112,2048]{1,0:T(8,128)(2,1)S(1)}, u32[]{:S(2)}, u32[]{:S(2)}) collective-permute-start(bf16[112,2048]{1,0:T(8,128)(2,1)S(1)} %bitcast.7), channel_id=1, source_target_pairs={{0,4},{1,5},{2,10},{3,11},{4,1},{5,0},{6,14},{7,15},{8,12},{9,13},... | collective-permute-start | bytes 1376264 | tf_op jit(solution)/shard_map/ppermute | solution.py:95
  32.4 9.7 %collective-permute-start.9 = (bf16[112,2048]{1,0:T(8,128)(2,1)S(1)}, bf16[112,2048]{1,0:T(8,128)(2,1)S(1)}, u32[]{:S(2)}, u32[]{:S(2)}) collective-permute-start(bf16[112,2048]{1,0:T(8,128)(2,1)S(1)} %bitcast.5), channel_id=1, source_target_pairs={{0,5},{1,4},{2,26},{3,27},{4,0},{5,1},{6,30},{7,31},{8,13},{9,12},... | collective-permute-start | bytes 1376264 | tf_op jit(solution)/shard_map/ppermute | solution.py:95
  33.9 13.1 %collective-permute-start.8 = (bf16[112,2048]{1,0:T(8,128)(2,1)S(1)}, bf16[112,2048]{1,0:T(8,128)(2,1)S(1)}, u32[]{:S(2)}, u32[]{:S(2)}) collective-permute-start(bf16[112,2048]{1,0:T(8,128)(2,1)S(1)} %bitcast.8), channel_id=1, source_target_pairs={{0,5},{1,4},{2,26},{3,27},{4,0},{5,1},{6,30},{7,31},{8,13},{9,12},... | collective-permute-start | bytes 1376264 | tf_op jit(solution)/shard_map/ppermute | solution.py:95
  35.1 11.9 %collective-permute-start.7 = (bf16[112,2048]{1,0:T(8,128)(2,1)S(1)}, bf16[112,2048]{1,0:T(8,128)(2,1)S(1)}, u32[]{:S(2)}, u32[]{:S(2)}) collective-permute-start(bf16[112,2048]{1,0:T(8,128)(2,1)S(1)} %bitcast.6), channel_id=1, source_target_pairs={{0,4},{1,5},{2,10},{3,11},{4,1},{5,0},{6,14},{7,15},{8,12},{9,13},... | collective-permute-start | bytes 1376264 | tf_op jit(solution)/shard_map/ppermute | solution.py:95
  40.4 9.8 %collective-permute-start.10 = (bf16[112,2048]{1,0:T(8,128)(2,1)S(1)}, bf16[112,2048]{1,0:T(8,128)(2,1)S(1)}, u32[]{:S(2)}, u32[]{:S(2)}) collective-permute-start(bf16[112,2048]{1,0:T(8,128)(2,1)S(1)} %collective-permute-done.6.refs_0_), channel_id=1, source_target_pairs={{0,4},{1,5},{2,10},{3,11},{4,1},{5,0},{6,14},{7,15},{8,12},{9,13},... | collective-permute-start | bytes 1376264 | tf_op jit(solution)/shard_map/ppermute | solution.py:95
  42.1 9.8 %collective-permute-start.11 = (bf16[112,2048]{1,0:T(8,128)(2,1)S(1)}, bf16[112,2048]{1,0:T(8,128)(2,1)S(1)}, u32[]{:S(2)}, u32[]{:S(2)}) collective-permute-start(bf16[112,2048]{1,0:T(8,128)(2,1)S(1)} %collective-permute-done.9.refs_3_), channel_id=1, source_target_pairs={{0,5},{1,4},{2,26},{3,27},{4,0},{5,1},{6,30},{7,31},{8,13},{9,12},... | collective-permute-start | bytes 1376264 | tf_op jit(solution)/shard_map/ppermute | solution.py:95
  54.4 3.0 %collective-permute-start.14 = (f32[224,1024]{1,0:T(8,128)S(1)}, f32[224,1024]{1,0:T(8,128)S(1)}, u32[]{:S(2)}, u32[]{:S(2)}) collective-permute-start(f32[224,1024]{1,0:T(8,128)S(1)} %get-tuple-element.12), channel_id=1, source_target_pairs={{0,2},{2,0},{1,3},{3,1},{4,6},{6,4},{5,7},{7,5},{8,10},{10,8},{9,1... | collective-permute-start | bytes 2752520 | tf_op jit(solution)/shard_map/ppermute | solution.py:178
  54.6 5.6 %collective-permute-start.13 = (f32[224,1024]{1,0:T(8,128)S(1)}, f32[224,1024]{1,0:T(8,128)S(1)}, u32[]{:S(2)}, u32[]{:S(2)}) collective-permute-start(f32[224,1024]{1,0:T(8,128)S(1)} %get-tuple-element.10), channel_id=1, source_target_pairs={{0,2},{2,0},{1,3},{3,1},{4,6},{6,4},{5,7},{7,5},{8,10},{10,8},{9,1... | collective-permute-start | bytes 2752520 | tf_op jit(solution)/shard_map/ppermute | solution.py:179
  57.6 4.9 %collective-permute-start.19 = (f32[24,1024]{1,0:T(8,128)S(1)}, f32[24,1024]{1,0:T(8,128)S(1)}, u32[]{:S(2)}, u32[]{:S(2)}) collective-permute-start(f32[24,1024]{1,0:T(8,128)S(1)} %slice.100), channel_id=1, source_target_pairs={{0,224},{32,0},{64,32},{96,64},{128,96},{160,128},{192,160},{224,1... | collective-permute-start | bytes 294920 | tf_op jit(solution)/shard_map/ppermute | solution.py:99
  60.4 6.5 %collective-permute-start.15 = (f32[32,1024]{1,0:T(8,128)S(1)}, f32[32,1024]{1,0:T(8,128)S(1)}, u32[]{:S(2)}, u32[]{:S(2)}) collective-permute-start(f32[32,1024]{1,0:T(8,128)S(1)} %get-tuple-element.13), channel_id=1, source_target_pairs={{0,32},{32,64},{64,96},{96,128},{128,160},{160,192},{192,224},{224... | collective-permute-start | bytes 393224 | tf_op jit(solution)/shard_map/ppermute | solution.py:99
  62.5 8.6 %collective-permute-start.20 = (f32[56,1024]{1,0:T(8,128)S(1)}, f32[56,1024]{1,0:T(8,128)S(1)}, u32[]{:S(2)}, u32[]{:S(2)}) collective-permute-start(f32[56,1024]{1,0:T(8,128)S(1)} %pad_maximum_fusion.3), channel_id=1, source_target_pairs={{0,224},{32,0},{64,32},{96,64},{128,96},{160,128},{192,160},{224,1... | collective-permute-start | bytes 688136 | tf_op jit(solution)/shard_map/ppermute | solution.py:99
  66.9 7.8 %collective-permute-start.16 = (f32[56,1024]{1,0:T(8,128)S(1)}, f32[56,1024]{1,0:T(8,128)S(1)}, u32[]{:S(2)}, u32[]{:S(2)}) collective-permute-start(f32[56,1024]{1,0:T(8,128)S(1)} %pad_maximum_fusion.2), channel_id=1, source_target_pairs={{0,32},{32,64},{64,96},{96,128},{128,160},{160,192},{192,224},{224... | collective-permute-start | bytes 688136 | tf_op jit(solution)/shard_map/ppermute | solution.py:99
  71.1 6.8 %collective-permute-start.21 = (f32[56,1024]{1,0:T(8,128)S(1)}, f32[56,1024]{1,0:T(8,128)S(1)}, u32[]{:S(2)}, u32[]{:S(2)}) collective-permute-start(f32[56,1024]{1,0:T(8,128)S(1)} %slice_add_fusion), channel_id=1, source_target_pairs={{0,224},{32,0},{64,32},{96,64},{128,96},{160,128},{192,160},{224,1... | collective-permute-start | bytes 688136 | tf_op jit(solution)/shard_map/ppermute | solution.py:99
  74.7 7.3 %collective-permute-start.17 = (f32[56,1024]{1,0:T(8,128)S(1)}, f32[56,1024]{1,0:T(8,128)S(1)}, u32[]{:S(2)}, u32[]{:S(2)}) collective-permute-start(f32[56,1024]{1,0:T(8,128)S(1)} %slice_add_fusion.2), channel_id=1, source_target_pairs={{0,32},{32,64},{64,96},{96,128},{128,160},{160,192},{192,224},{224... | collective-permute-start | bytes 688136 | tf_op jit(solution)/shard_map/ppermute | solution.py:99
  78.0 7.3 %collective-permute-start.22 = (f32[56,1024]{1,0:T(8,128)S(1)}, f32[56,1024]{1,0:T(8,128)S(1)}, u32[]{:S(2)}, u32[]{:S(2)}) collective-permute-start(f32[56,1024]{1,0:T(8,128)S(1)} %slice_add_fusion.1), channel_id=1, source_target_pairs={{0,224},{32,0},{64,32},{96,64},{128,96},{160,128},{192,160},{224,1... | collective-permute-start | bytes 688136 | tf_op jit(solution)/shard_map/ppermute | solution.py:99
  82.1 7.3 %collective-permute-start.18 = (f32[56,1024]{1,0:T(8,128)S(1)}, f32[56,1024]{1,0:T(8,128)S(1)}, u32[]{:S(2)}, u32[]{:S(2)}) collective-permute-start(f32[56,1024]{1,0:T(8,128)S(1)} %slice_add_fusion.3), channel_id=1, source_target_pairs={{0,32},{32,64},{64,96},{96,128},{128,160},{160,192},{192,224},{224... | collective-permute-start | bytes 688136 | tf_op jit(solution)/shard_map/ppermute | solution.py:99
